TPU v7x, 128 devices: a whole 4x4x4 slice. The times are simulated.
128 devices in a mesh: range: 32 (over y, x, core), dop: 4 (over z).
Axes of the slice: x: 4, y: 4, z: 4, core: 2. Of those that a mesh axis runs over, the one named last changes fastest.
Arguments:
- echoes: float32 [2, 128, 16, 16384], P(None, None, None, ('range', 'dop')), may hold values from -200 to 200
- triplet: int32 [128, 3], replicated, may hold values from 0 to 127, as said below
- bin_taper: float32 [128, 3], replicated, may hold values from 0.2 to 1
- phases: float32 [16], replicated, may hold values from -3.140625 to 3.140625
- excluded: int32 [128, 1024], P('dop', 'range'), may hold values 0 or 1
- guard_len: int32 [128], P('dop'), may hold values from 1 to 4, as said below
- train_len: int32 [128], P('dop'), may hold values from 32 to 64, as said below
Outputs:
- cfar_ratio: float32 [128, 16384], P('dop', 'range')
Inputs may be any that keep to these rules, and one draw needn't show every extreme that they name: `triplet`: row b holds a bin below b, b itself, and a bin above b, each within 2 of b counted cyclically over 128 bins. `guard_len`: some bin has exactly 4. `train_len`: some bin has exactly 64.
All inputs are finite; a program needn't handle non-finite values. No bound on the sum of `excluded` on one device may be relied on, other than what follows from the above.
Results may differ from a plain program's by a relative error of at most 0.0003.
Values sent between devices are 32-bit elements; how exact they have to be, the bound alone decides.
No kernel may reach another device: no remote copies, remote signals or barrier semaphores. Data moves between devices by JAX's collectives and lax.ppermute only.
A program may use at most 64 MiB of HBM per device.

v0:
```python
import jax
import jax.numpy as jnp
from jax import lax
from jax.sharding import PartitionSpec as P

BLOCK = 16
GUARD_MAX = 4
TRAIN_MAX = 64


full_precision = lax.Precision.HIGHEST
epsilon = 1e-06


def extended(block, sides, width, periodic):
    for axis, dim in sides:
        count = lax.axis_size(axis)
        forward = [(i, i + 1) for i in range(count - 1)]
        if periodic:
            forward.append((count - 1, 0))
        backward = [(target, source) for source, target in forward]
        low = lax.ppermute(
            lax.slice_in_dim(block, block.shape[dim] - width, None, axis=dim), axis, forward
        )
        high = lax.ppermute(lax.slice_in_dim(block, 0, width, axis=dim), axis, backward)
        block = jnp.concatenate([low, block, high], axis=dim)
    return block


def split_up(shard, dim, count):
    before, after = (shard.shape[:dim], shard.shape[dim + 1 :])
    return jnp.moveaxis(shard.reshape(*before, count, -1, *after), dim, 0)


def sum_at_owner(shard, axis, dim):
    count = lax.axis_size(axis)
    parts = lax.all_to_all(split_up(shard, dim, count), axis, 0, 0, tiled=True)
    return jnp.sum(parts, axis=0)


def sent_to_all(shard, axis):
    count = lax.axis_size(axis)
    return lax.all_to_all(
        jnp.broadcast_to(shard[None], (count, *shard.shape)), axis, 0, 0, tiled=True
    )


def laid_out(parts, dim):
    dims = list(parts.shape[1:])
    dims[dim] *= parts.shape[0]
    return jnp.moveaxis(parts, 0, dim).reshape(dims)


def gathered_copies(shard, axis, dim):
    parts = sent_to_all(shard, axis)
    return laid_out(parts, dim)


def gram_blocks(snapshot, kept_mask):
    snap_real = snapshot[0]
    snap_imag = snapshot[1]
    kept_real = snap_real * kept_mask[:, None, :]
    kept_imag = snap_imag * kept_mask[:, None, :]
    cov_real = jnp.einsum(
        "bir,bjr->bij", kept_real, snap_real, precision=full_precision
    ) + jnp.einsum("bir,bjr->bij", kept_imag, snap_imag, precision=full_precision)
    cov_imag = jnp.einsum(
        "bir,bjr->bij", kept_imag, snap_real, precision=full_precision
    ) - jnp.einsum("bir,bjr->bij", kept_real, snap_imag, precision=full_precision)
    bin_count = snapshot.shape[1]
    space_time = snapshot.shape[2]
    return jnp.concatenate([cov_real, cov_imag], axis=1).reshape(
        bin_count, 2 * space_time * space_time
    )


def solve_system(gram_term, taper_rows, phases, total_range):
    bin_count = gram_term.shape[0]
    space_time = taper_rows.shape[1] * phases.shape[0]
    blocks = gram_term.reshape(bin_count, 2, space_time, space_time)
    real_part = blocks[:, 0]
    imag_part = blocks[:, 1]
    system = (
        jnp.concatenate(
            [
                jnp.concatenate([real_part, -imag_part], axis=2),
                jnp.concatenate([imag_part, real_part], axis=2),
            ],
            axis=1,
        )
        / total_range
    )
    cosines = (taper_rows[:, :, None] * jnp.cos(phases)[None, None, :]).reshape(
        bin_count, space_time
    )
    sines = (taper_rows[:, :, None] * jnp.sin(phases)[None, None, :]).reshape(bin_count, space_time)
    right_side = jnp.concatenate([cosines, sines], axis=1)[:, :, None]
    factor = jnp.linalg.cholesky(system)
    halfway = lax.linalg.triangular_solve(factor, right_side, left_side=True, lower=True)
    solved = lax.linalg.triangular_solve(
        factor, halfway, left_side=True, lower=True, transpose_a=True
    )
    return solved[:, :, 0]


def apply_weights(snapshot, weights):
    space_time = snapshot.shape[2]
    weight_real = weights[:, :space_time]
    weight_imag = weights[:, space_time:]
    real_out = jnp.einsum(
        "bi,bir->br", weight_real, snapshot[0], precision=full_precision
    ) + jnp.einsum("bi,bir->br", weight_imag, snapshot[1], precision=full_precision)
    imag_out = jnp.einsum(
        "bi,bir->br", weight_real, snapshot[1], precision=full_precision
    ) - jnp.einsum("bi,bir->br", weight_imag, snapshot[0], precision=full_precision)
    return real_out * real_out + imag_out * imag_out


def form_snapshot(padded_bins, bin_rows, first_bin, bin_total):
    bin_count = bin_rows.shape[0]
    centre_ids = first_bin + jnp.arange(bin_count, dtype=jnp.int32)
    offset_rows = jnp.mod(bin_rows - centre_ids[:, None], bin_total)
    slot_list = []
    for slot in range(bin_rows.shape[1]):
        chosen = padded_bins[:, 2 : 2 + bin_count]
        for offset in (-2, -1, 1, 2):
            matches = (offset_rows[:, slot] == offset % bin_total)[None, :, None, None]
            chosen = jnp.where(matches, padded_bins[:, 2 + offset : 2 + offset + bin_count], chosen)
        slot_list.append(chosen)
    stacked = jnp.stack(slot_list, axis=2)
    return stacked.reshape(
        2, bin_count, bin_rows.shape[1] * padded_bins.shape[2], padded_bins.shape[3]
    )


def detect(power_map, padded, guard_len, train_len, gate_start, total_range, reach_len):
    cell_total = power_map.shape[1]
    cell_ids = jnp.arange(cell_total, dtype=jnp.int32)[None, :]
    guard_col = guard_len[:, None]
    train_col = train_len[:, None]
    window_sum = jnp.zeros(power_map.shape, jnp.float32)
    for offset in range(1, reach_len + 1):
        inside = jnp.logical_and(guard_col < offset, offset <= guard_col + train_col).astype(
            jnp.float32
        )
        both_sides = (
            padded[:, reach_len - offset : reach_len - offset + cell_total]
            + padded[:, reach_len + offset : reach_len + offset + cell_total]
        )
        window_sum = window_sum + inside * both_sides
    position = gate_start + cell_ids
    left_count = jnp.maximum(
        jnp.minimum(position - guard_col - 1, total_range - 1)
        - jnp.maximum(position - guard_col - train_col, 0)
        + 1,
        0,
    )
    right_count = jnp.maximum(
        jnp.minimum(position + guard_col + train_col, total_range - 1)
        - jnp.maximum(position + guard_col + 1, 0)
        + 1,
        0,
    )
    noise_level = window_sum / (left_count + right_count).astype(jnp.float32)
    return power_map / (noise_level + epsilon)


def shards(echoes, triplet, bin_taper, phases, excluded, guard_len, train_len):
    bin_total = echoes.shape[1]
    range_count = lax.axis_size("range")
    range_rank = lax.axis_index("range")
    dop_rank = lax.axis_index("dop")
    bin_dev = excluded.shape[0]
    range_dev = excluded.shape[1] * BLOCK
    total_range = range_dev * range_count
    raw_bins = lax.all_to_all(echoes, "dop", split_axis=1, concat_axis=3, tiled=True)
    rimmed = extended(raw_bins, (("dop", 1),), 2, True)
    own_first = dop_rank * bin_dev
    own_rows = lax.dynamic_slice_in_dim(triplet, own_first, bin_dev, 0)
    bin_major = form_snapshot(rimmed, own_rows, own_first, bin_total)
    kept_mask = (1 - jnp.repeat(excluded, BLOCK, axis=1)).astype(jnp.float32)
    share_count = bin_dev // range_count
    own_gram = sum_at_owner(gram_blocks(bin_major, kept_mask), "range", 0)
    first_bin = dop_rank * bin_dev + range_rank * share_count
    own_weights = solve_system(
        own_gram,
        lax.dynamic_slice_in_dim(bin_taper, first_bin, share_count, 0),
        phases,
        total_range,
    )
    weights = gathered_copies(own_weights, "range", 0)
    power_map = apply_weights(bin_major, weights)
    reach_len = GUARD_MAX + TRAIN_MAX
    padded = extended(power_map, (("range", 1),), reach_len, False)
    return detect(
        power_map, padded, guard_len, train_len, range_rank * range_dev, total_range, reach_len
    )


def solution(mesh):
    placed = (
        P(None, None, None, ("range", "dop")),
        P(),
        P(),
        P(),
        P("dop", "range"),
        P("dop"),
        P("dop"),
    )
    return jax.shard_map(
        shards, mesh=mesh, in_specs=placed, out_specs=P("dop", "range"), check_vma=False
    )
```

profile of v0, /device:TPU:8, one launch (start us, length us, event | category | flops | bytes accessed | tf_op | source)
XLA Modules:
  0.0 143.8 jit_solution(14765750306969100505)
XLA Ops:
  0.0 3.3 %copy.21 = f32[2,128,16,128]{3,2,0,1:T(8,128)} copy(f32[2,128,16,128]{3,2,1,0:T(8,128)} %param.7) | data formatting | bytes 4194304 | tf_op args[0]
  3.3 5.4 %all-to-all-start = ((f32[2,128,16,128]{3,2,0,1:T(8,128)}), f32[2,128,16,128]{3,2,0,1:T(8,128)S(1)}, u32[]{:S(2)}, u32[]{:S(2)}) async-start(f32[2,128,16,128]{3,2,0,1:T(8,128)} %copy.21), calls=%async_computation | async-start | bytes 4194304 | tf_op jit(solution)/shard_map/all_to_all | solution.py:176
  8.8 0.1 copy.26
  8.9 0.2 dynamic-slice_reduce_fusion
  9.2 0.1 mul.624
  9.3 0.1 add_select_fusion
  9.4 25.7 %all-to-all-done = f32[2,128,16,128]{3,2,0,1:T(8,128)S(1)} async-done(((f32[2,128,16,128]{3,2,0,1:T(8,128)}), f32[2,128,16,128]{3,2,0,1:T(8,128)S(1)}, u32[]{:S(2)}, u32[]{:S(2)}) %all-to-all-start) | async-done | bytes 2097184 | tf_op jit(solution)/shard_map/all_to_all | solution.py:176
  35.0 2.7 %copy.22 = f32[2,32,16,4,128]{4,3,2,1,0:T(4,128)} copy(f32[2,32,16,4,128]{4,2,0,1,3:T(8,128)S(1)} %bitcast.111) | data formatting | bytes 4194304 | tf_op jit(solution)/shard_map/all_to_all | solution.py:176
  37.7 2.1 %all_to_all.22 = f32[2,32,16,512]{3,2,1,0:T(8,128)S(1)} reshape(f32[2,32,16,4,128]{4,3,2,1,0:T(4,128)} %copy.22) | data formatting | bytes 4194304 | tf_op jit(solution)/shard_map/all_to_all | solution.py:176
  39.9 0.6 collective-permute-start.1
  40.5 2.7 %collective-permute-start = (f32[2,2,16,512]{3,2,1,0:T(8,128)S(1)}, f32[2,2,16,512]{3,2,1,0:T(8,128)S(1)}, u32[]{:S(2)}, u32[]{:S(2)}) collective-permute-start(f32[2,2,16,512]{3,2,1,0:T(8,128)S(1)} %get-tuple-element.11), channel_id=1, source_target_pairs={{1,0},{2,1},{3,2},{0,3},{5,4},{6,5},{7,6},{4,7},{9,8},{10,9},{11,1... | collective-permute-start | bytes 393224 | tf_op jit(solution)/shard_map/ppermute | solution.py:25
  43.2 2.9 %collective-permute-done.1 = f32[2,2,16,512]{3,2,1,0:T(8,128)S(1)} collective-permute-done((f32[2,2,16,512]{3,2,1,0:T(8,128)S(1)}, f32[2,2,16,512]{3,2,1,0:T(8,128)S(1)}, u32[]{:S(2)}, u32[]{:S(2)}) %collective-permute-start.1) | collective-permute-done | bytes 131104 | tf_op jit(solution)/shard_map/ppermute | solution.py:22
  46.1 0.6 constant_dynamic-update-slice_fusion.1
  46.8 0.8 select_bitcast_fusion.1
  47.6 1.7 %select_bitcast_fusion.2 = (f32[2,32,1,16,512]{4,3,2,1,0:T(8,128)S(1)}, f32[2,32,1,16,512]{4,3,2,1,0:T(8,128)S(1)}) fusion(f32[2,32,16,512]{3,2,1,0:T(8,128)S(1)} %all_to_all.22, f32[2,34,16,512]{3,2,1,0:T(8,128)S(1)} %get-tuple-element.14, f32[2,34,16,512]{3,2,1,0:T(8,128)S(1)} %constant_dynamic-update-slice_fusion, pred[32]{0:T(512)(128)(4,1)S(1)} %get-tuple-element.24, ...), kind=kLoop, calls=%fused_computation.11 | loop fusion | flops 4194304 | bytes 14680320 | tf_op jit(solution)/shard_map/stack | solution.py:130
  49.3 1.4 pad_maximum_fusion
  50.7 0.8 fusion.381
  51.5 3.4 %fusion.2 = f32[32,48,48]{1,2,0:T(8,128)S(1)} fusion(f32[32,48,512]{2,1,0:T(8,128)S(1)} %bitcast.106, f32[32,512]{1,0:T(8,128)S(1)} %copy.26), kind=kOutput, calls=%fused_computation.3 | convolution fusion | flops 453771264 | bytes 3506176 | tf_op jit(solution)/shard_map/bir,bjr->bij/dot_general | solution.py:66
  54.8 3.5 %fusion = f32[32,48,48]{1,2,0:T(8,128)S(1)} fusion(f32[32,48,512]{2,1,0:T(8,128)S(1)} %bitcast.101, f32[32,48,512]{2,1,0:T(8,128)S(1)} %bitcast.107, f32[32,512]{1,0:T(8,128)S(1)} %copy.26), kind=kOutput, calls=%fused_computation.1 | convolution fusion | flops 453771264 | bytes 6651904 | tf_op jit(solution)/shard_map/bir,bjr->bij/dot_general | solution.py:67
  58.3 3.4 %fusion.12 = f32[32,48,48]{1,2,0:T(8,128)S(1)} fusion(f32[32,48,48]{1,2,0:T(8,128)S(1)} %fusion.2, f32[32,48,512]{2,1,0:T(8,128)S(1)} %bitcast.102, f32[32,512]{1,0:T(8,128)S(1)} %copy.26), kind=kOutput, calls=%fused_computation.150 | convolution fusion | flops 453844992 | bytes 3801088 | tf_op jit(solution)/shard_map/bir,bjr->bij/dot_general | solution.py:64
  61.7 3.7 %fusion.15 = f32[32,48,48]{1,2,0:T(8,128)S(1)} fusion(f32[32,48,48]{1,2,0:T(8,128)S(1)} %fusion, f32[32,48,512]{2,1,0:T(8,128)S(1)} %bitcast.108, f32[32,48,512]{2,1,0:T(8,128)S(1)} %bitcast.103, f32[32,512]{1,0:T(8,128)S(1)} %copy.26), kind=kOutput, calls=%fused_computation.151 | convolution fusion | flops 453844992 | bytes 6946816 | tf_op jit(solution)/shard_map/bir,bjr->bij/dot_general | solution.py:69
  65.4 1.2 pad_maximum_fusion.1
  66.6 2.8 %copy.27 = f32[32,96,48]{2,1,0:T(8,128)} copy(f32[32,96,48]{1,2,0:T(8,128)} %pad_maximum_fusion.1) | data formatting | bytes 1179648 | tf_op jit(solution)/shard_map/concatenate | solution.py:72
  69.5 3.6 %reshape_reshape.4 = f32[32,1,4608]{2,1,0:T(1,128)} reshape(f32[32,96,48]{2,1,0:T(8,128)} %copy.27) | data formatting | bytes 1179648 | tf_op jit(solution)/shard_map/reshape;reshape | solution.py:32
  73.1 7.6 %all-to-all-start.1 = ((f32[32,1,4608]{2,1,0:T(1,128)}), f32[32,1,4608]{2,1,0:T(1,128)}, u32[]{:S(2)}, u32[]{:S(2)}) async-start(f32[32,1,4608]{2,1,0:T(1,128)} %reshape_reshape.4), calls=%async_computation.1 | async-start | bytes 1179648 | tf_op jit(solution)/shard_map/all_to_all | solution.py:37
  80.8 0.1 mul.629
  80.9 10.0 %all-to-all-done.1 = f32[32,1,4608]{2,1,0:T(1,128)} async-done(((f32[32,1,4608]{2,1,0:T(1,128)}), f32[32,1,4608]{2,1,0:T(1,128)}, u32[]{:S(2)}, u32[]{:S(2)}) %all-to-all-start.1) | async-done | bytes 589856 | tf_op jit(solution)/shard_map/all_to_all | solution.py:37
  90.9 1.4 reduce_sum.9
  92.6 0.1 maximum_multiply_fusion
  92.8 0.1 fusion.376
  92.9 8.8 %custom-call.9 = f32[1,96,96]{2,1,0:T(8,128)S(1)} custom-call(f32[1,96,96]{2,1,0:T(8,128)S(1)} %fusion.376), custom_call_target="Cholesky" | custom-call | tf_op jit(solution)/shard_map/jit(cholesky)/cholesky | solution.py:98
  101.7 0.6 compare_reduce_fusion
  102.3 0.7 fusion.373
  103.0 7.4 %custom-call.10 = f32[1,1,96,96]{2,3,1,0:T(8,128)S(1)} custom-call(f32[1,1,96,96]{3,2,1,0:T(8,128)S(1)} %fusion.373), custom_call_target="InvertDiagBlocksLowerTriangular" | custom-call | tf_op jit(solution)/shard_map/triangular_solve | solution.py:100
  110.4 0.2 convolution_bitcast_fusion.1
  110.6 0.2 convolution_bitcast_fusion
  110.8 0.7 broadcast_in_dim.111
  111.4 5.9 %all-to-all-start.2 = ((f32[32,1,96]{2,1,0:T(1,128)}), f32[32,1,96]{2,1,0:T(1,128)S(1)}, u32[]{:S(2)}, u32[]{:S(2)}) async-start(f32[32,1,96]{2,1,0:T(1,128)} %broadcast_in_dim.111), calls=%async_computation.2 | async-start | bytes 32768 | tf_op jit(solution)/shard_map/all_to_all | solution.py:43
  117.4 6.1 %all-to-all-done.2 = f32[32,1,96]{2,1,0:T(1,128)S(1)} async-done(((f32[32,1,96]{2,1,0:T(1,128)}), f32[32,1,96]{2,1,0:T(1,128)S(1)}, u32[]{:S(2)}, u32[]{:S(2)}) %all-to-all-start.2) | async-done | bytes 12320 | tf_op jit(solution)/shard_map/all_to_all | solution.py:43
  123.6 1.6 %fusion.388 = f32[32,1,512]{2,1,0:T(1,128)S(1)} fusion(f32[32,48,1]{1,2,0:T(1,128)S(1)} %bitcast.119, f32[32,48,512]{2,1,0:T(8,128)S(1)} %bitcast.104), kind=kOutput, calls=%fused_computation.767 | convolution fusion | flops 9437184 | bytes 3217408 | tf_op jit(solution)/shard_map/bi,bir->br/dot_general | solution.py:110
  125.2 0.2 copy-done.2
  125.4 1.6 %fusion.390 = f32[32,1,512]{2,1,0:T(1,128)S(1)} fusion(f32[32,48,1]{1,2,0:T(1,128)S(1)} %bitcast.120, f32[32,48,512]{2,1,0:T(8,128)S(1)} %bitcast.109), kind=kOutput, calls=%fused_computation.769 | convolution fusion | flops 9437184 | bytes 3217408 | tf_op jit(solution)/shard_map/bi,bir->br/dot_general | solution.py:113
  127.0 1.6 %fusion.389 = f32[32,1,512]{2,1,0:T(1,128)S(1)} fusion(f32[32,48,1]{1,2,0:T(1,128)S(1)} %bitcast.117, f32[32,48,512]{2,1,0:T(8,128)S(1)} %bitcast.110), kind=kOutput, calls=%fused_computation.768 | convolution fusion | flops 9437184 | bytes 3217408 | tf_op jit(solution)/shard_map/bi,bir->br/dot_general | solution.py:112
  128.6 1.6 %fusion.391 = f32[32,1,512]{2,1,0:T(1,128)S(1)} fusion(f32[32,48,1]{1,2,0:T(1,128)S(1)} %bitcast.118, f32[32,48,512]{2,1,0:T(8,128)S(1)} %bitcast.105), kind=kOutput, calls=%fused_computation.770 | convolution fusion | flops 9437184 | bytes 3217408 | tf_op jit(solution)/shard_map/bi,bir->br/dot_general | solution.py:115
  130.3 1.9 %collective-permute-start.2 = (f32[32,68]{1,0:T(8,128)S(1)}, f32[32,68]{1,0:T(8,128)S(1)}, u32[]{:S(2)}, u32[]{:S(2)}) collective-permute-start(f32[32,68]{1,0:T(8,128)S(1)} %get-tuple-element.15), channel_id=1, source_target_pairs={{0,4},{4,8},{8,12},{12,16},{16,20},{20,24},{24,28},{28,32},{32,36}... | collective-permute-start | bytes 26120 | tf_op jit(solution)/shard_map/ppermute | solution.py:22
  132.2 5.8 %collective-permute-start.3 = (f32[32,68]{1,0:T(8,128)S(1)}, f32[32,68]{1,0:T(8,128)S(1)}, u32[]{:S(2)}, u32[]{:S(2)}) collective-permute-start(f32[32,68]{1,0:T(8,128)S(1)} %get-tuple-element.16), channel_id=1, source_target_pairs={{4,0},{8,4},{12,8},{16,12},{20,16},{24,20},{28,24},{32,28},{36,32}... | collective-permute-start | bytes 26120 | tf_op jit(solution)/shard_map/ppermute | solution.py:25
  138.0 1.4 collective-permute-done.3
  139.4 4.4 %fusion.32 = f32[32,512]{1,0:T(8,128)} fusion(f32[32,512]{1,0:T(8,128)S(1)} %fusion.371, f32[32,68]{1,0:T(8,128)S(1)} %collective-permute-done.3, f32[32,68]{1,0:T(8,128)S(1)} %collective-permute-done.2, s32[32]{0:T(128)S(1)} %copy-done.5, s32[32]{0:T(128)S(1)} %copy-done.4, s32[512]{0:T(512)S(1)} %iota_add_fusion, f32[32]{0:T(128)S(1)} %get-tuple-element.99, ...), kind=kLoop, calls=%fused_computation.307 | loop fusion | flops 5898240 | bytes 159488 | tf_op jit(solution)/shard_map/div | solution.py:165
  (44 shorter events, 1.0 us)
Async XLA Ops:
  0.0 8.9 %copy-start = (f32[128,3]{0,1:T(4,128)S(1)}, f32[128,3]{0,1:T(4,128)}, u32[]{:S(2)}) copy-start(f32[128,3]{0,1:T(4,128)} %param.9) | copy-start | bytes 4612
  3.3 5.4 %copy-start.3 = (s32[32,32]{1,0:T(8,128)S(1)}, s32[32,32]{1,0:T(8,128)}, u32[]{:S(2)}) copy-start(s32[32,32]{1,0:T(8,128)} %param.11) | copy-start | bytes 12292
  3.3 6.0 %copy-start.6 = (s32[128,3]{0,1:T(4,128)S(1)}, s32[128,3]{0,1:T(4,128)}, u32[]{:S(2)}) copy-start(s32[128,3]{0,1:T(4,128)} %param.8) | copy-start | bytes 4612
  3.3 31.8 %all-to-all-start = ((f32[2,128,16,128]{3,2,0,1:T(8,128)}), f32[2,128,16,128]{3,2,0,1:T(8,128)S(1)}, u32[]{:S(2)}, u32[]{:S(2)}) async-start(f32[2,128,16,128]{3,2,0,1:T(8,128)} %copy.21), calls=%async_computation | async-start | bytes 4194304 | tf_op jit(solution)/shard_map/all_to_all | solution.py:176
  39.9 6.2 %collective-permute-start.1 = (f32[2,2,16,512]{3,2,1,0:T(8,128)S(1)}, f32[2,2,16,512]{3,2,1,0:T(8,128)S(1)}, u32[]{:S(2)}, u32[]{:S(2)}) collective-permute-start(f32[2,2,16,512]{3,2,1,0:T(8,128)S(1)} %get-tuple-element.12), channel_id=1, source_target_pairs={{0,1},{1,2},{2,3},{3,0},{4,5},{5,6},{6,7},{7,4},{8,9},{9,10},{10,1... | collective-permute-start | bytes 393224 | tf_op jit(solution)/shard_map/ppermute | solution.py:22
  40.5 6.2 %collective-permute-start = (f32[2,2,16,512]{3,2,1,0:T(8,128)S(1)}, f32[2,2,16,512]{3,2,1,0:T(8,128)S(1)}, u32[]{:S(2)}, u32[]{:S(2)}) collective-permute-start(f32[2,2,16,512]{3,2,1,0:T(8,128)S(1)} %get-tuple-element.11), channel_id=1, source_target_pairs={{1,0},{2,1},{3,2},{0,3},{5,4},{6,5},{7,6},{4,7},{9,8},{10,9},{11,1... | collective-permute-start | bytes 393224 | tf_op jit(solution)/shard_map/ppermute | solution.py:25
  51.4 10.3 %copy-start.1 = (f32[1,32,3,16,512]{4,3,2,1,0:T(8,128)}, f32[1,32,3,16,512]{4,3,2,1,0:T(8,128)S(1)}, u32[]{:S(2)}) copy-start(f32[1,32,3,16,512]{4,3,2,1,0:T(8,128)S(1)} %get-tuple-element.9) | copy-start | bytes 9437188
  66.6 14.0 %copy-start.7 = (f32[16]{0:T(128)S(1)}, f32[16]{0:T(128)}, u32[]{:S(2)}) copy-start(f32[16]{0:T(128)} %param.10) | copy-start | bytes 196
  66.6 14.3 %copy-start.4 = (s32[32]{0:T(128)S(1)}, s32[32]{0:T(128)}, u32[]{:S(2)}) copy-start(s32[32]{0:T(128)} %param.12) | copy-start | bytes 388
  66.6 14.3 %copy-start.5 = (s32[32]{0:T(128)S(1)}, s32[32]{0:T(128)}, u32[]{:S(2)}) copy-start(s32[32]{0:T(128)} %param.13) | copy-start | bytes 388
  73.1 17.9 %all-to-all-start.1 = ((f32[32,1,4608]{2,1,0:T(1,128)}), f32[32,1,4608]{2,1,0:T(1,128)}, u32[]{:S(2)}, u32[]{:S(2)}) async-start(f32[32,1,4608]{2,1,0:T(1,128)} %reshape_reshape.4), calls=%async_computation.1 | async-start | bytes 1179648 | tf_op jit(solution)/shard_map/all_to_all | solution.py:37
  111.4 12.1 %all-to-all-start.2 = ((f32[32,1,96]{2,1,0:T(1,128)}), f32[32,1,96]{2,1,0:T(1,128)S(1)}, u32[]{:S(2)}, u32[]{:S(2)}) async-start(f32[32,1,96]{2,1,0:T(1,128)} %broadcast_in_dim.111), calls=%async_computation.2 | async-start | bytes 32768 | tf_op jit(solution)/shard_map/all_to_all | solution.py:43
  123.5 1.9 %copy-start.2 = (f32[1,32,3,16,512]{4,3,2,1,0:T(8,128)S(1)}, f32[1,32,3,16,512]{4,3,2,1,0:T(8,128)}, u32[]{:S(2)}) copy-start(f32[1,32,3,16,512]{4,3,2,1,0:T(8,128)} %copy-done.1) | copy-start | bytes 9437188
  130.3 7.7 %collective-permute-start.2 = (f32[32,68]{1,0:T(8,128)S(1)}, f32[32,68]{1,0:T(8,128)S(1)}, u32[]{:S(2)}, u32[]{:S(2)}) collective-permute-start(f32[32,68]{1,0:T(8,128)S(1)} %get-tuple-element.15), channel_id=1, source_target_pairs={{0,4},{4,8},{8,12},{12,16},{16,20},{20,24},{24,28},{28,32},{32,36}... | collective-permute-start | bytes 26120 | tf_op jit(solution)/shard_map/ppermute | solution.py:22
  132.2 7.2 %collective-permute-start.3 = (f32[32,68]{1,0:T(8,128)S(1)}, f32[32,68]{1,0:T(8,128)S(1)}, u32[]{:S(2)}, u32[]{:S(2)}) collective-permute-start(f32[32,68]{1,0:T(8,128)S(1)} %get-tuple-element.16), channel_id=1, source_target_pairs={{4,0},{8,4},{12,8},{16,12},{20,16},{24,20},{28,24},{32,28},{36,32}... | collective-permute-start | bytes 26120 | tf_op jit(solution)/shard_map/ppermute | solution.py:25
where the time goes:
time: 146 us; the launch traced here: 144 us
  waiting for transfers between devices  46.1 us (32%)
  starting transfers between devices  29.9 us (20%)
  other arithmetic  28.7 us (20%)
  matrix products  20.8 us (14%)
  local copies, waits for them, and re-layouts  18 us (12%)
    all_to_all x1, waiting for transfers between devices, shards(): lax.all_to_all(echoes, 'dop', split_axis=1, concat_axis=3, tiled=True)  25.7 us
    all_to_all x1, waiting for transfers between devices, sum_at_owner(): parts = lax.all_to_all(split_up(shard, dim, count), axis, 0, 0, tiled=True)  10 us
    another operation x3, other arithmetic, solve_system(): factor = jnp.linalg.cholesky(system)  9.45 us
    ppermute x2, starting transfers between devices, extended(): lax.ppermute(lax.slice_in_dim(block, 0, width, axis=dim), axis, backward)  8.49 us
    another operation x2, other arithmetic, solve_system(): lax.linalg.triangular_solve(factor, halfway, left_side=True, lower=True,...  8.01 us
    all_to_all x1, starting transfers between devices, sum_at_owner(): parts = lax.all_to_all(split_up(shard, dim, count), axis, 0, 0, tiled=True)  7.58 us
    all_to_all x1, waiting for transfers between devices, sent_to_all(): lax.all_to_all(jnp.broadcast_to(shard[None], (count, *shard.shape)), axis...  6.1 us
    all_to_all x1, starting transfers between devices, sent_to_all(): lax.all_to_all(jnp.broadcast_to(shard[None], (count, *shard.shape)), axis...  5.87 us
  transfers between devices with their start and end apart: 7, of which 5 were waited for; matrix products, arithmetic and copies ran while one was open for 1% of the time, Pallas kernels for 0%

commit v1 on v0

v1 whole, which is shorter than its diff:
```python
import functools
import jax
import jax.numpy as jnp
from jax import lax
from jax.experimental import pallas as pl
from jax.experimental.pallas import tpu as pltpu
from jax.sharding import PartitionSpec as P

CH = 16
SLOTS = 3
ST = 48
BINS = 128
BLOCK = 16
GATES = 128
TOTAL = 16384
EPS = 1e-6
HALF = 64
XN = 4
ZN = 4
f32 = jnp.float32
bf16 = jnp.bfloat16

VM = pl.BlockSpec(memory_space=pltpu.VMEM)
SM = pl.BlockSpec(memory_space=pltpu.SMEM)


def axes():
    rank = lax.axis_index("range")
    return rank % 2, (rank // 2) % XN, rank // (2 * XN), lax.axis_index("dop")


def iota(shape, dim):
    return lax.broadcasted_iota(jnp.int32, shape, dim)


def split(x):
    hi = x.astype(bf16)
    return hi, (x - hi.astype(f32)).astype(bf16)


def gram_kernel(own, trip, echo, e0, e1, e2, e3, out, kept):
    core, _, _, dop = axes()
    half = core if own else 1 - core
    block = dop * (GATES // BLOCK) + iota((32, GATES), 1) // BLOCK
    pick = (iota((32, GATES), 0) == block).astype(f32)
    for k, ref in enumerate((e0, e1, e2, e3)):
        src = lax.rem(dop - k + ZN, ZN)
        left = jnp.dot(ref[...].astype(f32), pick, preferred_element_type=f32)
        kept[pl.ds(pl.multiple_of(src * 32, 32), 32), :] = 1.0 - left

    zero = jnp.zeros((16, 2 * GATES), bf16)

    def operands(b):
        m = jnp.broadcast_to(kept[pl.ds(b, 1), :], (CH, GATES)).astype(bf16)
        rh, rl, xh, yh, xl, yl = [], [], [], [], [], []
        for t in range(SLOTS):
            s = trip[b * SLOTS + t]
            uh, ul = split(echo[0, s])
            vh, vl = split(echo[1, s])
            rh.append(jnp.concatenate([uh, vh], 1))
            rl.append(jnp.concatenate([ul, vl], 1))
            muh, mul, mvh, mvl = uh * m, ul * m, vh * m, vl * m
            xh.append(jnp.concatenate([muh, mvh], 1))
            yh.append(jnp.concatenate([mvh, -muh], 1))
            xl.append(jnp.concatenate([mul, mvl], 1))
            yl.append(jnp.concatenate([mvl, -mul], 1))
        return rh, rl, jnp.concatenate(xh + yh + xl + yl, 0)

    row = iota((ST, GATES), 0)
    lane = iota((ST, GATES), 1)
    low = row >= lane % HALF

    def pair(q):
        b = (q // 8) * 32 + half * 16 + (q % 8) * 2
        rha, rla, la = operands(b)
        rhb, rlb, lb = operands(b + 1)
        rhs = jnp.concatenate(rha + [zero] + rhb + [zero] + rla + [zero] + rlb + [zero], 0)
        dims = (((1,), (1,)), ((), ()))
        ga = lax.dot_general(la, rhs, dims, preferred_element_type=f32)
        gb = lax.dot_general(lb, rhs, dims, preferred_element_type=f32)
        ga = ga[:96] + ga[96:]
        gb = gb[:96] + gb[96:]
        ga = ga[:, :GATES] + ga[:, GATES:]
        gb = gb[:, :GATES] + gb[:, GATES:]
        re = jnp.where(lane < HALF, ga[:ST], gb[:ST])
        im = jnp.where(lane < HALF, ga[ST:], gb[ST:])
        out[q] = jnp.where(low, re, im)

    unroll = 2

    def step(i, c):
        for j in range(unroll):
            pair(i * unroll + j)
        return c

    lax.fori_loop(0, 32 // unroll, step, 0)


def gram(own, trip, echo, ex):
    return pl.pallas_call(
        functools.partial(gram_kernel, own),
        out_shape=jax.ShapeDtypeStruct((32, ST, GATES), f32),
        in_specs=[SM] + [VM] * 5,
        out_specs=VM,
        scratch_shapes=[pltpu.VMEM((BINS, GATES), f32)],
        name="gram_own" if own else "gram_peer",
    )(trip, echo, *ex)


def merge_kernel(axis, count, n_in, *refs):
    ins, outs = refs[:n_in], refs[n_in:]
    core, x, _, dop = axes()
    me = dop if axis == "z" else x
    size = outs[0].shape[0]
    for k, ref in enumerate(outs):
        base = lax.rem(me + k, count) * size if count > 1 else 0

        def step(i, c):
            total = ins[0][base + i]
            for r in ins[1:]:
                total = total + r[base + i]
            ref[i] = total
            return c

        if size <= 2:
            for i in range(size):
                step(i, 0)
        else:
            lax.fori_loop(0, size, step, 0)


def merge(axis, count, parts):
    size = parts[0].shape[0] // count
    return pl.pallas_call(
        functools.partial(merge_kernel, axis, count, len(parts)),
        out_shape=[jax.ShapeDtypeStruct((size, ST, GATES), f32)] * count,
        in_specs=[VM] * len(parts),
        out_specs=[VM] * count,
        name="merge_" + axis,
    )(*parts)


def solve_kernel(p0, p1, p2, p3, sr, si, out):
    row = iota((ST, GATES), 0)
    lane = iota((ST, GATES), 1)
    col = lane % HALF
    first = lane < HALF
    are, aim = [], []
    for q in range(2):
        p = (p0[q] + p1[q] + p2[q] + p3[q]) * (1.0 / TOTAL)
        full = jnp.concatenate([p, jnp.zeros((GATES - ST, GATES), f32)], 0).T
        pt = jnp.where(first, full[:ST], pltpu.roll(full[HALF : HALF + ST], HALF, 1))
        re = jnp.where(row >= col, p, pt)
        im = jnp.where(row < col, p, jnp.where(row == col, 0.0, -pt))
        aug = col >= ST
        are.append(jnp.where(aug, sr[q], re))
        aim.append(jnp.where(aug, si[q], im))
    base = jnp.where(first, 0, HALF)
    for k in range(ST):
        idx = base + k
        hit = row == k
        for q in range(2):
            cr = jnp.take_along_axis(are[q], idx, 1)
            ci = jnp.take_along_axis(aim[q], idx, 1)
            inv = 1.0 / cr[k : k + 1]
            nr = are[q][k : k + 1] * inv
            ni = aim[q][k : k + 1] * inv
            are[q] = jnp.where(hit, nr, are[q] - (cr * nr - ci * ni))
            aim[q] = jnp.where(hit, ni, aim[q] - (cr * ni + ci * nr))
    rows = []
    pad = jnp.zeros((GATES - ST, GATES), f32)
    lane1 = iota((1, GATES), 1)
    for q in range(2):
        wr = jnp.concatenate([are[q], pad], 0).T
        wi = jnp.concatenate([aim[q], pad], 0).T
        for h in (ST, HALF + ST):
            rows.append(
                jnp.where(lane1 < HALF, wr[h : h + 1], pltpu.roll(wi[h : h + 1], HALF, 1))
            )
    out[...] = jnp.concatenate(rows + [jnp.zeros((4, GATES), f32)], 0)


def solve(parts, sr, si):
    return pl.pallas_call(
        solve_kernel,
        out_shape=jax.ShapeDtypeStruct((8, GATES), f32),
        in_specs=[VM] * 6,
        out_specs=VM,
        name="solve",
    )(*parts, sr, si)


def power_kernel(trip, echo, w0, w1, o0, o1, o2, o3, wt):
    core, x, _, dop = axes()
    wt[0] = w0[...].T
    wt[1] = w1[...].T

    def one(b):
        z = b // 32
        c = lax.rem(b // 16, 2)
        bx = lax.rem(b // 4, XN)
        slot = lax.rem(dop - z + ZN, ZN) * 4 + lax.rem(x - bx + XN, XN)
        col = slot * 8 + lax.rem(b, 4)
        cc = lax.rem(c + core, 2)
        idx = jnp.full((CH, GATES), col, jnp.int32)
        re = jnp.zeros((CH, GATES), f32)
        im = jnp.zeros((CH, GATES), f32)
        for t in range(SLOTS):
            s = trip[b * SLOTS + t]
            u = echo[0, s]
            v = echo[1, s]
            wr = jnp.take_along_axis(wt[cc, t * CH : (t + 1) * CH, :], idx, 1)
            wi = jnp.take_along_axis(wt[cc, HALF + t * CH : HALF + (t + 1) * CH, :], idx, 1)
            re = re + wr * u + wi * v
            im = im + wr * v - wi * u
        re = jnp.sum(re, 0, keepdims=True)
        im = jnp.sum(im, 0, keepdims=True)
        return re * re + im * im

    for k, ref in enumerate((o0, o1, o2, o3)):
        first = lax.rem(dop + k, ZN) * 32

        def step(i, c):
            rows = [one(first + i * 8 + j) for j in range(8)]
            ref[pl.ds(pl.multiple_of(i * 8, 8), 8), :] = jnp.concatenate(rows, 0)
            return c

        lax.fori_loop(0, 4, step, 0)


def power(trip, echo, w0, w1):
    return pl.pallas_call(
        power_kernel,
        out_shape=[jax.ShapeDtypeStruct((32, GATES), f32)] * 4,
        in_specs=[SM] + [VM] * 3,
        out_specs=[VM] * 4,
        scratch_shapes=[pltpu.VMEM((2, GATES, GATES), f32)],
        name="power",
    )(trip, echo, w0, w1)


def cfar_kernel(p0, p1, p2, p3, h0, h1, h2, h3, guard, train, out, line):
    _, _, _, dop = axes()
    rank = lax.axis_index("range")
    for k, ref in enumerate((p0, p1, p2, p3)):
        line[1 + lax.rem(dop - k + ZN, ZN)] = ref[...]
    for j, ref in enumerate((h0, h1, h2, h3)):

        @pl.when(dop == (j + 3) % 4)
        def _():
            line[0] = ref[...]

        @pl.when(dop == j)
        def _():
            line[5] = ref[...]

    width = 6 * GATES
    p = jnp.concatenate([line[j] for j in range(6)], 1)
    g = guard[...]
    t = train[...]
    total = p
    acc = jnp.where((t & 1) == 1, p, 0.0)
    for k in range(1, 7):
        total = total + pltpu.roll(total, width - (1 << (k - 1)), 1)
        acc = jnp.where((t >> k) & 1 == 1, total + pltpu.roll(acc, width - (1 << k), 1), acc)
    right = acc
    shift = g + 1
    for k in range(3):
        right = jnp.where((shift >> k) & 1 == 1, pltpu.roll(right, width - (1 << k), 1), right)
    left = acc
    shift = g + t
    for k in range(7):
        left = jnp.where((shift >> k) & 1 == 1, pltpu.roll(left, 1 << k, 1), left)
    lo, hi = GATES, GATES + 4 * GATES
    both = left[:, lo:hi] + right[:, lo:hi]
    pos = rank * (4 * GATES) + iota((32, 4 * GATES), 1)
    left_count = jnp.maximum(jnp.minimum(pos - g - 1, TOTAL - 1) - jnp.maximum(pos - g - t, 0) + 1, 0)
    right_count = jnp.maximum(jnp.minimum(pos + g + t, TOTAL - 1) - jnp.maximum(pos + g + 1, 0) + 1, 0)
    noise = both / (left_count + right_count).astype(f32)
    out[...] = p[:, lo:hi] / (noise + EPS)


def cfar(parts, halos, guard, train):
    return pl.pallas_call(
        cfar_kernel,
        out_shape=jax.ShapeDtypeStruct((32, 4 * GATES), f32),
        in_specs=[VM] * 10,
        out_specs=VM,
        scratch_shapes=[pltpu.VMEM((6, 32, GATES), f32)],
        name="cfar",
    )(*parts, *halos, guard, train)


def turn(axis, k):
    if axis == "z":
        return "dop", [(i, (i + k) % ZN) for i in range(ZN)]
    pairs = []
    for y in range(4):
        for x in range(XN):
            for c in range(2):
                to = {"x": (y, (x + k) % XN, c), "y": ((y + k) % 4, x, c), "core": (y, x, 1 - c)}[axis]
                pairs.append(((y * XN + x) * 2 + c, (to[0] * XN + to[1]) * 2 + to[2]))
    return "range", pairs


def send(value, axis, k):
    return lax.ppermute(value, *turn(axis, k))


def steering(bin_taper, phases):
    core, x, _, dop = axes()
    first = dop * 32 + core * 16 + x * 4
    taper = lax.dynamic_slice_in_dim(bin_taper, first, 4, 0)

    def lay(values):
        full = (taper[:, :, None] * values[None, None, :]).reshape(2, 2, ST)
        full = jnp.broadcast_to(full[:, :, :, None], (2, 2, ST, HALF))
        return jnp.concatenate([full[:, 0], full[:, 1]], axis=2)

    return lay(jnp.cos(phases)), lay(jnp.sin(phases))


def shards(echoes, triplet, bin_taper, phases, excluded, guard_len, train_len):
    trip = triplet.reshape(-1)
    ex = [excluded] + [send(excluded, "z", k) for k in (1, 2, 3)]
    peer = gram(False, trip, echoes, ex)
    got = send(peer, "core", 1)
    mine = gram(True, trip, echoes, ex)
    pieces = merge("z", ZN, [mine, got])
    parts = [pieces[0]] + [send(pieces[k], "z", k) for k in (1, 2, 3)]
    pieces = merge("x", XN, parts)
    parts = [pieces[0]] + [send(pieces[k], "x", k) for k in (1, 2, 3)]
    (total,) = merge("y", 1, parts)
    parts = [total] + [send(total, "y", k) for k in (1, 2, 3)]
    sr, si = steering(bin_taper, phases)
    w = solve(parts, sr, si)
    w = jnp.concatenate([w] + [send(w, "x", k) for k in (1, 2, 3)], 0)
    w = jnp.concatenate([w] + [send(w, "z", k) for k in (1, 2, 3)], 0)
    other = send(w, "core", 1)
    pw = power(trip, echoes, w, other)
    parts = [pw[0]] + [send(pw[k], "z", k) for k in (1, 2, 3)]
    halos = []
    ranges = lax.axis_size("range")
    for j in range(4):
        pairs = [(r * ZN + 3, (r + 1) * ZN + (3 + j) % 4) for r in range(ranges - 1)]
        pairs += [(r * ZN, (r - 1) * ZN + j) for r in range(1, ranges)]
        halos.append(lax.ppermute(pw[j], ("range", "dop"), pairs))
    return cfar(parts, halos, guard_len[:, None], train_len[:, None])


def solution(mesh):
    placed = (
        P(None, None, None, ("range", "dop")),
        P(),
        P(),
        P(),
        P("dop", "range"),
        P("dop"),
        P("dop"),
    )
    return jax.shard_map(
        shards, mesh=mesh, in_specs=placed, out_specs=P("dop", "range"), check_vma=False
    )
```

time: 146 us -> 121 us (0.83); the launches traced: 144 us -> 121 us
  Pallas kernels: 0 us -> 37.6 us
  other arithmetic: 28.7 us -> 2.13 us
  waiting for transfers between devices: 46.1 us -> 21.3 us
  matrix products: 20.8 us -> 0 us
  starting transfers between devices: 29.9 us -> 49.3 us
  local copies, waits for them, and re-layouts: 18 us -> 10.2 us
    all_to_all x3 -> x0, waiting for transfers between devices: 41.8 us -> none  [the longest x1 25.7 us: shards(): lax.all_to_all(echoes, 'dop', split_axis=1, concat_axis=3, tiled=True)]
    ppermute x4 -> x27, starting transfers between devices: 11 us -> 49.3 us  [the longest x23 35.2 us: send(): return lax.ppermute(value, *turn(axis, k))]
    pallas_call x0 -> x8, Pallas kernels: none -> 37.6 us  [the longest x2 15.8 us: gram(): pl.pallas_call(functools.partial(gram_kernel, own), out_shape=jax.ShapeDt...]
    another operation x8 -> x0, other arithmetic: 21.4 us -> none  [the longest x3 9.45 us: solve_system(): factor = jnp.linalg.cholesky(system)]
    dot_general x8 -> x0, matrix products: 20.4 us -> none  [the longest x1 3.71 us: gram_blocks(): jnp.einsum('bir,bjr->bij', kept_real, snap_imag, precision=full_precision)]
    all_to_all x3 -> x0, starting transfers between devices: 18.9 us -> none  [the longest x1 7.58 us: sum_at_owner(): parts = lax.all_to_all(split_up(shard, dim, count), axis, 0, 0, tiled=True)]
    ppermute x4 -> x27, waiting for transfers between devices: 4.26 us -> 21.3 us  [the longest x23 21.1 us: send(): return lax.ppermute(value, *turn(axis, k))]
    all_to_all x2 -> x0, local copies, waits for them, and re-layouts: 4.78 us -> none  [shards(): lax.all_to_all(echoes, 'dop', split_axis=1, concat_axis=3, tiled=True)]
  transfers between devices with their start and end apart: 7 -> 27, of which waited for: 5 -> 15; matrix products, arithmetic and copies ran while one was open for 1% -> 5% of each run, Pallas kernels for 0% -> 7%
where the time goes in v1:
time: 121 us
  starting transfers between devices  49.3 us (41%)
  Pallas kernels  37.6 us (31%)
  waiting for transfers between devices  21.3 us (18%)
  local copies, waits for them, and re-layouts  10.2 us (8%)
  other arithmetic  2.13 us (2%)
    ppermute x23, starting transfers between devices, send(): return lax.ppermute(value, *turn(axis, k))  35.2 us
    ppermute x23, waiting for transfers between devices, send(): return lax.ppermute(value, *turn(axis, k))  21.1 us
    pallas_call x2, Pallas kernels, gram(): pl.pallas_call(functools.partial(gram_kernel, own), out_shape=jax.ShapeDt...  15.8 us
    ppermute x4, starting transfers between devices, shards(): halos.append(lax.ppermute(pw[j], ('range', 'dop'), pairs))  14.1 us
    unnamed x59, local copies, waits for them, and re-layouts  7.2 us
    pallas_call x1, Pallas kernels, power(): pl.pallas_call(power_kernel, out_shape=[jax.ShapeDtypeStruct((32, GATES),...  6.96 us
    pallas_call x1, Pallas kernels, solve(): pl.pallas_call(solve_kernel, out_shape=jax.ShapeDtypeStruct((8, GATES), f...  6.16 us
    pallas_call x3, Pallas kernels, merge(): pl.pallas_call(functools.partial(merge_kernel, axis, count, len(parts)),...  5.88 us
  transfers between devices with their start and end apart: 27, of which 15 were waited for; matrix products, arithmetic and copies ran while one was open for 5% of the time, Pallas kernels for 7%

profile of v1, /device:TPU:8, one launch (start us, length us, event | category | flops | bytes accessed | tf_op | source)
XLA Modules:
  0.0 120.7 jit_solution(17487124125769539622)
XLA Ops:
  0.0 1.9 %collective-permute-start = (s32[32,32]{1,0:T(8,128)}, s32[32,32]{1,0:T(8,128)S(1)}, u32[]{:S(2)}, u32[]{:S(2)}) collective-permute-start(s32[32,32]{1,0:T(8,128)} %e0.3), channel_id=1, source_target_pairs={{0,1},{1,2},{2,3},{3,0},{4,5},{5,6},{6,7},{7,4},{8,9},{9,10},{10,1... | collective-permute-start | bytes 12296 | tf_op jit(solution)/shard_map/ppermute | solution.py:307
  1.9 3.6 %collective-permute-start.1 = (s32[32,32]{1,0:T(8,128)}, s32[32,32]{1,0:T(8,128)S(1)}, u32[]{:S(2)}, u32[]{:S(2)}) collective-permute-start(s32[32,32]{1,0:T(8,128)} %e0.3), channel_id=1, source_target_pairs={{0,2},{1,3},{2,0},{3,1},{4,6},{5,7},{6,4},{7,5},{8,10},{9,11},{10,... | collective-permute-start | bytes 12296 | tf_op jit(solution)/shard_map/ppermute | solution.py:307
  5.5 1.0 collective-permute-start.2
  6.5 0.8 copy.11
  7.3 0.8 reshape.26.trip
  8.1 1.3 %collective-permute-done.2.e3 = s32[32,32]{1,0:T(8,128)S(1)} collective-permute-done((s32[32,32]{1,0:T(8,128)}, s32[32,32]{1,0:T(8,128)S(1)}, u32[]{:S(2)}, u32[]{:S(2)}) %collective-permute-start.2) | collective-permute-done | bytes 4128 | tf_op jit(solution)/shard_map/ppermute | solution.py:307
  10.1 7.9 %gram_peer.1 = f32[32,48,128]{2,1,0:T(8,128)} custom-call(s32[384]{0:T(512)} %reshape.26.trip, f32[2,128,16,128]{3,2,1,0:T(8,128)} %echo.5, s32[32,32]{1,0:T(8,128)} %e0.3, s32[32,32]{1,0:T(8,128)} %copy-done.6, s32[32,32]{1,0:T(8,128)} %copy-done.7, s32[32,32]{1,0:T(8,128)} %copy-done.8), custom_call_target="tpu_custom_call" | custom-call | tf_op jit(solution)/shard_map/gram_peer/pallas_call | solution.py:100
  18.5 7.9 %gram_own.1.refs_0_ = f32[32,48,128]{2,1,0:T(8,128)} custom-call(s32[384]{0:T(512)} %reshape.26.trip, f32[2,128,16,128]{3,2,1,0:T(8,128)} %echo.5, s32[32,32]{1,0:T(8,128)} %e0.3, s32[32,32]{1,0:T(8,128)} %copy-done.6, s32[32,32]{1,0:T(8,128)} %copy-done.7, s32[32,32]{1,0:T(8,128)} %copy-done.8), custom_call_target="tpu_custom_call" | custom-call | tf_op jit(solution)/shard_map/gram_own/pallas_call | solution.py:100
  26.5 0.9 copy-done.1
  27.3 2.5 %merge_z.1 = (f32[8,48,128]{2,1,0:T(8,128)}, f32[8,48,128]{2,1,0:T(8,128)}, f32[8,48,128]{2,1,0:T(8,128)}, f32[8,48,128]{2,1,0:T(8,128)}) custom-call(f32[32,48,128]{2,1,0:T(8,128)} %gram_own.1.refs_0_, f32[32,48,128]{2,1,0:T(8,128)} %copy-done.1), custom_call_target="tpu_custom_call" | custom-call | tf_op jit(solution)/shard_map/merge_z/pallas_call | solution.py:134
  30.2 3.3 %collective-permute-start.5 = (f32[8,48,128]{2,1,0:T(8,128)}, f32[8,48,128]{2,1,0:T(8,128)S(1)}, u32[]{:S(2)}, u32[]{:S(2)}) collective-permute-start(f32[8,48,128]{2,1,0:T(8,128)} %get-tuple-element.19), channel_id=1, source_target_pairs={{0,2},{1,3},{2,0},{3,1},{4,6},{5,7},{6,4},{7,5},{8,10},{9,11},{10,... | collective-permute-start | bytes 589832 | tf_op jit(solution)/shard_map/ppermute | solution.py:307
  33.5 1.0 collective-permute-start.6
  34.5 4.0 %collective-permute-done.4.refs_1_ = f32[8,48,128]{2,1,0:T(8,128)S(1)} collective-permute-done((f32[8,48,128]{2,1,0:T(8,128)}, f32[8,48,128]{2,1,0:T(8,128)S(1)}, u32[]{:S(2)}, u32[]{:S(2)}) %collective-permute-start.4) | collective-permute-done | bytes 196640 | tf_op jit(solution)/shard_map/ppermute | solution.py:307
  38.6 4.6 %collective-permute-done.5.refs_2_ = f32[8,48,128]{2,1,0:T(8,128)S(1)} collective-permute-done((f32[8,48,128]{2,1,0:T(8,128)}, f32[8,48,128]{2,1,0:T(8,128)S(1)}, u32[]{:S(2)}, u32[]{:S(2)}) %collective-permute-start.5) | collective-permute-done | bytes 196640 | tf_op jit(solution)/shard_map/ppermute | solution.py:307
  44.1 1.9 %merge_x.1 = (f32[2,48,128]{2,1,0:T(8,128)}, f32[2,48,128]{2,1,0:T(8,128)}, f32[2,48,128]{2,1,0:T(8,128)}, f32[2,48,128]{2,1,0:T(8,128)}) custom-call(f32[8,48,128]{2,1,0:T(8,128)} %get-tuple-element.17.refs_0_, f32[8,48,128]{2,1,0:T(8,128)} %copy-done.2, f32[8,48,128]{2,1,0:T(8,128)} %copy-done.3, f32[8,48,128]{2,1,0:T(8,128)} %copy-done.4), custom_call_target="tpu_custom_call" | custom-call | tf_op jit(solution)/shard_map/merge_x/pallas_call | solution.py:134
  46.0 1.5 %collective-permute-start.7 = (f32[2,48,128]{2,1,0:T(8,128)}, f32[2,48,128]{2,1,0:T(8,128)S(1)}, u32[]{:S(2)}, u32[]{:S(2)}) collective-permute-start(f32[2,48,128]{2,1,0:T(8,128)} %get-tuple-element.22), channel_id=1, source_target_pairs={{0,8},{4,12},{8,16},{12,20},{16,24},{20,28},{24,0},{28,4},{32,40},... | collective-permute-start | bytes 147464 | tf_op jit(solution)/shard_map/ppermute | solution.py:307
  47.5 2.7 %collective-permute-start.8 = (f32[2,48,128]{2,1,0:T(8,128)}, f32[2,48,128]{2,1,0:T(8,128)S(1)}, u32[]{:S(2)}, u32[]{:S(2)}) collective-permute-start(f32[2,48,128]{2,1,0:T(8,128)} %get-tuple-element.23), channel_id=1, source_target_pairs={{0,16},{4,20},{8,24},{12,28},{16,0},{20,4},{24,8},{28,12},{32,48},... | collective-permute-start | bytes 147464 | tf_op jit(solution)/shard_map/ppermute | solution.py:307
  50.2 1.4 %collective-permute-start.9 = (f32[2,48,128]{2,1,0:T(8,128)}, f32[2,48,128]{2,1,0:T(8,128)S(1)}, u32[]{:S(2)}, u32[]{:S(2)}) collective-permute-start(f32[2,48,128]{2,1,0:T(8,128)} %get-tuple-element.24), channel_id=1, source_target_pairs={{0,24},{4,28},{8,0},{12,4},{16,8},{20,12},{24,16},{28,20},{32,56},... | collective-permute-start | bytes 147464 | tf_op jit(solution)/shard_map/ppermute | solution.py:307
  51.8 0.7 pad_maximum_fusion.sr
  52.5 0.8 collective-permute-done.8.refs_2_
  53.3 1.2 %collective-permute-done.9.refs_3_ = f32[2,48,128]{2,1,0:T(8,128)S(1)} collective-permute-done((f32[2,48,128]{2,1,0:T(8,128)}, f32[2,48,128]{2,1,0:T(8,128)S(1)}, u32[]{:S(2)}, u32[]{:S(2)}) %collective-permute-start.9) | collective-permute-done | bytes 49184 | tf_op jit(solution)/shard_map/ppermute | solution.py:307
  55.1 1.5 %merge_y.1.p0 = f32[2,48,128]{2,1,0:T(8,128)} custom-call(f32[2,48,128]{2,1,0:T(8,128)} %get-tuple-element.21.refs_0_, f32[2,48,128]{2,1,0:T(8,128)} %copy-done.13, f32[2,48,128]{2,1,0:T(8,128)} %copy-done.14, f32[2,48,128]{2,1,0:T(8,128)} %copy-done.15), custom_call_target="tpu_custom_call" | custom-call | tf_op jit(solution)/shard_map/merge_y/pallas_call | solution.py:134
  56.6 1.6 %collective-permute-start.10 = (f32[2,48,128]{2,1,0:T(8,128)}, f32[2,48,128]{2,1,0:T(8,128)S(1)}, u32[]{:S(2)}, u32[]{:S(2)}) collective-permute-start(f32[2,48,128]{2,1,0:T(8,128)} %merge_y.1.p0), channel_id=1, source_target_pairs={{0,32},{4,36},{8,40},{12,44},{16,48},{20,52},{24,56},{28,60},{32,6... | collective-permute-start | bytes 147464 | tf_op jit(solution)/shard_map/ppermute | solution.py:307
  58.2 0.9 collective-permute-start.11
  59.2 2.4 %collective-permute-start.12 = (f32[2,48,128]{2,1,0:T(8,128)}, f32[2,48,128]{2,1,0:T(8,128)S(1)}, u32[]{:S(2)}, u32[]{:S(2)}) collective-permute-start(f32[2,48,128]{2,1,0:T(8,128)} %merge_y.1.p0), channel_id=1, source_target_pairs={{0,96},{4,100},{8,104},{12,108},{16,112},{20,116},{24,120},{28,124... | collective-permute-start | bytes 147464 | tf_op jit(solution)/shard_map/ppermute | solution.py:307
  61.7 0.7 pad_maximum_fusion.1.si
  62.4 1.6 %collective-permute-done.11.p2 = f32[2,48,128]{2,1,0:T(8,128)S(1)} collective-permute-done((f32[2,48,128]{2,1,0:T(8,128)}, f32[2,48,128]{2,1,0:T(8,128)S(1)}, u32[]{:S(2)}, u32[]{:S(2)}) %collective-permute-start.11) | collective-permute-done | bytes 49184 | tf_op jit(solution)/shard_map/ppermute | solution.py:307
  65.2 6.2 %solve.1 = f32[8,128]{1,0:T(8,128)} custom-call(f32[2,48,128]{2,1,0:T(8,128)} %merge_y.1.p0, f32[2,48,128]{2,1,0:T(8,128)} %copy-done.10, f32[2,48,128]{2,1,0:T(8,128)} %copy-done.11, f32[2,48,128]{2,1,0:T(8,128)} %copy-done.12, f32[2,48,128]{2,1,0:T(8,128)} %pad_maximum_fusion.sr, f32[2,48,128]{2,1,0:T(8,128)} %pad_maximum_fusion.1.si), custom_call_target="tpu_custom_call" | custom-call | tf_op jit(solution)/shard_map/solve/pallas_call | solution.py:184
  71.8 3.7 %collective-permute-start.14 = (f32[8,128]{1,0:T(8,128)}, f32[8,128]{1,0:T(8,128)S(1)}, u32[]{:S(2)}, u32[]{:S(2)}) collective-permute-start(f32[8,128]{1,0:T(8,128)} %solve.1), channel_id=1, source_target_pairs={{0,16},{4,20},{8,24},{12,28},{16,0},{20,4},{24,8},{28,12},{32,48},... | collective-permute-start | bytes 12296 | tf_op jit(solution)/shard_map/ppermute | solution.py:307
  75.6 0.7 constant_dynamic-update-slice_fusion.6
  76.4 0.9 collective-permute-done.14
  77.3 2.0 %collective-permute-done.15 = f32[8,128]{1,0:T(8,128)S(1)} collective-permute-done((f32[8,128]{1,0:T(8,128)}, f32[8,128]{1,0:T(8,128)S(1)}, u32[]{:S(2)}, u32[]{:S(2)}) %collective-permute-start.15) | collective-permute-done | bytes 4128 | tf_op jit(solution)/shard_map/ppermute | solution.py:307
  79.3 0.7 pad_maximum_fusion.2
  80.0 1.5 %collective-permute-start.16 = (f32[32,128]{1,0:T(8,128)S(1)}, f32[32,128]{1,0:T(8,128)S(1)}, u32[]{:S(2)}, u32[]{:S(2)}) collective-permute-start(f32[32,128]{1,0:T(8,128)S(1)} %pad_maximum_fusion.2), channel_id=1, source_target_pairs={{0,1},{1,2},{2,3},{3,0},{4,5},{5,6},{6,7},{7,4},{8,9},{9,10},{10,1... | collective-permute-start | bytes 49160 | tf_op jit(solution)/shard_map/ppermute | solution.py:307
  81.5 2.6 %collective-permute-start.17 = (f32[32,128]{1,0:T(8,128)S(1)}, f32[32,128]{1,0:T(8,128)S(1)}, u32[]{:S(2)}, u32[]{:S(2)}) collective-permute-start(f32[32,128]{1,0:T(8,128)S(1)} %pad_maximum_fusion.2), channel_id=1, source_target_pairs={{0,2},{1,3},{2,0},{3,1},{4,6},{5,7},{6,4},{7,5},{8,10},{9,11},{10,... | collective-permute-start | bytes 49160 | tf_op jit(solution)/shard_map/ppermute | solution.py:307
  85.0 1.7 %collective-permute-done.17 = f32[32,128]{1,0:T(8,128)S(1)} collective-permute-done((f32[32,128]{1,0:T(8,128)S(1)}, f32[32,128]{1,0:T(8,128)S(1)}, u32[]{:S(2)}, u32[]{:S(2)}) %collective-permute-start.17) | collective-permute-done | bytes 16416 | tf_op jit(solution)/shard_map/ppermute | solution.py:307
  86.7 1.1 collective-permute-done.18
  87.8 1.2 %collective-permute-done.19.w1 = f32[128,128]{1,0:T(8,128)S(1)} collective-permute-done((f32[128,128]{1,0:T(8,128)S(1)}, f32[128,128]{1,0:T(8,128)S(1)}, u32[]{:S(2)}, u32[]{:S(2)}) %collective-permute-start.19) | collective-permute-done | bytes 65568 | tf_op jit(solution)/shard_map/ppermute | solution.py:307
  89.7 7.0 %power.1 = (f32[32,128]{1,0:T(8,128)}, f32[32,128]{1,0:T(8,128)}, f32[32,128]{1,0:T(8,128)}, f32[32,128]{1,0:T(8,128)}) custom-call(s32[384]{0:T(512)} %reshape.26.trip, f32[2,128,16,128]{3,2,1,0:T(8,128)} %echo.5, f32[128,128]{1,0:T(8,128)} %copy-done.5, f32[128,128]{1,0:T(8,128)} %copy-done.9), custom_call_target="tpu_custom_call" | custom-call | tf_op jit(solution)/shard_map/power/pallas_call | solution.py:232
  96.7 3.3 %collective-permute-start.21 = (f32[32,128]{1,0:T(8,128)}, f32[32,128]{1,0:T(8,128)S(1)}, u32[]{:S(2)}, u32[]{:S(2)}) collective-permute-start(f32[32,128]{1,0:T(8,128)} %get-tuple-element.27), channel_id=1, source_target_pairs={{0,2},{1,3},{2,0},{3,1},{4,6},{5,7},{6,4},{7,5},{8,10},{9,11},{10,... | collective-permute-start | bytes 49160 | tf_op jit(solution)/shard_map/ppermute | solution.py:307
  100.0 3.3 %collective-permute-start.24 = (f32[32,128]{1,0:T(8,128)}, f32[32,128]{1,0:T(8,128)S(1)}, u32[]{:S(2)}, u32[]{:S(2)}) collective-permute-start(f32[32,128]{1,0:T(8,128)} %get-tuple-element.26), channel_id=1, source_target_pairs={{3,4},{7,8},{11,12},{15,16},{19,20},{23,24},{27,28},{31,32},{35,36... | collective-permute-start | bytes 49160 | tf_op jit(solution)/shard_map/ppermute | solution.py:347
  103.3 1.1 collective-permute-start.22
  104.4 5.7 %collective-permute-start.23 = (f32[32,128]{1,0:T(8,128)}, f32[32,128]{1,0:T(8,128)S(1)}, u32[]{:S(2)}, u32[]{:S(2)}) collective-permute-start(f32[32,128]{1,0:T(8,128)} %get-tuple-element.25.p0), channel_id=1, source_target_pairs={{3,7},{7,11},{11,15},{15,19},{19,23},{23,27},{27,31},{31,35},{35,3... | collective-permute-start | bytes 49160 | tf_op jit(solution)/shard_map/ppermute | solution.py:347
  110.2 1.3 %collective-permute-start.25 = (f32[32,128]{1,0:T(8,128)}, f32[32,128]{1,0:T(8,128)S(1)}, u32[]{:S(2)}, u32[]{:S(2)}) collective-permute-start(f32[32,128]{1,0:T(8,128)} %get-tuple-element.27), channel_id=1, source_target_pairs={{3,5},{7,9},{11,13},{15,17},{19,21},{23,25},{27,29},{31,33},{35,37... | collective-permute-start | bytes 49160 | tf_op jit(solution)/shard_map/ppermute | solution.py:347
  111.5 3.8 %collective-permute-start.26 = (f32[32,128]{1,0:T(8,128)}, f32[32,128]{1,0:T(8,128)S(1)}, u32[]{:S(2)}, u32[]{:S(2)}) collective-permute-start(f32[32,128]{1,0:T(8,128)} %get-tuple-element.28), channel_id=1, source_target_pairs={{3,6},{7,10},{11,14},{15,18},{19,22},{23,26},{27,30},{31,34},{35,3... | collective-permute-start | bytes 49160 | tf_op jit(solution)/shard_map/ppermute | solution.py:347
  115.3 0.7 copy.13.guard
  116.0 0.7 copy.14.train
  117.9 2.8 %cfar.1 = f32[32,512]{1,0:T(8,128)} custom-call(f32[32,128]{1,0:T(8,128)} %get-tuple-element.25.p0, f32[32,128]{1,0:T(8,128)} %copy-done.16, f32[32,128]{1,0:T(8,128)} %copy-done.17, f32[32,128]{1,0:T(8,128)} %copy-done.19, f32[32,128]{1,0:T(8,128)} %copy-done.20, f32[32,128]{1,0:T(8,128)} %copy-done.18, f32[32,128]{1,0:T(8,128)} %copy-done.21, ...), custom_call_target="tpu_custom_call" | custom-call | tf_op jit(solution)/shard_map/cfar/pallas_call | solution.py:284
  (95 shorter events, 7.9 us)
Async XLA Ops:
  0.0 18.0 %copy-start = (f32[128,3]{0,1:T(4,128)S(1)}, f32[128,3]{0,1:T(4,128)}, u32[]{:S(2)}) copy-start(f32[128,3]{0,1:T(4,128)} %param.9) | copy-start | bytes 4612
  0.0 18.3 %copy-start.25 = (f32[16]{0:T(128)S(1)}, f32[16]{0:T(128)}, u32[]{:S(2)}) copy-start(f32[16]{0:T(128)} %param.10) | copy-start | bytes 196
  0.0 8.1 %collective-permute-start = (s32[32,32]{1,0:T(8,128)}, s32[32,32]{1,0:T(8,128)S(1)}, u32[]{:S(2)}, u32[]{:S(2)}) collective-permute-start(s32[32,32]{1,0:T(8,128)} %e0.3), channel_id=1, source_target_pairs={{0,1},{1,2},{2,3},{3,0},{4,5},{5,6},{6,7},{7,4},{8,9},{9,10},{10,1... | collective-permute-start | bytes 12296 | tf_op jit(solution)/shard_map/ppermute | solution.py:307
  1.9 6.2 %collective-permute-start.1 = (s32[32,32]{1,0:T(8,128)}, s32[32,32]{1,0:T(8,128)S(1)}, u32[]{:S(2)}, u32[]{:S(2)}) collective-permute-start(s32[32,32]{1,0:T(8,128)} %e0.3), channel_id=1, source_target_pairs={{0,2},{1,3},{2,0},{3,1},{4,6},{5,7},{6,4},{7,5},{8,10},{9,11},{10,... | collective-permute-start | bytes 12296 | tf_op jit(solution)/shard_map/ppermute | solution.py:307
  5.5 3.9 %collective-permute-start.2 = (s32[32,32]{1,0:T(8,128)}, s32[32,32]{1,0:T(8,128)S(1)}, u32[]{:S(2)}, u32[]{:S(2)}) collective-permute-start(s32[32,32]{1,0:T(8,128)} %e0.3), channel_id=1, source_target_pairs={{0,3},{1,0},{2,1},{3,2},{4,7},{5,4},{6,5},{7,6},{8,11},{9,8},{10,9... | collective-permute-start | bytes 12296 | tf_op jit(solution)/shard_map/ppermute | solution.py:307
  8.1 1.4 %copy-start.6 = (s32[32,32]{1,0:T(8,128)}, s32[32,32]{1,0:T(8,128)S(1)}, u32[]{:S(2)}) copy-start(s32[32,32]{1,0:T(8,128)S(1)} %collective-permute-done.e1) | copy-start | bytes 12292
  8.1 1.4 %copy-start.7 = (s32[32,32]{1,0:T(8,128)}, s32[32,32]{1,0:T(8,128)S(1)}, u32[]{:S(2)}) copy-start(s32[32,32]{1,0:T(8,128)S(1)} %collective-permute-done.1.e2) | copy-start | bytes 12292
  18.0 8.5 %collective-permute-start.3 = (f32[32,48,128]{2,1,0:T(8,128)}, f32[32,48,128]{2,1,0:T(8,128)S(1)}, u32[]{:S(2)}, u32[]{:S(2)}) collective-permute-start(f32[32,48,128]{2,1,0:T(8,128)} %gram_peer.1), channel_id=1, source_target_pairs={{0,4},{4,0},{8,12},{12,8},{16,20},{20,16},{24,28},{28,24},{32,36},... | collective-permute-start | bytes 2359304 | tf_op jit(solution)/shard_map/ppermute | solution.py:307
  26.5 0.9 copy-start.1
  29.8 8.8 %collective-permute-start.4 = (f32[8,48,128]{2,1,0:T(8,128)}, f32[8,48,128]{2,1,0:T(8,128)S(1)}, u32[]{:S(2)}, u32[]{:S(2)}) collective-permute-start(f32[8,48,128]{2,1,0:T(8,128)} %get-tuple-element.18), channel_id=1, source_target_pairs={{0,1},{1,2},{2,3},{3,0},{4,5},{5,6},{6,7},{7,4},{8,9},{9,10},{10,1... | collective-permute-start | bytes 589832 | tf_op jit(solution)/shard_map/ppermute | solution.py:307
  30.2 13.0 %collective-permute-start.5 = (f32[8,48,128]{2,1,0:T(8,128)}, f32[8,48,128]{2,1,0:T(8,128)S(1)}, u32[]{:S(2)}, u32[]{:S(2)}) collective-permute-start(f32[8,48,128]{2,1,0:T(8,128)} %get-tuple-element.19), channel_id=1, source_target_pairs={{0,2},{1,3},{2,0},{3,1},{4,6},{5,7},{6,4},{7,5},{8,10},{9,11},{10,... | collective-permute-start | bytes 589832 | tf_op jit(solution)/shard_map/ppermute | solution.py:307
  33.5 9.9 %collective-permute-start.6 = (f32[8,48,128]{2,1,0:T(8,128)}, f32[8,48,128]{2,1,0:T(8,128)S(1)}, u32[]{:S(2)}, u32[]{:S(2)}) collective-permute-start(f32[8,48,128]{2,1,0:T(8,128)} %get-tuple-element.20), channel_id=1, source_target_pairs={{0,3},{1,0},{2,1},{3,2},{4,7},{5,4},{6,5},{7,6},{8,11},{9,8},{10,9... | collective-permute-start | bytes 589832 | tf_op jit(solution)/shard_map/ppermute | solution.py:307
  38.6 4.8 %copy-start.2 = (f32[8,48,128]{2,1,0:T(8,128)}, f32[8,48,128]{2,1,0:T(8,128)S(1)}, u32[]{:S(2)}) copy-start(f32[8,48,128]{2,1,0:T(8,128)S(1)} %collective-permute-done.4.refs_1_) | copy-start | bytes 589828
  43.2 0.7 copy-start.3
  43.4 0.7 copy-start.4
  44.1 71.2 %copy-start.23 = (s32[32]{0:T(128)S(1)}, s32[32]{0:T(128)}, u32[]{:S(2)}) copy-start(s32[32]{0:T(128)} %param.12) | copy-start | bytes 388
  44.1 71.9 %copy-start.24 = (s32[32]{0:T(128)S(1)}, s32[32]{0:T(128)}, u32[]{:S(2)}) copy-start(s32[32]{0:T(128)} %param.13) | copy-start | bytes 388
  46.0 6.5 %collective-permute-start.7 = (f32[2,48,128]{2,1,0:T(8,128)}, f32[2,48,128]{2,1,0:T(8,128)S(1)}, u32[]{:S(2)}, u32[]{:S(2)}) collective-permute-start(f32[2,48,128]{2,1,0:T(8,128)} %get-tuple-element.22), channel_id=1, source_target_pairs={{0,8},{4,12},{8,16},{12,20},{16,24},{20,28},{24,0},{28,4},{32,40},... | collective-permute-start | bytes 147464 | tf_op jit(solution)/shard_map/ppermute | solution.py:307
  47.5 5.8 %collective-permute-start.8 = (f32[2,48,128]{2,1,0:T(8,128)}, f32[2,48,128]{2,1,0:T(8,128)S(1)}, u32[]{:S(2)}, u32[]{:S(2)}) collective-permute-start(f32[2,48,128]{2,1,0:T(8,128)} %get-tuple-element.23), channel_id=1, source_target_pairs={{0,16},{4,20},{8,24},{12,28},{16,0},{20,4},{24,8},{28,12},{32,48},... | collective-permute-start | bytes 147464 | tf_op jit(solution)/shard_map/ppermute | solution.py:307
  50.2 4.3 %collective-permute-start.9 = (f32[2,48,128]{2,1,0:T(8,128)}, f32[2,48,128]{2,1,0:T(8,128)S(1)}, u32[]{:S(2)}, u32[]{:S(2)}) collective-permute-start(f32[2,48,128]{2,1,0:T(8,128)} %get-tuple-element.24), channel_id=1, source_target_pairs={{0,24},{4,28},{8,0},{12,4},{16,8},{20,12},{24,16},{28,20},{32,56},... | collective-permute-start | bytes 147464 | tf_op jit(solution)/shard_map/ppermute | solution.py:307
  52.5 2.0 %copy-start.13 = (f32[2,48,128]{2,1,0:T(8,128)}, f32[2,48,128]{2,1,0:T(8,128)S(1)}, u32[]{:S(2)}) copy-start(f32[2,48,128]{2,1,0:T(8,128)S(1)} %collective-permute-done.7.refs_1_) | copy-start | bytes 147460
  53.3 1.2 %copy-start.14 = (f32[2,48,128]{2,1,0:T(8,128)}, f32[2,48,128]{2,1,0:T(8,128)S(1)}, u32[]{:S(2)}) copy-start(f32[2,48,128]{2,1,0:T(8,128)S(1)} %collective-permute-done.8.refs_2_) | copy-start | bytes 147460
  54.5 0.6 copy-start.15
  56.6 5.8 %collective-permute-start.10 = (f32[2,48,128]{2,1,0:T(8,128)}, f32[2,48,128]{2,1,0:T(8,128)S(1)}, u32[]{:S(2)}, u32[]{:S(2)}) collective-permute-start(f32[2,48,128]{2,1,0:T(8,128)} %merge_y.1.p0), channel_id=1, source_target_pairs={{0,32},{4,36},{8,40},{12,44},{16,48},{20,52},{24,56},{28,60},{32,6... | collective-permute-start | bytes 147464 | tf_op jit(solution)/shard_map/ppermute | solution.py:307
  58.2 5.8 %collective-permute-start.11 = (f32[2,48,128]{2,1,0:T(8,128)}, f32[2,48,128]{2,1,0:T(8,128)S(1)}, u32[]{:S(2)}, u32[]{:S(2)}) collective-permute-start(f32[2,48,128]{2,1,0:T(8,128)} %merge_y.1.p0), channel_id=1, source_target_pairs={{0,64},{4,68},{8,72},{12,76},{16,80},{20,84},{24,88},{28,92},{32,9... | collective-permute-start | bytes 147464 | tf_op jit(solution)/shard_map/ppermute | solution.py:307
  59.2 4.9 %collective-permute-start.12 = (f32[2,48,128]{2,1,0:T(8,128)}, f32[2,48,128]{2,1,0:T(8,128)S(1)}, u32[]{:S(2)}, u32[]{:S(2)}) collective-permute-start(f32[2,48,128]{2,1,0:T(8,128)} %merge_y.1.p0), channel_id=1, source_target_pairs={{0,96},{4,100},{8,104},{12,108},{16,112},{20,116},{24,120},{28,124... | collective-permute-start | bytes 147464 | tf_op jit(solution)/shard_map/ppermute | solution.py:307
  62.4 1.6 %copy-start.10 = (f32[2,48,128]{2,1,0:T(8,128)}, f32[2,48,128]{2,1,0:T(8,128)S(1)}, u32[]{:S(2)}) copy-start(f32[2,48,128]{2,1,0:T(8,128)S(1)} %collective-permute-done.10.p1) | copy-start | bytes 147460
  64.0 0.6 copy-start.11
  64.6 0.6 copy-start.12
  71.4 5.0 %collective-permute-start.13 = (f32[8,128]{1,0:T(8,128)}, f32[8,128]{1,0:T(8,128)S(1)}, u32[]{:S(2)}, u32[]{:S(2)}) collective-permute-start(f32[8,128]{1,0:T(8,128)} %solve.1), channel_id=1, source_target_pairs={{0,8},{4,12},{8,16},{12,20},{16,24},{20,28},{24,0},{28,4},{32,40},... | collective-permute-start | bytes 12296 | tf_op jit(solution)/shard_map/ppermute | solution.py:307
  71.8 5.5 %collective-permute-start.14 = (f32[8,128]{1,0:T(8,128)}, f32[8,128]{1,0:T(8,128)S(1)}, u32[]{:S(2)}, u32[]{:S(2)}) collective-permute-start(f32[8,128]{1,0:T(8,128)} %solve.1), channel_id=1, source_target_pairs={{0,16},{4,20},{8,24},{12,28},{16,0},{20,4},{24,8},{28,12},{32,48},... | collective-permute-start | bytes 12296 | tf_op jit(solution)/shard_map/ppermute | solution.py:307
  75.5 3.8 %collective-permute-start.15 = (f32[8,128]{1,0:T(8,128)}, f32[8,128]{1,0:T(8,128)S(1)}, u32[]{:S(2)}, u32[]{:S(2)}) collective-permute-start(f32[8,128]{1,0:T(8,128)} %solve.1), channel_id=1, source_target_pairs={{0,24},{4,28},{8,0},{12,4},{16,8},{20,12},{24,16},{28,20},{32,56},... | collective-permute-start | bytes 12296 | tf_op jit(solution)/shard_map/ppermute | solution.py:307
  80.0 4.9 %collective-permute-start.16 = (f32[32,128]{1,0:T(8,128)S(1)}, f32[32,128]{1,0:T(8,128)S(1)}, u32[]{:S(2)}, u32[]{:S(2)}) collective-permute-start(f32[32,128]{1,0:T(8,128)S(1)} %pad_maximum_fusion.2), channel_id=1, source_target_pairs={{0,1},{1,2},{2,3},{3,0},{4,5},{5,6},{6,7},{7,4},{8,9},{9,10},{10,1... | collective-permute-start | bytes 49160 | tf_op jit(solution)/shard_map/ppermute | solution.py:307
  81.5 5.2 %collective-permute-start.17 = (f32[32,128]{1,0:T(8,128)S(1)}, f32[32,128]{1,0:T(8,128)S(1)}, u32[]{:S(2)}, u32[]{:S(2)}) collective-permute-start(f32[32,128]{1,0:T(8,128)S(1)} %pad_maximum_fusion.2), channel_id=1, source_target_pairs={{0,2},{1,3},{2,0},{3,1},{4,6},{5,7},{6,4},{7,5},{8,10},{9,11},{10,... | collective-permute-start | bytes 49160 | tf_op jit(solution)/shard_map/ppermute | solution.py:307
  84.1 3.7 %collective-permute-start.18 = (f32[32,128]{1,0:T(8,128)S(1)}, f32[32,128]{1,0:T(8,128)S(1)}, u32[]{:S(2)}, u32[]{:S(2)}) collective-permute-start(f32[32,128]{1,0:T(8,128)S(1)} %pad_maximum_fusion.2), channel_id=1, source_target_pairs={{0,3},{1,0},{2,1},{3,2},{4,7},{5,4},{6,5},{7,6},{8,11},{9,8},{10,9... | collective-permute-start | bytes 49160 | tf_op jit(solution)/shard_map/ppermute | solution.py:307
  87.8 1.3 %copy-start.5 = (f32[128,128]{1,0:T(8,128)}, f32[128,128]{1,0:T(8,128)S(1)}, u32[]{:S(2)}) copy-start(f32[128,128]{1,0:T(8,128)S(1)} %constant_dynamic-update-slice_fusion.w0) | copy-start | bytes 196612
  87.8 1.3 %collective-permute-start.19 = (f32[128,128]{1,0:T(8,128)S(1)}, f32[128,128]{1,0:T(8,128)S(1)}, u32[]{:S(2)}, u32[]{:S(2)}) collective-permute-start(f32[128,128]{1,0:T(8,128)S(1)} %constant_dynamic-update-slice_fusion.w0), channel_id=1, source_target_pairs={{0,4},{4,0},{8,12},{12,8},{16,20},{20,16},{24,28},{28,24},{32,36},... | collective-permute-start | bytes 196616 | tf_op jit(solution)/shard_map/ppermute | solution.py:307
  89.1 0.6 copy-start.9
  96.7 13.4 %collective-permute-start.20 = (f32[32,128]{1,0:T(8,128)}, f32[32,128]{1,0:T(8,128)S(1)}, u32[]{:S(2)}, u32[]{:S(2)}) collective-permute-start(f32[32,128]{1,0:T(8,128)} %get-tuple-element.26), channel_id=1, source_target_pairs={{0,1},{1,2},{2,3},{3,0},{4,5},{5,6},{6,7},{7,4},{8,9},{9,10},{10,1... | collective-permute-start | bytes 49160 | tf_op jit(solution)/shard_map/ppermute | solution.py:307
  96.7 14.8 %collective-permute-start.21 = (f32[32,128]{1,0:T(8,128)}, f32[32,128]{1,0:T(8,128)S(1)}, u32[]{:S(2)}, u32[]{:S(2)}) collective-permute-start(f32[32,128]{1,0:T(8,128)} %get-tuple-element.27), channel_id=1, source_target_pairs={{0,2},{1,3},{2,0},{3,1},{4,6},{5,7},{6,4},{7,5},{8,10},{9,11},{10,... | collective-permute-start | bytes 49160 | tf_op jit(solution)/shard_map/ppermute | solution.py:307
  100.0 16.7 %collective-permute-start.24 = (f32[32,128]{1,0:T(8,128)}, f32[32,128]{1,0:T(8,128)S(1)}, u32[]{:S(2)}, u32[]{:S(2)}) collective-permute-start(f32[32,128]{1,0:T(8,128)} %get-tuple-element.26), channel_id=1, source_target_pairs={{3,4},{7,8},{11,12},{15,16},{19,20},{23,24},{27,28},{31,32},{35,36... | collective-permute-start | bytes 49160 | tf_op jit(solution)/shard_map/ppermute | solution.py:347
  103.3 13.4 %collective-permute-start.22 = (f32[32,128]{1,0:T(8,128)}, f32[32,128]{1,0:T(8,128)S(1)}, u32[]{:S(2)}, u32[]{:S(2)}) collective-permute-start(f32[32,128]{1,0:T(8,128)} %get-tuple-element.28), channel_id=1, source_target_pairs={{0,3},{1,0},{2,1},{3,2},{4,7},{5,4},{6,5},{7,6},{8,11},{9,8},{10,9... | collective-permute-start | bytes 49160 | tf_op jit(solution)/shard_map/ppermute | solution.py:307
  104.4 12.3 %collective-permute-start.23 = (f32[32,128]{1,0:T(8,128)}, f32[32,128]{1,0:T(8,128)S(1)}, u32[]{:S(2)}, u32[]{:S(2)}) collective-permute-start(f32[32,128]{1,0:T(8,128)} %get-tuple-element.25.p0), channel_id=1, source_target_pairs={{3,7},{7,11},{11,15},{15,19},{19,23},{23,27},{27,31},{31,35},{35,3... | collective-permute-start | bytes 49160 | tf_op jit(solution)/shard_map/ppermute | solution.py:347
  110.1 6.8 %copy-start.16 = (f32[32,128]{1,0:T(8,128)}, f32[32,128]{1,0:T(8,128)S(1)}, u32[]{:S(2)}) copy-start(f32[32,128]{1,0:T(8,128)S(1)} %collective-permute-done.20.p1) | copy-start | bytes 49156
  110.2 6.6 %collective-permute-start.25 = (f32[32,128]{1,0:T(8,128)}, f32[32,128]{1,0:T(8,128)S(1)}, u32[]{:S(2)}, u32[]{:S(2)}) collective-permute-start(f32[32,128]{1,0:T(8,128)} %get-tuple-element.27), channel_id=1, source_target_pairs={{3,5},{7,9},{11,13},{15,17},{19,21},{23,25},{27,29},{31,33},{35,37... | collective-permute-start | bytes 49160 | tf_op jit(solution)/shard_map/ppermute | solution.py:347
  111.5 5.5 %copy-start.17 = (f32[32,128]{1,0:T(8,128)}, f32[32,128]{1,0:T(8,128)S(1)}, u32[]{:S(2)}) copy-start(f32[32,128]{1,0:T(8,128)S(1)} %collective-permute-done.21.p2) | copy-start | bytes 49156
  111.5 5.5 %collective-permute-start.26 = (f32[32,128]{1,0:T(8,128)}, f32[32,128]{1,0:T(8,128)S(1)}, u32[]{:S(2)}, u32[]{:S(2)}) collective-permute-start(f32[32,128]{1,0:T(8,128)} %get-tuple-element.28), channel_id=1, source_target_pairs={{3,6},{7,10},{11,14},{15,18},{19,22},{23,26},{27,30},{31,34},{35,3... | collective-permute-start | bytes 49160 | tf_op jit(solution)/shard_map/ppermute | solution.py:347
  116.7 0.6 copy-start.19
  (5 other events, 3.0 us)

commit v2 on v1

v2 whole, which is shorter than its diff:
```python
import functools
import jax
import jax.numpy as jnp
from jax import lax
from jax.experimental import pallas as pl
from jax.experimental.pallas import tpu as pltpu
from jax.sharding import PartitionSpec as P

CH = 16
SLOTS = 3
ST = 48
BINS = 128
BLOCK = 16
GATES = 128
TOTAL = 16384
EPS = 1e-6
HALF = 64
XN = 4
YN = 4
ZN = 4
f32 = jnp.float32
bf16 = jnp.bfloat16

VM = pl.BlockSpec(memory_space=pltpu.VMEM)
SM = pl.BlockSpec(memory_space=pltpu.SMEM)


def core_and_dop():
    return lax.axis_index("range") % 2, lax.axis_index("dop")


def iota(shape, dim):
    return lax.broadcasted_iota(jnp.int32, shape, dim)


def split(x):
    hi = x.astype(bf16)
    return hi, (x - hi.astype(f32)).astype(bf16)


def lanes(*parts):
    return jnp.concatenate(parts, 1)


def rows(*parts):
    return jnp.concatenate(parts, 0)


def gram_kernel(trip, near, far, m0, m1, m2, out, kept):
    core, dop = core_and_dop()
    block = dop * (GATES // BLOCK) + (iota((64, 2 * GATES), 1) % GATES) // BLOCK
    block = block + 32 * (iota((64, 2 * GATES), 1) // GATES)
    pick = (iota((64, 2 * GATES), 0) == block).astype(f32)
    masks = rows(m0[...], m1[...], m2[...]).astype(f32)
    left = 1.0 - jnp.dot(masks, pick, preferred_element_type=f32)
    for k in range(4):
        kept[dop ^ k] = left[16 * k : 16 * k + 16]

    zero = jnp.zeros((16, 4 * GATES), bf16)

    def operands(z, i):
        b = z * 32 + core * 16 + i
        m = kept[z, pl.ds(i, 1), :]
        mn = jnp.broadcast_to(m[:, :GATES], (CH, GATES)).astype(bf16)
        mf = jnp.broadcast_to(m[:, GATES:], (CH, GATES)).astype(bf16)
        rh, rl, xh, yh, xl, yl = [], [], [], [], [], []
        for t in range(SLOTS):
            s = trip[b, t]
            unh, unl = split(near[0, s])
            ufh, ufl = split(far[0, s])
            vnh, vnl = split(near[1, s])
            vfh, vfl = split(far[1, s])
            rh.append(lanes(unh, ufh, vnh, vfh))
            rl.append(lanes(unl, ufl, vnl, vfl))
            a, c, d, e = unh * mn, ufh * mf, vnh * mn, vfh * mf
            xh.append(lanes(a, c, d, e))
            yh.append(lanes(d, e, -a, -c))
            a, c, d, e = unl * mn, ufl * mf, vnl * mn, vfl * mf
            xl.append(lanes(a, c, d, e))
            yl.append(lanes(d, e, -a, -c))
        return rh, rl, rows(*xh, *yh, *xl, *yl)

    row = iota((ST, GATES), 0)
    lane = iota((ST, GATES), 1)
    low = row >= lane % HALF
    first = lane < HALF
    first24 = first[:24]

    def pair(z, i):
        rha, rla, la = operands(z, i)
        rhb, rlb, lb = operands(z, i + 1)
        rhs = rows(*rha, zero, *rhb, zero, *rla, zero, *rlb, zero)
        dims = (((1,), (1,)), ((), ()))
        ga = lax.dot_general(la, rhs, dims, preferred_element_type=f32)
        gb = lax.dot_general(lb, rhs, dims, preferred_element_type=f32)
        ga = ga[:96] + ga[96:]
        gb = gb[:96] + gb[96:]
        ga = ga[:, :GATES] + ga[:, GATES:]
        gb = gb[:, :GATES] + gb[:, GATES:]
        re = jnp.where(first, ga[:ST], gb[:ST])
        im = jnp.where(first, ga[ST:], gb[ST:])
        p = jnp.where(low, re, im)
        r = pltpu.roll(p, HALF, 1)
        out[i * ZN + z] = jnp.where(first24, p[:24], r[24:])
        out[(i + 1) * ZN + z] = jnp.where(first24, r[:24], p[24:])

    def step(j, c):
        z = j // 8
        pair(z, (j % 8) * 2)
        return c

    lax.fori_loop(0, 32, step, 0)


def gram(trip, near, far, masks):
    return pl.pallas_call(
        gram_kernel,
        out_shape=jax.ShapeDtypeStruct((64, 24, GATES), f32),
        in_specs=[SM] + [VM] * 5,
        out_specs=VM,
        scratch_shapes=[pltpu.VMEM((ZN, 16, 2 * GATES), f32)],
        name="gram",
    )(trip, near, far, *masks)


def solve_kernel(parts, taper, trig, out):
    core, dop = core_and_dop()
    b = dop * 32 + core * 16 + lax.axis_index("range") // 2
    row = iota((ST, GATES), 0)
    lane = iota((ST, GATES), 1)
    total = parts[0]
    for j in range(1, 64):
        total = total + parts[j]
    total = total * (1.0 / TOTAL)
    p = rows(total, pltpu.roll(total, HALF, 1))
    full = rows(p, jnp.zeros((GATES - ST, GATES), f32)).T[:ST]
    re = jnp.where(row >= lane, p, full)
    im = jnp.where(row < lane, p, jnp.where(row == lane, 0.0, -full))
    chan = iota((CH, GATES), 0)
    cosine = jnp.zeros((CH, GATES), f32)
    sine = jnp.zeros((CH, GATES), f32)
    for j in range(CH):
        cosine = jnp.where(chan == j, trig[j], cosine)
        sine = jnp.where(chan == j, trig[CH + j], sine)
    sr = rows(*[taper[b, t] * cosine for t in range(SLOTS)])
    si = rows(*[taper[b, t] * sine for t in range(SLOTS)])
    are = jnp.where(lane < ST, re, sr)
    aim = jnp.where(lane < ST, im, si)
    for k in range(0, ST, 2):
        i0 = jnp.full((ST, GATES), k, jnp.int32)
        i1 = jnp.full((ST, GATES), k + 1, jnp.int32)
        c0r = jnp.take_along_axis(are, i0, 1)
        c0i = jnp.take_along_axis(aim, i0, 1)
        c1r = jnp.take_along_axis(are, i1, 1)
        c1i = jnp.take_along_axis(aim, i1, 1)
        r0, q0 = are[k : k + 1], aim[k : k + 1]
        r1, q1 = are[k + 1 : k + 2], aim[k + 1 : k + 2]
        a, d = c0r[k : k + 1], c1r[k + 1 : k + 2]
        br, bi = c1r[k : k + 1], c1i[k : k + 1]
        inv = 1.0 / (a * d - (br * br + bi * bi))
        a, d, br, bi = a * inv, d * inv, br * inv, bi * inv
        n0r = d * r0 - (br * r1 - bi * q1)
        n0i = d * q0 - (br * q1 + bi * r1)
        n1r = a * r1 - (br * r0 + bi * q0)
        n1i = a * q1 - (br * q0 - bi * r0)
        ur = (c0r * n0r - c0i * n0i) + (c1r * n1r - c1i * n1i)
        ui = (c0r * n0i + c0i * n0r) + (c1r * n1i + c1i * n1r)
        are = jnp.where(row == k, n0r, jnp.where(row == k + 1, n1r, are - ur))
        aim = jnp.where(row == k, n0i, jnp.where(row == k + 1, n1i, aim - ui))
    pad = jnp.zeros((GATES - ST, GATES), f32)
    wr = rows(are, pad).T[ST : ST + 1]
    wi = rows(aim, pad).T[ST : ST + 1]
    lane1 = iota((1, GATES), 1)
    top = jnp.where(lane1 < ST, wr, pltpu.roll(wi, ST, 1))
    low = jnp.where(lane1 < ST, -wi, pltpu.roll(wr, ST, 1))
    live = lane1 < 2 * ST
    tile = rows(jnp.where(live, top, 0.0), jnp.where(live, low, 0.0), jnp.zeros((6, GATES), f32))
    for j in range(64):
        out[j] = tile


def solve(parts, taper, trig):
    return pl.pallas_call(
        solve_kernel,
        out_shape=jax.ShapeDtypeStruct((64, 8, GATES), f32),
        in_specs=[VM, SM, SM],
        out_specs=VM,
        name="solve",
    )(parts, taper, trig)


def power_kernel(trip, near, far, w, out):
    core, dop = core_and_dop()
    zero = jnp.zeros((32, 2 * GATES), bf16)

    def one(z, i):
        b = z * 32 + core * 16 + i
        uh, ul, vh, vl = [], [], [], []
        for t in range(SLOTS):
            s = trip[b, t]
            h, l = split(lanes(near[0, s], far[0, s]))
            uh.append(h)
            ul.append(l)
            h, l = split(lanes(near[1, s], far[1, s]))
            vh.append(h)
            vl.append(l)
        rhs = rows(*uh, *vh, zero, *ul, *vl, zero)
        wt = w[i * ZN + z]
        hi = wt.astype(bf16).astype(f32)
        lhs = rows(hi, wt - hi).astype(bf16)
        y = jnp.dot(lanes(lhs, lhs), rhs, preferred_element_type=f32)
        y = y[:8] + y[8:]
        y = y * y
        return y[0:1] + y[1:2]

    def step(j, c):
        z = j // 2
        i = (j % 2) * 8
        y = rows(*[one(z, i + k) for k in range(8)])
        at = pl.ds(pl.multiple_of(i, 8), 8)
        out[core * ZN + z, at, :] = y[:, :GATES]
        out[(1 - core) * ZN + z, at, :] = y[:, GATES:]
        return c

    lax.fori_loop(0, 8, step, 0)


def power(trip, near, far, w):
    return pl.pallas_call(
        power_kernel,
        out_shape=jax.ShapeDtypeStruct((8, 16, GATES), f32),
        in_specs=[SM] + [VM] * 3,
        out_specs=VM,
        name="power",
    )(trip, near, far, w)


def cfar_kernel(p, before, after, guard, train, out):
    rank = lax.axis_index("range")
    width = 6 * GATES
    pieces = [before[...]] + [rows(p[z], p[ZN + z]) for z in range(ZN)] + [after[...]]
    p = lanes(*pieces)
    row = iota((32, 1), 0)
    g = jnp.zeros((32, 1), jnp.int32)
    t = jnp.zeros((32, 1), jnp.int32)
    for j in range(32):
        g = jnp.where(row == j, guard[j], g)
        t = jnp.where(row == j, train[j], t)
    total = p
    acc = jnp.where((t & 1) == 1, p, 0.0)
    for k in range(1, 7):
        total = total + pltpu.roll(total, width - (1 << (k - 1)), 1)
        acc = jnp.where((t >> k) & 1 == 1, total + pltpu.roll(acc, width - (1 << k), 1), acc)
    right = acc
    shift = g + 1
    for k in range(3):
        right = jnp.where((shift >> k) & 1 == 1, pltpu.roll(right, width - (1 << k), 1), right)
    left = acc
    shift = g + t
    for k in range(7):
        left = jnp.where((shift >> k) & 1 == 1, pltpu.roll(left, 1 << k, 1), left)
    lo, hi = GATES, GATES + 4 * GATES
    both = left[:, lo:hi] + right[:, lo:hi]
    pos = rank * (4 * GATES) + iota((32, 4 * GATES), 1)
    left_count = jnp.maximum(jnp.minimum(pos - g - 1, TOTAL - 1) - jnp.maximum(pos - g - t, 0) + 1, 0)
    right_count = jnp.maximum(jnp.minimum(pos + g + t, TOTAL - 1) - jnp.maximum(pos + g + 1, 0) + 1, 0)
    noise = both / (left_count + right_count).astype(f32)
    out[...] = p[:, lo:hi] / (noise + EPS)


def cfar(p, before, after, guard, train):
    return pl.pallas_call(
        cfar_kernel,
        out_shape=jax.ShapeDtypeStruct((32, 4 * GATES), f32),
        in_specs=[VM] * 3 + [SM] * 2,
        out_specs=VM,
        name="cfar",
    )(p, before, after, guard, train)


BOTH = ("range", "dop")
CORE_SWAP = [(i, i ^ 1) for i in range(32)]
SAME_CORE = [
    [((y * XN + x) * 2 + c) * ZN + z for y in range(YN) for x in range(XN) for z in range(ZN)]
    for c in range(2)
]
CHIP_LINE = [[8 * i + j for j in range(8)] for i in range(16)]


def flipped(bit):
    return [(i, i ^ bit) for i in range(ZN)]


def shards(echoes, triplet, bin_taper, phases, excluded, guard_len, train_len):
    core, dop = core_and_dop()
    other = lax.ppermute(excluded, "range", CORE_SWAP)
    far = lax.ppermute(echoes, "range", CORE_SWAP)
    mine = lax.dynamic_slice_in_dim(lanes(excluded, other), core * 16, 16, 0)
    m1 = lax.ppermute(mine, "dop", flipped(1))
    m2 = lax.ppermute(rows(mine, m1), "dop", flipped(2))
    part = gram(triplet, echoes, far, [mine, m1, m2])
    part = lax.all_to_all(part, BOTH, 0, 0, tiled=True, axis_index_groups=SAME_CORE)
    trig = jnp.concatenate([jnp.cos(phases), jnp.sin(phases)])
    w = solve(part, bin_taper, trig)
    w = lax.all_to_all(w, BOTH, 0, 0, tiled=True, axis_index_groups=SAME_CORE)
    pw = power(triplet, echoes, far, w)
    pw = lax.all_to_all(pw, BOTH, 0, 0, tiled=True, axis_index_groups=CHIP_LINE)
    ranges = lax.axis_size("range")
    up = [(i, i + 1) for i in range(ranges - 1)]
    down = [(i + 1, i) for i in range(ranges - 1)]
    before = lax.ppermute(rows(pw[ZN - 1], pw[2 * ZN - 1]), "range", up)
    after = lax.ppermute(rows(pw[0], pw[ZN]), "range", down)
    return cfar(pw, before, after, guard_len, train_len)


def solution(mesh):
    placed = (
        P(None, None, None, ("range", "dop")),
        P(),
        P(),
        P(),
        P("dop", "range"),
        P("dop"),
        P("dop"),
    )
    return jax.shard_map(
        shards, mesh=mesh, in_specs=placed, out_specs=P("dop", "range"), check_vma=False
    )
```

time: 121 us -> 106 us (0.88)
  starting transfers between devices: 49.3 us -> 22.8 us
  blocking collectives: 0 us -> 24.7 us
  Pallas kernels: 37.6 us -> 29 us
  local copies, waits for them, and re-layouts: 10.2 us -> 5.62 us
    ppermute x27 -> x6, starting transfers between devices: 49.3 us -> 11.8 us  [the longest x1 3.88 us: shards(): m2 = lax.ppermute(rows(mine, m1), 'dop', flipped(2))]
    all_to_all x0 -> x2, blocking collectives: none -> 24.7 us  [the longest x1 16.1 us: shards(): w = lax.all_to_all(w, BOTH, 0, 0, tiled=True, axis_index_groups=SAME_CORE)]
    all_to_all x0 -> x1, waiting for transfers between devices: none -> 11.3 us  [shards(): lax.all_to_all(part, BOTH, 0, 0, tiled=True, axis_index_groups=SAME_CORE)]
    all_to_all x0 -> x1, starting transfers between devices: none -> 11.1 us  [shards(): lax.all_to_all(part, BOTH, 0, 0, tiled=True, axis_index_groups=SAME_CORE)]
    ppermute x27 -> x6, waiting for transfers between devices: 21.3 us -> 11.1 us  [the longest x1 5.22 us: shards(): before = lax.ppermute(rows(pw[ZN - 1], pw[2 * ZN - 1]), 'range', up)]
    pallas_call x7 -> x3, Pallas kernels: 34.8 us -> 26.4 us  [the longest x1 15.7 us: gram(): pl.pallas_call(gram_kernel, out_shape=jax.ShapeDtypeStruct((64, 24, GATES...]
    broadcast_in_dim x6 -> x0, local copies, waits for them, and re-layouts: 1.66 us -> none  [the longest x2 1.37 us: shards(): return cfar(parts, halos, guard_len[:, None], train_len[:, None])]
    unnamed x59 -> x22, local copies, waits for them, and re-layouts: 7.2 us -> 5.58 us
  transfers between devices with their start and end apart: 27 -> 7, of which waited for: 15 -> 5; matrix products, arithmetic and copies ran while one was open for 5% -> 3% of each run, Pallas kernels for 7% -> 0%
where the time goes in v2:
time: 106 us
  Pallas kernels  29 us (27%)
  blocking collectives  24.7 us (23%)
  starting transfers between devices  22.8 us (22%)
  waiting for transfers between devices  22.4 us (21%)
  local copies, waits for them, and re-layouts  5.62 us (5%)
  other arithmetic  1.37 us (1%)
    all_to_all x1, blocking collectives, shards(): w = lax.all_to_all(w, BOTH, 0, 0, tiled=True, axis_index_groups=SAME_CORE)  16.1 us
    pallas_call x1, Pallas kernels, gram(): pl.pallas_call(gram_kernel, out_shape=jax.ShapeDtypeStruct((64, 24, GATES...  15.7 us
    all_to_all x1, waiting for transfers between devices, shards(): lax.all_to_all(part, BOTH, 0, 0, tiled=True, axis_index_groups=SAME_CORE)  11.3 us
    all_to_all x1, starting transfers between devices, shards(): lax.all_to_all(part, BOTH, 0, 0, tiled=True, axis_index_groups=SAME_CORE)  11.1 us
    all_to_all x1, blocking collectives, shards(): pw = lax.all_to_all(pw, BOTH, 0, 0, tiled=True, axis_index_groups=CHIP_LINE)  8.6 us
    pallas_call x1, Pallas kernels, solve(): pl.pallas_call(solve_kernel, out_shape=jax.ShapeDtypeStruct((64, 8, GATES...  5.8 us
    unnamed x22, local copies, waits for them, and re-layouts  5.58 us
    ppermute x1, waiting for transfers between devices, shards(): before = lax.ppermute(rows(pw[ZN - 1], pw[2 * ZN - 1]), 'range', up)  5.22 us
  transfers between devices with their start and end apart: 7, of which 5 were waited for; matrix products, arithmetic and copies ran while one was open for 3% of the time, Pallas kernels for 0%

profile of v2, /device:TPU:8, one launch (start us, length us, event | category | flops | bytes accessed | tf_op | source)
XLA Modules:
  0.0 105.9 jit_solution(3653650173652012418)
XLA Ops:
  0.0 0.0 collective-permute-start
  0.0 0.5 collective-permute-start.1
  0.5 3.9 %collective-permute-done.1 = s32[32,32]{1,0:T(8,128)S(1)} collective-permute-done((s32[32,32]{1,0:T(8,128)}, s32[32,32]{1,0:T(8,128)S(1)}, u32[]{:S(2)}, u32[]{:S(2)}) %collective-permute-start.1) | collective-permute-done | bytes 4128 | tf_op jit(solution)/shard_map/ppermute | solution.py:296
  4.4 0.8 fusion.m0
  5.2 0.0 copy-start.3
  5.2 1.9 %collective-permute-start.2 = (s32[16,64]{1,0:T(8,128)S(1)}, s32[16,64]{1,0:T(8,128)S(1)}, u32[]{:S(2)}, u32[]{:S(2)}) collective-permute-start(s32[16,64]{1,0:T(8,128)S(1)} %fusion.m0), channel_id=1, source_target_pairs={{0,1},{1,0},{2,3},{3,2},{4,5},{5,4},{6,7},{7,6},{8,9},{9,8},{10,11... | collective-permute-start | bytes 12296 | tf_op jit(solution)/shard_map/ppermute | solution.py:299
  7.1 1.7 %collective-permute-done.2.m1 = s32[16,64]{1,0:T(8,128)S(1)} collective-permute-done((s32[16,64]{1,0:T(8,128)S(1)}, s32[16,64]{1,0:T(8,128)S(1)}, u32[]{:S(2)}, u32[]{:S(2)}) %collective-permute-start.2) | collective-permute-done | bytes 4128 | tf_op jit(solution)/shard_map/ppermute | solution.py:299
  8.8 0.0 copy-start.4
  8.9 3.9 %collective-permute-start.3 = (s32[32,64]{1,0:T(8,128)S(1)}, s32[32,64]{1,0:T(8,128)S(1)}, u32[]{:S(2)}, u32[]{:S(2)}) collective-permute-start(s32[32,64]{1,0:T(8,128)S(1)} %pad_add_fusion), channel_id=1, source_target_pairs={{0,2},{1,3},{2,0},{3,1},{4,6},{5,7},{6,4},{7,5},{8,10},{9,11},{10,... | collective-permute-start | bytes 24584 | tf_op jit(solution)/shard_map/ppermute | solution.py:300
  12.7 1.4 %copy.10.trip = s32[128,3]{1,0:T(8,128)} copy(s32[128,3]{0,1:T(4,128)} %param.8) | data formatting | bytes 3072 | tf_op args[1]
  14.1 0.0 copy-start.8
  14.1 0.0 copy-start.9
  14.2 0.3 collective-permute-done.3.m2
  14.4 0.0 copy-start.5
  14.4 0.0 collective-permute-done.far
  14.5 0.0 copy-done.3
  14.5 0.0 copy-done.4
  14.5 0.6 copy-done.5
  15.0 0.0 copy-start
  15.0 1.3 %copy-done = f32[2,128,16,128]{3,2,1,0:T(8,128)} copy-done((f32[2,128,16,128]{3,2,1,0:T(8,128)}, f32[2,128,16,128]{3,2,1,0:T(8,128)S(1)}, u32[]{:S(2)}) %copy-start) | copy-done | bytes 2097176
  16.4 15.7 %gram.1 = f32[64,24,128]{2,1,0:T(8,128)} custom-call(s32[128,3]{1,0:T(8,128)} %copy.10.trip, f32[2,128,16,128]{3,2,1,0:T(8,128)} %near.3, f32[2,128,16,128]{3,2,1,0:T(8,128)} %copy-done, s32[16,64]{1,0:T(8,128)} %copy-done.3, s32[16,64]{1,0:T(8,128)} %copy-done.4, s32[32,64]{1,0:T(8,128)} %copy-done.5), custom_call_target="tpu_custom_call" | custom-call | tf_op jit(solution)/shard_map/gram/pallas_call | solution.py:116
  32.1 11.1 %all-to-all-start = ((f32[64,24,128]{2,1,0:T(8,128)}), f32[64,24,128]{2,1,0:T(8,128)S(1)}, u32[]{:S(2)}, u32[]{:S(2)}) async-start(f32[64,24,128]{2,1,0:T(8,128)} %gram.1), calls=%async_computation | async-start | bytes 1572864 | tf_op jit(solution)/shard_map/all_to_all | solution.py:302
  43.1 0.0 copy-done.8
  43.2 0.7 copy.9.taper
  43.9 0.0 copy-done.9
  43.9 0.6 pad_maximum_fusion.2.trig
  44.5 11.3 %all-to-all-done.parts = f32[64,24,128]{2,1,0:T(8,128)S(1)} async-done(((f32[64,24,128]{2,1,0:T(8,128)}), f32[64,24,128]{2,1,0:T(8,128)S(1)}, u32[]{:S(2)}, u32[]{:S(2)}) %all-to-all-start) | async-done | bytes 786464 | tf_op jit(solution)/shard_map/all_to_all | solution.py:302
  55.8 0.0 copy-start.1
  55.8 0.9 copy-done.1
  56.7 5.8 %solve.1 = f32[64,8,128]{2,1,0:T(8,128)} custom-call(f32[64,24,128]{2,1,0:T(8,128)} %copy-done.1, f32[128,3]{1,0:T(8,128)} %copy.9.taper, f32[32]{0:T(128)} %pad_maximum_fusion.2.trig), custom_call_target="tpu_custom_call" | custom-call | tf_op jit(solution)/shard_map/solve/pallas_call | solution.py:183
  62.5 16.1 %all_to_all.15.w = f32[64,8,128]{2,1,0:T(8,128)} all-to-all(f32[64,8,128]{2,1,0:T(8,128)} %solve.1), channel_id=1, replica_groups={{0,1,2,3,8,9,10,11,16,17,18,19,24,25,26,27,32,33,34,35,40,41,42,43,48,4..., dimensions={0} | all-to-all | bytes 524288 | tf_op jit(solution)/shard_map/all_to_all | solution.py:305
  78.5 4.9 %power.1 = f32[8,16,128]{2,1,0:T(8,128)} custom-call(s32[128,3]{1,0:T(8,128)} %copy.10.trip, f32[2,128,16,128]{3,2,1,0:T(8,128)} %near.3, f32[2,128,16,128]{3,2,1,0:T(8,128)} %copy-done, f32[64,8,128]{2,1,0:T(8,128)} %all_to_all.15.w), custom_call_target="tpu_custom_call" | custom-call | tf_op jit(solution)/shard_map/power/pallas_call | solution.py:229
  83.4 8.6 %all_to_all.16.p = f32[8,16,128]{2,1,0:T(8,128)S(1)} all-to-all(f32[8,16,128]{2,1,0:T(8,128)} %power.1), channel_id=1, replica_groups={{0,1,2,3,4,5,6,7},{8,9,10,11,12,13,14,15},{16,17,18,19,20,21,22,23},{24..., dimensions={0} | all-to-all | bytes 131072 | tf_op jit(solution)/shard_map/all_to_all | solution.py:307
  92.0 0.0 copy-start.2
  92.0 3.5 %collective-permute-start.5 = (f32[32,128]{1,0:T(8,128)S(1)}, f32[32,128]{1,0:T(8,128)S(1)}, u32[]{:S(2)}, u32[]{:S(2)}) collective-permute-start(f32[32,128]{1,0:T(8,128)S(1)} %pad_maximum_fusion.1), channel_id=1, source_target_pairs={{4,0},{8,4},{12,8},{16,12},{20,16},{24,20},{28,24},{32,28},{36,32}... | collective-permute-start | bytes 49160 | tf_op jit(solution)/shard_map/ppermute | solution.py:312
  95.5 1.9 %collective-permute-start.4 = (f32[32,128]{1,0:T(8,128)S(1)}, f32[32,128]{1,0:T(8,128)S(1)}, u32[]{:S(2)}, u32[]{:S(2)}) collective-permute-start(f32[32,128]{1,0:T(8,128)S(1)} %pad_maximum_fusion), channel_id=1, source_target_pairs={{0,4},{4,8},{8,12},{12,16},{16,20},{20,24},{24,28},{28,32},{32,36}... | collective-permute-start | bytes 49160 | tf_op jit(solution)/shard_map/ppermute | solution.py:311
  97.5 0.0 collective-permute-done.5.after
  97.5 0.0 copy-start.6
  97.5 5.2 %collective-permute-done.4.before = f32[32,128]{1,0:T(8,128)S(1)} collective-permute-done((f32[32,128]{1,0:T(8,128)S(1)}, f32[32,128]{1,0:T(8,128)S(1)}, u32[]{:S(2)}, u32[]{:S(2)}) %collective-permute-start.4) | collective-permute-done | bytes 16416 | tf_op jit(solution)/shard_map/ppermute | solution.py:311
  102.7 0.0 copy-done.2
  102.7 0.0 copy-done.6
  102.7 0.0 copy-start.7
  102.7 0.6 copy-done.7
  103.3 2.6 %cfar.1 = f32[32,512]{1,0:T(8,128)} custom-call(f32[8,16,128]{2,1,0:T(8,128)} %copy-done.2, f32[32,128]{1,0:T(8,128)} %copy-done.7, f32[32,128]{1,0:T(8,128)} %copy-done.6, s32[32]{0:T(128)} %guard.1, s32[32]{0:T(128)} %train.1), custom_call_target="tpu_custom_call" | custom-call | tf_op jit(solution)/shard_map/cfar/pallas_call | solution.py:272
  (5 shorter events, 0.1 us)
Async XLA Ops:
  0.0 14.5 %collective-permute-start = (f32[2,128,16,128]{3,2,1,0:T(8,128)}, f32[2,128,16,128]{3,2,1,0:T(8,128)S(1)}, u32[]{:S(2)}, u32[]{:S(2)}) collective-permute-start(f32[2,128,16,128]{3,2,1,0:T(8,128)} %near.3), channel_id=1, source_target_pairs={{0,4},{4,0},{8,12},{12,8},{16,20},{20,16},{24,28},{28,24},{32,36},... | collective-permute-start | bytes 6291464 | tf_op jit(solution)/shard_map/ppermute | solution.py:297
  0.0 4.4 %collective-permute-start.1 = (s32[32,32]{1,0:T(8,128)}, s32[32,32]{1,0:T(8,128)S(1)}, u32[]{:S(2)}, u32[]{:S(2)}) collective-permute-start(s32[32,32]{1,0:T(8,128)} %param.11), channel_id=1, source_target_pairs={{0,4},{4,0},{8,12},{12,8},{16,20},{20,16},{24,28},{28,24},{32,36},... | collective-permute-start | bytes 12296 | tf_op jit(solution)/shard_map/ppermute | solution.py:296
  5.2 9.3 %copy-start.3 = (s32[16,64]{1,0:T(8,128)}, s32[16,64]{1,0:T(8,128)S(1)}, u32[]{:S(2)}) copy-start(s32[16,64]{1,0:T(8,128)S(1)} %fusion.m0) | copy-start | bytes 12292
  5.2 3.7 %collective-permute-start.2 = (s32[16,64]{1,0:T(8,128)S(1)}, s32[16,64]{1,0:T(8,128)S(1)}, u32[]{:S(2)}, u32[]{:S(2)}) collective-permute-start(s32[16,64]{1,0:T(8,128)S(1)} %fusion.m0), channel_id=1, source_target_pairs={{0,1},{1,0},{2,3},{3,2},{4,5},{5,4},{6,7},{7,6},{8,9},{9,8},{10,11... | collective-permute-start | bytes 12296 | tf_op jit(solution)/shard_map/ppermute | solution.py:299
  8.8 5.6 %copy-start.4 = (s32[16,64]{1,0:T(8,128)}, s32[16,64]{1,0:T(8,128)S(1)}, u32[]{:S(2)}) copy-start(s32[16,64]{1,0:T(8,128)S(1)} %collective-permute-done.2.m1) | copy-start | bytes 12292
  8.9 5.6 %collective-permute-start.3 = (s32[32,64]{1,0:T(8,128)S(1)}, s32[32,64]{1,0:T(8,128)S(1)}, u32[]{:S(2)}, u32[]{:S(2)}) collective-permute-start(s32[32,64]{1,0:T(8,128)S(1)} %pad_add_fusion), channel_id=1, source_target_pairs={{0,2},{1,3},{2,0},{3,1},{4,6},{5,7},{6,4},{7,5},{8,10},{9,11},{10,... | collective-permute-start | bytes 24584 | tf_op jit(solution)/shard_map/ppermute | solution.py:300
  14.1 29.0 %copy-start.8 = (f32[128,3]{0,1:T(4,128)S(1)}, f32[128,3]{0,1:T(4,128)}, u32[]{:S(2)}) copy-start(f32[128,3]{0,1:T(4,128)} %param.9) | copy-start | bytes 4612
  14.1 29.7 %copy-start.9 = (f32[16]{0:T(128)S(1)}, f32[16]{0:T(128)}, u32[]{:S(2)}) copy-start(f32[16]{0:T(128)} %param.10) | copy-start | bytes 196
  14.4 0.6 copy-start.5
  15.0 1.3 %copy-start = (f32[2,128,16,128]{3,2,1,0:T(8,128)}, f32[2,128,16,128]{3,2,1,0:T(8,128)S(1)}, u32[]{:S(2)}) copy-start(f32[2,128,16,128]{3,2,1,0:T(8,128)S(1)} %collective-permute-done.far) | copy-start | bytes 6291460
  32.1 23.7 %all-to-all-start = ((f32[64,24,128]{2,1,0:T(8,128)}), f32[64,24,128]{2,1,0:T(8,128)S(1)}, u32[]{:S(2)}, u32[]{:S(2)}) async-start(f32[64,24,128]{2,1,0:T(8,128)} %gram.1), calls=%async_computation | async-start | bytes 1572864 | tf_op jit(solution)/shard_map/all_to_all | solution.py:302
  55.8 0.9 copy-start.1
  92.0 10.7 %copy-start.2 = (f32[8,16,128]{2,1,0:T(8,128)}, f32[8,16,128]{2,1,0:T(8,128)S(1)}, u32[]{:S(2)}) copy-start(f32[8,16,128]{2,1,0:T(8,128)S(1)} %all_to_all.16.p) | copy-start | bytes 196612
  92.0 5.5 %collective-permute-start.5 = (f32[32,128]{1,0:T(8,128)S(1)}, f32[32,128]{1,0:T(8,128)S(1)}, u32[]{:S(2)}, u32[]{:S(2)}) collective-permute-start(f32[32,128]{1,0:T(8,128)S(1)} %pad_maximum_fusion.1), channel_id=1, source_target_pairs={{4,0},{8,4},{12,8},{16,12},{20,16},{24,20},{28,24},{32,28},{36,32}... | collective-permute-start | bytes 49160 | tf_op jit(solution)/shard_map/ppermute | solution.py:312
  95.5 7.2 %collective-permute-start.4 = (f32[32,128]{1,0:T(8,128)S(1)}, f32[32,128]{1,0:T(8,128)S(1)}, u32[]{:S(2)}, u32[]{:S(2)}) collective-permute-start(f32[32,128]{1,0:T(8,128)S(1)} %pad_maximum_fusion), channel_id=1, source_target_pairs={{0,4},{4,8},{8,12},{12,16},{16,20},{20,24},{24,28},{28,32},{32,36}... | collective-permute-start | bytes 49160 | tf_op jit(solution)/shard_map/ppermute | solution.py:311
  97.5 5.2 %copy-start.6 = (f32[32,128]{1,0:T(8,128)}, f32[32,128]{1,0:T(8,128)S(1)}, u32[]{:S(2)}) copy-start(f32[32,128]{1,0:T(8,128)S(1)} %collective-permute-done.5.after) | copy-start | bytes 49156
  102.7 0.6 copy-start.7

commit v3 on v2

v3 whole, which is shorter than its diff:
```python
import functools
import jax
import jax.numpy as jnp
from jax import lax
from jax.experimental import pallas as pl
from jax.experimental.pallas import tpu as pltpu
from jax.sharding import PartitionSpec as P

CH = 16
SLOTS = 3
ST = 48
BINS = 128
BLOCK = 16
GATES = 128
TOTAL = 16384
EPS = 1e-6
HALF = 64
XN = 4
YN = 4
ZN = 4
f32 = jnp.float32
bf16 = jnp.bfloat16
VMEM_LIMIT = 16 * 2**20

VM = pl.BlockSpec(memory_space=pltpu.VMEM)
SM = pl.BlockSpec(memory_space=pltpu.SMEM)


def core_and_dop():
    return lax.axis_index("range") % 2, lax.axis_index("dop")


def iota(shape, dim):
    return lax.broadcasted_iota(jnp.int32, shape, dim)


def split(x):
    hi = x.astype(bf16)
    return hi, (x - hi.astype(f32)).astype(bf16)


def lanes(*parts):
    return jnp.concatenate(parts, 1)


def rows(*parts):
    return jnp.concatenate(parts, 0)


def prep_kernel(echo, out):
    def step(i, c):
        for j in range(4):
            for p in range(2):
                x = echo[p, i * 4 + j]
                hi, rest = split(x)
                x = x - hi.astype(f32)
                out[0, p, i * 4 + j] = hi
                out[1, p, i * 4 + j] = rest
                out[2, p, i * 4 + j] = (x - rest.astype(f32)).astype(bf16)
        return c

    lax.fori_loop(0, BINS // 4, step, 0)


def prep(echo, name):
    return pl.pallas_call(
        prep_kernel,
        out_shape=jax.ShapeDtypeStruct((3, 2, BINS, CH, GATES), bf16),
        in_specs=[VM],
        out_specs=VM,
        name=name,
        compiler_params=pltpu.CompilerParams(vmem_limit_bytes=VMEM_LIMIT),
    )(echo)


def gram_kernel(second, trip, near, far, *refs):
    masks = refs[: 1 if second else 2]
    done, out, kept = (refs[1], refs[2], refs[3]) if second else (None, refs[2], refs[3])
    core, dop = core_and_dop()
    block = dop * (GATES // BLOCK) + (iota((64, 2 * GATES), 1) % GATES) // BLOCK
    block = block + 32 * (iota((64, 2 * GATES), 1) // GATES)
    pick = (iota((64, 2 * GATES), 0) == block).astype(f32)
    left = 1.0 - jnp.dot(rows(*[m[...] for m in masks]).astype(f32), pick, preferred_element_type=f32)
    for k in range(2):
        kept[k] = left[16 * k : 16 * k + 16]
    zero = jnp.zeros((16, 4 * GATES), bf16)
    base = 2 if second else 0

    def operands(k, i):
        b = (dop ^ (base + k)) * 32 + core * 16 + i
        m = kept[k, pl.ds(i, 1), :]
        mn = jnp.broadcast_to(m[:, :GATES], (CH, GATES)).astype(bf16)
        mf = jnp.broadcast_to(m[:, GATES:], (CH, GATES)).astype(bf16)
        plain, left, right = [[], []], [[], []], [[], []]
        for t in range(SLOTS):
            s = trip[b, t]
            for h in range(2):
                un, uf, vn, vf = near[h, 0, s], far[h, 0, s], near[h, 1, s], far[h, 1, s]
                plain[h].append(lanes(un, uf, vn, vf))
                un, uf, vn, vf = un * mn, uf * mf, vn * mn, vf * mf
                left[h].append(lanes(un, uf, vn, vf))
                right[h].append(lanes(vn, vf, -un, -uf))
        return plain[0], plain[1], rows(*left[0], *right[0], *left[1], *right[1])

    row = iota((ST, GATES), 0)
    lane = iota((ST, GATES), 1)
    low = row >= lane % HALF
    first = lane < HALF
    first24 = first[:24]

    def store(k, i, value):
        if second:
            out[i * ZN + (dop ^ (2 + k))] = value
        else:
            out[k * 16 + i] = value

    def pair(k, i):
        rha, rla, la = operands(k, i)
        rhb, rlb, lb = operands(k, i + 1)
        rhs = rows(*rha, zero, *rhb, zero, *rla, zero, *rlb, zero)
        dims = (((1,), (1,)), ((), ()))
        g = lax.dot_general(rows(la, lb), rhs, dims, preferred_element_type=f32)
        ga, gb = g[:192], g[192:]
        ga = ga[:96] + ga[96:]
        gb = gb[:96] + gb[96:]
        ga = ga[:, :GATES] + ga[:, GATES:]
        gb = gb[:, :GATES] + gb[:, GATES:]
        re = jnp.where(first, ga[:ST], gb[:ST])
        im = jnp.where(first, ga[ST:], gb[ST:])
        p = jnp.where(low, re, im)
        r = pltpu.roll(p, HALF, 1)
        store(k, i, jnp.where(first24, p[:24], r[24:]))
        store(k, i + 1, jnp.where(first24, r[:24], p[24:]))

    def step(k, c):
        for i in range(0, 16, 2):
            pair(k, i)
        return c

    lax.fori_loop(0, 2, step, 0)
    if second:
        for k in range(2):
            for i in range(16):
                out[i * ZN + (dop ^ k)] = done[k * 16 + i]


def gram(second, trip, near, far, extra):
    return pl.pallas_call(
        functools.partial(gram_kernel, second),
        out_shape=jax.ShapeDtypeStruct((64 if second else 32, 24, GATES), f32),
        in_specs=[SM] + [VM] * 4,
        out_specs=VM,
        scratch_shapes=[pltpu.VMEM((2, 16, 2 * GATES), f32)],
        name="gram_b" if second else "gram_a",
        compiler_params=pltpu.CompilerParams(vmem_limit_bytes=VMEM_LIMIT),
    )(trip, near, far, *extra)


def solve_kernel(parts, taper, trig, out):
    core, dop = core_and_dop()
    b = dop * 32 + core * 16 + lax.axis_index("range") // 2
    row = iota((ST, GATES), 0)
    lane = iota((ST, GATES), 1)
    total = parts[0]
    for j in range(1, 64):
        total = total + parts[j]
    total = total * (1.0 / TOTAL)
    p = rows(total, pltpu.roll(total, HALF, 1))
    full = rows(p, jnp.zeros((GATES - ST, GATES), f32)).T[:ST]
    re = jnp.where(row >= lane, p, full)
    im = jnp.where(row < lane, p, jnp.where(row == lane, 0.0, -full))
    chan = iota((CH, GATES), 0)
    cosine = jnp.zeros((CH, GATES), f32)
    sine = jnp.zeros((CH, GATES), f32)
    for j in range(CH):
        cosine = jnp.where(chan == j, trig[j], cosine)
        sine = jnp.where(chan == j, trig[CH + j], sine)
    sr = rows(*[taper[b, t] * cosine for t in range(SLOTS)])
    si = rows(*[taper[b, t] * sine for t in range(SLOTS)])
    are = jnp.where(lane < ST, re, sr)
    aim = jnp.where(lane < ST, im, si)
    for k in range(0, ST, 2):
        i0 = jnp.full((ST, GATES), k, jnp.int32)
        i1 = jnp.full((ST, GATES), k + 1, jnp.int32)
        c0r = jnp.take_along_axis(are, i0, 1)
        c0i = jnp.take_along_axis(aim, i0, 1)
        c1r = jnp.take_along_axis(are, i1, 1)
        c1i = jnp.take_along_axis(aim, i1, 1)
        r0, q0 = are[k : k + 1], aim[k : k + 1]
        r1, q1 = are[k + 1 : k + 2], aim[k + 1 : k + 2]
        a, d = c0r[k : k + 1], c1r[k + 1 : k + 2]
        br, bi = c1r[k : k + 1], c1i[k : k + 1]
        inv = 1.0 / (a * d - (br * br + bi * bi))
        a, d, br, bi = a * inv, d * inv, br * inv, bi * inv
        n0r = d * r0 - (br * r1 - bi * q1)
        n0i = d * q0 - (br * q1 + bi * r1)
        n1r = a * r1 - (br * r0 + bi * q0)
        n1i = a * q1 - (br * q0 - bi * r0)
        ur = (c0r * n0r - c0i * n0i) + (c1r * n1r - c1i * n1i)
        ui = (c0r * n0i + c0i * n0r) + (c1r * n1i + c1i * n1r)
        are = jnp.where(row == k, n0r, jnp.where(row == k + 1, n1r, are - ur))
        aim = jnp.where(row == k, n0i, jnp.where(row == k + 1, n1i, aim - ui))
    pad = jnp.zeros((GATES - ST, GATES), f32)
    wr = rows(are, pad).T[ST : ST + 1]
    wi = rows(aim, pad).T[ST : ST + 1]
    lane1 = iota((1, GATES), 1)
    w = jnp.where(lane1 < ST, wr, jnp.where(lane1 < 2 * ST, pltpu.roll(wi, ST, 1), 0.0))
    for j in range(64):
        out[j] = w


def solve(parts, taper, trig):
    return pl.pallas_call(
        solve_kernel,
        out_shape=jax.ShapeDtypeStruct((64, 1, GATES), f32),
        in_specs=[VM, SM, SM],
        out_specs=VM,
        name="solve",
        compiler_params=pltpu.CompilerParams(vmem_limit_bytes=VMEM_LIMIT),
    )(parts, taper, trig)


def power_kernel(trip, near, far, w, own, other):
    core, dop = core_and_dop()
    zero = jnp.zeros((32, 2 * GATES), bf16)
    row = iota((8, GATES), 0)
    lane = iota((8, GATES), 1)

    def one(k, i):
        z = dop ^ k
        b = z * 32 + core * 16 + i
        wt = jnp.broadcast_to(w[i * ZN + z], (8, GATES))
        turned = jnp.where(
            lane < ST,
            -pltpu.roll(wt, GATES - ST, 1),
            jnp.where(lane < 2 * ST, pltpu.roll(wt, ST, 1), 0.0),
        )
        wt = jnp.where(row % 2 == 0, wt, turned)
        hi = wt.astype(bf16).astype(f32)
        mid = (wt - hi).astype(bf16).astype(f32)
        lo = wt - hi - mid
        wt = jnp.where(row < 2, hi, jnp.where(row < 4, mid, jnp.where(row < 6, lo, 0.0)))
        lhs = rows(wt, jnp.zeros((8, GATES), f32)).astype(bf16)
        rhs = []
        for h in range(3):
            for p in range(2):
                for t in range(SLOTS):
                    s = trip[b, t]
                    rhs.append(lanes(near[h, p, s], far[h, p, s]))
            rhs.append(zero)
        y = jnp.dot(lanes(lhs, lhs, lhs), rows(*rhs), preferred_element_type=f32)
        re = y[0:1] + y[2:3] + y[4:5]
        im = y[1:2] + y[3:4] + y[5:6]
        return re * re + im * im

    def step(j, c):
        k = j // 2
        i = (j % 2) * 8
        y = rows(*[one(k, i + n) for n in range(8)])
        at = pl.ds(pl.multiple_of(i, 8), 8)
        own[k, at, :] = y[:, :GATES]
        other[k, at, :] = y[:, GATES:]
        return c

    lax.fori_loop(0, 8, step, 0)


def power(trip, near, far, w):
    return pl.pallas_call(
        power_kernel,
        out_shape=[jax.ShapeDtypeStruct((ZN, 16, GATES), f32)] * 2,
        in_specs=[SM] + [VM] * 3,
        out_specs=[VM] * 2,
        name="power",
        compiler_params=pltpu.CompilerParams(vmem_limit_bytes=VMEM_LIMIT),
    )(trip, near, far, w)


def cfar_kernel(p0, p1, p2, p3, before, after, guard, train, out, line):
    core, dop = core_and_dop()
    rank = lax.axis_index("range")
    width = 6 * GATES
    for k, ref in enumerate((p0, p1, p2, p3)):
        at = 1 + (dop ^ k)
        line[at, core] = ref[0]
        line[at, 1 - core] = ref[1]
    for at, ref in ((0, before), (5, after)):
        line[at, 1 - core] = ref[0]
        line[at, core] = ref[1]
    p = lanes(*[rows(line[j, 0], line[j, 1]) for j in range(6)])
    row = iota((32, 1), 0)
    g = jnp.zeros((32, 1), jnp.int32)
    t = jnp.zeros((32, 1), jnp.int32)
    for j in range(32):
        g = jnp.where(row == j, guard[j], g)
        t = jnp.where(row == j, train[j], t)
    total = p
    acc = jnp.where((t & 1) == 1, p, 0.0)
    for k in range(1, 7):
        total = total + pltpu.roll(total, width - (1 << (k - 1)), 1)
        acc = jnp.where((t >> k) & 1 == 1, total + pltpu.roll(acc, width - (1 << k), 1), acc)
    right = acc
    shift = g + 1
    for k in range(3):
        right = jnp.where((shift >> k) & 1 == 1, pltpu.roll(right, width - (1 << k), 1), right)
    left = acc
    shift = g + t
    for k in range(7):
        left = jnp.where((shift >> k) & 1 == 1, pltpu.roll(left, 1 << k, 1), left)
    lo, hi = GATES, GATES + 4 * GATES
    both = left[:, lo:hi] + right[:, lo:hi]
    pos = rank * (4 * GATES) + iota((32, 4 * GATES), 1)
    left_count = jnp.maximum(jnp.minimum(pos - g - 1, TOTAL - 1) - jnp.maximum(pos - g - t, 0) + 1, 0)
    right_count = jnp.maximum(jnp.minimum(pos + g + t, TOTAL - 1) - jnp.maximum(pos + g + 1, 0) + 1, 0)
    noise = both / (left_count + right_count).astype(f32)
    out[...] = p[:, lo:hi] / (noise + EPS)


def cfar(pieces, before, after, guard, train):
    return pl.pallas_call(
        cfar_kernel,
        out_shape=jax.ShapeDtypeStruct((32, 4 * GATES), f32),
        in_specs=[VM] * 6 + [SM] * 2,
        out_specs=VM,
        scratch_shapes=[pltpu.VMEM((6, 2, 16, GATES), f32)],
        name="cfar",
        compiler_params=pltpu.CompilerParams(vmem_limit_bytes=VMEM_LIMIT),
    )(*pieces, before, after, guard, train)


BOTH = ("range", "dop")
CORE_SWAP = [(i, i ^ 1) for i in range(32)]
SAME_CORE = [
    [((y * XN + x) * 2 + c) * ZN + z for y in range(YN) for x in range(XN) for z in range(ZN)]
    for c in range(2)
]


def flipped(bit):
    return [(i, i ^ bit) for i in range(ZN)]


def swap(value):
    return lax.ppermute(value, "range", CORE_SWAP)


def shards(echoes, triplet, bin_taper, phases, excluded, guard_len, train_len):
    core, dop = core_and_dop()
    other = swap(excluded)
    ready, other = lax.optimization_barrier((echoes, other))
    far = prep(swap(ready), "prep_far")
    near = prep(echoes, "prep_near")
    mine = lax.dynamic_slice_in_dim(lanes(excluded, other), core * 16, 16, 0)
    m1 = lax.ppermute(mine, "dop", flipped(1))
    m2 = lax.ppermute(rows(mine, m1), "dop", flipped(2))
    part = gram(False, triplet, near, far, [mine, m1])
    part = gram(True, triplet, near, far, [m2, part])
    part = lax.all_to_all(part, BOTH, 0, 0, tiled=True, axis_index_groups=SAME_CORE)
    trig = jnp.concatenate([jnp.cos(phases), jnp.sin(phases)])
    w = solve(part, bin_taper, trig)
    w = lax.all_to_all(w, BOTH, 0, 0, tiled=True, axis_index_groups=SAME_CORE)
    own, away = power(triplet, near, far, w)
    came = swap(away)
    pieces = [jnp.stack([own[k], came[k]]) for k in range(ZN)]
    pieces = [pieces[0]] + [lax.ppermute(pieces[k], "dop", flipped(k)) for k in (1, 2, 3)]
    p0, p1, p2, p3 = pieces
    ranges = lax.axis_size("range")
    up = [(i, i + 1) for i in range(ranges - 1)]
    down = [(i + 1, i) for i in range(ranges - 1)]
    last = jnp.where(dop == 0, p3, jnp.where(dop == 1, p2, jnp.where(dop == 2, p1, p0)))
    head = jnp.where(dop == 0, p0, jnp.where(dop == 1, p1, jnp.where(dop == 2, p2, p3)))
    before = lax.ppermute(last, "range", up)
    after = lax.ppermute(head, "range", down)
    return cfar(pieces, before, after, guard_len, train_len)


def solution(mesh):
    placed = (
        P(None, None, None, ("range", "dop")),
        P(),
        P(),
        P(),
        P("dop", "range"),
        P("dop"),
        P("dop"),
    )
    return jax.shard_map(
        shards, mesh=mesh, in_specs=placed, out_specs=P("dop", "range"), check_vma=False
    )
```

time: 106 us -> 92.6 us (0.87)
  the two profiles are of different devices: /device:TPU:8 before, /device:TPU:7 now
where the time goes in v3:
time: 92.6 us; the launch traced here: 92.1 us
  starting transfers between devices  28.4 us (31%)
  Pallas kernels  22.3 us (24%)
  waiting for transfers between devices  21.2 us (23%)
  blocking collectives  14.5 us (16%)
  local copies, waits for them, and re-layouts  4.66 us (5%)
    all_to_all x1, blocking collectives, shards(): w = lax.all_to_all(w, BOTH, 0, 0, tiled=True, axis_index_groups=SAME_CORE)  14.5 us
    all_to_all x1, waiting for transfers between devices, shards(): lax.all_to_all(part, BOTH, 0, 0, tiled=True, axis_index_groups=SAME_CORE)  11.2 us
    all_to_all x1, starting transfers between devices, shards(): lax.all_to_all(part, BOTH, 0, 0, tiled=True, axis_index_groups=SAME_CORE)  8.02 us
    pallas_call x2, Pallas kernels, gram(): pl.pallas_call(functools.partial(gram_kernel, second), out_shape=jax.Shap...  7.96 us
    ppermute x1, starting transfers between devices, shards(): before = lax.ppermute(last, 'range', up)  5.36 us
    ppermute x1, waiting for transfers between devices, shards(): after = lax.ppermute(head, 'range', down)  5.23 us
    pallas_call x1, Pallas kernels, solve(): pl.pallas_call(solve_kernel, out_shape=jax.ShapeDtypeStruct((64, 1, GATES...  4.83 us
    ppermute x3, starting transfers between devices, swap(): return lax.ppermute(value, 'range', CORE_SWAP)  4.75 us
  transfers between devices with their start and end apart: 11, of which 7 were waited for; matrix products, arithmetic and copies ran while one was open for 1% of the time, Pallas kernels for 7%

profile of v3, /device:TPU:7, one launch (start us, length us, event | category | flops | bytes accessed | tf_op | source)
XLA Modules:
  0.0 92.1 jit_solution(15025378847178983189)
XLA Ops:
  0.0 0.0 copy-start.6
  0.0 0.7 collective-permute-start
  0.7 1.0 %collective-permute-done = s32[32,32]{1,0:T(8,128)S(1)} collective-permute-done((s32[32,32]{1,0:T(8,128)}, s32[32,32]{1,0:T(8,128)S(1)}, u32[]{:S(2)}, u32[]{:S(2)}) %collective-permute-start) | collective-permute-done | bytes 4128 | tf_op jit(solution)/shard_map/ppermute | solution.py:344
  1.7 0.3 collective-permute-start.1
  2.1 0.8 fusion.refs_0_
  2.8 1.7 %collective-permute-start.2 = (s32[16,64]{1,0:T(8,128)S(1)}, s32[16,64]{1,0:T(8,128)S(1)}, u32[]{:S(2)}, u32[]{:S(2)}) collective-permute-start(s32[16,64]{1,0:T(8,128)S(1)} %fusion.refs_0_), channel_id=1, source_target_pairs={{0,1},{1,0},{2,3},{3,2},{4,5},{5,4},{6,7},{7,6},{8,9},{9,8},{10,11... | collective-permute-start | bytes 12296 | tf_op jit(solution)/shard_map/ppermute | solution.py:354
  4.5 1.0 %collective-permute-done.2.refs_1_ = s32[16,64]{1,0:T(8,128)S(1)} collective-permute-done((s32[16,64]{1,0:T(8,128)S(1)}, s32[16,64]{1,0:T(8,128)S(1)}, u32[]{:S(2)}, u32[]{:S(2)}) %collective-permute-start.2) | collective-permute-done | bytes 4128 | tf_op jit(solution)/shard_map/ppermute | solution.py:354
  5.5 3.4 %collective-permute-start.3 = (s32[32,64]{1,0:T(8,128)S(1)}, s32[32,64]{1,0:T(8,128)S(1)}, u32[]{:S(2)}, u32[]{:S(2)}) collective-permute-start(s32[32,64]{1,0:T(8,128)S(1)} %pad_add_fusion), channel_id=1, source_target_pairs={{0,2},{1,3},{2,0},{3,1},{4,6},{5,7},{6,4},{7,5},{8,10},{9,11},{10,... | collective-permute-start | bytes 24584 | tf_op jit(solution)/shard_map/ppermute | solution.py:355
  9.0 1.6 %copy-done.3 = f32[2,128,16,128]{3,2,1,0:T(8,128)S(1)} copy-done((f32[2,128,16,128]{3,2,1,0:T(8,128)S(1)}, f32[2,128,16,128]{3,2,1,0:T(8,128)}, u32[]{:S(2)}) %copy-start.3) | copy-done | bytes 2097176
  10.6 0.6 prep_near.1.near
  11.1 0.0 copy-done.6
  11.1 0.1 copy.11.trip
  11.2 0.0 collective-permute-done.1.echo
  11.2 2.1 %prep_far.1.far = bf16[3,2,128,16,128]{4,3,2,1,0:T(8,128)(2,1)S(1)} custom-call(f32[2,128,16,128]{3,2,1,0:T(8,128)} %collective-permute-done.1.echo), custom_call_target="tpu_custom_call" | custom-call | tf_op jit(solution)/shard_map/prep_far/pallas_call | solution.py:66
  13.4 0.0 copy-start
  13.4 4.0 %gram_a.1.refs_1_ = f32[32,24,128]{2,1,0:T(8,128)S(1)} custom-call(s32[128,3]{1,0:T(8,128)S(1)} %copy.11.trip, bf16[3,2,128,16,128]{4,3,2,1,0:T(8,128)(2,1)S(1)} %prep_near.1.near, bf16[3,2,128,16,128]{4,3,2,1,0:T(8,128)(2,1)S(1)} %prep_far.1.far, s32[16,64]{1,0:T(8,128)S(1)} %fusion.refs_0_, s32[16,64]{1,0:T(8,128)S(1)} %collective-permute-done.2.refs_1_), custom_call_target="tpu_custom_call" | custom-call | tf_op jit(solution)/shard_map/gram_a/pallas_call | solution.py:148
  17.4 0.0 copy-start.7
  17.4 0.0 copy-start.8
  17.4 0.0 collective-permute-done.3.refs_0_
  17.4 0.0 copy-done
  17.4 4.0 %gram_b.1 = f32[64,24,128]{2,1,0:T(8,128)S(1)} custom-call(s32[128,3]{1,0:T(8,128)S(1)} %copy.11.trip, bf16[3,2,128,16,128]{4,3,2,1,0:T(8,128)(2,1)S(1)} %prep_near.1.near, bf16[3,2,128,16,128]{4,3,2,1,0:T(8,128)(2,1)S(1)} %prep_far.1.far, s32[32,64]{1,0:T(8,128)S(1)} %collective-permute-done.3.refs_0_, f32[32,24,128]{2,1,0:T(8,128)S(1)} %gram_a.1.refs_1_), custom_call_target="tpu_custom_call" | custom-call | tf_op jit(solution)/shard_map/gram_b/pallas_call | solution.py:148
  21.4 0.0 copy-start.2
  21.4 0.9 copy-done.2
  22.3 8.0 %all-to-all-start = ((f32[64,24,128]{2,1,0:T(8,128)}), f32[64,24,128]{2,1,0:T(8,128)}, u32[]{:S(2)}, u32[]{:S(2)}) async-start(f32[64,24,128]{2,1,0:T(8,128)} %copy-done.2), calls=%async_computation | async-start | bytes 1572864 | tf_op jit(solution)/shard_map/all_to_all | solution.py:358
  30.3 0.0 copy-done.7
  30.3 0.1 copy.10.taper
  30.5 0.0 copy-done.8
  30.5 0.1 pad_maximum_fusion.4.trig
  30.6 11.2 %all-to-all-done.parts = f32[64,24,128]{2,1,0:T(8,128)} async-done(((f32[64,24,128]{2,1,0:T(8,128)}), f32[64,24,128]{2,1,0:T(8,128)}, u32[]{:S(2)}, u32[]{:S(2)}) %all-to-all-start) | async-done | bytes 786464 | tf_op jit(solution)/shard_map/all_to_all | solution.py:358
  41.8 4.8 %solve.1 = f32[64,1,128]{2,1,0:T(1,128)S(1)} custom-call(f32[64,24,128]{2,1,0:T(8,128)} %all-to-all-done.parts, f32[128,3]{1,0:T(8,128)S(1)} %copy.10.taper, f32[32]{0:T(128)S(1)} %pad_maximum_fusion.4.trig), custom_call_target="tpu_custom_call" | custom-call | tf_op jit(solution)/shard_map/solve/pallas_call | solution.py:213
  46.6 14.5 %all_to_all.10.w = f32[64,1,128]{2,1,0:T(1,128)S(1)} all-to-all(f32[64,1,128]{2,1,0:T(1,128)S(1)} %solve.1), channel_id=1, replica_groups={{0,1,2,3,8,9,10,11,16,17,18,19,24,25,26,27,32,33,34,35,40,41,42,43,48,4..., dimensions={0} | all-to-all | bytes 65536 | tf_op jit(solution)/shard_map/all_to_all | solution.py:361
  61.1 1.9 %copy-done.1 = bf16[3,2,128,16,128]{4,3,2,1,0:T(8,128)(2,1)S(1)} copy-done((bf16[3,2,128,16,128]{4,3,2,1,0:T(8,128)(2,1)S(1)}, bf16[3,2,128,16,128]{4,3,2,1,0:T(8,128)(2,1)}, u32[]{:S(2)}) %copy-start.1) | copy-done | bytes 3145752
  63.0 4.5 %power.1 = (f32[4,16,128]{2,1,0:T(8,128)S(1)}, f32[4,16,128]{2,1,0:T(8,128)S(1)}) custom-call(s32[128,3]{1,0:T(8,128)S(1)} %copy.11.trip, bf16[3,2,128,16,128]{4,3,2,1,0:T(8,128)(2,1)S(1)} %prep_near.1.near, bf16[3,2,128,16,128]{4,3,2,1,0:T(8,128)(2,1)S(1)} %copy-done.1, f32[64,1,128]{2,1,0:T(1,128)S(1)} %all_to_all.10.w), custom_call_target="tpu_custom_call" | custom-call | tf_op jit(solution)/shard_map/power/pallas_call | solution.py:269
  67.5 3.7 %collective-permute-start.4 = (f32[4,16,128]{2,1,0:T(8,128)S(1)}, f32[4,16,128]{2,1,0:T(8,128)S(1)}, u32[]{:S(2)}, u32[]{:S(2)}) collective-permute-start(f32[4,16,128]{2,1,0:T(8,128)S(1)} %get-tuple-element.12), channel_id=1, source_target_pairs={{0,4},{4,0},{8,12},{12,8},{16,20},{20,16},{24,28},{28,24},{32,36},... | collective-permute-start | bytes 98312 | tf_op jit(solution)/shard_map/ppermute | solution.py:344
  71.2 0.9 collective-permute-done.4
  72.1 1.0 %collective-permute-start.7 = (f32[2,16,128]{2,1,0:T(8,128)S(1)}, f32[2,16,128]{2,1,0:T(8,128)S(1)}, u32[]{:S(2)}, u32[]{:S(2)}) collective-permute-start(f32[2,16,128]{2,1,0:T(8,128)S(1)} %pad_maximum_fusion.3), channel_id=1, source_target_pairs={{0,3},{1,2},{2,1},{3,0},{4,7},{5,6},{6,5},{7,4},{8,11},{9,10},{10,... | collective-permute-start | bytes 49160 | tf_op jit(solution)/shard_map/ppermute | solution.py:365
  73.2 1.0 %collective-permute-start.6 = (f32[2,16,128]{2,1,0:T(8,128)S(1)}, f32[2,16,128]{2,1,0:T(8,128)S(1)}, u32[]{:S(2)}, u32[]{:S(2)}) collective-permute-start(f32[2,16,128]{2,1,0:T(8,128)S(1)} %pad_maximum_fusion.2), channel_id=1, source_target_pairs={{0,2},{1,3},{2,0},{3,1},{4,6},{5,7},{6,4},{7,5},{8,10},{9,11},{10,... | collective-permute-start | bytes 49160 | tf_op jit(solution)/shard_map/ppermute | solution.py:365
  74.2 1.2 %collective-permute-start.5 = (f32[2,16,128]{2,1,0:T(8,128)S(1)}, f32[2,16,128]{2,1,0:T(8,128)S(1)}, u32[]{:S(2)}, u32[]{:S(2)}) collective-permute-start(f32[2,16,128]{2,1,0:T(8,128)S(1)} %pad_maximum_fusion.1), channel_id=1, source_target_pairs={{0,1},{1,0},{2,3},{3,2},{4,5},{5,4},{6,7},{7,6},{8,9},{9,8},{10,11... | collective-permute-start | bytes 49160 | tf_op jit(solution)/shard_map/ppermute | solution.py:365
  75.4 0.5 collective-permute-done.7.p3
  75.9 1.3 %collective-permute-done.6.p2 = f32[2,16,128]{2,1,0:T(8,128)S(1)} collective-permute-done((f32[2,16,128]{2,1,0:T(8,128)S(1)}, f32[2,16,128]{2,1,0:T(8,128)S(1)}, u32[]{:S(2)}, u32[]{:S(2)}) %collective-permute-start.6) | collective-permute-done | bytes 16416 | tf_op jit(solution)/shard_map/ppermute | solution.py:365
  77.2 0.0 collective-permute-done.5.p1
  77.3 5.4 %collective-permute-start.8 = (f32[2,16,128]{2,1,0:T(8,128)S(1)}, f32[2,16,128]{2,1,0:T(8,128)S(1)}, u32[]{:S(2)}, u32[]{:S(2)}) collective-permute-start(f32[2,16,128]{2,1,0:T(8,128)S(1)} %get-tuple-element.14), channel_id=1, source_target_pairs={{0,4},{4,8},{8,12},{12,16},{16,20},{20,24},{24,28},{28,32},{32,36}... | collective-permute-start | bytes 49160 | tf_op jit(solution)/shard_map/ppermute | solution.py:372
  82.6 1.9 %collective-permute-start.9 = (f32[2,16,128]{2,1,0:T(8,128)S(1)}, f32[2,16,128]{2,1,0:T(8,128)S(1)}, u32[]{:S(2)}, u32[]{:S(2)}) collective-permute-start(f32[2,16,128]{2,1,0:T(8,128)S(1)} %get-tuple-element.13), channel_id=1, source_target_pairs={{4,0},{8,4},{12,8},{16,12},{20,16},{24,20},{28,24},{32,28},{36,32}... | collective-permute-start | bytes 49160 | tf_op jit(solution)/shard_map/ppermute | solution.py:373
  84.6 0.0 collective-permute-done.8.before
  84.6 5.2 %collective-permute-done.9.after = f32[2,16,128]{2,1,0:T(8,128)S(1)} collective-permute-done((f32[2,16,128]{2,1,0:T(8,128)S(1)}, f32[2,16,128]{2,1,0:T(8,128)S(1)}, u32[]{:S(2)}, u32[]{:S(2)}) %collective-permute-start.9) | collective-permute-done | bytes 16416 | tf_op jit(solution)/shard_map/ppermute | solution.py:373
  89.8 0.0 copy-done.4
  89.8 0.0 copy-done.5
  89.8 2.3 %cfar.1 = f32[32,512]{1,0:T(8,128)} custom-call(f32[2,16,128]{2,1,0:T(8,128)S(1)} %get-tuple-element.23.p0, f32[2,16,128]{2,1,0:T(8,128)S(1)} %collective-permute-done.5.p1, f32[2,16,128]{2,1,0:T(8,128)S(1)} %collective-permute-done.6.p2, f32[2,16,128]{2,1,0:T(8,128)S(1)} %collective-permute-done.7.p3, f32[2,16,128]{2,1,0:T(8,128)S(1)} %collective-permute-done.8.before, ...), custom_call_target="tpu_custom_call" | custom-call | tf_op jit(solution)/shard_map/cfar/pallas_call | solution.py:320
  (12 shorter events, 0.1 us)
Async XLA Ops:
  0.0 11.1 %copy-start.6 = (s32[128,3]{0,1:T(4,128)S(1)}, s32[128,3]{0,1:T(4,128)}, u32[]{:S(2)}) copy-start(s32[128,3]{0,1:T(4,128)} %param.8) | copy-start | bytes 4612
  0.0 1.7 %collective-permute-start = (s32[32,32]{1,0:T(8,128)}, s32[32,32]{1,0:T(8,128)S(1)}, u32[]{:S(2)}, u32[]{:S(2)}) collective-permute-start(s32[32,32]{1,0:T(8,128)} %param.11), channel_id=1, source_target_pairs={{0,4},{4,0},{8,12},{12,8},{16,20},{20,16},{24,28},{28,24},{32,36},... | collective-permute-start | bytes 12296 | tf_op jit(solution)/shard_map/ppermute | solution.py:344
  1.7 9.5 %collective-permute-start.1 = (f32[2,128,16,128]{3,2,1,0:T(8,128)}, f32[2,128,16,128]{3,2,1,0:T(8,128)}, u32[]{:S(2)}, u32[]{:S(2)}) collective-permute-start(f32[2,128,16,128]{3,2,1,0:T(8,128)} %echo.1), channel_id=1, source_target_pairs={{0,4},{4,0},{8,12},{12,8},{16,20},{20,16},{24,28},{28,24},{32,36},... | collective-permute-start | bytes 6291464 | tf_op jit(solution)/shard_map/ppermute | solution.py:344
  2.8 2.7 %collective-permute-start.2 = (s32[16,64]{1,0:T(8,128)S(1)}, s32[16,64]{1,0:T(8,128)S(1)}, u32[]{:S(2)}, u32[]{:S(2)}) collective-permute-start(s32[16,64]{1,0:T(8,128)S(1)} %fusion.refs_0_), channel_id=1, source_target_pairs={{0,1},{1,0},{2,3},{3,2},{4,5},{5,4},{6,7},{7,6},{8,9},{9,8},{10,11... | collective-permute-start | bytes 12296 | tf_op jit(solution)/shard_map/ppermute | solution.py:354
  5.5 11.9 %collective-permute-start.3 = (s32[32,64]{1,0:T(8,128)S(1)}, s32[32,64]{1,0:T(8,128)S(1)}, u32[]{:S(2)}, u32[]{:S(2)}) collective-permute-start(s32[32,64]{1,0:T(8,128)S(1)} %pad_add_fusion), channel_id=1, source_target_pairs={{0,2},{1,3},{2,0},{3,1},{4,6},{5,7},{6,4},{7,5},{8,10},{9,11},{10,... | collective-permute-start | bytes 24584 | tf_op jit(solution)/shard_map/ppermute | solution.py:355
  9.0 1.6 %copy-start.3 = (f32[2,128,16,128]{3,2,1,0:T(8,128)S(1)}, f32[2,128,16,128]{3,2,1,0:T(8,128)}, u32[]{:S(2)}) copy-start(f32[2,128,16,128]{3,2,1,0:T(8,128)} %echo.1) | copy-start | bytes 6291460
  13.4 4.0 %copy-start = (bf16[3,2,128,16,128]{4,3,2,1,0:T(8,128)(2,1)}, bf16[3,2,128,16,128]{4,3,2,1,0:T(8,128)(2,1)S(1)}, u32[]{:S(2)}) copy-start(bf16[3,2,128,16,128]{4,3,2,1,0:T(8,128)(2,1)S(1)} %prep_far.1.far) | copy-start | bytes 9437188
  17.4 13.0 %copy-start.7 = (f32[128,3]{0,1:T(4,128)S(1)}, f32[128,3]{0,1:T(4,128)}, u32[]{:S(2)}) copy-start(f32[128,3]{0,1:T(4,128)} %param.9) | copy-start | bytes 4612
  17.4 13.1 %copy-start.8 = (f32[16]{0:T(128)S(1)}, f32[16]{0:T(128)}, u32[]{:S(2)}) copy-start(f32[16]{0:T(128)} %param.10) | copy-start | bytes 196
  21.4 0.9 copy-start.2
  22.3 19.4 %all-to-all-start = ((f32[64,24,128]{2,1,0:T(8,128)}), f32[64,24,128]{2,1,0:T(8,128)}, u32[]{:S(2)}, u32[]{:S(2)}) async-start(f32[64,24,128]{2,1,0:T(8,128)} %copy-done.2), calls=%async_computation | async-start | bytes 1572864 | tf_op jit(solution)/shard_map/all_to_all | solution.py:358
  61.1 1.9 %copy-start.1 = (bf16[3,2,128,16,128]{4,3,2,1,0:T(8,128)(2,1)S(1)}, bf16[3,2,128,16,128]{4,3,2,1,0:T(8,128)(2,1)}, u32[]{:S(2)}) copy-start(bf16[3,2,128,16,128]{4,3,2,1,0:T(8,128)(2,1)} %copy-done) | copy-start | bytes 9437188
  63.0 26.8 %copy-start.4 = (s32[32]{0:T(128)S(1)}, s32[32]{0:T(128)}, u32[]{:S(2)}) copy-start(s32[32]{0:T(128)} %guard.1) | copy-start | bytes 388
  63.0 26.8 %copy-start.5 = (s32[32]{0:T(128)S(1)}, s32[32]{0:T(128)}, u32[]{:S(2)}) copy-start(s32[32]{0:T(128)} %train.1) | copy-start | bytes 388
  67.5 4.6 %collective-permute-start.4 = (f32[4,16,128]{2,1,0:T(8,128)S(1)}, f32[4,16,128]{2,1,0:T(8,128)S(1)}, u32[]{:S(2)}, u32[]{:S(2)}) collective-permute-start(f32[4,16,128]{2,1,0:T(8,128)S(1)} %get-tuple-element.12), channel_id=1, source_target_pairs={{0,4},{4,0},{8,12},{12,8},{16,20},{20,16},{24,28},{28,24},{32,36},... | collective-permute-start | bytes 98312 | tf_op jit(solution)/shard_map/ppermute | solution.py:344
  72.1 3.8 %collective-permute-start.7 = (f32[2,16,128]{2,1,0:T(8,128)S(1)}, f32[2,16,128]{2,1,0:T(8,128)S(1)}, u32[]{:S(2)}, u32[]{:S(2)}) collective-permute-start(f32[2,16,128]{2,1,0:T(8,128)S(1)} %pad_maximum_fusion.3), channel_id=1, source_target_pairs={{0,3},{1,2},{2,1},{3,0},{4,7},{5,6},{6,5},{7,4},{8,11},{9,10},{10,... | collective-permute-start | bytes 49160 | tf_op jit(solution)/shard_map/ppermute | solution.py:365
  73.2 4.1 %collective-permute-start.6 = (f32[2,16,128]{2,1,0:T(8,128)S(1)}, f32[2,16,128]{2,1,0:T(8,128)S(1)}, u32[]{:S(2)}, u32[]{:S(2)}) collective-permute-start(f32[2,16,128]{2,1,0:T(8,128)S(1)} %pad_maximum_fusion.2), channel_id=1, source_target_pairs={{0,2},{1,3},{2,0},{3,1},{4,6},{5,7},{6,4},{7,5},{8,10},{9,11},{10,... | collective-permute-start | bytes 49160 | tf_op jit(solution)/shard_map/ppermute | solution.py:365
  74.2 3.1 %collective-permute-start.5 = (f32[2,16,128]{2,1,0:T(8,128)S(1)}, f32[2,16,128]{2,1,0:T(8,128)S(1)}, u32[]{:S(2)}, u32[]{:S(2)}) collective-permute-start(f32[2,16,128]{2,1,0:T(8,128)S(1)} %pad_maximum_fusion.1), channel_id=1, source_target_pairs={{0,1},{1,0},{2,3},{3,2},{4,5},{5,4},{6,7},{7,6},{8,9},{9,8},{10,11... | collective-permute-start | bytes 49160 | tf_op jit(solution)/shard_map/ppermute | solution.py:365
  77.3 7.3 %collective-permute-start.8 = (f32[2,16,128]{2,1,0:T(8,128)S(1)}, f32[2,16,128]{2,1,0:T(8,128)S(1)}, u32[]{:S(2)}, u32[]{:S(2)}) collective-permute-start(f32[2,16,128]{2,1,0:T(8,128)S(1)} %get-tuple-element.14), channel_id=1, source_target_pairs={{0,4},{4,8},{8,12},{12,16},{16,20},{20,24},{24,28},{28,32},{32,36}... | collective-permute-start | bytes 49160 | tf_op jit(solution)/shard_map/ppermute | solution.py:372
  82.6 7.2 %collective-permute-start.9 = (f32[2,16,128]{2,1,0:T(8,128)S(1)}, f32[2,16,128]{2,1,0:T(8,128)S(1)}, u32[]{:S(2)}, u32[]{:S(2)}) collective-permute-start(f32[2,16,128]{2,1,0:T(8,128)S(1)} %get-tuple-element.13), channel_id=1, source_target_pairs={{4,0},{8,4},{12,8},{16,12},{20,16},{24,20},{28,24},{32,28},{36,32}... | collective-permute-start | bytes 49160 | tf_op jit(solution)/shard_map/ppermute | solution.py:373

commit v4 on v3

--- a/solution.py
+++ b/solution.py
@@ -18,6 +18,7 @@
 XN = 4
 YN = 4
 ZN = 4
+WINDOW = 20
 f32 = jnp.float32
 bf16 = jnp.bfloat16
 VMEM_LIMIT = 16 * 2**20
@@ -47,30 +48,44 @@
     return jnp.concatenate(parts, 0)
 
 
-def prep_kernel(echo, out):
-    def step(i, c):
-        for j in range(4):
-            for p in range(2):
-                x = echo[p, i * 4 + j]
-                hi, rest = split(x)
-                x = x - hi.astype(f32)
-                out[0, p, i * 4 + j] = hi
-                out[1, p, i * 4 + j] = rest
-                out[2, p, i * 4 + j] = (x - rest.astype(f32)).astype(bf16)
-        return c
-
-    lax.fori_loop(0, BINS // 4, step, 0)
-
-
-def prep(echo, name):
+def pack_kernel(echo, near, send, sems):
+    core, _ = core_and_dop()
+    copies = []
+    for out, half in ((near, core), (send, 1 - core)):
+        for z in range(ZN):
+            first = z * 32 + half * 16
+            for start, at, count in (
+                (first, 2, 16),
+                ((first + BINS - 2) % BINS, 0, 2),
+                ((first + 16) % BINS, 18, 2),
+            ):
+                copies.append(
+                    pltpu.make_async_copy(
+                        echo.at[:, pl.ds(start, count)],
+                        out.at[:, pl.ds(z * WINDOW + at, count)],
+                        sems.at[len(copies)],
+                    )
+                )
+    for c in copies:
+        c.start()
+    for c in copies:
+        c.wait()
+
+
+def pack(echo):
     return pl.pallas_call(
-        prep_kernel,
-        out_shape=jax.ShapeDtypeStruct((3, 2, BINS, CH, GATES), bf16),
-        in_specs=[VM],
-        out_specs=VM,
-        name=name,
+        pack_kernel,
+        out_shape=[jax.ShapeDtypeStruct((2, ZN * WINDOW, CH, GATES), f32)] * 2,
+        in_specs=[pl.BlockSpec(memory_space=pltpu.HBM)],
+        out_specs=[VM] * 2,
+        scratch_shapes=[pltpu.SemaphoreType.DMA((6 * ZN,))],
+        name="pack",
         compiler_params=pltpu.CompilerParams(vmem_limit_bytes=VMEM_LIMIT),
     )(echo)
+
+
+def place(trip, b, t, z, core):
+    return z * WINDOW + ((trip[b, t] - (z * 32 + core * 16) + BINS + 2) & (BINS - 1))
 
 
 def gram_kernel(second, trip, near, far, *refs):
@@ -87,19 +102,20 @@
     base = 2 if second else 0
 
     def operands(k, i):
-        b = (dop ^ (base + k)) * 32 + core * 16 + i
+        z = dop ^ (base + k)
+        b = z * 32 + core * 16 + i
         m = kept[k, pl.ds(i, 1), :]
         mn = jnp.broadcast_to(m[:, :GATES], (CH, GATES)).astype(bf16)
         mf = jnp.broadcast_to(m[:, GATES:], (CH, GATES)).astype(bf16)
         plain, left, right = [[], []], [[], []], [[], []]
         for t in range(SLOTS):
-            s = trip[b, t]
+            s = place(trip, b, t, z, core)
+            un, uf, vn, vf = split(near[0, s]), split(far[0, s]), split(near[1, s]), split(far[1, s])
             for h in range(2):
-                un, uf, vn, vf = near[h, 0, s], far[h, 0, s], near[h, 1, s], far[h, 1, s]
-                plain[h].append(lanes(un, uf, vn, vf))
-                un, uf, vn, vf = un * mn, uf * mf, vn * mn, vf * mf
-                left[h].append(lanes(un, uf, vn, vf))
-                right[h].append(lanes(vn, vf, -un, -uf))
+                plain[h].append(lanes(un[h], uf[h], vn[h], vf[h]))
+                a, c, d, e = un[h] * mn, uf[h] * mf, vn[h] * mn, vf[h] * mf
+                left[h].append(lanes(a, c, d, e))
+                right[h].append(lanes(d, e, -a, -c))
         return plain[0], plain[1], rows(*left[0], *right[0], *left[1], *right[1])
 
     row = iota((ST, GATES), 0)
@@ -241,13 +257,17 @@
         lo = wt - hi - mid
         wt = jnp.where(row < 2, hi, jnp.where(row < 4, mid, jnp.where(row < 6, lo, 0.0)))
         lhs = rows(wt, jnp.zeros((8, GATES), f32)).astype(bf16)
-        rhs = []
-        for h in range(3):
-            for p in range(2):
-                for t in range(SLOTS):
-                    s = trip[b, t]
-                    rhs.append(lanes(near[h, p, s], far[h, p, s]))
-            rhs.append(zero)
+        rhs = [[], [], []]
+        for p in range(2):
+            for t in range(SLOTS):
+                s = place(trip, b, t, z, core)
+                x = lanes(near[p, s], far[p, s])
+                hi, rest = split(x)
+                x = x - hi.astype(f32)
+                rhs[0].append(hi)
+                rhs[1].append(rest)
+                rhs[2].append((x - rest.astype(f32)).astype(bf16))
+        rhs = [*rhs[0], zero, *rhs[1], zero, *rhs[2], zero]
         y = jnp.dot(lanes(lhs, lhs, lhs), rows(*rhs), preferred_element_type=f32)
         re = y[0:1] + y[2:3] + y[4:5]
         im = y[1:2] + y[3:4] + y[5:6]
@@ -276,7 +296,7 @@
     )(trip, near, far, w)
 
 
-def cfar_kernel(p0, p1, p2, p3, before, after, guard, train, out, line):
+def cfar_kernel(p0, p1, p2, p3, inner, outer, guard, train, out, line):
     core, dop = core_and_dop()
     rank = lax.axis_index("range")
     width = 6 * GATES
@@ -284,7 +304,7 @@
         at = 1 + (dop ^ k)
         line[at, core] = ref[0]
         line[at, 1 - core] = ref[1]
-    for at, ref in ((0, before), (5, after)):
+    for at, ref in ((5 * (1 - core), inner), (5 * core, outer)):
         line[at, 1 - core] = ref[0]
         line[at, core] = ref[1]
     p = lanes(*[rows(line[j, 0], line[j, 1]) for j in range(6)])
@@ -316,7 +336,7 @@
     out[...] = p[:, lo:hi] / (noise + EPS)
 
 
-def cfar(pieces, before, after, guard, train):
+def cfar(pieces, inner, outer, guard, train):
     return pl.pallas_call(
         cfar_kernel,
         out_shape=jax.ShapeDtypeStruct((32, 4 * GATES), f32),
@@ -325,7 +345,7 @@
         scratch_shapes=[pltpu.VMEM((6, 2, 16, GATES), f32)],
         name="cfar",
         compiler_params=pltpu.CompilerParams(vmem_limit_bytes=VMEM_LIMIT),
-    )(*pieces, before, after, guard, train)
+    )(*pieces, inner, outer, guard, train)
 
 
 BOTH = ("range", "dop")
@@ -347,9 +367,9 @@
 def shards(echoes, triplet, bin_taper, phases, excluded, guard_len, train_len):
     core, dop = core_and_dop()
     other = swap(excluded)
-    ready, other = lax.optimization_barrier((echoes, other))
-    far = prep(swap(ready), "prep_far")
-    near = prep(echoes, "prep_near")
+    near, far = pack(echoes)
+    far, other = lax.optimization_barrier((far, other))
+    far = swap(far)
     mine = lax.dynamic_slice_in_dim(lanes(excluded, other), core * 16, 16, 0)
     m1 = lax.ppermute(mine, "dop", flipped(1))
     m2 = lax.ppermute(rows(mine, m1), "dop", flipped(2))
@@ -365,13 +385,12 @@
     pieces = [pieces[0]] + [lax.ppermute(pieces[k], "dop", flipped(k)) for k in (1, 2, 3)]
     p0, p1, p2, p3 = pieces
     ranges = lax.axis_size("range")
-    up = [(i, i + 1) for i in range(ranges - 1)]
-    down = [(i + 1, i) for i in range(ranges - 1)]
-    last = jnp.where(dop == 0, p3, jnp.where(dop == 1, p2, jnp.where(dop == 2, p1, p0)))
+    tail = jnp.where(dop == 0, p3, jnp.where(dop == 1, p2, jnp.where(dop == 2, p1, p0)))
     head = jnp.where(dop == 0, p0, jnp.where(dop == 1, p1, jnp.where(dop == 2, p2, p3)))
-    before = lax.ppermute(last, "range", up)
-    after = lax.ppermute(head, "range", down)
-    return cfar(pieces, before, after, guard_len, train_len)
+    inner = swap(jnp.where(core == 0, tail, head))
+    pairs = [(i, i + 1 if i % 2 else i - 1) for i in range(1, ranges - 1)]
+    outer = lax.ppermute(jnp.where(core == 0, head, tail), "range", pairs)
+    return cfar(pieces, inner, outer, guard_len, train_len)
 
 
 def solution(mesh):

time: 92.6 us -> 84.3 us (0.910)
  the two profiles are of different devices: /device:TPU:7 before, /device:TPU:8 now
where the time goes in v4:
time: 84.3 us; the launch traced here: 83.7 us
  starting transfers between devices  23.6 us (28%)
  Pallas kernels  21.3 us (25%)
  waiting for transfers between devices  21.2 us (25%)
  blocking collectives  14.5 us (17%)
  local copies, waits for them, and re-layouts  2.76 us (3%)
    all_to_all x1, blocking collectives, shards(): w = lax.all_to_all(w, BOTH, 0, 0, tiled=True, axis_index_groups=SAME_CORE)  14.5 us
    all_to_all x1, waiting for transfers between devices, shards(): lax.all_to_all(part, BOTH, 0, 0, tiled=True, axis_index_groups=SAME_CORE)  12.8 us
    all_to_all x1, starting transfers between devices, shards(): lax.all_to_all(part, BOTH, 0, 0, tiled=True, axis_index_groups=SAME_CORE)  8.84 us
    pallas_call x2, Pallas kernels, gram(): pl.pallas_call(functools.partial(gram_kernel, second), out_shape=jax.Shap...  7.89 us
    pallas_call x1, Pallas kernels, solve(): pl.pallas_call(solve_kernel, out_shape=jax.ShapeDtypeStruct((64, 1, GATES...  4.83 us
    pallas_call x1, Pallas kernels, power(): pl.pallas_call(power_kernel, out_shape=[jax.ShapeDtypeStruct((ZN, 16, GAT...  4.5 us
    ppermute x3, starting transfers between devices, shards(): lax.ppermute(pieces[k], 'dop', flipped(k))  4.09 us
    ppermute x1, starting transfers between devices, shards(): outer = lax.ppermute(jnp.where(core == 0, head, tail), 'range', pairs)  4.06 us
  transfers between devices with their start and end apart: 11, of which 6 were waited for; matrix products, arithmetic and copies ran while one was open for 1% of the time, Pallas kernels for 7%

profile of v4, /device:TPU:8, one launch (start us, length us, event | category | flops | bytes accessed | tf_op | source)
XLA Modules:
  0.0 83.7 jit_solution(13132336883543153063)
XLA Ops:
  0.0 0.0 collective-permute-start
  0.0 0.0 copy-start.1
  0.0 1.6 %copy-done.1 = f32[2,128,16,128]{3,2,1,0:T(8,128)S(1)} copy-done((f32[2,128,16,128]{3,2,1,0:T(8,128)S(1)}, f32[2,128,16,128]{3,2,1,0:T(8,128)}, u32[]{:S(2)}) %copy-start.1) | copy-done | bytes 2097176
  1.6 0.0 copy-start.4
  1.6 0.0 copy-start.5
  1.6 1.8 %pack.1 = (f32[2,80,16,128]{3,2,1,0:T(8,128)S(1)}, f32[2,80,16,128]{3,2,1,0:T(8,128)}) custom-call(f32[2,128,16,128]{3,2,1,0:T(8,128)S(1)} %copy-done.1), custom_call_target="tpu_custom_call" | custom-call | tf_op jit(solution)/shard_map/pack/pallas_call | solution.py:76
  3.4 0.0 collective-permute-done
  3.4 0.6 collective-permute-start.1
  4.0 0.0 copy-done.4
  4.0 0.1 fusion.refs_0_
  4.1 1.9 %collective-permute-start.2 = (s32[16,64]{1,0:T(8,128)S(1)}, s32[16,64]{1,0:T(8,128)S(1)}, u32[]{:S(2)}, u32[]{:S(2)}) collective-permute-start(s32[16,64]{1,0:T(8,128)S(1)} %fusion.refs_0_), channel_id=1, source_target_pairs={{0,1},{1,0},{2,3},{3,2},{4,5},{5,4},{6,7},{7,6},{8,9},{9,8},{10,11... | collective-permute-start | bytes 12296 | tf_op jit(solution)/shard_map/ppermute | solution.py:374
  6.0 1.7 %collective-permute-done.2.refs_1_ = s32[16,64]{1,0:T(8,128)S(1)} collective-permute-done((s32[16,64]{1,0:T(8,128)S(1)}, s32[16,64]{1,0:T(8,128)S(1)}, u32[]{:S(2)}, u32[]{:S(2)}) %collective-permute-start.2) | collective-permute-done | bytes 4128 | tf_op jit(solution)/shard_map/ppermute | solution.py:374
  7.8 3.9 %collective-permute-start.3 = (s32[32,64]{1,0:T(8,128)S(1)}, s32[32,64]{1,0:T(8,128)S(1)}, u32[]{:S(2)}, u32[]{:S(2)}) collective-permute-start(s32[32,64]{1,0:T(8,128)S(1)} %pad_add_fusion), channel_id=1, source_target_pairs={{0,2},{1,3},{2,0},{3,1},{4,6},{5,7},{6,4},{7,5},{8,10},{9,11},{10,... | collective-permute-start | bytes 24584 | tf_op jit(solution)/shard_map/ppermute | solution.py:375
  11.7 0.0 copy-done.5
  11.7 0.1 copy.11.trip
  11.8 0.0 collective-permute-done.1.far
  11.8 3.9 %gram_a.1.refs_1_ = f32[32,24,128]{2,1,0:T(8,128)S(1)} custom-call(s32[128,3]{1,0:T(8,128)S(1)} %copy.11.trip, f32[2,80,16,128]{3,2,1,0:T(8,128)S(1)} %get-tuple-element.11.near, f32[2,80,16,128]{3,2,1,0:T(8,128)S(1)} %collective-permute-done.1.far, s32[16,64]{1,0:T(8,128)S(1)} %fusion.refs_0_, s32[16,64]{1,0:T(8,128)S(1)} %collective-permute-done.2.refs_1_), custom_call_target="tpu_custom_call" | custom-call | tf_op jit(solution)/shard_map/gram_a/pallas_call | solution.py:164
  15.7 0.0 collective-permute-done.3.refs_0_
  15.7 4.0 %gram_b.1 = f32[64,24,128]{2,1,0:T(8,128)S(1)} custom-call(s32[128,3]{1,0:T(8,128)S(1)} %copy.11.trip, f32[2,80,16,128]{3,2,1,0:T(8,128)S(1)} %get-tuple-element.11.near, f32[2,80,16,128]{3,2,1,0:T(8,128)S(1)} %collective-permute-done.1.far, s32[32,64]{1,0:T(8,128)S(1)} %collective-permute-done.3.refs_0_, f32[32,24,128]{2,1,0:T(8,128)S(1)} %gram_a.1.refs_1_), custom_call_target="tpu_custom_call" | custom-call | tf_op jit(solution)/shard_map/gram_b/pallas_call | solution.py:164
  19.7 0.0 copy-start
  19.7 0.9 %copy-done = f32[64,24,128]{2,1,0:T(8,128)} copy-done((f32[64,24,128]{2,1,0:T(8,128)}, f32[64,24,128]{2,1,0:T(8,128)S(1)}, u32[]{:S(2)}) %copy-start) | copy-done | bytes 786456
  20.6 0.0 copy-start.6
  20.6 0.0 copy-start.7
  20.6 8.8 %all-to-all-start = ((f32[64,24,128]{2,1,0:T(8,128)}), f32[64,24,128]{2,1,0:T(8,128)S(1)}, u32[]{:S(2)}, u32[]{:S(2)}) async-start(f32[64,24,128]{2,1,0:T(8,128)} %copy-done), calls=%async_computation | async-start | bytes 1572864 | tf_op jit(solution)/shard_map/all_to_all | solution.py:378
  29.4 0.0 copy-done.6
  29.4 0.1 copy.10.taper
  29.6 0.0 copy-done.7
  29.6 0.1 pad_maximum_fusion.4.trig
  29.7 12.8 %all-to-all-done.parts = f32[64,24,128]{2,1,0:T(8,128)S(1)} async-done(((f32[64,24,128]{2,1,0:T(8,128)}), f32[64,24,128]{2,1,0:T(8,128)S(1)}, u32[]{:S(2)}, u32[]{:S(2)}) %all-to-all-start) | async-done | bytes 786464 | tf_op jit(solution)/shard_map/all_to_all | solution.py:378
  42.5 4.8 %solve.1 = f32[64,1,128]{2,1,0:T(1,128)S(1)} custom-call(f32[64,24,128]{2,1,0:T(8,128)S(1)} %all-to-all-done.parts, f32[128,3]{1,0:T(8,128)S(1)} %copy.10.taper, f32[32]{0:T(128)S(1)} %pad_maximum_fusion.4.trig), custom_call_target="tpu_custom_call" | custom-call | tf_op jit(solution)/shard_map/solve/pallas_call | solution.py:229
  47.3 14.5 %all_to_all.10.w = f32[64,1,128]{2,1,0:T(1,128)S(1)} all-to-all(f32[64,1,128]{2,1,0:T(1,128)S(1)} %solve.1), channel_id=1, replica_groups={{0,1,2,3,8,9,10,11,16,17,18,19,24,25,26,27,32,33,34,35,40,41,42,43,48,4..., dimensions={0} | all-to-all | bytes 65536 | tf_op jit(solution)/shard_map/all_to_all | solution.py:381
  61.8 0.0 copy-start.3
  61.8 4.5 %power.1 = (f32[4,16,128]{2,1,0:T(8,128)S(1)}, f32[4,16,128]{2,1,0:T(8,128)S(1)}) custom-call(s32[128,3]{1,0:T(8,128)S(1)} %copy.11.trip, f32[2,80,16,128]{3,2,1,0:T(8,128)S(1)} %get-tuple-element.11.near, f32[2,80,16,128]{3,2,1,0:T(8,128)S(1)} %collective-permute-done.1.far, f32[64,1,128]{2,1,0:T(1,128)S(1)} %all_to_all.10.w), custom_call_target="tpu_custom_call" | custom-call | tf_op jit(solution)/shard_map/power/pallas_call | solution.py:289
  66.3 0.1 collective-permute-start.4
  66.4 1.2 %collective-permute-done.4 = f32[4,16,128]{2,1,0:T(8,128)S(1)} collective-permute-done((f32[4,16,128]{2,1,0:T(8,128)S(1)}, f32[4,16,128]{2,1,0:T(8,128)S(1)}, u32[]{:S(2)}, u32[]{:S(2)}) %collective-permute-start.4) | collective-permute-done | bytes 32800 | tf_op jit(solution)/shard_map/ppermute | solution.py:364
  67.6 1.2 %collective-permute-start.7 = (f32[2,16,128]{2,1,0:T(8,128)S(1)}, f32[2,16,128]{2,1,0:T(8,128)S(1)}, u32[]{:S(2)}, u32[]{:S(2)}) collective-permute-start(f32[2,16,128]{2,1,0:T(8,128)S(1)} %pad_maximum_fusion.3), channel_id=1, source_target_pairs={{0,3},{1,2},{2,1},{3,0},{4,7},{5,6},{6,5},{7,4},{8,11},{9,10},{10,... | collective-permute-start | bytes 49160 | tf_op jit(solution)/shard_map/ppermute | solution.py:385
  68.9 1.4 %collective-permute-start.6 = (f32[2,16,128]{2,1,0:T(8,128)S(1)}, f32[2,16,128]{2,1,0:T(8,128)S(1)}, u32[]{:S(2)}, u32[]{:S(2)}) collective-permute-start(f32[2,16,128]{2,1,0:T(8,128)S(1)} %pad_maximum_fusion.2), channel_id=1, source_target_pairs={{0,2},{1,3},{2,0},{3,1},{4,6},{5,7},{6,4},{7,5},{8,10},{9,11},{10,... | collective-permute-start | bytes 49160 | tf_op jit(solution)/shard_map/ppermute | solution.py:385
  70.3 1.5 %collective-permute-start.5 = (f32[2,16,128]{2,1,0:T(8,128)S(1)}, f32[2,16,128]{2,1,0:T(8,128)S(1)}, u32[]{:S(2)}, u32[]{:S(2)}) collective-permute-start(f32[2,16,128]{2,1,0:T(8,128)S(1)} %pad_maximum_fusion.1), channel_id=1, source_target_pairs={{0,1},{1,0},{2,3},{3,2},{4,5},{5,4},{6,7},{7,6},{8,9},{9,8},{10,11... | collective-permute-start | bytes 49160 | tf_op jit(solution)/shard_map/ppermute | solution.py:385
  71.7 0.8 %collective-permute-done.7.p3 = f32[2,16,128]{2,1,0:T(8,128)S(1)} collective-permute-done((f32[2,16,128]{2,1,0:T(8,128)S(1)}, f32[2,16,128]{2,1,0:T(8,128)S(1)}, u32[]{:S(2)}, u32[]{:S(2)}) %collective-permute-start.7) | collective-permute-done | bytes 16416 | tf_op jit(solution)/shard_map/ppermute | solution.py:385
  72.6 1.5 %collective-permute-done.6.p2 = f32[2,16,128]{2,1,0:T(8,128)S(1)} collective-permute-done((f32[2,16,128]{2,1,0:T(8,128)S(1)}, f32[2,16,128]{2,1,0:T(8,128)S(1)}, u32[]{:S(2)}, u32[]{:S(2)}) %collective-permute-start.6) | collective-permute-done | bytes 16416 | tf_op jit(solution)/shard_map/ppermute | solution.py:385
  74.1 0.0 collective-permute-done.5.p1
  74.2 0.1 collective-permute-start.8
  74.3 4.1 %collective-permute-start.9 = (f32[2,16,128]{2,1,0:T(8,128)S(1)}, f32[2,16,128]{2,1,0:T(8,128)S(1)}, u32[]{:S(2)}, u32[]{:S(2)}) collective-permute-start(f32[2,16,128]{2,1,0:T(8,128)S(1)} %get-tuple-element.17), channel_id=1, source_target_pairs={{4,8},{8,4},{12,16},{16,12},{20,24},{24,20},{28,32},{32,28},{36,40... | collective-permute-start | bytes 49160 | tf_op jit(solution)/shard_map/ppermute | solution.py:392
  78.3 0.0 collective-permute-done.8.inner
  78.3 3.1 %collective-permute-done.9.outer = f32[2,16,128]{2,1,0:T(8,128)S(1)} collective-permute-done((f32[2,16,128]{2,1,0:T(8,128)S(1)}, f32[2,16,128]{2,1,0:T(8,128)S(1)}, u32[]{:S(2)}, u32[]{:S(2)}) %collective-permute-start.9) | collective-permute-done | bytes 16416 | tf_op jit(solution)/shard_map/ppermute | solution.py:392
  81.4 0.0 copy-done.2
  81.4 0.0 copy-done.3
  81.4 2.3 %cfar.1 = f32[32,512]{1,0:T(8,128)} custom-call(f32[2,16,128]{2,1,0:T(8,128)S(1)} %get-tuple-element.28.p0, f32[2,16,128]{2,1,0:T(8,128)S(1)} %collective-permute-done.5.p1, f32[2,16,128]{2,1,0:T(8,128)S(1)} %collective-permute-done.6.p2, f32[2,16,128]{2,1,0:T(8,128)S(1)} %collective-permute-done.7.p3, f32[2,16,128]{2,1,0:T(8,128)S(1)} %collective-permute-done.8.inner, ...), custom_call_target="tpu_custom_call" | custom-call | tf_op jit(solution)/shard_map/cfar/pallas_call | solution.py:340
  (10 shorter events, 0.1 us)
Async XLA Ops:
  0.0 3.4 %collective-permute-start = (s32[32,32]{1,0:T(8,128)}, s32[32,32]{1,0:T(8,128)S(1)}, u32[]{:S(2)}, u32[]{:S(2)}) collective-permute-start(s32[32,32]{1,0:T(8,128)} %param.11), channel_id=1, source_target_pairs={{0,4},{4,0},{8,12},{12,8},{16,20},{20,16},{24,28},{28,24},{32,36},... | collective-permute-start | bytes 12296 | tf_op jit(solution)/shard_map/ppermute | solution.py:364
  0.0 1.6 %copy-start.1 = (f32[2,128,16,128]{3,2,1,0:T(8,128)S(1)}, f32[2,128,16,128]{3,2,1,0:T(8,128)}, u32[]{:S(2)}) copy-start(f32[2,128,16,128]{3,2,1,0:T(8,128)} %echo.1) | copy-start | bytes 6291460
  1.6 2.4 %copy-start.4 = (s32[32,32]{1,0:T(8,128)S(1)}, s32[32,32]{1,0:T(8,128)}, u32[]{:S(2)}) copy-start(s32[32,32]{1,0:T(8,128)} %param.11) | copy-start | bytes 12292
  1.6 10.1 %copy-start.5 = (s32[128,3]{0,1:T(4,128)S(1)}, s32[128,3]{0,1:T(4,128)}, u32[]{:S(2)}) copy-start(s32[128,3]{0,1:T(4,128)} %param.8) | copy-start | bytes 4612
  3.4 8.3 %collective-permute-start.1 = (f32[2,80,16,128]{3,2,1,0:T(8,128)}, f32[2,80,16,128]{3,2,1,0:T(8,128)S(1)}, u32[]{:S(2)}, u32[]{:S(2)}) collective-permute-start(f32[2,80,16,128]{3,2,1,0:T(8,128)} %get-tuple-element.13), channel_id=1, source_target_pairs={{0,4},{4,0},{8,12},{12,8},{16,20},{20,16},{24,28},{28,24},{32,36},... | collective-permute-start | bytes 3932168 | tf_op jit(solution)/shard_map/ppermute | solution.py:364
  4.1 3.7 %collective-permute-start.2 = (s32[16,64]{1,0:T(8,128)S(1)}, s32[16,64]{1,0:T(8,128)S(1)}, u32[]{:S(2)}, u32[]{:S(2)}) collective-permute-start(s32[16,64]{1,0:T(8,128)S(1)} %fusion.refs_0_), channel_id=1, source_target_pairs={{0,1},{1,0},{2,3},{3,2},{4,5},{5,4},{6,7},{7,6},{8,9},{9,8},{10,11... | collective-permute-start | bytes 12296 | tf_op jit(solution)/shard_map/ppermute | solution.py:374
  7.8 7.9 %collective-permute-start.3 = (s32[32,64]{1,0:T(8,128)S(1)}, s32[32,64]{1,0:T(8,128)S(1)}, u32[]{:S(2)}, u32[]{:S(2)}) collective-permute-start(s32[32,64]{1,0:T(8,128)S(1)} %pad_add_fusion), channel_id=1, source_target_pairs={{0,2},{1,3},{2,0},{3,1},{4,6},{5,7},{6,4},{7,5},{8,10},{9,11},{10,... | collective-permute-start | bytes 24584 | tf_op jit(solution)/shard_map/ppermute | solution.py:375
  19.7 0.9 %copy-start = (f32[64,24,128]{2,1,0:T(8,128)}, f32[64,24,128]{2,1,0:T(8,128)S(1)}, u32[]{:S(2)}) copy-start(f32[64,24,128]{2,1,0:T(8,128)S(1)} %gram_b.1) | copy-start | bytes 2359300
  20.6 8.9 %copy-start.6 = (f32[128,3]{0,1:T(4,128)S(1)}, f32[128,3]{0,1:T(4,128)}, u32[]{:S(2)}) copy-start(f32[128,3]{0,1:T(4,128)} %param.9) | copy-start | bytes 4612
  20.6 9.0 %copy-start.7 = (f32[16]{0:T(128)S(1)}, f32[16]{0:T(128)}, u32[]{:S(2)}) copy-start(f32[16]{0:T(128)} %param.10) | copy-start | bytes 196
  20.6 21.9 %all-to-all-start = ((f32[64,24,128]{2,1,0:T(8,128)}), f32[64,24,128]{2,1,0:T(8,128)S(1)}, u32[]{:S(2)}, u32[]{:S(2)}) async-start(f32[64,24,128]{2,1,0:T(8,128)} %copy-done), calls=%async_computation | async-start | bytes 1572864 | tf_op jit(solution)/shard_map/all_to_all | solution.py:378
  61.8 19.6 %copy-start.2 = (s32[32]{0:T(128)S(1)}, s32[32]{0:T(128)}, u32[]{:S(2)}) copy-start(s32[32]{0:T(128)} %guard.1) | copy-start | bytes 388
  61.8 19.6 %copy-start.3 = (s32[32]{0:T(128)S(1)}, s32[32]{0:T(128)}, u32[]{:S(2)}) copy-start(s32[32]{0:T(128)} %train.1) | copy-start | bytes 388
  66.3 1.3 %collective-permute-start.4 = (f32[4,16,128]{2,1,0:T(8,128)S(1)}, f32[4,16,128]{2,1,0:T(8,128)S(1)}, u32[]{:S(2)}, u32[]{:S(2)}) collective-permute-start(f32[4,16,128]{2,1,0:T(8,128)S(1)} %get-tuple-element.16), channel_id=1, source_target_pairs={{0,4},{4,0},{8,12},{12,8},{16,20},{20,16},{24,28},{28,24},{32,36},... | collective-permute-start | bytes 98312 | tf_op jit(solution)/shard_map/ppermute | solution.py:364
  67.6 4.9 %collective-permute-start.7 = (f32[2,16,128]{2,1,0:T(8,128)S(1)}, f32[2,16,128]{2,1,0:T(8,128)S(1)}, u32[]{:S(2)}, u32[]{:S(2)}) collective-permute-start(f32[2,16,128]{2,1,0:T(8,128)S(1)} %pad_maximum_fusion.3), channel_id=1, source_target_pairs={{0,3},{1,2},{2,1},{3,0},{4,7},{5,6},{6,5},{7,4},{8,11},{9,10},{10,... | collective-permute-start | bytes 49160 | tf_op jit(solution)/shard_map/ppermute | solution.py:385
  68.9 5.2 %collective-permute-start.6 = (f32[2,16,128]{2,1,0:T(8,128)S(1)}, f32[2,16,128]{2,1,0:T(8,128)S(1)}, u32[]{:S(2)}, u32[]{:S(2)}) collective-permute-start(f32[2,16,128]{2,1,0:T(8,128)S(1)} %pad_maximum_fusion.2), channel_id=1, source_target_pairs={{0,2},{1,3},{2,0},{3,1},{4,6},{5,7},{6,4},{7,5},{8,10},{9,11},{10,... | collective-permute-start | bytes 49160 | tf_op jit(solution)/shard_map/ppermute | solution.py:385
  70.3 3.9 %collective-permute-start.5 = (f32[2,16,128]{2,1,0:T(8,128)S(1)}, f32[2,16,128]{2,1,0:T(8,128)S(1)}, u32[]{:S(2)}, u32[]{:S(2)}) collective-permute-start(f32[2,16,128]{2,1,0:T(8,128)S(1)} %pad_maximum_fusion.1), channel_id=1, source_target_pairs={{0,1},{1,0},{2,3},{3,2},{4,5},{5,4},{6,7},{7,6},{8,9},{9,8},{10,11... | collective-permute-start | bytes 49160 | tf_op jit(solution)/shard_map/ppermute | solution.py:385
  74.2 4.2 %collective-permute-start.8 = (f32[2,16,128]{2,1,0:T(8,128)S(1)}, f32[2,16,128]{2,1,0:T(8,128)S(1)}, u32[]{:S(2)}, u32[]{:S(2)}) collective-permute-start(f32[2,16,128]{2,1,0:T(8,128)S(1)} %broadcast_select_fusion.1), channel_id=1, source_target_pairs={{0,4},{4,0},{8,12},{12,8},{16,20},{20,16},{24,28},{28,24},{32,36},... | collective-permute-start | bytes 49160 | tf_op jit(solution)/shard_map/ppermute | solution.py:364
  74.3 7.2 %collective-permute-start.9 = (f32[2,16,128]{2,1,0:T(8,128)S(1)}, f32[2,16,128]{2,1,0:T(8,128)S(1)}, u32[]{:S(2)}, u32[]{:S(2)}) collective-permute-start(f32[2,16,128]{2,1,0:T(8,128)S(1)} %get-tuple-element.17), channel_id=1, source_target_pairs={{4,8},{8,4},{12,16},{16,12},{20,24},{24,20},{28,32},{32,28},{36,40... | collective-permute-start | bytes 49160 | tf_op jit(solution)/shard_map/ppermute | solution.py:392

commit v5 on v4

--- a/solution.py
+++ b/solution.py
@@ -19,6 +19,7 @@
 YN = 4
 ZN = 4
 WINDOW = 20
+PACKED = ST * ST
 f32 = jnp.float32
 bf16 = jnp.bfloat16
 VMEM_LIMIT = 16 * 2**20
@@ -122,13 +123,22 @@
     lane = iota((ST, GATES), 1)
     low = row >= lane % HALF
     first = lane < HALF
-    first24 = first[:24]
-
-    def store(k, i, value):
-        if second:
-            out[i * ZN + (dop ^ (2 + k))] = value
-        else:
-            out[k * 16 + i] = value
+    lane16 = iota((CH, GATES), 1)
+    mine8 = iota((8, GATES), 1) // 16 == iota((8, GATES), 0)
+
+    def store(k, i, p, at):
+        q = i * ZN + (dop ^ (2 + k)) if second else k * 16 + i
+        p0, p1, p2 = p[:16], p[16:32], p[32:]
+        p0 = p0 if at == 0 else pltpu.roll(p0, GATES - at, 1)
+        p1 = pltpu.roll(p1, (GATES + 48 - at) % GATES, 1)
+        p2 = pltpu.roll(p2, (GATES + 96 - at) % GATES, 1)
+        tail = [pltpu.roll(p2[h : h + 8], 0, 1, stride=16, stride_axis=0) for h in (0, 8)]
+        main = jnp.where(lane16 < 48, p0, jnp.where(lane16 < 96, p1, p2))
+        for j in range(16):
+            out[q, :, j * GATES : (j + 1) * GATES] = main[j : j + 1]
+        for j in range(2):
+            extra = jnp.sum(jnp.where(mine8, tail[j], 0.0), 0, keepdims=True)
+            out[q, :, (16 + j) * GATES : (17 + j) * GATES] = extra
 
     def pair(k, i):
         rha, rla, la = operands(k, i)
@@ -144,9 +154,8 @@
         re = jnp.where(first, ga[:ST], gb[:ST])
         im = jnp.where(first, ga[ST:], gb[ST:])
         p = jnp.where(low, re, im)
-        r = pltpu.roll(p, HALF, 1)
-        store(k, i, jnp.where(first24, p[:24], r[24:]))
-        store(k, i + 1, jnp.where(first24, r[:24], p[24:]))
+        store(k, i, p, 0)
+        store(k, i + 1, p, HALF)
 
     def step(k, c):
         for i in range(0, 16, 2):
@@ -163,7 +172,7 @@
 def gram(second, trip, near, far, extra):
     return pl.pallas_call(
         functools.partial(gram_kernel, second),
-        out_shape=jax.ShapeDtypeStruct((64 if second else 32, 24, GATES), f32),
+        out_shape=jax.ShapeDtypeStruct((64 if second else 32, 1, PACKED), f32),
         in_specs=[SM] + [VM] * 4,
         out_specs=VM,
         scratch_shapes=[pltpu.VMEM((2, 16, 2 * GATES), f32)],
@@ -177,11 +186,13 @@
     b = dop * 32 + core * 16 + lax.axis_index("range") // 2
     row = iota((ST, GATES), 0)
     lane = iota((ST, GATES), 1)
-    total = parts[0]
-    for j in range(1, 64):
-        total = total + parts[j]
-    total = total * (1.0 / TOTAL)
-    p = rows(total, pltpu.roll(total, HALF, 1))
+    line = []
+    for j in range(PACKED // GATES):
+        line.append(jnp.sum(parts[:, 0, j * GATES : (j + 1) * GATES], 0, keepdims=True) * (1.0 / TOTAL))
+    main = rows(*line[:16])
+    corner = rows(*[pltpu.roll(line[16 + j // 8], (GATES + 32 - 16 * (j % 8)) % GATES, 1) for j in range(16)])
+    p2 = jnp.where(lane[:16] < 32, pltpu.roll(main, 32, 1), corner)
+    p = rows(main, pltpu.roll(main, GATES - 48, 1), p2)
     full = rows(p, jnp.zeros((GATES - ST, GATES), f32)).T[:ST]
     re = jnp.where(row >= lane, p, full)
     im = jnp.where(row < lane, p, jnp.where(row == lane, 0.0, -full))

time: 84.3 us -> 82.6 us (0.980)
  waiting for transfers between devices: 21.2 us -> 19.5 us
  Pallas kernels: 21.3 us -> 22.7 us
  local copies, waits for them, and re-layouts: 2.76 us -> 1.89 us
    all_to_all x1, waiting for transfers between devices: 12.8 us -> 11.1 us  [shards(): lax.all_to_all(part, BOTH, 0, 0, tiled=True, axis_index_groups=SAME_CORE)]
    pallas_call x2, Pallas kernels: 7.89 us -> 9.08 us  [gram(): pl.pallas_call(functools.partial(gram_kernel, second), out_shape=jax.Shap...]
    unnamed x18 -> x16, local copies, waits for them, and re-layouts: 2.71 us -> 1.84 us
where the time goes in v5:
time: 82.6 us; the launch traced here: 82.1 us
  starting transfers between devices  23.2 us (28%)
  Pallas kernels  22.7 us (27%)
  waiting for transfers between devices  19.5 us (24%)
  blocking collectives  14.4 us (17%)
  local copies, waits for them, and re-layouts  1.89 us (2%)
    all_to_all x1, blocking collectives, shards(): w = lax.all_to_all(w, BOTH, 0, 0, tiled=True, axis_index_groups=SAME_CORE)  14.4 us
    all_to_all x1, waiting for transfers between devices, shards(): lax.all_to_all(part, BOTH, 0, 0, tiled=True, axis_index_groups=SAME_CORE)  11.1 us
    pallas_call x2, Pallas kernels, gram(): pl.pallas_call(functools.partial(gram_kernel, second), out_shape=jax.Shap...  9.08 us
    all_to_all x1, starting transfers between devices, shards(): lax.all_to_all(part, BOTH, 0, 0, tiled=True, axis_index_groups=SAME_CORE)  8.51 us
    pallas_call x1, Pallas kernels, solve(): pl.pallas_call(solve_kernel, out_shape=jax.ShapeDtypeStruct((64, 1, GATES...  4.98 us
    pallas_call x1, Pallas kernels, power(): pl.pallas_call(power_kernel, out_shape=[jax.ShapeDtypeStruct((ZN, 16, GAT...  4.5 us
    ppermute x3, starting transfers between devices, shards(): lax.ppermute(pieces[k], 'dop', flipped(k))  4.09 us
    ppermute x1, starting transfers between devices, shards(): outer = lax.ppermute(jnp.where(core == 0, head, tail), 'range', pairs)  4.06 us
  transfers between devices with their start and end apart: 11, of which 6 were waited for; matrix products, arithmetic and copies ran while one was open for 1% of the time, Pallas kernels for 7%

profile of v5, /device:TPU:8, one launch (start us, length us, event | category | flops | bytes accessed | tf_op | source)
XLA Modules:
  0.0 82.1 jit_solution(14633439538675804428)
XLA Ops:
  0.0 0.0 collective-permute-start
  0.0 0.0 copy-start
  0.0 1.6 %copy-done = f32[2,128,16,128]{3,2,1,0:T(8,128)S(1)} copy-done((f32[2,128,16,128]{3,2,1,0:T(8,128)S(1)}, f32[2,128,16,128]{3,2,1,0:T(8,128)}, u32[]{:S(2)}) %copy-start) | copy-done | bytes 2097176
  1.6 0.0 copy-start.3
  1.6 0.0 copy-start.4
  1.6 1.8 %pack.1 = (f32[2,80,16,128]{3,2,1,0:T(8,128)S(1)}, f32[2,80,16,128]{3,2,1,0:T(8,128)}) custom-call(f32[2,128,16,128]{3,2,1,0:T(8,128)S(1)} %copy-done), custom_call_target="tpu_custom_call" | custom-call | tf_op jit(solution)/shard_map/pack/pallas_call | solution.py:77
  3.4 0.0 collective-permute-done
  3.4 0.6 collective-permute-start.1
  4.0 0.0 copy-done.3
  4.0 0.1 fusion.refs_0_
  4.1 1.9 %collective-permute-start.2 = (s32[16,64]{1,0:T(8,128)S(1)}, s32[16,64]{1,0:T(8,128)S(1)}, u32[]{:S(2)}, u32[]{:S(2)}) collective-permute-start(s32[16,64]{1,0:T(8,128)S(1)} %fusion.refs_0_), channel_id=1, source_target_pairs={{0,1},{1,0},{2,3},{3,2},{4,5},{5,4},{6,7},{7,6},{8,9},{9,8},{10,11... | collective-permute-start | bytes 12296 | tf_op jit(solution)/shard_map/ppermute | solution.py:385
  6.0 1.7 %collective-permute-done.2.refs_1_ = s32[16,64]{1,0:T(8,128)S(1)} collective-permute-done((s32[16,64]{1,0:T(8,128)S(1)}, s32[16,64]{1,0:T(8,128)S(1)}, u32[]{:S(2)}, u32[]{:S(2)}) %collective-permute-start.2) | collective-permute-done | bytes 4128 | tf_op jit(solution)/shard_map/ppermute | solution.py:385
  7.8 3.9 %collective-permute-start.3 = (s32[32,64]{1,0:T(8,128)S(1)}, s32[32,64]{1,0:T(8,128)S(1)}, u32[]{:S(2)}, u32[]{:S(2)}) collective-permute-start(s32[32,64]{1,0:T(8,128)S(1)} %pad_add_fusion), channel_id=1, source_target_pairs={{0,2},{1,3},{2,0},{3,1},{4,6},{5,7},{6,4},{7,5},{8,10},{9,11},{10,... | collective-permute-start | bytes 24584 | tf_op jit(solution)/shard_map/ppermute | solution.py:386
  11.7 0.0 copy-done.4
  11.7 0.1 copy.11.trip
  11.8 0.0 collective-permute-done.1.far
  11.8 4.1 %gram_a.1.refs_1_ = f32[32,1,2304]{2,1,0:T(1,128)S(1)} custom-call(s32[128,3]{1,0:T(8,128)S(1)} %copy.11.trip, f32[2,80,16,128]{3,2,1,0:T(8,128)S(1)} %get-tuple-element.11.near, f32[2,80,16,128]{3,2,1,0:T(8,128)S(1)} %collective-permute-done.1.far, s32[16,64]{1,0:T(8,128)S(1)} %fusion.refs_0_, s32[16,64]{1,0:T(8,128)S(1)} %collective-permute-done.2.refs_1_), custom_call_target="tpu_custom_call" | custom-call | tf_op jit(solution)/shard_map/gram_a/pallas_call | solution.py:173
  15.9 0.0 copy-start.5
  15.9 0.0 copy-start.6
  15.9 0.0 collective-permute-done.3.refs_0_
  15.9 5.0 %gram_b.1 = f32[64,1,2304]{2,1,0:T(1,128)} custom-call(s32[128,3]{1,0:T(8,128)S(1)} %copy.11.trip, f32[2,80,16,128]{3,2,1,0:T(8,128)S(1)} %get-tuple-element.11.near, f32[2,80,16,128]{3,2,1,0:T(8,128)S(1)} %collective-permute-done.1.far, s32[32,64]{1,0:T(8,128)S(1)} %collective-permute-done.3.refs_0_, f32[32,1,2304]{2,1,0:T(1,128)S(1)} %gram_a.1.refs_1_), custom_call_target="tpu_custom_call" | custom-call | tf_op jit(solution)/shard_map/gram_b/pallas_call | solution.py:173
  20.9 8.5 %all-to-all-start = ((f32[64,1,2304]{2,1,0:T(1,128)}), f32[64,1,2304]{2,1,0:T(1,128)S(1)}, u32[]{:S(2)}, u32[]{:S(2)}) async-start(f32[64,1,2304]{2,1,0:T(1,128)} %gram_b.1), calls=%async_computation | async-start | bytes 1179648 | tf_op jit(solution)/shard_map/all_to_all | solution.py:389
  29.4 0.0 copy-done.5
  29.4 0.1 copy.10.taper
  29.5 0.0 copy-done.6
  29.6 0.1 pad_maximum_fusion.4.trig
  29.7 11.1 %all-to-all-done.parts = f32[64,1,2304]{2,1,0:T(1,128)S(1)} async-done(((f32[64,1,2304]{2,1,0:T(1,128)}), f32[64,1,2304]{2,1,0:T(1,128)S(1)}, u32[]{:S(2)}, u32[]{:S(2)}) %all-to-all-start) | async-done | bytes 589856 | tf_op jit(solution)/shard_map/all_to_all | solution.py:389
  40.8 5.0 %solve.1 = f32[64,1,128]{2,1,0:T(1,128)S(1)} custom-call(f32[64,1,2304]{2,1,0:T(1,128)S(1)} %all-to-all-done.parts, f32[128,3]{1,0:T(8,128)S(1)} %copy.10.taper, f32[32]{0:T(128)S(1)} %pad_maximum_fusion.4.trig), custom_call_target="tpu_custom_call" | custom-call | tf_op jit(solution)/shard_map/solve/pallas_call | solution.py:240
  45.7 14.4 %all_to_all.10.w = f32[64,1,128]{2,1,0:T(1,128)S(1)} all-to-all(f32[64,1,128]{2,1,0:T(1,128)S(1)} %solve.1), channel_id=1, replica_groups={{0,1,2,3,8,9,10,11,16,17,18,19,24,25,26,27,32,33,34,35,40,41,42,43,48,4..., dimensions={0} | all-to-all | bytes 65536 | tf_op jit(solution)/shard_map/all_to_all | solution.py:392
  60.2 0.0 copy-start.1
  60.2 0.0 copy-start.2
  60.2 4.5 %power.1 = (f32[4,16,128]{2,1,0:T(8,128)S(1)}, f32[4,16,128]{2,1,0:T(8,128)S(1)}) custom-call(s32[128,3]{1,0:T(8,128)S(1)} %copy.11.trip, f32[2,80,16,128]{3,2,1,0:T(8,128)S(1)} %get-tuple-element.11.near, f32[2,80,16,128]{3,2,1,0:T(8,128)S(1)} %collective-permute-done.1.far, f32[64,1,128]{2,1,0:T(1,128)S(1)} %all_to_all.10.w), custom_call_target="tpu_custom_call" | custom-call | tf_op jit(solution)/shard_map/power/pallas_call | solution.py:300
  64.7 0.1 collective-permute-start.4
  64.8 1.2 %collective-permute-done.4 = f32[4,16,128]{2,1,0:T(8,128)S(1)} collective-permute-done((f32[4,16,128]{2,1,0:T(8,128)S(1)}, f32[4,16,128]{2,1,0:T(8,128)S(1)}, u32[]{:S(2)}, u32[]{:S(2)}) %collective-permute-start.4) | collective-permute-done | bytes 32800 | tf_op jit(solution)/shard_map/ppermute | solution.py:375
  66.0 1.2 %collective-permute-start.7 = (f32[2,16,128]{2,1,0:T(8,128)S(1)}, f32[2,16,128]{2,1,0:T(8,128)S(1)}, u32[]{:S(2)}, u32[]{:S(2)}) collective-permute-start(f32[2,16,128]{2,1,0:T(8,128)S(1)} %pad_maximum_fusion.3), channel_id=1, source_target_pairs={{0,3},{1,2},{2,1},{3,0},{4,7},{5,6},{6,5},{7,4},{8,11},{9,10},{10,... | collective-permute-start | bytes 49160 | tf_op jit(solution)/shard_map/ppermute | solution.py:396
  67.2 1.4 %collective-permute-start.6 = (f32[2,16,128]{2,1,0:T(8,128)S(1)}, f32[2,16,128]{2,1,0:T(8,128)S(1)}, u32[]{:S(2)}, u32[]{:S(2)}) collective-permute-start(f32[2,16,128]{2,1,0:T(8,128)S(1)} %pad_maximum_fusion.2), channel_id=1, source_target_pairs={{0,2},{1,3},{2,0},{3,1},{4,6},{5,7},{6,4},{7,5},{8,10},{9,11},{10,... | collective-permute-start | bytes 49160 | tf_op jit(solution)/shard_map/ppermute | solution.py:396
  68.6 1.5 %collective-permute-start.5 = (f32[2,16,128]{2,1,0:T(8,128)S(1)}, f32[2,16,128]{2,1,0:T(8,128)S(1)}, u32[]{:S(2)}, u32[]{:S(2)}) collective-permute-start(f32[2,16,128]{2,1,0:T(8,128)S(1)} %pad_maximum_fusion.1), channel_id=1, source_target_pairs={{0,1},{1,0},{2,3},{3,2},{4,5},{5,4},{6,7},{7,6},{8,9},{9,8},{10,11... | collective-permute-start | bytes 49160 | tf_op jit(solution)/shard_map/ppermute | solution.py:396
  70.1 0.8 %collective-permute-done.7.p3 = f32[2,16,128]{2,1,0:T(8,128)S(1)} collective-permute-done((f32[2,16,128]{2,1,0:T(8,128)S(1)}, f32[2,16,128]{2,1,0:T(8,128)S(1)}, u32[]{:S(2)}, u32[]{:S(2)}) %collective-permute-start.7) | collective-permute-done | bytes 16416 | tf_op jit(solution)/shard_map/ppermute | solution.py:396
  71.0 1.5 %collective-permute-done.6.p2 = f32[2,16,128]{2,1,0:T(8,128)S(1)} collective-permute-done((f32[2,16,128]{2,1,0:T(8,128)S(1)}, f32[2,16,128]{2,1,0:T(8,128)S(1)}, u32[]{:S(2)}, u32[]{:S(2)}) %collective-permute-start.6) | collective-permute-done | bytes 16416 | tf_op jit(solution)/shard_map/ppermute | solution.py:396
  72.5 0.0 collective-permute-done.5.p1
  72.5 0.1 collective-permute-start.8
  72.6 4.1 %collective-permute-start.9 = (f32[2,16,128]{2,1,0:T(8,128)S(1)}, f32[2,16,128]{2,1,0:T(8,128)S(1)}, u32[]{:S(2)}, u32[]{:S(2)}) collective-permute-start(f32[2,16,128]{2,1,0:T(8,128)S(1)} %get-tuple-element.17), channel_id=1, source_target_pairs={{4,8},{8,4},{12,16},{16,12},{20,24},{24,20},{28,32},{32,28},{36,40... | collective-permute-start | bytes 49160 | tf_op jit(solution)/shard_map/ppermute | solution.py:403
  76.7 0.0 collective-permute-done.8.inner
  76.7 3.1 %collective-permute-done.9.outer = f32[2,16,128]{2,1,0:T(8,128)S(1)} collective-permute-done((f32[2,16,128]{2,1,0:T(8,128)S(1)}, f32[2,16,128]{2,1,0:T(8,128)S(1)}, u32[]{:S(2)}, u32[]{:S(2)}) %collective-permute-start.9) | collective-permute-done | bytes 16416 | tf_op jit(solution)/shard_map/ppermute | solution.py:403
  79.8 0.0 copy-done.1
  79.8 0.0 copy-done.2
  79.8 2.3 %cfar.1 = f32[32,512]{1,0:T(8,128)} custom-call(f32[2,16,128]{2,1,0:T(8,128)S(1)} %get-tuple-element.28.p0, f32[2,16,128]{2,1,0:T(8,128)S(1)} %collective-permute-done.5.p1, f32[2,16,128]{2,1,0:T(8,128)S(1)} %collective-permute-done.6.p2, f32[2,16,128]{2,1,0:T(8,128)S(1)} %collective-permute-done.7.p3, f32[2,16,128]{2,1,0:T(8,128)S(1)} %collective-permute-done.8.inner, ...), custom_call_target="tpu_custom_call" | custom-call | tf_op jit(solution)/shard_map/cfar/pallas_call | solution.py:351
  (9 shorter events, 0.1 us)
Async XLA Ops:
  0.0 3.4 %collective-permute-start = (s32[32,32]{1,0:T(8,128)}, s32[32,32]{1,0:T(8,128)S(1)}, u32[]{:S(2)}, u32[]{:S(2)}) collective-permute-start(s32[32,32]{1,0:T(8,128)} %param.11), channel_id=1, source_target_pairs={{0,4},{4,0},{8,12},{12,8},{16,20},{20,16},{24,28},{28,24},{32,36},... | collective-permute-start | bytes 12296 | tf_op jit(solution)/shard_map/ppermute | solution.py:375
  0.0 1.6 %copy-start = (f32[2,128,16,128]{3,2,1,0:T(8,128)S(1)}, f32[2,128,16,128]{3,2,1,0:T(8,128)}, u32[]{:S(2)}) copy-start(f32[2,128,16,128]{3,2,1,0:T(8,128)} %echo.1) | copy-start | bytes 6291460
  1.6 2.4 %copy-start.3 = (s32[32,32]{1,0:T(8,128)S(1)}, s32[32,32]{1,0:T(8,128)}, u32[]{:S(2)}) copy-start(s32[32,32]{1,0:T(8,128)} %param.11) | copy-start | bytes 12292
  1.6 10.1 %copy-start.4 = (s32[128,3]{0,1:T(4,128)S(1)}, s32[128,3]{0,1:T(4,128)}, u32[]{:S(2)}) copy-start(s32[128,3]{0,1:T(4,128)} %param.8) | copy-start | bytes 4612
  3.4 8.3 %collective-permute-start.1 = (f32[2,80,16,128]{3,2,1,0:T(8,128)}, f32[2,80,16,128]{3,2,1,0:T(8,128)S(1)}, u32[]{:S(2)}, u32[]{:S(2)}) collective-permute-start(f32[2,80,16,128]{3,2,1,0:T(8,128)} %get-tuple-element.13), channel_id=1, source_target_pairs={{0,4},{4,0},{8,12},{12,8},{16,20},{20,16},{24,28},{28,24},{32,36},... | collective-permute-start | bytes 3932168 | tf_op jit(solution)/shard_map/ppermute | solution.py:375
  4.1 3.7 %collective-permute-start.2 = (s32[16,64]{1,0:T(8,128)S(1)}, s32[16,64]{1,0:T(8,128)S(1)}, u32[]{:S(2)}, u32[]{:S(2)}) collective-permute-start(s32[16,64]{1,0:T(8,128)S(1)} %fusion.refs_0_), channel_id=1, source_target_pairs={{0,1},{1,0},{2,3},{3,2},{4,5},{5,4},{6,7},{7,6},{8,9},{9,8},{10,11... | collective-permute-start | bytes 12296 | tf_op jit(solution)/shard_map/ppermute | solution.py:385
  7.8 8.1 %collective-permute-start.3 = (s32[32,64]{1,0:T(8,128)S(1)}, s32[32,64]{1,0:T(8,128)S(1)}, u32[]{:S(2)}, u32[]{:S(2)}) collective-permute-start(s32[32,64]{1,0:T(8,128)S(1)} %pad_add_fusion), channel_id=1, source_target_pairs={{0,2},{1,3},{2,0},{3,1},{4,6},{5,7},{6,4},{7,5},{8,10},{9,11},{10,... | collective-permute-start | bytes 24584 | tf_op jit(solution)/shard_map/ppermute | solution.py:386
  15.9 13.5 %copy-start.5 = (f32[128,3]{0,1:T(4,128)S(1)}, f32[128,3]{0,1:T(4,128)}, u32[]{:S(2)}) copy-start(f32[128,3]{0,1:T(4,128)} %param.9) | copy-start | bytes 4612
  15.9 13.6 %copy-start.6 = (f32[16]{0:T(128)S(1)}, f32[16]{0:T(128)}, u32[]{:S(2)}) copy-start(f32[16]{0:T(128)} %param.10) | copy-start | bytes 196
  20.9 19.8 %all-to-all-start = ((f32[64,1,2304]{2,1,0:T(1,128)}), f32[64,1,2304]{2,1,0:T(1,128)S(1)}, u32[]{:S(2)}, u32[]{:S(2)}) async-start(f32[64,1,2304]{2,1,0:T(1,128)} %gram_b.1), calls=%async_computation | async-start | bytes 1179648 | tf_op jit(solution)/shard_map/all_to_all | solution.py:389
  60.2 19.6 %copy-start.1 = (s32[32]{0:T(128)S(1)}, s32[32]{0:T(128)}, u32[]{:S(2)}) copy-start(s32[32]{0:T(128)} %guard.1) | copy-start | bytes 388
  60.2 19.6 %copy-start.2 = (s32[32]{0:T(128)S(1)}, s32[32]{0:T(128)}, u32[]{:S(2)}) copy-start(s32[32]{0:T(128)} %train.1) | copy-start | bytes 388
  64.7 1.3 %collective-permute-start.4 = (f32[4,16,128]{2,1,0:T(8,128)S(1)}, f32[4,16,128]{2,1,0:T(8,128)S(1)}, u32[]{:S(2)}, u32[]{:S(2)}) collective-permute-start(f32[4,16,128]{2,1,0:T(8,128)S(1)} %get-tuple-element.16), channel_id=1, source_target_pairs={{0,4},{4,0},{8,12},{12,8},{16,20},{20,16},{24,28},{28,24},{32,36},... | collective-permute-start | bytes 98312 | tf_op jit(solution)/shard_map/ppermute | solution.py:375
  66.0 4.9 %collective-permute-start.7 = (f32[2,16,128]{2,1,0:T(8,128)S(1)}, f32[2,16,128]{2,1,0:T(8,128)S(1)}, u32[]{:S(2)}, u32[]{:S(2)}) collective-permute-start(f32[2,16,128]{2,1,0:T(8,128)S(1)} %pad_maximum_fusion.3), channel_id=1, source_target_pairs={{0,3},{1,2},{2,1},{3,0},{4,7},{5,6},{6,5},{7,4},{8,11},{9,10},{10,... | collective-permute-start | bytes 49160 | tf_op jit(solution)/shard_map/ppermute | solution.py:396
  67.2 5.2 %collective-permute-start.6 = (f32[2,16,128]{2,1,0:T(8,128)S(1)}, f32[2,16,128]{2,1,0:T(8,128)S(1)}, u32[]{:S(2)}, u32[]{:S(2)}) collective-permute-start(f32[2,16,128]{2,1,0:T(8,128)S(1)} %pad_maximum_fusion.2), channel_id=1, source_target_pairs={{0,2},{1,3},{2,0},{3,1},{4,6},{5,7},{6,4},{7,5},{8,10},{9,11},{10,... | collective-permute-start | bytes 49160 | tf_op jit(solution)/shard_map/ppermute | solution.py:396
  68.6 3.9 %collective-permute-start.5 = (f32[2,16,128]{2,1,0:T(8,128)S(1)}, f32[2,16,128]{2,1,0:T(8,128)S(1)}, u32[]{:S(2)}, u32[]{:S(2)}) collective-permute-start(f32[2,16,128]{2,1,0:T(8,128)S(1)} %pad_maximum_fusion.1), channel_id=1, source_target_pairs={{0,1},{1,0},{2,3},{3,2},{4,5},{5,4},{6,7},{7,6},{8,9},{9,8},{10,11... | collective-permute-start | bytes 49160 | tf_op jit(solution)/shard_map/ppermute | solution.py:396
  72.5 4.2 %collective-permute-start.8 = (f32[2,16,128]{2,1,0:T(8,128)S(1)}, f32[2,16,128]{2,1,0:T(8,128)S(1)}, u32[]{:S(2)}, u32[]{:S(2)}) collective-permute-start(f32[2,16,128]{2,1,0:T(8,128)S(1)} %broadcast_select_fusion.1), channel_id=1, source_target_pairs={{0,4},{4,0},{8,12},{12,8},{16,20},{20,16},{24,28},{28,24},{32,36},... | collective-permute-start | bytes 49160 | tf_op jit(solution)/shard_map/ppermute | solution.py:375
  72.6 7.2 %collective-permute-start.9 = (f32[2,16,128]{2,1,0:T(8,128)S(1)}, f32[2,16,128]{2,1,0:T(8,128)S(1)}, u32[]{:S(2)}, u32[]{:S(2)}) collective-permute-start(f32[2,16,128]{2,1,0:T(8,128)S(1)} %get-tuple-element.17), channel_id=1, source_target_pairs={{4,8},{8,4},{12,16},{16,12},{20,24},{24,20},{28,32},{32,28},{36,40... | collective-permute-start | bytes 49160 | tf_op jit(solution)/shard_map/ppermute | solution.py:403

commit v6 on v5

--- a/solution.py
+++ b/solution.py
@@ -81,15 +81,19 @@
         out_specs=[VM] * 2,
         scratch_shapes=[pltpu.SemaphoreType.DMA((6 * ZN,))],
         name="pack",
-        compiler_params=pltpu.CompilerParams(vmem_limit_bytes=VMEM_LIMIT),
+        compiler_params=pltpu.CompilerParams(vmem_limit_bytes=52 * 2**20),
     )(echo)
 
 
-def place(trip, b, t, z, core):
-    return z * WINDOW + ((trip[b, t] - (z * 32 + core * 16) + BINS + 2) & (BINS - 1))
-
-
-def gram_kernel(second, trip, near, far, *refs):
+def places(triplet):
+    core, _ = core_and_dop()
+    mine = lax.dynamic_index_in_dim(triplet.reshape(ZN, 2, 16, SLOTS), core, 1, keepdims=False)
+    group = iota((ZN, 16, SLOTS), 0)
+    where = group * WINDOW + ((mine - (group * 32 + core * 16) + BINS + 2) & (BINS - 1))
+    return where.reshape(ZN * 16 * SLOTS)
+
+
+def gram_kernel(second, place, near, far, *refs):
     masks = refs[: 1 if second else 2]
     done, out, kept = (refs[1], refs[2], refs[3]) if second else (None, refs[2], refs[3])
     core, dop = core_and_dop()
@@ -104,34 +108,35 @@
 
     def operands(k, i):
         z = dop ^ (base + k)
-        b = z * 32 + core * 16 + i
         m = kept[k, pl.ds(i, 1), :]
         mn = jnp.broadcast_to(m[:, :GATES], (CH, GATES)).astype(bf16)
         mf = jnp.broadcast_to(m[:, GATES:], (CH, GATES)).astype(bf16)
-        plain, left, right = [[], []], [[], []], [[], []]
+        hi, lo, left, right, rest, last = [], [], [], [], [], []
         for t in range(SLOTS):
-            s = place(trip, b, t, z, core)
+            s = place[(z * 16 + i) * SLOTS + t]
             un, uf, vn, vf = split(near[0, s]), split(far[0, s]), split(near[1, s]), split(far[1, s])
-            for h in range(2):
-                plain[h].append(lanes(un[h], uf[h], vn[h], vf[h]))
-                a, c, d, e = un[h] * mn, uf[h] * mf, vn[h] * mn, vf[h] * mf
-                left[h].append(lanes(a, c, d, e))
-                right[h].append(lanes(d, e, -a, -c))
-        return plain[0], plain[1], rows(*left[0], *right[0], *left[1], *right[1])
+            hi.append(lanes(un[0], uf[0], vn[0], vf[0]))
+            lo.append(lanes(un[1], uf[1], vn[1], vf[1]))
+            a, c, d, e = un[0] * mn, uf[0] * mf, vn[0] * mn, vf[0] * mf
+            left.append(lanes(a, c, d, e))
+            right.append(lanes(d, e, -a, -c))
+            a, c, d, e = un[1] * mn, uf[1] * mf, vn[1] * mn, vf[1] * mf
+            rest.append(lanes(a, c, d, e))
+            last.append(lanes(d, e, -a, -c))
+        return hi, lo, rows(*left, *right, *rest, *last)
 
     row = iota((ST, GATES), 0)
     lane = iota((ST, GATES), 1)
     low = row >= lane % HALF
+    high = row <= lane % HALF
     first = lane < HALF
     lane16 = iota((CH, GATES), 1)
     mine8 = iota((8, GATES), 1) // 16 == iota((8, GATES), 0)
 
-    def store(k, i, p, at):
+    def store(k, i, p):
         q = i * ZN + (dop ^ (2 + k)) if second else k * 16 + i
-        p0, p1, p2 = p[:16], p[16:32], p[32:]
-        p0 = p0 if at == 0 else pltpu.roll(p0, GATES - at, 1)
-        p1 = pltpu.roll(p1, (GATES + 48 - at) % GATES, 1)
-        p2 = pltpu.roll(p2, (GATES + 96 - at) % GATES, 1)
+        p0, p1 = p[:16], pltpu.roll(p[16:32], 48, 1)
+        p2 = pltpu.roll(p[32:], 96, 1)
         tail = [pltpu.roll(p2[h : h + 8], 0, 1, stride=16, stride_axis=0) for h in (0, 8)]
         main = jnp.where(lane16 < 48, p0, jnp.where(lane16 < 96, p1, p2))
         for j in range(16):
@@ -141,9 +146,9 @@
             out[q, :, (16 + j) * GATES : (17 + j) * GATES] = extra
 
     def pair(k, i):
-        rha, rla, la = operands(k, i)
-        rhb, rlb, lb = operands(k, i + 1)
-        rhs = rows(*rha, zero, *rhb, zero, *rla, zero, *rlb, zero)
+        ha, wa, la = operands(k, i)
+        hb, wb, lb = operands(k, i + 1)
+        rhs = rows(*ha, zero, *hb, zero, *wa, zero, *wb, zero)
         dims = (((1,), (1,)), ((), ()))
         g = lax.dot_general(rows(la, lb), rhs, dims, preferred_element_type=f32)
         ga, gb = g[:192], g[192:]
@@ -154,8 +159,8 @@
         re = jnp.where(first, ga[:ST], gb[:ST])
         im = jnp.where(first, ga[ST:], gb[ST:])
         p = jnp.where(low, re, im)
-        store(k, i, p, 0)
-        store(k, i + 1, p, HALF)
+        store(k, i, p)
+        store(k, i + 1, pltpu.roll(p, HALF, 1))
 
     def step(k, c):
         for i in range(0, 16, 2):
@@ -169,7 +174,7 @@
                 out[i * ZN + (dop ^ k)] = done[k * 16 + i]
 
 
-def gram(second, trip, near, far, extra):
+def gram(second, place, near, far, extra):
     return pl.pallas_call(
         functools.partial(gram_kernel, second),
         out_shape=jax.ShapeDtypeStruct((64 if second else 32, 1, PACKED), f32),
@@ -178,12 +183,10 @@
         scratch_shapes=[pltpu.VMEM((2, 16, 2 * GATES), f32)],
         name="gram_b" if second else "gram_a",
         compiler_params=pltpu.CompilerParams(vmem_limit_bytes=VMEM_LIMIT),
-    )(trip, near, far, *extra)
-
-
-def solve_kernel(parts, taper, trig, out):
-    core, dop = core_and_dop()
-    b = dop * 32 + core * 16 + lax.axis_index("range") // 2
+    )(place, near, far, *extra)
+
+
+def solve_kernel(parts, sr, si, out):
     row = iota((ST, GATES), 0)
     lane = iota((ST, GATES), 1)
     line = []
@@ -196,16 +199,8 @@
     full = rows(p, jnp.zeros((GATES - ST, GATES), f32)).T[:ST]
     re = jnp.where(row >= lane, p, full)
     im = jnp.where(row < lane, p, jnp.where(row == lane, 0.0, -full))
-    chan = iota((CH, GATES), 0)
-    cosine = jnp.zeros((CH, GATES), f32)
-    sine = jnp.zeros((CH, GATES), f32)
-    for j in range(CH):
-        cosine = jnp.where(chan == j, trig[j], cosine)
-        sine = jnp.where(chan == j, trig[CH + j], sine)
-    sr = rows(*[taper[b, t] * cosine for t in range(SLOTS)])
-    si = rows(*[taper[b, t] * sine for t in range(SLOTS)])
-    are = jnp.where(lane < ST, re, sr)
-    aim = jnp.where(lane < ST, im, si)
+    are = jnp.where(lane < ST, re, sr[...])
+    aim = jnp.where(lane < ST, im, si[...])
     for k in range(0, ST, 2):
         i0 = jnp.full((ST, GATES), k, jnp.int32)
         i1 = jnp.full((ST, GATES), k + 1, jnp.int32)
@@ -236,18 +231,18 @@
         out[j] = w
 
 
-def solve(parts, taper, trig):
+def solve(parts, sr, si):
     return pl.pallas_call(
         solve_kernel,
         out_shape=jax.ShapeDtypeStruct((64, 1, GATES), f32),
-        in_specs=[VM, SM, SM],
+        in_specs=[VM] * 3,
         out_specs=VM,
         name="solve",
         compiler_params=pltpu.CompilerParams(vmem_limit_bytes=VMEM_LIMIT),
-    )(parts, taper, trig)
-
-
-def power_kernel(trip, near, far, w, own, other):
+    )(parts, sr, si)
+
+
+def power_kernel(place, near, far, w, out, edge):
     core, dop = core_and_dop()
     zero = jnp.zeros((32, 2 * GATES), bf16)
     row = iota((8, GATES), 0)
@@ -255,7 +250,6 @@
 
     def one(k, i):
         z = dop ^ k
-        b = z * 32 + core * 16 + i
         wt = jnp.broadcast_to(w[i * ZN + z], (8, GATES))
         turned = jnp.where(
             lane < ST,
@@ -271,7 +265,7 @@
         rhs = [[], [], []]
         for p in range(2):
             for t in range(SLOTS):
-                s = place(trip, b, t, z, core)
+                s = place[(z * 16 + i) * SLOTS + t]
                 x = lanes(near[p, s], far[p, s])
                 hi, rest = split(x)
                 x = x - hi.astype(f32)
@@ -289,42 +283,75 @@
         i = (j % 2) * 8
         y = rows(*[one(k, i + n) for n in range(8)])
         at = pl.ds(pl.multiple_of(i, 8), 8)
-        own[k, at, :] = y[:, :GATES]
-        other[k, at, :] = y[:, GATES:]
+        mine, away = y[:, :GATES], y[:, GATES:]
+        out[k, 0, at, :] = mine
+        out[k, 1, at, :] = away
+        edge[k ^ 3, at, :] = jnp.where((dop == 3) == (core == 1), mine, away)
         return c
 
     lax.fori_loop(0, 8, step, 0)
 
 
-def power(trip, near, far, w):
+def power(place, near, far, w):
     return pl.pallas_call(
         power_kernel,
-        out_shape=[jax.ShapeDtypeStruct((ZN, 16, GATES), f32)] * 2,
+        out_shape=[
+            jax.ShapeDtypeStruct((ZN, 2, 16, GATES), f32),
+            jax.ShapeDtypeStruct((ZN, 16, GATES), f32),
+        ],
         in_specs=[SM] + [VM] * 3,
         out_specs=[VM] * 2,
         name="power",
         compiler_params=pltpu.CompilerParams(vmem_limit_bytes=VMEM_LIMIT),
-    )(trip, near, far, w)
-
-
-def cfar_kernel(p0, p1, p2, p3, inner, outer, guard, train, out, line):
+    )(place, near, far, w)
+
+
+def chosen(refs, slot, index):
+    value = refs[0][slot]
+    for k in range(1, ZN):
+        value = jnp.where(index == k, refs[k][slot], value)
+    return value
+
+
+def leave_kernel(r0, r1, r2, r3, out):
+    core, dop = core_and_dop()
+    refs = (r0, r1, r2, r3)
+    for k in range(ZN):
+        out[k] = refs[k][1]
+    index = dop ^ (3 * (1 - core))
+    out[4] = chosen(refs, 0, index)
+    out[5] = chosen(refs, 2, index)
+
+
+def leave(pieces):
+    return pl.pallas_call(
+        leave_kernel,
+        out_shape=jax.ShapeDtypeStruct((6, 16, GATES), f32),
+        in_specs=[VM] * 4,
+        out_specs=VM,
+        name="leave",
+        compiler_params=pltpu.CompilerParams(vmem_limit_bytes=VMEM_LIMIT),
+    )(*pieces)
+
+
+def cfar_kernel(r0, r1, r2, r3, came, guard, train, out, line):
     core, dop = core_and_dop()
     rank = lax.axis_index("range")
     width = 6 * GATES
-    for k, ref in enumerate((p0, p1, p2, p3)):
+    refs = (r0, r1, r2, r3)
+    for k in range(ZN):
         at = 1 + (dop ^ k)
-        line[at, core] = ref[0]
-        line[at, 1 - core] = ref[1]
-    for at, ref in ((5 * (1 - core), inner), (5 * core, outer)):
-        line[at, 1 - core] = ref[0]
-        line[at, core] = ref[1]
+        line[at, core] = refs[k][0]
+        line[at, 1 - core] = came[k]
+    index = dop ^ (3 * core)
+    inner, outer = 5 * (1 - core), 5 * core
+    line[inner, core] = chosen(refs, 1, index)
+    line[inner, 1 - core] = came[4]
+    line[outer, core] = chosen(refs, 2, index)
+    line[outer, 1 - core] = came[5]
     p = lanes(*[rows(line[j, 0], line[j, 1]) for j in range(6)])
-    row = iota((32, 1), 0)
-    g = jnp.zeros((32, 1), jnp.int32)
-    t = jnp.zeros((32, 1), jnp.int32)
-    for j in range(32):
-        g = jnp.where(row == j, guard[j], g)
-        t = jnp.where(row == j, train[j], t)
+    g = guard[:, :1]
+    t = train[:, :1]
     total = p
     acc = jnp.where((t & 1) == 1, p, 0.0)
     for k in range(1, 7):
@@ -347,16 +374,16 @@
     out[...] = p[:, lo:hi] / (noise + EPS)
 
 
-def cfar(pieces, inner, outer, guard, train):
+def cfar(pieces, came, guard, train):
     return pl.pallas_call(
         cfar_kernel,
         out_shape=jax.ShapeDtypeStruct((32, 4 * GATES), f32),
-        in_specs=[VM] * 6 + [SM] * 2,
+        in_specs=[VM] * 7,
         out_specs=VM,
         scratch_shapes=[pltpu.VMEM((6, 2, 16, GATES), f32)],
         name="cfar",
         compiler_params=pltpu.CompilerParams(vmem_limit_bytes=VMEM_LIMIT),
-    )(*pieces, inner, outer, guard, train)
+    )(*pieces, came, guard, train)
 
 
 BOTH = ("range", "dop")
@@ -375,8 +402,20 @@
     return lax.ppermute(value, "range", CORE_SWAP)
 
 
+def steering(bin_taper, phases):
+    core, dop = core_and_dop()
+    b = dop * 32 + core * 16 + lax.axis_index("range") // 2
+    taper = lax.dynamic_index_in_dim(bin_taper, b, 0, keepdims=False)
+
+    def lay(values):
+        return jnp.broadcast_to((taper[:, None] * values[None, :]).reshape(ST, 1), (ST, GATES))
+
+    return lay(jnp.cos(phases)), lay(jnp.sin(phases))
+
+
 def shards(echoes, triplet, bin_taper, phases, excluded, guard_len, train_len):
     core, dop = core_and_dop()
+    place = places(triplet)
     other = swap(excluded)
     near, far = pack(echoes)
     far, other = lax.optimization_barrier((far, other))
@@ -384,24 +423,30 @@
     mine = lax.dynamic_slice_in_dim(lanes(excluded, other), core * 16, 16, 0)
     m1 = lax.ppermute(mine, "dop", flipped(1))
     m2 = lax.ppermute(rows(mine, m1), "dop", flipped(2))
-    part = gram(False, triplet, near, far, [mine, m1])
-    part = gram(True, triplet, near, far, [m2, part])
+    part = gram(False, place, near, far, [mine, m1])
+    part = gram(True, place, near, far, [m2, part])
     part = lax.all_to_all(part, BOTH, 0, 0, tiled=True, axis_index_groups=SAME_CORE)
-    trig = jnp.concatenate([jnp.cos(phases), jnp.sin(phases)])
-    w = solve(part, bin_taper, trig)
+    sr, si = steering(bin_taper, phases)
+    guard = jnp.broadcast_to(guard_len[:, None], (32, GATES))
+    train = jnp.broadcast_to(train_len[:, None], (32, GATES))
+    sr, si, guard, train = lax.optimization_barrier((sr, si, guard, train))
+    w = solve(part, sr, si)
     w = lax.all_to_all(w, BOTH, 0, 0, tiled=True, axis_index_groups=SAME_CORE)
-    own, away = power(triplet, near, far, w)
-    came = swap(away)
-    pieces = [jnp.stack([own[k], came[k]]) for k in range(ZN)]
+    pw, edge = power(place, near, far, w)
+    chips = lax.axis_size("range") // 2
+    pairs = []
+    for chip in range(chips):
+        for c in range(2):
+            here = (chip * 2 + c) * ZN
+            if chip + 1 < chips:
+                pairs.append((here + ZN - 1, here + 2 * ZN))
+            if chip > 0:
+                pairs.append((here, here - ZN - 1))
+    edge = lax.ppermute(edge, BOTH, pairs)
+    pieces = [jnp.concatenate([pw[k], edge[k : k + 1]]) for k in range(ZN)]
     pieces = [pieces[0]] + [lax.ppermute(pieces[k], "dop", flipped(k)) for k in (1, 2, 3)]
-    p0, p1, p2, p3 = pieces
-    ranges = lax.axis_size("range")
-    tail = jnp.where(dop == 0, p3, jnp.where(dop == 1, p2, jnp.where(dop == 2, p1, p0)))
-    head = jnp.where(dop == 0, p0, jnp.where(dop == 1, p1, jnp.where(dop == 2, p2, p3)))
-    inner = swap(jnp.where(core == 0, tail, head))
-    pairs = [(i, i + 1 if i % 2 else i - 1) for i in range(1, ranges - 1)]
-    outer = lax.ppermute(jnp.where(core == 0, head, tail), "range", pairs)
-    return cfar(pieces, inner, outer, guard_len, train_len)
+    came = swap(leave(pieces))
+    return cfar(pieces, came, guard, train)
 
 
 def solution(mesh):

time: 82.6 us -> 80.5 us (0.975)
  Pallas kernels: 22.7 us -> 18.1 us
  starting transfers between devices: 23.2 us -> 24.8 us
    pallas_call x2, Pallas kernels: 9.08 us -> 6.46 us  [gram(): pl.pallas_call(functools.partial(gram_kernel, second), out_shape=jax.Shap...]
    ppermute x1, waiting for transfers between devices: 3.09 us -> 5.35 us  [shards(): edge = lax.ppermute(edge, BOTH, pairs)]
    pallas_call x1, Pallas kernels: 4.98 us -> 3.37 us  [solve(): pl.pallas_call(solve_kernel, out_shape=jax.ShapeDtypeStruct((64, 1, GATES...]
    pallas_call x1, Pallas kernels: 1.82 us -> 3 us  [pack(): pl.pallas_call(pack_kernel, out_shape=[jax.ShapeDtypeStruct((2, ZN * WIND...]
    pallas_call x1 -> x2, Pallas kernels: 4.5 us -> 3.46 us  [the longest x1 3.45 us: power(): pl.pallas_call(power_kernel, out_shape=[jax.ShapeDtypeStruct((ZN, 2, 16,...]
    all_to_all x1, starting transfers between devices: 8.51 us -> 9.5 us  [shards(): lax.all_to_all(part, BOTH, 0, 0, tiled=True, axis_index_groups=SAME_CORE)]
    all_to_all x1, waiting for transfers between devices: 11.1 us -> 10.1 us  [shards(): lax.all_to_all(part, BOTH, 0, 0, tiled=True, axis_index_groups=SAME_CORE)]
    unnamed x16 -> x15, local copies, waits for them, and re-layouts: 1.84 us -> 0.95 us
  transfers between devices with their start and end apart: 11 -> 10, of which waited for: 6 -> 7; matrix products, arithmetic and copies ran while one was open for 1% -> 2% of each run, Pallas kernels for 7% -> 8%
where the time goes in v6:
time: 80.5 us; the launch traced here: 79.9 us
  starting transfers between devices  24.8 us (31%)
  waiting for transfers between devices  19.8 us (25%)
  Pallas kernels  18.1 us (22%)
  blocking collectives  14.4 us (18%)
  local copies, waits for them, and re-layouts  2.28 us (3%)
    all_to_all x1, blocking collectives, shards(): w = lax.all_to_all(w, BOTH, 0, 0, tiled=True, axis_index_groups=SAME_CORE)  14.4 us
    all_to_all x1, waiting for transfers between devices, shards(): lax.all_to_all(part, BOTH, 0, 0, tiled=True, axis_index_groups=SAME_CORE)  10.1 us
    all_to_all x1, starting transfers between devices, shards(): lax.all_to_all(part, BOTH, 0, 0, tiled=True, axis_index_groups=SAME_CORE)  9.5 us
    pallas_call x2, Pallas kernels, gram(): pl.pallas_call(functools.partial(gram_kernel, second), out_shape=jax.Shap...  6.46 us
    ppermute x1, waiting for transfers between devices, shards(): edge = lax.ppermute(edge, BOTH, pairs)  5.35 us
    ppermute x1, starting transfers between devices, shards(): edge = lax.ppermute(edge, BOTH, pairs)  4.66 us
    ppermute x3, starting transfers between devices, shards(): lax.ppermute(pieces[k], 'dop', flipped(k))  4.06 us
    ppermute x1, starting transfers between devices, shards(): m2 = lax.ppermute(rows(mine, m1), 'dop', flipped(2))  3.88 us
  transfers between devices with their start and end apart: 10, of which 7 were waited for; matrix products, arithmetic and copies ran while one was open for 2% of the time, Pallas kernels for 8%

profile of v6, /device:TPU:8, one launch (start us, length us, event | category | flops | bytes accessed | tf_op | source)
XLA Modules:
  0.0 79.9 jit_solution(15971598402988619910)
XLA Ops:
  0.0 0.1 collective-permute-start
  0.1 3.0 %pack.1 = (f32[2,80,16,128]{3,2,1,0:T(8,128)S(1)}, f32[2,80,16,128]{3,2,1,0:T(8,128)}) custom-call(f32[2,128,16,128]{3,2,1,0:T(8,128)} %echo.1), custom_call_target="tpu_custom_call" | custom-call | tf_op jit(solution)/shard_map/pack/pallas_call | solution.py:77
  3.1 0.0 collective-permute-done
  3.1 0.6 collective-permute-start.1
  3.7 0.1 reshape.43
  3.8 0.0 copy-done.2
  3.8 0.1 fusion.refs_0_
  3.9 1.9 %collective-permute-start.2 = (s32[16,64]{1,0:T(8,128)S(1)}, s32[16,64]{1,0:T(8,128)S(1)}, u32[]{:S(2)}, u32[]{:S(2)}) collective-permute-start(s32[16,64]{1,0:T(8,128)S(1)} %fusion.refs_0_), channel_id=1, source_target_pairs={{0,1},{1,0},{2,3},{3,2},{4,5},{5,4},{6,7},{7,6},{8,9},{9,8},{10,11... | collective-permute-start | bytes 12296 | tf_op jit(solution)/shard_map/ppermute | solution.py:424
  5.8 0.1 copy.9
  5.9 0.1 squeeze.18
  6.1 0.1 iota.18
  6.2 0.1 iota.19
  6.3 0.1 iota.15
  6.4 0.1 iota.16
  6.5 1.1 %collective-permute-done.2.refs_1_ = s32[16,64]{1,0:T(8,128)S(1)} collective-permute-done((s32[16,64]{1,0:T(8,128)S(1)}, s32[16,64]{1,0:T(8,128)S(1)}, u32[]{:S(2)}, u32[]{:S(2)}) %collective-permute-start.2) | collective-permute-done | bytes 4128 | tf_op jit(solution)/shard_map/ppermute | solution.py:424
  7.6 3.9 %collective-permute-start.3 = (s32[32,64]{1,0:T(8,128)S(1)}, s32[32,64]{1,0:T(8,128)S(1)}, u32[]{:S(2)}, u32[]{:S(2)}) collective-permute-start(s32[32,64]{1,0:T(8,128)S(1)} %pad_add_fusion), channel_id=1, source_target_pairs={{0,2},{1,3},{2,0},{3,1},{4,6},{5,7},{6,4},{7,5},{8,10},{9,11},{10,... | collective-permute-start | bytes 24584 | tf_op jit(solution)/shard_map/ppermute | solution.py:425
  11.5 0.0 collective-permute-done.1.far
  11.5 3.2 %gram_a.1.refs_1_ = f32[32,1,2304]{2,1,0:T(1,128)S(1)} custom-call(s32[192]{0:T(256)S(1)} %and_add_fusion.place, f32[2,80,16,128]{3,2,1,0:T(8,128)S(1)} %get-tuple-element.15.near, f32[2,80,16,128]{3,2,1,0:T(8,128)S(1)} %collective-permute-done.1.far, s32[16,64]{1,0:T(8,128)S(1)} %fusion.refs_0_, s32[16,64]{1,0:T(8,128)S(1)} %collective-permute-done.2.refs_1_), custom_call_target="tpu_custom_call" | custom-call | tf_op jit(solution)/shard_map/gram_a/pallas_call | solution.py:178
  14.7 0.0 copy-start.6
  14.7 0.0 copy-start.4
  14.7 0.0 copy-start.5
  14.7 0.0 collective-permute-done.3.refs_0_
  14.7 3.2 %gram_b.1 = f32[64,1,2304]{2,1,0:T(1,128)S(1)} custom-call(s32[192]{0:T(256)S(1)} %and_add_fusion.place, f32[2,80,16,128]{3,2,1,0:T(8,128)S(1)} %get-tuple-element.15.near, f32[2,80,16,128]{3,2,1,0:T(8,128)S(1)} %collective-permute-done.1.far, s32[32,64]{1,0:T(8,128)S(1)} %collective-permute-done.3.refs_0_, f32[32,1,2304]{2,1,0:T(1,128)S(1)} %gram_a.1.refs_1_), custom_call_target="tpu_custom_call" | custom-call | tf_op jit(solution)/shard_map/gram_b/pallas_call | solution.py:178
  18.0 0.8 %copy-done.1 = f32[64,1,2304]{2,1,0:T(1,128)} copy-done((f32[64,1,2304]{2,1,0:T(1,128)}, f32[64,1,2304]{2,1,0:T(1,128)S(1)}, u32[]{:S(2)}) %copy-start.1) | copy-done | bytes 589848
  18.8 9.5 %all-to-all-start = ((f32[64,1,2304]{2,1,0:T(1,128)}), f32[64,1,2304]{2,1,0:T(1,128)S(1)}, u32[]{:S(2)}, u32[]{:S(2)}) async-start(f32[64,1,2304]{2,1,0:T(1,128)} %copy-done.1), calls=%async_computation | async-start | bytes 1179648 | tf_op jit(solution)/shard_map/all_to_all | solution.py:428
  28.4 0.2 dynamic-slice_reduce_fusion
  28.6 0.1 broadcast_multiply_fusion
  28.7 0.1 mul.72
  28.7 0.1 mul.75
  28.8 0.1 broadcast_in_dim.8.sr
  28.9 0.1 broadcast_in_dim.9.si
  29.0 0.1 broadcast_in_dim.10.guard
  29.0 0.1 broadcast_in_dim.11.train
  29.1 10.1 %all-to-all-done.parts = f32[64,1,2304]{2,1,0:T(1,128)S(1)} async-done(((f32[64,1,2304]{2,1,0:T(1,128)}), f32[64,1,2304]{2,1,0:T(1,128)S(1)}, u32[]{:S(2)}, u32[]{:S(2)}) %all-to-all-start) | async-done | bytes 589856 | tf_op jit(solution)/shard_map/all_to_all | solution.py:428
  39.2 3.4 %solve.1 = f32[64,1,128]{2,1,0:T(1,128)S(1)} custom-call(f32[64,1,2304]{2,1,0:T(1,128)S(1)} %all-to-all-done.parts, f32[48,128]{1,0:T(8,128)S(1)} %broadcast_in_dim.8.sr, f32[48,128]{1,0:T(8,128)S(1)} %broadcast_in_dim.9.si), custom_call_target="tpu_custom_call" | custom-call | tf_op jit(solution)/shard_map/solve/pallas_call | solution.py:235
  42.6 14.4 %all_to_all.10.w = f32[64,1,128]{2,1,0:T(1,128)S(1)} all-to-all(f32[64,1,128]{2,1,0:T(1,128)S(1)} %solve.1), channel_id=1, replica_groups={{0,1,2,3,8,9,10,11,16,17,18,19,24,25,26,27,32,33,34,35,40,41,42,43,48,4..., dimensions={0} | all-to-all | bytes 65536 | tf_op jit(solution)/shard_map/all_to_all | solution.py:434
  57.1 3.4 %power.1 = (f32[4,2,16,128]{3,2,1,0:T(8,128)S(1)}, f32[4,16,128]{2,1,0:T(8,128)S(1)}) custom-call(s32[192]{0:T(256)S(1)} %and_add_fusion.place, f32[2,80,16,128]{3,2,1,0:T(8,128)S(1)} %get-tuple-element.15.near, f32[2,80,16,128]{3,2,1,0:T(8,128)S(1)} %collective-permute-done.1.far, f32[64,1,128]{2,1,0:T(1,128)S(1)} %all_to_all.10.w), custom_call_target="tpu_custom_call" | custom-call | tf_op jit(solution)/shard_map/power/pallas_call | solution.py:296
  60.5 4.7 %collective-permute-start.4 = (f32[4,16,128]{2,1,0:T(8,128)S(1)}, f32[4,16,128]{2,1,0:T(8,128)S(1)}, u32[]{:S(2)}, u32[]{:S(2)}) collective-permute-start(f32[4,16,128]{2,1,0:T(8,128)S(1)} %get-tuple-element.22), channel_id=1, source_target_pairs={{3,8},{7,12},{11,16},{8,3},{15,20},{12,7},{19,24},{16,11},{23,28},... | collective-permute-start | bytes 98312 | tf_op jit(solution)/shard_map/ppermute | solution.py:445
  65.2 5.3 %collective-permute-done.4 = f32[4,16,128]{2,1,0:T(8,128)S(1)} collective-permute-done((f32[4,16,128]{2,1,0:T(8,128)S(1)}, f32[4,16,128]{2,1,0:T(8,128)S(1)}, u32[]{:S(2)}, u32[]{:S(2)}) %collective-permute-start.4) | collective-permute-done | bytes 32800 | tf_op jit(solution)/shard_map/ppermute | solution.py:445
  70.6 0.0 collective-permute-start.7
  70.6 0.1 collective-permute-start.6
  70.7 4.0 %collective-permute-start.5 = (f32[3,16,128]{2,1,0:T(8,128)S(1)}, f32[3,16,128]{2,1,0:T(8,128)S(1)}, u32[]{:S(2)}, u32[]{:S(2)}) collective-permute-start(f32[3,16,128]{2,1,0:T(8,128)S(1)} %pad_maximum_fusion.1), channel_id=1, source_target_pairs={{0,1},{1,0},{2,3},{3,2},{4,5},{5,4},{6,7},{7,6},{8,9},{9,8},{10,11... | collective-permute-start | bytes 73736 | tf_op jit(solution)/shard_map/ppermute | solution.py:447
  74.7 0.9 %collective-permute-done.7.r3 = f32[3,16,128]{2,1,0:T(8,128)S(1)} collective-permute-done((f32[3,16,128]{2,1,0:T(8,128)S(1)}, f32[3,16,128]{2,1,0:T(8,128)S(1)}, u32[]{:S(2)}, u32[]{:S(2)}) %collective-permute-start.7) | collective-permute-done | bytes 24608 | tf_op jit(solution)/shard_map/ppermute | solution.py:447
  75.6 0.4 collective-permute-done.6.r2
  76.0 0.7 collective-permute-done.5.r1
  76.7 0.1 collective-permute-start.8
  76.8 1.2 %collective-permute-done.8.came = f32[6,16,128]{2,1,0:T(8,128)S(1)} collective-permute-done((f32[6,16,128]{2,1,0:T(8,128)S(1)}, f32[6,16,128]{2,1,0:T(8,128)S(1)}, u32[]{:S(2)}, u32[]{:S(2)}) %collective-permute-start.8) | collective-permute-done | bytes 49184 | tf_op jit(solution)/shard_map/ppermute | solution.py:402
  78.0 1.8 %cfar.1 = f32[32,512]{1,0:T(8,128)} custom-call(f32[3,16,128]{2,1,0:T(8,128)S(1)} %pad_maximum_fusion.r0, f32[3,16,128]{2,1,0:T(8,128)S(1)} %collective-permute-done.5.r1, f32[3,16,128]{2,1,0:T(8,128)S(1)} %collective-permute-done.6.r2, f32[3,16,128]{2,1,0:T(8,128)S(1)} %collective-permute-done.7.r3, f32[6,16,128]{2,1,0:T(8,128)S(1)} %collective-permute-done.8.came, ...), custom_call_target="tpu_custom_call" | custom-call | tf_op jit(solution)/shard_map/cfar/pallas_call | solution.py:378
  (22 shorter events, 0.1 us)
Async XLA Ops:
  0.0 28.3 %copy-start = (f32[128,3]{0,1:T(4,128)S(1)}, f32[128,3]{0,1:T(4,128)}, u32[]{:S(2)}) copy-start(f32[128,3]{0,1:T(4,128)} %param.9) | copy-start | bytes 4612
  0.0 3.8 %copy-start.2 = (s32[32,32]{1,0:T(8,128)S(1)}, s32[32,32]{1,0:T(8,128)}, u32[]{:S(2)}) copy-start(s32[32,32]{1,0:T(8,128)} %param.11) | copy-start | bytes 12292
  0.0 3.7 %copy-start.3 = (s32[128,3]{0,1:T(4,128)S(1)}, s32[128,3]{0,1:T(4,128)}, u32[]{:S(2)}) copy-start(s32[128,3]{0,1:T(4,128)} %param.8) | copy-start | bytes 4612
  0.0 3.1 %collective-permute-start = (s32[32,32]{1,0:T(8,128)}, s32[32,32]{1,0:T(8,128)S(1)}, u32[]{:S(2)}, u32[]{:S(2)}) collective-permute-start(s32[32,32]{1,0:T(8,128)} %param.11), channel_id=1, source_target_pairs={{0,4},{4,0},{8,12},{12,8},{16,20},{20,16},{24,28},{28,24},{32,36},... | collective-permute-start | bytes 12296 | tf_op jit(solution)/shard_map/ppermute | solution.py:402
  3.1 8.3 %collective-permute-start.1 = (f32[2,80,16,128]{3,2,1,0:T(8,128)}, f32[2,80,16,128]{3,2,1,0:T(8,128)S(1)}, u32[]{:S(2)}, u32[]{:S(2)}) collective-permute-start(f32[2,80,16,128]{3,2,1,0:T(8,128)} %get-tuple-element.17), channel_id=1, source_target_pairs={{0,4},{4,0},{8,12},{12,8},{16,20},{20,16},{24,28},{28,24},{32,36},... | collective-permute-start | bytes 3932168 | tf_op jit(solution)/shard_map/ppermute | solution.py:402
  3.9 3.7 %collective-permute-start.2 = (s32[16,64]{1,0:T(8,128)S(1)}, s32[16,64]{1,0:T(8,128)S(1)}, u32[]{:S(2)}, u32[]{:S(2)}) collective-permute-start(s32[16,64]{1,0:T(8,128)S(1)} %fusion.refs_0_), channel_id=1, source_target_pairs={{0,1},{1,0},{2,3},{3,2},{4,5},{5,4},{6,7},{7,6},{8,9},{9,8},{10,11... | collective-permute-start | bytes 12296 | tf_op jit(solution)/shard_map/ppermute | solution.py:424
  7.6 7.1 %collective-permute-start.3 = (s32[32,64]{1,0:T(8,128)S(1)}, s32[32,64]{1,0:T(8,128)S(1)}, u32[]{:S(2)}, u32[]{:S(2)}) collective-permute-start(s32[32,64]{1,0:T(8,128)S(1)} %pad_add_fusion), channel_id=1, source_target_pairs={{0,2},{1,3},{2,0},{3,1},{4,6},{5,7},{6,4},{7,5},{8,10},{9,11},{10,... | collective-permute-start | bytes 24584 | tf_op jit(solution)/shard_map/ppermute | solution.py:425
  14.7 13.8 %copy-start.6 = (f32[16]{0:T(128)S(1)}, f32[16]{0:T(128)}, u32[]{:S(2)}) copy-start(f32[16]{0:T(128)} %param.10) | copy-start | bytes 196
  14.7 14.3 %copy-start.4 = (s32[32]{0:T(128)S(1)}, s32[32]{0:T(128)}, u32[]{:S(2)}) copy-start(s32[32]{0:T(128)} %param.12) | copy-start | bytes 388
  14.7 14.3 %copy-start.5 = (s32[32]{0:T(128)S(1)}, s32[32]{0:T(128)}, u32[]{:S(2)}) copy-start(s32[32]{0:T(128)} %param.13) | copy-start | bytes 388
  18.0 0.8 %copy-start.1 = (f32[64,1,2304]{2,1,0:T(1,128)}, f32[64,1,2304]{2,1,0:T(1,128)S(1)}, u32[]{:S(2)}) copy-start(f32[64,1,2304]{2,1,0:T(1,128)S(1)} %gram_b.1) | copy-start | bytes 1769476
  18.8 20.4 %all-to-all-start = ((f32[64,1,2304]{2,1,0:T(1,128)}), f32[64,1,2304]{2,1,0:T(1,128)S(1)}, u32[]{:S(2)}, u32[]{:S(2)}) async-start(f32[64,1,2304]{2,1,0:T(1,128)} %copy-done.1), calls=%async_computation | async-start | bytes 1179648 | tf_op jit(solution)/shard_map/all_to_all | solution.py:428
  60.5 10.0 %collective-permute-start.4 = (f32[4,16,128]{2,1,0:T(8,128)S(1)}, f32[4,16,128]{2,1,0:T(8,128)S(1)}, u32[]{:S(2)}, u32[]{:S(2)}) collective-permute-start(f32[4,16,128]{2,1,0:T(8,128)S(1)} %get-tuple-element.22), channel_id=1, source_target_pairs={{3,8},{7,12},{11,16},{8,3},{15,20},{12,7},{19,24},{16,11},{23,28},... | collective-permute-start | bytes 98312 | tf_op jit(solution)/shard_map/ppermute | solution.py:445
  70.6 5.0 %collective-permute-start.7 = (f32[3,16,128]{2,1,0:T(8,128)S(1)}, f32[3,16,128]{2,1,0:T(8,128)S(1)}, u32[]{:S(2)}, u32[]{:S(2)}) collective-permute-start(f32[3,16,128]{2,1,0:T(8,128)S(1)} %pad_maximum_fusion.3), channel_id=1, source_target_pairs={{0,3},{1,2},{2,1},{3,0},{4,7},{5,6},{6,5},{7,4},{8,11},{9,10},{10,... | collective-permute-start | bytes 73736 | tf_op jit(solution)/shard_map/ppermute | solution.py:447
  70.6 5.4 %collective-permute-start.6 = (f32[3,16,128]{2,1,0:T(8,128)S(1)}, f32[3,16,128]{2,1,0:T(8,128)S(1)}, u32[]{:S(2)}, u32[]{:S(2)}) collective-permute-start(f32[3,16,128]{2,1,0:T(8,128)S(1)} %pad_maximum_fusion.2), channel_id=1, source_target_pairs={{0,2},{1,3},{2,0},{3,1},{4,6},{5,7},{6,4},{7,5},{8,10},{9,11},{10,... | collective-permute-start | bytes 73736 | tf_op jit(solution)/shard_map/ppermute | solution.py:447
  70.7 6.0 %collective-permute-start.5 = (f32[3,16,128]{2,1,0:T(8,128)S(1)}, f32[3,16,128]{2,1,0:T(8,128)S(1)}, u32[]{:S(2)}, u32[]{:S(2)}) collective-permute-start(f32[3,16,128]{2,1,0:T(8,128)S(1)} %pad_maximum_fusion.1), channel_id=1, source_target_pairs={{0,1},{1,0},{2,3},{3,2},{4,5},{5,4},{6,7},{7,6},{8,9},{9,8},{10,11... | collective-permute-start | bytes 73736 | tf_op jit(solution)/shard_map/ppermute | solution.py:447
  76.7 1.3 %collective-permute-start.8 = (f32[6,16,128]{2,1,0:T(8,128)S(1)}, f32[6,16,128]{2,1,0:T(8,128)S(1)}, u32[]{:S(2)}, u32[]{:S(2)}) collective-permute-start(f32[6,16,128]{2,1,0:T(8,128)S(1)} %leave.1), channel_id=1, source_target_pairs={{0,4},{4,0},{8,12},{12,8},{16,20},{20,16},{24,28},{28,24},{32,36},... | collective-permute-start | bytes 147464 | tf_op jit(solution)/shard_map/ppermute | solution.py:402

commit v7 on v6

v7 whole, which is shorter than its diff:
```python
import functools
import jax
import jax.numpy as jnp
from jax import lax
from jax.experimental import pallas as pl
from jax.experimental.pallas import tpu as pltpu
from jax.sharding import PartitionSpec as P

CH = 16
SLOTS = 3
ST = 48
BINS = 128
BLOCK = 16
GATES = 128
TOTAL = 16384
EPS = 1e-6
HALF = 64
XN = 4
YN = 4
ZN = 4
WINDOW = 68
PACKED = ST * ST
f32 = jnp.float32
bf16 = jnp.bfloat16
VMEM_LIMIT = 16 * 2**20

VM = pl.BlockSpec(memory_space=pltpu.VMEM)
SM = pl.BlockSpec(memory_space=pltpu.SMEM)


def core_and_dop():
    return lax.axis_index("range") % 2, lax.axis_index("dop")


def iota(shape, dim):
    return lax.broadcasted_iota(jnp.int32, shape, dim)


def split(x):
    hi = x.astype(bf16)
    return hi, (x - hi.astype(f32)).astype(bf16)


def lanes(*parts):
    return jnp.concatenate(parts, 1)


def rows(*parts):
    return jnp.concatenate(parts, 0)


def pack_kernel(echo, near, send, sems):
    core, _ = core_and_dop()
    copies = []
    for out, half in ((near, core), (send, 1 - core)):
        first = half * 64
        for start, at, count in (
            (first, 2, 64),
            ((first + BINS - 2) % BINS, 0, 2),
            ((first + 64) % BINS, 66, 2),
        ):
            copies.append(
                pltpu.make_async_copy(
                    echo.at[:, pl.ds(start, count)],
                    out.at[:, pl.ds(at, count)],
                    sems.at[len(copies)],
                )
            )
    for c in copies:
        c.start()
    for c in copies:
        c.wait()


def pack(echo):
    return pl.pallas_call(
        pack_kernel,
        out_shape=[jax.ShapeDtypeStruct((2, WINDOW, CH, GATES), f32)] * 2,
        in_specs=[pl.BlockSpec(memory_space=pltpu.HBM)],
        out_specs=[VM] * 2,
        scratch_shapes=[pltpu.SemaphoreType.DMA((6,))],
        name="pack",
        compiler_params=pltpu.CompilerParams(vmem_limit_bytes=52 * 2**20),
    )(echo)


def places(triplet):
    core, _ = core_and_dop()
    mine = lax.dynamic_slice_in_dim(triplet, core * 64, 64, 0)
    return ((mine - core * 64 + BINS + 2) & (BINS - 1)).reshape(64 * SLOTS)


def gram_kernel(place, near, far, m0, m1, m2, m3, out, kept):
    core, dop = core_and_dop()
    block = dop * (GATES // BLOCK) + iota((32, GATES), 1) // BLOCK
    pick = (iota((32, GATES), 0) == block).astype(f32)
    for k, ref in enumerate((m0, m1, m2, m3)):
        m = dop ^ k
        left = 1.0 - jnp.dot(ref[...].astype(f32), pick, preferred_element_type=f32)
        kept[(m // 2) ^ core, pl.ds(pl.multiple_of((m % 2) * 32, 32), 32), :] = left
    zero = jnp.zeros((16, 4 * GATES), bf16)

    def operands(i):
        mn = jnp.broadcast_to(kept[0, pl.ds(i, 1), :], (CH, GATES)).astype(bf16)
        mf = jnp.broadcast_to(kept[1, pl.ds(i, 1), :], (CH, GATES)).astype(bf16)
        hi, lo, left, right, rest, last = [], [], [], [], [], []
        for t in range(SLOTS):
            s = place[i * SLOTS + t]
            un, uf, vn, vf = split(near[0, s]), split(far[0, s]), split(near[1, s]), split(far[1, s])
            hi.append(lanes(un[0], uf[0], vn[0], vf[0]))
            lo.append(lanes(un[1], uf[1], vn[1], vf[1]))
            a, c, d, e = un[0] * mn, uf[0] * mf, vn[0] * mn, vf[0] * mf
            left.append(lanes(a, c, d, e))
            right.append(lanes(d, e, -a, -c))
            a, c, d, e = un[1] * mn, uf[1] * mf, vn[1] * mn, vf[1] * mf
            rest.append(lanes(a, c, d, e))
            last.append(lanes(d, e, -a, -c))
        return hi, lo, rows(*left, *right, *rest, *last)

    row = iota((ST, GATES), 0)
    lane = iota((ST, GATES), 1)
    low = row >= lane % HALF
    high = row <= lane % HALF
    first = lane < HALF
    lane16 = iota((CH, GATES), 1)
    mine8 = iota((8, GATES), 1) // 16 == iota((8, GATES), 0)

    def store(q, p):
        p0, p1 = p[:16], pltpu.roll(p[16:32], 48, 1)
        p2 = pltpu.roll(p[32:], 96, 1)
        tail = [pltpu.roll(p2[h : h + 8], 0, 1, stride=16, stride_axis=0) for h in (0, 8)]
        main = jnp.where(lane16 < 48, p0, jnp.where(lane16 < 96, p1, p2))
        for j in range(16):
            out[q, :, j * GATES : (j + 1) * GATES] = main[j : j + 1]
        for j in range(2):
            extra = jnp.sum(jnp.where(mine8, tail[j], 0.0), 0, keepdims=True)
            out[q, :, (16 + j) * GATES : (17 + j) * GATES] = extra

    def pair(i):
        ha, wa, la = operands(i)
        hb, wb, lb = operands(i + 1)
        rhs = rows(*ha, zero, *hb, zero, *wa, zero, *wb, zero)
        dims = (((1,), (1,)), ((), ()))
        g = lax.dot_general(rows(la, lb), rhs, dims, preferred_element_type=f32)
        ga, gb = g[:192], g[192:]
        ga = ga[:96] + ga[96:]
        gb = gb[:96] + gb[96:]
        ga = ga[:, :GATES] + ga[:, GATES:]
        gb = gb[:, :GATES] + gb[:, GATES:]
        re = jnp.where(first, ga[:ST], gb[:ST])
        im = jnp.where(first, ga[ST:], gb[ST:])
        p = jnp.where(low, re, im)
        store(i, p)
        store(i + 1, pltpu.roll(p, HALF, 1))

    def step(j, c):
        for n in range(0, 16, 2):
            pair(j * 16 + n)
        return c

    lax.fori_loop(0, 4, step, 0)


def gram(place, near, far, masks):
    return pl.pallas_call(
        gram_kernel,
        out_shape=jax.ShapeDtypeStruct((64, 1, PACKED), f32),
        in_specs=[SM] + [VM] * 6,
        out_specs=VM,
        scratch_shapes=[pltpu.VMEM((2, 64, GATES), f32)],
        name="gram",
        compiler_params=pltpu.CompilerParams(vmem_limit_bytes=VMEM_LIMIT),
    )(place, near, far, *masks)


def solve_kernel(parts, sr, si, out):
    row = iota((ST, GATES), 0)
    lane = iota((ST, GATES), 1)
    line = []
    for j in range(PACKED // GATES):
        line.append(jnp.sum(parts[:, 0, j * GATES : (j + 1) * GATES], 0, keepdims=True) * (1.0 / TOTAL))
    main = rows(*line[:16])
    corner = rows(*[pltpu.roll(line[16 + j // 8], (GATES + 32 - 16 * (j % 8)) % GATES, 1) for j in range(16)])
    p2 = jnp.where(lane[:16] < 32, pltpu.roll(main, 32, 1), corner)
    p = rows(main, pltpu.roll(main, GATES - 48, 1), p2)
    full = rows(p, jnp.zeros((GATES - ST, GATES), f32)).T[:ST]
    re = jnp.where(row >= lane, p, full)
    im = jnp.where(row < lane, p, jnp.where(row == lane, 0.0, -full))
    are = jnp.where(lane < ST, re, sr[...])
    aim = jnp.where(lane < ST, im, si[...])
    for k in range(0, ST, 2):
        i0 = jnp.full((ST, GATES), k, jnp.int32)
        i1 = jnp.full((ST, GATES), k + 1, jnp.int32)
        c0r = jnp.take_along_axis(are, i0, 1)
        c0i = jnp.take_along_axis(aim, i0, 1)
        c1r = jnp.take_along_axis(are, i1, 1)
        c1i = jnp.take_along_axis(aim, i1, 1)
        r0, q0 = are[k : k + 1], aim[k : k + 1]
        r1, q1 = are[k + 1 : k + 2], aim[k + 1 : k + 2]
        a, d = c0r[k : k + 1], c1r[k + 1 : k + 2]
        br, bi = c1r[k : k + 1], c1i[k : k + 1]
        inv = 1.0 / (a * d - (br * br + bi * bi))
        a, d, br, bi = a * inv, d * inv, br * inv, bi * inv
        n0r = d * r0 - (br * r1 - bi * q1)
        n0i = d * q0 - (br * q1 + bi * r1)
        n1r = a * r1 - (br * r0 + bi * q0)
        n1i = a * q1 - (br * q0 - bi * r0)
        ur = (c0r * n0r - c0i * n0i) + (c1r * n1r - c1i * n1i)
        ui = (c0r * n0i + c0i * n0r) + (c1r * n1i + c1i * n1r)
        are = jnp.where(row == k, n0r, jnp.where(row == k + 1, n1r, are - ur))
        aim = jnp.where(row == k, n0i, jnp.where(row == k + 1, n1i, aim - ui))
    pad = jnp.zeros((GATES - ST, GATES), f32)
    wr = rows(are, pad).T[ST : ST + 1]
    wi = rows(aim, pad).T[ST : ST + 1]
    lane1 = iota((1, GATES), 1)
    w = jnp.where(lane1 < ST, wr, jnp.where(lane1 < 2 * ST, pltpu.roll(wi, ST, 1), 0.0))
    for j in range(64):
        out[j] = w


def solve(parts, sr, si):
    return pl.pallas_call(
        solve_kernel,
        out_shape=jax.ShapeDtypeStruct((64, 1, GATES), f32),
        in_specs=[VM] * 3,
        out_specs=VM,
        name="solve",
        compiler_params=pltpu.CompilerParams(vmem_limit_bytes=VMEM_LIMIT),
    )(parts, sr, si)


def power_kernel(place, near, far, w, out):
    core, dop = core_and_dop()
    zero = jnp.zeros((32, 2 * GATES), bf16)
    row = iota((8, GATES), 0)
    lane = iota((8, GATES), 1)

    def one(i):
        wt = jnp.broadcast_to(w[i], (8, GATES))
        turned = jnp.where(
            lane < ST,
            -pltpu.roll(wt, GATES - ST, 1),
            jnp.where(lane < 2 * ST, pltpu.roll(wt, ST, 1), 0.0),
        )
        wt = jnp.where(row % 2 == 0, wt, turned)
        hi = wt.astype(bf16).astype(f32)
        mid = (wt - hi).astype(bf16).astype(f32)
        lo = wt - hi - mid
        wt = jnp.where(row < 2, hi, jnp.where(row < 4, mid, jnp.where(row < 6, lo, 0.0)))
        lhs = rows(wt, jnp.zeros((8, GATES), f32)).astype(bf16)
        rhs = [[], [], []]
        for p in range(2):
            for t in range(SLOTS):
                s = place[i * SLOTS + t]
                x = lanes(near[p, s], far[p, s])
                hi, rest = split(x)
                x = x - hi.astype(f32)
                rhs[0].append(hi)
                rhs[1].append(rest)
                rhs[2].append((x - rest.astype(f32)).astype(bf16))
        rhs = [*rhs[0], zero, *rhs[1], zero, *rhs[2], zero]
        y = jnp.dot(lanes(lhs, lhs, lhs), rows(*rhs), preferred_element_type=f32)
        re = y[0:1] + y[2:3] + y[4:5]
        im = y[1:2] + y[3:4] + y[5:6]
        return re * re + im * im

    def step(j, c):
        group = j // 4
        y = rows(*[one(j * 8 + n) for n in range(8)])
        at = pl.ds(pl.multiple_of((j % 4) * 8, 8), 8)
        out[(2 * core + group) ^ dop, at, :] = y[:, :GATES]
        out[(2 - 2 * core + group) ^ dop, at, :] = y[:, GATES:]
        return c

    lax.fori_loop(0, 8, step, 0)


def power(place, near, far, w):
    return pl.pallas_call(
        power_kernel,
        out_shape=jax.ShapeDtypeStruct((ZN, 32, GATES), f32),
        in_specs=[SM] + [VM] * 3,
        out_specs=VM,
        name="power",
        compiler_params=pltpu.CompilerParams(vmem_limit_bytes=VMEM_LIMIT),
    )(place, near, far, w)


def cfar_kernel(p0, p1, p2, p3, inner, outer, guard, train, out, line):
    core, dop = core_and_dop()
    rank = lax.axis_index("range")
    width = 6 * GATES
    for k, ref in enumerate((p0, p1, p2, p3)):
        line[1 + (k ^ (2 * core + dop % 2))] = ref[...]
    line[5 * (1 - core)] = inner[...]
    line[5 * core] = outer[...]
    p = lanes(*[line[j] for j in range(6)])
    g = guard[:, :1]
    t = train[:, :1]
    total = p
    acc = jnp.where((t & 1) == 1, p, 0.0)
    for k in range(1, 7):
        total = total + pltpu.roll(total, width - (1 << (k - 1)), 1)
        acc = jnp.where((t >> k) & 1 == 1, total + pltpu.roll(acc, width - (1 << k), 1), acc)
    right = acc
    shift = g + 1
    for k in range(3):
        right = jnp.where((shift >> k) & 1 == 1, pltpu.roll(right, width - (1 << k), 1), right)
    left = acc
    shift = g + t
    for k in range(7):
        left = jnp.where((shift >> k) & 1 == 1, pltpu.roll(left, 1 << k, 1), left)
    lo, hi = GATES, GATES + 4 * GATES
    both = left[:, lo:hi] + right[:, lo:hi]
    pos = rank * (4 * GATES) + iota((32, 4 * GATES), 1)
    left_count = jnp.maximum(jnp.minimum(pos - g - 1, TOTAL - 1) - jnp.maximum(pos - g - t, 0) + 1, 0)
    right_count = jnp.maximum(jnp.minimum(pos + g + t, TOTAL - 1) - jnp.maximum(pos + g + 1, 0) + 1, 0)
    noise = both / (left_count + right_count).astype(f32)
    out[...] = p[:, lo:hi] / (noise + EPS)


def cfar(pieces, inner, outer, guard, train):
    return pl.pallas_call(
        cfar_kernel,
        out_shape=jax.ShapeDtypeStruct((32, 4 * GATES), f32),
        in_specs=[VM] * 8,
        out_specs=VM,
        scratch_shapes=[pltpu.VMEM((6, 32, GATES), f32)],
        name="cfar",
        compiler_params=pltpu.CompilerParams(vmem_limit_bytes=VMEM_LIMIT),
    )(*pieces, inner, outer, guard, train)


BOTH = ("range", "dop")
CORE_SWAP = [(i, i ^ 1) for i in range(32)]
SAME_CORE = [
    [((y * XN + x) * 2 + c) * ZN + z for y in range(YN) for x in range(XN) for z in range(ZN)]
    for c in range(2)
]


def flipped(bit):
    return [(i, i ^ bit) for i in range(ZN)]


def swap(value):
    return lax.ppermute(value, "range", CORE_SWAP)


def steering(bin_taper, phases):
    core, dop = core_and_dop()
    b = core * 64 + (lax.axis_index("range") // 2) * ZN + dop
    taper = lax.dynamic_index_in_dim(bin_taper, b, 0, keepdims=False)

    def lay(values):
        return jnp.broadcast_to((taper[:, None] * values[None, :]).reshape(ST, 1), (ST, GATES))

    return lay(jnp.cos(phases)), lay(jnp.sin(phases))


def chip_pairs(target):
    pairs = []
    for chip in range(XN * YN):
        for c in range(2):
            for z in range(ZN):
                to = target(c, z)
                pairs.append(((chip * 2 + c) * ZN + z, (chip * 2 + to[0]) * ZN + to[1]))
    return pairs


def shards(echoes, triplet, bin_taper, phases, excluded, guard_len, train_len):
    core, dop = core_and_dop()
    near, far = pack(echoes)
    far = swap(far)
    masks = [
        lax.ppermute(excluded, BOTH, chip_pairs(lambda c, z: (z // 2, (2 * c + z % 2) ^ k)))
        for k in range(ZN)
    ]
    place = places(triplet)
    part = gram(place, near, far, masks)
    part = lax.all_to_all(part, BOTH, 0, 0, tiled=True, axis_index_groups=SAME_CORE)
    sr, si = steering(bin_taper, phases)
    guard = jnp.broadcast_to(guard_len[:, None], (32, GATES))
    train = jnp.broadcast_to(train_len[:, None], (32, GATES))
    sr, si, guard, train = lax.optimization_barrier((sr, si, guard, train))
    w = solve(part, sr, si)
    w = lax.all_to_all(w, BOTH, 0, 0, tiled=True, axis_index_groups=SAME_CORE)
    pw = power(place, near, far, w)
    pieces = [
        lax.ppermute(pw[k], BOTH, chip_pairs(lambda c, z: ((z ^ k) // 2, 2 * c + (z ^ k) % 2)))
        for k in range(ZN)
    ]
    at = 2 * core + dop % 2
    at_tail = at ^ 3

    def chosen(index):
        value = pieces[0]
        for k in range(1, ZN):
            value = jnp.where(index == k, pieces[k], value)
        return value

    tail, head = chosen(at_tail), chosen(at)
    ranges = lax.axis_size("range")
    inner = swap(jnp.where(core == 0, tail, head))
    pairs = [(i, i + 1 if i % 2 else i - 1) for i in range(1, ranges - 1)]
    outer = lax.ppermute(jnp.where(core == 0, head, tail), "range", pairs)
    return cfar(pieces, inner, outer, guard, train)


def solution(mesh):
    placed = (
        P(None, None, None, ("range", "dop")),
        P(),
        P(),
        P(),
        P("dop", "range"),
        P("dop"),
        P("dop"),
    )
    return jax.shard_map(
        shards, mesh=mesh, in_specs=placed, out_specs=P("dop", "range"), check_vma=False
    )
```

time: 80.5 us -> 82.6 us (1.026)
  starting transfers between devices: 24.8 us -> 26.7 us
  waiting for transfers between devices: 19.8 us -> 21.6 us
  local copies, waits for them, and re-layouts: 2.28 us -> 0.93 us
    ppermute x6 -> x9, starting transfers between devices: 14.5 us -> 16.8 us  [the longest x4 8.82 us: shards(): lax.ppermute(excluded, BOTH, chip_pairs(lambda c, z: (z // 2, 2 * c + z %...]
    ppermute x6 -> x9, waiting for transfers between devices: 8.47 us -> 10.2 us  [the longest x4 4.36 us: shards(): lax.ppermute(pw[k], BOTH, chip_pairs(lambda c, z: ((z ^ k) // 2, 2 * c +...]
    all_to_all x1, waiting for transfers between devices: 10.1 us -> 11.5 us  [shards(): lax.all_to_all(part, BOTH, 0, 0, tiled=True, axis_index_groups=SAME_CORE)]
    ppermute x3 -> x2, waiting for transfers between devices: 1.22 us -> 0.01 us  [swap(): return lax.ppermute(value, 'range', CORE_SWAP)]
    unnamed x15 -> x12, local copies, waits for them, and re-layouts: 0.95 us -> 0.02 us
    pallas_call x5 -> x3, Pallas kernels: 12.9 us -> 12.7 us  [the longest x1 6.57 us: gram(): pl.pallas_call(gram_kernel, out_shape=jax.ShapeDtypeStruct((64, 1, PACKED...]
  transfers between devices with their start and end apart: 10 -> 12, of which waited for: 7 -> 7; matrix products, arithmetic and copies ran while one was open for 2% -> 1% of each run, Pallas kernels for 8% -> 0%
where the time goes in v7:
time: 82.6 us; the launch traced here: 82 us
  starting transfers between devices  26.7 us (32%)
  waiting for transfers between devices  21.6 us (26%)
  Pallas kernels  17.9 us (22%)
  blocking collectives  14.4 us (17%)
  local copies, waits for them, and re-layouts  0.93 us (1%)
    all_to_all x1, blocking collectives, shards(): w = lax.all_to_all(w, BOTH, 0, 0, tiled=True, axis_index_groups=SAME_CORE)  14.4 us
    all_to_all x1, waiting for transfers between devices, shards(): lax.all_to_all(part, BOTH, 0, 0, tiled=True, axis_index_groups=SAME_CORE)  11.5 us
    all_to_all x1, starting transfers between devices, shards(): lax.all_to_all(part, BOTH, 0, 0, tiled=True, axis_index_groups=SAME_CORE)  9.74 us
    ppermute x4, starting transfers between devices, shards(): lax.ppermute(excluded, BOTH, chip_pairs(lambda c, z: (z // 2, 2 * c + z %...  8.82 us
    pallas_call x1, Pallas kernels, gram(): pl.pallas_call(gram_kernel, out_shape=jax.ShapeDtypeStruct((64, 1, PACKED...  6.57 us
    ppermute x4, waiting for transfers between devices, shards(): lax.ppermute(pw[k], BOTH, chip_pairs(lambda c, z: ((z ^ k) // 2, 2 * c +...  4.36 us
    ppermute x1, starting transfers between devices, shards(): outer = lax.ppermute(jnp.where(core == 0, head, tail), 'range', pairs)  4.01 us
    ppermute x4, starting transfers between devices, shards(): lax.ppermute(pw[k], BOTH, chip_pairs(lambda c, z: ((z ^ k) // 2, 2 * c +...  3.99 us
  transfers between devices with their start and end apart: 12, of which 7 were waited for; matrix products, arithmetic and copies ran while one was open for 1% of the time, Pallas kernels for 0%

profile of v7, /device:TPU:8, one launch (start us, length us, event | category | flops | bytes accessed | tf_op | source)
XLA Modules:
  0.0 82.0 jit_solution(8928094370886377708)
XLA Ops:
  0.0 0.0 copy-start
  0.0 2.7 %pack.1 = (f32[2,68,16,128]{3,2,1,0:T(8,128)S(1)}, f32[2,68,16,128]{3,2,1,0:T(8,128)}) custom-call(f32[2,128,16,128]{3,2,1,0:T(8,128)} %echo.1), custom_call_target="tpu_custom_call" | custom-call | tf_op jit(solution)/shard_map/pack/pallas_call | solution.py:76
  2.7 0.1 collective-permute-start
  2.8 0.0 copy-done.4
  2.8 0.7 collective-permute-start.1
  3.5 2.0 %collective-permute-start.2 = (s32[32,32]{1,0:T(8,128)S(1)}, s32[32,32]{1,0:T(8,128)S(1)}, u32[]{:S(2)}, u32[]{:S(2)}) collective-permute-start(s32[32,32]{1,0:T(8,128)S(1)} %copy-done.4), channel_id=1, source_target_pairs={{0,1},{1,0},{2,5},{3,4},{4,3},{5,2},{6,7},{7,6},{8,9},{9,8},{10,13... | collective-permute-start | bytes 12296 | tf_op jit(solution)/shard_map/ppermute | solution.py:376
  5.5 6.0 %collective-permute-start.3 = (s32[32,32]{1,0:T(8,128)S(1)}, s32[32,32]{1,0:T(8,128)S(1)}, u32[]{:S(2)}, u32[]{:S(2)}) collective-permute-start(s32[32,32]{1,0:T(8,128)S(1)} %copy-done.4), channel_id=1, source_target_pairs={{0,2},{1,3},{2,6},{3,7},{4,0},{5,1},{6,4},{7,5},{8,10},{9,11},{10,... | collective-permute-start | bytes 12296 | tf_op jit(solution)/shard_map/ppermute | solution.py:376
  11.5 0.2 collective-permute-start.4
  11.6 0.0 copy-done.1
  11.6 0.1 add_and_fusion
  11.7 0.1 copy.8
  11.8 0.1 reshape.39.place
  12.0 0.0 collective-permute-done.1.m0
  12.0 0.0 collective-permute-done.2.m1
  12.0 1.0 %collective-permute-done.3.m2 = s32[32,32]{1,0:T(8,128)S(1)} collective-permute-done((s32[32,32]{1,0:T(8,128)S(1)}, s32[32,32]{1,0:T(8,128)S(1)}, u32[]{:S(2)}, u32[]{:S(2)}) %collective-permute-start.3) | collective-permute-done | bytes 4128 | tf_op jit(solution)/shard_map/ppermute | solution.py:376
  12.9 1.7 %collective-permute-done.4.m3 = s32[32,32]{1,0:T(8,128)S(1)} collective-permute-done((s32[32,32]{1,0:T(8,128)S(1)}, s32[32,32]{1,0:T(8,128)S(1)}, u32[]{:S(2)}, u32[]{:S(2)}) %collective-permute-start.4) | collective-permute-done | bytes 4128 | tf_op jit(solution)/shard_map/ppermute | solution.py:376
  14.7 0.0 collective-permute-done.far
  14.7 6.6 %gram.1 = f32[64,1,2304]{2,1,0:T(1,128)} custom-call(s32[192]{0:T(256)S(1)} %reshape.39.place, f32[2,68,16,128]{3,2,1,0:T(8,128)S(1)} %get-tuple-element.11.near, f32[2,68,16,128]{3,2,1,0:T(8,128)S(1)} %collective-permute-done.far, s32[32,32]{1,0:T(8,128)S(1)} %collective-permute-done.1.m0, s32[32,32]{1,0:T(8,128)S(1)} %collective-permute-done.2.m1, ...), custom_call_target="tpu_custom_call" | custom-call | tf_op jit(solution)/shard_map/gram/pallas_call | solution.py:165
  21.2 9.7 %all-to-all-start = ((f32[64,1,2304]{2,1,0:T(1,128)}), f32[64,1,2304]{2,1,0:T(1,128)S(1)}, u32[]{:S(2)}, u32[]{:S(2)}) async-start(f32[64,1,2304]{2,1,0:T(1,128)} %gram.1), calls=%async_computation | async-start | bytes 1179648 | tf_op jit(solution)/shard_map/all_to_all | solution.py:381
  31.0 0.0 copy-done
  31.0 0.2 dynamic-slice_reduce_fusion
  31.2 0.0 copy-done.5
  31.2 0.1 broadcast_multiply_fusion
  31.3 0.1 mul.57
  31.4 0.1 mul.60
  31.5 0.1 broadcast_in_dim.8.sr
  31.6 0.1 broadcast_in_dim.9.si
  31.6 0.0 copy-done.2
  31.6 0.1 broadcast_in_dim.10.guard
  31.7 0.0 copy-done.3
  31.7 0.1 broadcast_in_dim.11.train
  31.8 11.5 %all-to-all-done.parts = f32[64,1,2304]{2,1,0:T(1,128)S(1)} async-done(((f32[64,1,2304]{2,1,0:T(1,128)}), f32[64,1,2304]{2,1,0:T(1,128)S(1)}, u32[]{:S(2)}, u32[]{:S(2)}) %all-to-all-start) | async-done | bytes 589856 | tf_op jit(solution)/shard_map/all_to_all | solution.py:381
  43.2 3.4 %solve.1 = f32[64,1,128]{2,1,0:T(1,128)S(1)} custom-call(f32[64,1,2304]{2,1,0:T(1,128)S(1)} %all-to-all-done.parts, f32[48,128]{1,0:T(8,128)S(1)} %broadcast_in_dim.8.sr, f32[48,128]{1,0:T(8,128)S(1)} %broadcast_in_dim.9.si), custom_call_target="tpu_custom_call" | custom-call | tf_op jit(solution)/shard_map/solve/pallas_call | solution.py:222
  46.6 14.4 %all_to_all.10.w = f32[64,1,128]{2,1,0:T(1,128)S(1)} all-to-all(f32[64,1,128]{2,1,0:T(1,128)S(1)} %solve.1), channel_id=1, replica_groups={{0,1,2,3,8,9,10,11,16,17,18,19,24,25,26,27,32,33,34,35,40,41,42,43,48,4..., dimensions={0} | all-to-all | bytes 65536 | tf_op jit(solution)/shard_map/all_to_all | solution.py:387
  61.1 3.4 %power.1 = f32[4,32,128]{2,1,0:T(8,128)S(1)} custom-call(s32[192]{0:T(256)S(1)} %reshape.39.place, f32[2,68,16,128]{3,2,1,0:T(8,128)S(1)} %get-tuple-element.11.near, f32[2,68,16,128]{3,2,1,0:T(8,128)S(1)} %collective-permute-done.far, f32[64,1,128]{2,1,0:T(1,128)S(1)} %all_to_all.10.w), custom_call_target="tpu_custom_call" | custom-call | tf_op jit(solution)/shard_map/power/pallas_call | solution.py:279
  64.5 0.7 collective-permute-start.5
  65.2 0.7 collective-permute-start.6
  65.8 2.1 %collective-permute-start.7 = (f32[32,128]{1,0:T(8,128)S(1)}, f32[32,128]{1,0:T(8,128)S(1)}, u32[]{:S(2)}, u32[]{:S(2)}) collective-permute-start(f32[32,128]{1,0:T(8,128)S(1)} %get-tuple-element.21), channel_id=1, source_target_pairs={{0,4},{1,5},{2,0},{3,1},{4,6},{5,7},{6,2},{7,3},{8,12},{9,13},{10,... | collective-permute-start | bytes 49160 | tf_op jit(solution)/shard_map/ppermute | solution.py:390
  67.9 0.6 collective-permute-start.8
  68.5 0.0 collective-permute-done.5.p0
  68.5 0.5 collective-permute-done.6.p1
  69.0 3.1 %collective-permute-done.7.p2 = f32[32,128]{1,0:T(8,128)S(1)} collective-permute-done((f32[32,128]{1,0:T(8,128)S(1)}, f32[32,128]{1,0:T(8,128)S(1)}, u32[]{:S(2)}, u32[]{:S(2)}) %collective-permute-start.7) | collective-permute-done | bytes 16416 | tf_op jit(solution)/shard_map/ppermute | solution.py:390
  72.1 0.8 collective-permute-done.8.p3
  72.9 0.1 collective-permute-start.9
  73.0 4.0 %collective-permute-start.10 = (f32[32,128]{1,0:T(8,128)S(1)}, f32[32,128]{1,0:T(8,128)S(1)}, u32[]{:S(2)}, u32[]{:S(2)}) collective-permute-start(f32[32,128]{1,0:T(8,128)S(1)} %get-tuple-element.17), channel_id=1, source_target_pairs={{4,8},{8,4},{12,16},{16,12},{20,24},{24,20},{28,32},{32,28},{36,40... | collective-permute-start | bytes 49160 | tf_op jit(solution)/shard_map/ppermute | solution.py:406
  77.0 0.0 collective-permute-done.9.inner
  77.0 3.1 %collective-permute-done.10.outer = f32[32,128]{1,0:T(8,128)S(1)} collective-permute-done((f32[32,128]{1,0:T(8,128)S(1)}, f32[32,128]{1,0:T(8,128)S(1)}, u32[]{:S(2)}, u32[]{:S(2)}) %collective-permute-start.10) | collective-permute-done | bytes 16416 | tf_op jit(solution)/shard_map/ppermute | solution.py:406
  80.2 1.8 %cfar.1 = f32[32,512]{1,0:T(8,128)} custom-call(f32[32,128]{1,0:T(8,128)S(1)} %collective-permute-done.5.p0, f32[32,128]{1,0:T(8,128)S(1)} %collective-permute-done.6.p1, f32[32,128]{1,0:T(8,128)S(1)} %collective-permute-done.7.p2, f32[32,128]{1,0:T(8,128)S(1)} %collective-permute-done.8.p3, f32[32,128]{1,0:T(8,128)S(1)} %collective-permute-done.9.inner, ...), custom_call_target="tpu_custom_call" | custom-call | tf_op jit(solution)/shard_map/cfar/pallas_call | solution.py:323
  (9 shorter events, 0.1 us)
Async XLA Ops:
  0.0 31.0 %copy-start = (f32[128,3]{0,1:T(4,128)S(1)}, f32[128,3]{0,1:T(4,128)}, u32[]{:S(2)}) copy-start(f32[128,3]{0,1:T(4,128)} %param.9) | copy-start | bytes 4612
  0.0 2.8 %copy-start.4 = (s32[32,32]{1,0:T(8,128)S(1)}, s32[32,32]{1,0:T(8,128)}, u32[]{:S(2)}) copy-start(s32[32,32]{1,0:T(8,128)} %param.11) | copy-start | bytes 12292
  0.0 11.6 %copy-start.1 = (s32[128,3]{0,1:T(4,128)S(1)}, s32[128,3]{0,1:T(4,128)}, u32[]{:S(2)}) copy-start(s32[128,3]{0,1:T(4,128)} %param.8) | copy-start | bytes 4612
  2.7 11.9 %collective-permute-start = (f32[2,68,16,128]{3,2,1,0:T(8,128)}, f32[2,68,16,128]{3,2,1,0:T(8,128)S(1)}, u32[]{:S(2)}, u32[]{:S(2)}) collective-permute-start(f32[2,68,16,128]{3,2,1,0:T(8,128)} %get-tuple-element.12), channel_id=1, source_target_pairs={{0,4},{4,0},{8,12},{12,8},{16,20},{20,16},{24,28},{28,24},{32,36},... | collective-permute-start | bytes 3342344 | tf_op jit(solution)/shard_map/ppermute | solution.py:347
  2.8 9.2 %collective-permute-start.1 = (s32[32,32]{1,0:T(8,128)S(1)}, s32[32,32]{1,0:T(8,128)S(1)}, u32[]{:S(2)}, u32[]{:S(2)}) collective-permute-start(s32[32,32]{1,0:T(8,128)S(1)} %copy-done.4), channel_id=1, source_target_pairs={{0,0},{1,1},{2,4},{3,5},{4,2},{5,3},{6,6},{7,7},{8,8},{9,9},{10,12... | collective-permute-start | bytes 12296 | tf_op jit(solution)/shard_map/ppermute | solution.py:376
  3.5 8.5 %collective-permute-start.2 = (s32[32,32]{1,0:T(8,128)S(1)}, s32[32,32]{1,0:T(8,128)S(1)}, u32[]{:S(2)}, u32[]{:S(2)}) collective-permute-start(s32[32,32]{1,0:T(8,128)S(1)} %copy-done.4), channel_id=1, source_target_pairs={{0,1},{1,0},{2,5},{3,4},{4,3},{5,2},{6,7},{7,6},{8,9},{9,8},{10,13... | collective-permute-start | bytes 12296 | tf_op jit(solution)/shard_map/ppermute | solution.py:376
  5.5 7.5 %collective-permute-start.3 = (s32[32,32]{1,0:T(8,128)S(1)}, s32[32,32]{1,0:T(8,128)S(1)}, u32[]{:S(2)}, u32[]{:S(2)}) collective-permute-start(s32[32,32]{1,0:T(8,128)S(1)} %copy-done.4), channel_id=1, source_target_pairs={{0,2},{1,3},{2,6},{3,7},{4,0},{5,1},{6,4},{7,5},{8,10},{9,11},{10,... | collective-permute-start | bytes 12296 | tf_op jit(solution)/shard_map/ppermute | solution.py:376
  11.5 3.2 %collective-permute-start.4 = (s32[32,32]{1,0:T(8,128)S(1)}, s32[32,32]{1,0:T(8,128)S(1)}, u32[]{:S(2)}, u32[]{:S(2)}) collective-permute-start(s32[32,32]{1,0:T(8,128)S(1)} %copy-done.4), channel_id=1, source_target_pairs={{0,3},{1,2},{2,7},{3,6},{4,1},{5,0},{6,5},{7,4},{8,11},{9,10},{10,... | collective-permute-start | bytes 12296 | tf_op jit(solution)/shard_map/ppermute | solution.py:376
  21.2 10.0 %copy-start.5 = (f32[16]{0:T(128)S(1)}, f32[16]{0:T(128)}, u32[]{:S(2)}) copy-start(f32[16]{0:T(128)} %param.10) | copy-start | bytes 196
  21.2 10.4 %copy-start.2 = (s32[32]{0:T(128)S(1)}, s32[32]{0:T(128)}, u32[]{:S(2)}) copy-start(s32[32]{0:T(128)} %param.12) | copy-start | bytes 388
  21.2 10.5 %copy-start.3 = (s32[32]{0:T(128)S(1)}, s32[32]{0:T(128)}, u32[]{:S(2)}) copy-start(s32[32]{0:T(128)} %param.13) | copy-start | bytes 388
  21.2 22.0 %all-to-all-start = ((f32[64,1,2304]{2,1,0:T(1,128)}), f32[64,1,2304]{2,1,0:T(1,128)S(1)}, u32[]{:S(2)}, u32[]{:S(2)}) async-start(f32[64,1,2304]{2,1,0:T(1,128)} %gram.1), calls=%async_computation | async-start | bytes 1179648 | tf_op jit(solution)/shard_map/all_to_all | solution.py:381
  64.5 4.0 %collective-permute-start.5 = (f32[32,128]{1,0:T(8,128)S(1)}, f32[32,128]{1,0:T(8,128)S(1)}, u32[]{:S(2)}, u32[]{:S(2)}) collective-permute-start(f32[32,128]{1,0:T(8,128)S(1)} %get-tuple-element.23), channel_id=1, source_target_pairs={{0,0},{1,1},{2,4},{3,5},{4,2},{5,3},{6,6},{7,7},{8,8},{9,9},{10,12... | collective-permute-start | bytes 49160 | tf_op jit(solution)/shard_map/ppermute | solution.py:390
  65.2 3.8 %collective-permute-start.6 = (f32[32,128]{1,0:T(8,128)S(1)}, f32[32,128]{1,0:T(8,128)S(1)}, u32[]{:S(2)}, u32[]{:S(2)}) collective-permute-start(f32[32,128]{1,0:T(8,128)S(1)} %get-tuple-element.22), channel_id=1, source_target_pairs={{0,1},{1,0},{2,5},{3,4},{4,3},{5,2},{6,7},{7,6},{8,9},{9,8},{10,13... | collective-permute-start | bytes 49160 | tf_op jit(solution)/shard_map/ppermute | solution.py:390
  65.8 6.3 %collective-permute-start.7 = (f32[32,128]{1,0:T(8,128)S(1)}, f32[32,128]{1,0:T(8,128)S(1)}, u32[]{:S(2)}, u32[]{:S(2)}) collective-permute-start(f32[32,128]{1,0:T(8,128)S(1)} %get-tuple-element.21), channel_id=1, source_target_pairs={{0,4},{1,5},{2,0},{3,1},{4,6},{5,7},{6,2},{7,3},{8,12},{9,13},{10,... | collective-permute-start | bytes 49160 | tf_op jit(solution)/shard_map/ppermute | solution.py:390
  67.9 4.9 %collective-permute-start.8 = (f32[32,128]{1,0:T(8,128)S(1)}, f32[32,128]{1,0:T(8,128)S(1)}, u32[]{:S(2)}, u32[]{:S(2)}) collective-permute-start(f32[32,128]{1,0:T(8,128)S(1)} %get-tuple-element.20), channel_id=1, source_target_pairs={{0,5},{1,4},{2,1},{3,0},{4,7},{5,6},{6,3},{7,2},{8,13},{9,12},{10,... | collective-permute-start | bytes 49160 | tf_op jit(solution)/shard_map/ppermute | solution.py:390
  72.9 4.1 %collective-permute-start.9 = (f32[32,128]{1,0:T(8,128)S(1)}, f32[32,128]{1,0:T(8,128)S(1)}, u32[]{:S(2)}, u32[]{:S(2)}) collective-permute-start(f32[32,128]{1,0:T(8,128)S(1)} %broadcast_select_fusion.1), channel_id=1, source_target_pairs={{0,4},{4,0},{8,12},{12,8},{16,20},{20,16},{24,28},{28,24},{32,36},... | collective-permute-start | bytes 49160 | tf_op jit(solution)/shard_map/ppermute | solution.py:347
  73.0 7.2 %collective-permute-start.10 = (f32[32,128]{1,0:T(8,128)S(1)}, f32[32,128]{1,0:T(8,128)S(1)}, u32[]{:S(2)}, u32[]{:S(2)}) collective-permute-start(f32[32,128]{1,0:T(8,128)S(1)} %get-tuple-element.17), channel_id=1, source_target_pairs={{4,8},{8,4},{12,16},{16,12},{20,24},{24,20},{28,32},{32,28},{36,40... | collective-permute-start | bytes 49160 | tf_op jit(solution)/shard_map/ppermute | solution.py:406

commit v8 on v7

--- a/solution.py
+++ b/solution.py
@@ -20,6 +20,7 @@
 ZN = 4
 WINDOW = 68
 PACKED = ST * ST
+UNROLL = 4
 f32 = jnp.float32
 bf16 = jnp.bfloat16
 VMEM_LIMIT = 16 * 2**20
@@ -90,22 +91,26 @@
     return ((mine - core * 64 + BINS + 2) & (BINS - 1)).reshape(64 * SLOTS)
 
 
-def gram_kernel(place, near, far, m0, m1, m2, m3, out, kept):
+def gram_kernel(second, place, near, far, mask, *refs):
+    if second:
+        done, whole, kept, out, sems = refs
+    else:
+        out, kept = refs
     core, dop = core_and_dop()
-    block = dop * (GATES // BLOCK) + iota((32, GATES), 1) // BLOCK
-    pick = (iota((32, GATES), 0) == block).astype(f32)
-    for k, ref in enumerate((m0, m1, m2, m3)):
-        m = dop ^ k
-        left = 1.0 - jnp.dot(ref[...].astype(f32), pick, preferred_element_type=f32)
-        kept[(m // 2) ^ core, pl.ds(pl.multiple_of((m % 2) * 32, 32), 32), :] = left
+    group = (dop + 1) % 2 if second else dop % 2
+    block = dop * (GATES // BLOCK) + (iota((64, 2 * GATES), 1) % GATES) // BLOCK
+    block = block + 32 * (iota((64, 2 * GATES), 1) // GATES)
+    pick = (iota((64, 2 * GATES), 0) == block).astype(f32)
+    kept[...] = 1.0 - jnp.dot(mask[...].astype(f32), pick, preferred_element_type=f32)
     zero = jnp.zeros((16, 4 * GATES), bf16)
 
     def operands(i):
-        mn = jnp.broadcast_to(kept[0, pl.ds(i, 1), :], (CH, GATES)).astype(bf16)
-        mf = jnp.broadcast_to(kept[1, pl.ds(i, 1), :], (CH, GATES)).astype(bf16)
+        m = kept[i : i + 1]
+        mn = jnp.broadcast_to(m[:, :GATES], (CH, GATES)).astype(bf16)
+        mf = jnp.broadcast_to(m[:, GATES:], (CH, GATES)).astype(bf16)
         hi, lo, left, right, rest, last = [], [], [], [], [], []
         for t in range(SLOTS):
-            s = place[i * SLOTS + t]
+            s = place[(group * 32 + i) * SLOTS + t]
             un, uf, vn, vf = split(near[0, s]), split(far[0, s]), split(near[1, s]), split(far[1, s])
             hi.append(lanes(un[0], uf[0], vn[0], vf[0]))
             lo.append(lanes(un[1], uf[1], vn[1], vf[1]))
@@ -153,24 +158,40 @@
         store(i, p)
         store(i + 1, pltpu.roll(p, HALF, 1))
 
-    def step(j, c):
-        for n in range(0, 16, 2):
-            pair(j * 16 + n)
-        return c
-
-    lax.fori_loop(0, 4, step, 0)
-
-
-def gram(place, near, far, masks):
-    return pl.pallas_call(
-        gram_kernel,
-        out_shape=jax.ShapeDtypeStruct((64, 1, PACKED), f32),
-        in_specs=[SM] + [VM] * 6,
-        out_specs=VM,
-        scratch_shapes=[pltpu.VMEM((2, 64, GATES), f32)],
-        name="gram",
+    copies = []
+
+    def ship(value, first, at, count):
+        copies.append(
+            pltpu.make_async_copy(
+                value.at[pl.ds(first, count)],
+                whole.at[pl.ds(pl.multiple_of(at + first, 16), count)],
+                sems.at[len(copies)],
+            )
+        )
+        copies[-1].start()
+
+    if second:
+        ship(done, 0, (1 - group) * 32, 32)
+    for i in range(0, 32, 2):
+        pair(i)
+        if second and i in (14, 30):
+            ship(out, i - 14, group * 32, 16)
+    for c in copies:
+        c.wait()
+
+
+def gram(second, place, near, far, *extra):
+    block = (32, 1, PACKED)
+    kept = pltpu.VMEM((32, 2 * GATES), f32)
+    return pl.pallas_call(
+        functools.partial(gram_kernel, second),
+        out_shape=jax.ShapeDtypeStruct((64, 1, PACKED) if second else block, f32),
+        in_specs=[SM] + [VM] * (4 if second else 3),
+        out_specs=pl.BlockSpec(memory_space=pl.ANY) if second else VM,
+        scratch_shapes=[kept, pltpu.VMEM(block, f32), pltpu.SemaphoreType.DMA((3,))] if second else [kept],
+        name="gram_b" if second else "gram_a",
         compiler_params=pltpu.CompilerParams(vmem_limit_bytes=VMEM_LIMIT),
-    )(place, near, far, *masks)
+    )(place, near, far, *extra)
 
 
 def solve_kernel(parts, sr, si, out):
@@ -229,7 +250,7 @@
     )(parts, sr, si)
 
 
-def power_kernel(place, near, far, w, out):
+def power_kernel(place, near, far, w, own, other):
     core, dop = core_and_dop()
     zero = jnp.zeros((32, 2 * GATES), bf16)
     row = iota((8, GATES), 0)
@@ -265,38 +286,29 @@
         return re * re + im * im
 
     def step(j, c):
-        group = j // 4
+        k = (j // 4) ^ (dop % 2)
         y = rows(*[one(j * 8 + n) for n in range(8)])
         at = pl.ds(pl.multiple_of((j % 4) * 8, 8), 8)
-        out[(2 * core + group) ^ dop, at, :] = y[:, :GATES]
-        out[(2 - 2 * core + group) ^ dop, at, :] = y[:, GATES:]
+        own[k, at, :] = y[:, :GATES]
+        other[k, at, :] = y[:, GATES:]
         return c
 
-    lax.fori_loop(0, 8, step, 0)
+    lax.fori_loop(0, 8, step, 0, unroll=UNROLL)
 
 
 def power(place, near, far, w):
     return pl.pallas_call(
         power_kernel,
-        out_shape=jax.ShapeDtypeStruct((ZN, 32, GATES), f32),
+        out_shape=[jax.ShapeDtypeStruct((2, 32, GATES), f32)] * 2,
         in_specs=[SM] + [VM] * 3,
-        out_specs=VM,
+        out_specs=[VM] * 2,
         name="power",
         compiler_params=pltpu.CompilerParams(vmem_limit_bytes=VMEM_LIMIT),
     )(place, near, far, w)
 
 
-def cfar_kernel(p0, p1, p2, p3, inner, outer, guard, train, out, line):
-    core, dop = core_and_dop()
-    rank = lax.axis_index("range")
-    width = 6 * GATES
-    for k, ref in enumerate((p0, p1, p2, p3)):
-        line[1 + (k ^ (2 * core + dop % 2))] = ref[...]
-    line[5 * (1 - core)] = inner[...]
-    line[5 * core] = outer[...]
-    p = lanes(*[line[j] for j in range(6)])
-    g = guard[:, :1]
-    t = train[:, :1]
+def window_sums(p, g, t):
+    width = p.shape[1]
     total = p
     acc = jnp.where((t & 1) == 1, p, 0.0)
     for k in range(1, 7):
@@ -310,31 +322,70 @@
     shift = g + t
     for k in range(7):
         left = jnp.where((shift >> k) & 1 == 1, pltpu.roll(left, 1 << k, 1), left)
+    return left, right
+
+
+def noise_kernel(p0, p1, p2, p3, inner, guard, train, out, line):
+    core, dop = core_and_dop()
+    rank = lax.axis_index("range")
+    for k, ref in enumerate((p0, p1, p2, p3)):
+        line[1 + (dop ^ k)] = ref[...]
+    line[5 * (1 - core)] = inner[...]
+    line[5 * core] = jnp.zeros((32, GATES), f32)
+    p = lanes(*[line[j] for j in range(6)])
+    g = guard[:, :1]
+    t = train[:, :1]
+    left, right = window_sums(p, g, t)
     lo, hi = GATES, GATES + 4 * GATES
-    both = left[:, lo:hi] + right[:, lo:hi]
     pos = rank * (4 * GATES) + iota((32, 4 * GATES), 1)
     left_count = jnp.maximum(jnp.minimum(pos - g - 1, TOTAL - 1) - jnp.maximum(pos - g - t, 0) + 1, 0)
     right_count = jnp.maximum(jnp.minimum(pos + g + t, TOTAL - 1) - jnp.maximum(pos + g + 1, 0) + 1, 0)
-    noise = both / (left_count + right_count).astype(f32)
-    out[...] = p[:, lo:hi] / (noise + EPS)
-
-
-def cfar(pieces, inner, outer, guard, train):
+    out[0] = p[:, lo:hi]
+    out[1] = left[:, lo:hi] + right[:, lo:hi]
+    out[2] = (left_count + right_count).astype(f32)
+
+
+def noise(pieces, inner, guard, train):
+    return pl.pallas_call(
+        noise_kernel,
+        out_shape=jax.ShapeDtypeStruct((3, 32, 4 * GATES), f32),
+        in_specs=[VM] * 7,
+        out_specs=VM,
+        scratch_shapes=[pltpu.VMEM((6, 32, GATES), f32)],
+        name="noise",
+        compiler_params=pltpu.CompilerParams(vmem_limit_bytes=VMEM_LIMIT),
+    )(*pieces, inner, guard, train)
+
+
+def cfar_kernel(known, outer, guard, train, out, line):
+    core, _ = core_and_dop()
+    line[core] = outer[...]
+    line[1 - core] = jnp.zeros((32, GATES), f32)
+    p = lanes(line[0], line[1])
+    left, right = window_sums(p, guard[:, :1], train[:, :1])
+    sums = known[1]
+    head = sums[:, :GATES] + jnp.where(core == 0, left[:, GATES:], 0.0)
+    tail = sums[:, 3 * GATES :] + jnp.where(core == 1, right[:, :GATES], 0.0)
+    sums = lanes(head, sums[:, GATES : 3 * GATES], tail)
+    out[...] = known[0] / (sums / known[2] + EPS)
+
+
+def cfar(known, outer, guard, train):
     return pl.pallas_call(
         cfar_kernel,
         out_shape=jax.ShapeDtypeStruct((32, 4 * GATES), f32),
-        in_specs=[VM] * 8,
+        in_specs=[VM] * 4,
         out_specs=VM,
-        scratch_shapes=[pltpu.VMEM((6, 32, GATES), f32)],
+        scratch_shapes=[pltpu.VMEM((2, 32, GATES), f32)],
         name="cfar",
         compiler_params=pltpu.CompilerParams(vmem_limit_bytes=VMEM_LIMIT),
-    )(*pieces, inner, outer, guard, train)
+    )(known, outer, guard, train)
 
 
 BOTH = ("range", "dop")
 CORE_SWAP = [(i, i ^ 1) for i in range(32)]
 SAME_CORE = [
-    [((y * XN + x) * 2 + c) * ZN + z for y in range(YN) for x in range(XN) for z in range(ZN)]
+    [((y * XN + x) * 2 + c) * ZN + z for z in range(ZN) for y in range(YN) for x in range(XN)]
     for c in range(2)
 ]
 
@@ -349,7 +400,7 @@
 
 def steering(bin_taper, phases):
     core, dop = core_and_dop()
-    b = core * 64 + (lax.axis_index("range") // 2) * ZN + dop
+    b = core * 64 + dop * 16 + lax.axis_index("range") // 2
     taper = lax.dynamic_index_in_dim(bin_taper, b, 0, keepdims=False)
 
     def lay(values):
@@ -358,26 +409,19 @@
     return lay(jnp.cos(phases)), lay(jnp.sin(phases))
 
 
-def chip_pairs(target):
-    pairs = []
-    for chip in range(XN * YN):
-        for c in range(2):
-            for z in range(ZN):
-                to = target(c, z)
-                pairs.append(((chip * 2 + c) * ZN + z, (chip * 2 + to[0]) * ZN + to[1]))
-    return pairs
-
-
 def shards(echoes, triplet, bin_taper, phases, excluded, guard_len, train_len):
     core, dop = core_and_dop()
+    place = places(triplet)
+    other = swap(excluded)
     near, far = pack(echoes)
+    far, other = lax.optimization_barrier((far, other))
     far = swap(far)
-    masks = [
-        lax.ppermute(excluded, BOTH, chip_pairs(lambda c, z: (z // 2, (2 * c + z % 2) ^ k)))
-        for k in range(ZN)
-    ]
-    place = places(triplet)
-    part = gram(place, near, far, masks)
+    mine = lanes(excluded, other)
+    across = lax.ppermute(mine, "dop", flipped(2))
+    m0 = jnp.where(dop // 2 == core, mine, across)
+    m1 = lax.ppermute(m0, "dop", flipped(1))
+    part = gram(False, place, near, far, m0)
+    part = gram(True, place, near, far, m1, part)
     part = lax.all_to_all(part, BOTH, 0, 0, tiled=True, axis_index_groups=SAME_CORE)
     sr, si = steering(bin_taper, phases)
     guard = jnp.broadcast_to(guard_len[:, None], (32, GATES))
@@ -385,26 +429,20 @@
     sr, si, guard, train = lax.optimization_barrier((sr, si, guard, train))
     w = solve(part, sr, si)
     w = lax.all_to_all(w, BOTH, 0, 0, tiled=True, axis_index_groups=SAME_CORE)
-    pw = power(place, near, far, w)
+    own, away = power(place, near, far, w)
+    came = swap(away)
     pieces = [
-        lax.ppermute(pw[k], BOTH, chip_pairs(lambda c, z: ((z ^ k) // 2, 2 * c + (z ^ k) % 2)))
-        for k in range(ZN)
+        jnp.where((dop // 2) ^ (k // 2) == core, own[k % 2], came[k % 2]) for k in range(ZN)
     ]
-    at = 2 * core + dop % 2
-    at_tail = at ^ 3
-
-    def chosen(index):
-        value = pieces[0]
-        for k in range(1, ZN):
-            value = jnp.where(index == k, pieces[k], value)
-        return value
-
-    tail, head = chosen(at_tail), chosen(at)
+    pieces = [pieces[0]] + [lax.ppermute(pieces[k], "dop", flipped(k)) for k in (1, 2, 3)]
+    p0, p1, p2, p3 = pieces
     ranges = lax.axis_size("range")
+    tail = jnp.where(dop == 0, p3, jnp.where(dop == 1, p2, jnp.where(dop == 2, p1, p0)))
+    head = jnp.where(dop == 0, p0, jnp.where(dop == 1, p1, jnp.where(dop == 2, p2, p3)))
     inner = swap(jnp.where(core == 0, tail, head))
     pairs = [(i, i + 1 if i % 2 else i - 1) for i in range(1, ranges - 1)]
     outer = lax.ppermute(jnp.where(core == 0, head, tail), "range", pairs)
-    return cfar(pieces, inner, outer, guard, train)
+    return cfar(noise(pieces, inner, guard, train), outer, guard, train)
 
 
 def solution(mesh):

time: 82.6 us -> 78.5 us (0.950)
  waiting for transfers between devices: 21.6 us -> 18.4 us
    ppermute x8 -> x5, waiting for transfers between devices: 7.04 us -> 4.39 us  [the longest x3 2.67 us: shards(): lax.ppermute(pieces[k], 'dop', flipped(k))]
    ppermute x8 -> x5, starting transfers between devices: 12.8 us -> 10.2 us  [the longest x3 4.7 us: shards(): lax.ppermute(pieces[k], 'dop', flipped(k))]
    all_to_all x1, starting transfers between devices: 9.74 us -> 11.1 us  [shards(): lax.all_to_all(part, BOTH, 0, 0, tiled=True, axis_index_groups=SAME_CORE)]
    ppermute x1, waiting for transfers between devices: 3.13 us -> 1.81 us  [shards(): outer = lax.ppermute(jnp.where(core == 0, head, tail), 'range', pairs)]
    ppermute x2 -> x4, waiting for transfers between devices: 0.01 us -> 1.19 us  [swap(): return lax.ppermute(value, 'range', CORE_SWAP)]
    pallas_call x2 -> x4, Pallas kernels: 9.99 us -> 9.95 us  [the longest x2 6.19 us: gram(): pl.pallas_call(functools.partial(gram_kernel, second), out_shape=jax.Shap...]
  transfers between devices with their start and end apart: 12 -> 11, of which waited for: 7 -> 6; matrix products, arithmetic and copies ran while one was open for 1% -> 2% of each run, Pallas kernels for 0% -> 9%
where the time goes in v8:
time: 78.5 us; the launch traced here: 77.9 us
  starting transfers between devices  26.2 us (33%)
  waiting for transfers between devices  18.4 us (23%)
  Pallas kernels  17.7 us (23%)
  blocking collectives  14.1 us (18%)
  local copies, waits for them, and re-layouts  0.94 us (1%)
    all_to_all x1, blocking collectives, shards(): w = lax.all_to_all(w, BOTH, 0, 0, tiled=True, axis_index_groups=SAME_CORE)  14.1 us
    all_to_all x1, starting transfers between devices, shards(): lax.all_to_all(part, BOTH, 0, 0, tiled=True, axis_index_groups=SAME_CORE)  11.1 us
    all_to_all x1, waiting for transfers between devices, shards(): lax.all_to_all(part, BOTH, 0, 0, tiled=True, axis_index_groups=SAME_CORE)  11 us
    pallas_call x2, Pallas kernels, gram(): pl.pallas_call(functools.partial(gram_kernel, second), out_shape=jax.Shap...  6.19 us
    ppermute x3, starting transfers between devices, shards(): lax.ppermute(pieces[k], 'dop', flipped(k))  4.7 us
    ppermute x1, starting transfers between devices, shards(): outer = lax.ppermute(jnp.where(core == 0, head, tail), 'range', pairs)  4.11 us
    ppermute x1, starting transfers between devices, shards(): across = lax.ppermute(mine, 'dop', flipped(2))  3.89 us
    pallas_call x1, Pallas kernels, solve(): pl.pallas_call(solve_kernel, out_shape=jax.ShapeDtypeStruct((64, 1, GATES...  3.37 us
  transfers between devices with their start and end apart: 11, of which 6 were waited for; matrix products, arithmetic and copies ran while one was open for 2% of the time, Pallas kernels for 9%

profile of v8, /device:TPU:8, one launch (start us, length us, event | category | flops | bytes accessed | tf_op | source)
XLA Modules:
  0.0 77.9 jit_solution(6636293076586258838)
XLA Ops:
  0.0 0.0 copy-start
  0.0 0.1 collective-permute-start
  0.1 2.7 %pack.1 = (f32[2,68,16,128]{3,2,1,0:T(8,128)S(1)}, f32[2,68,16,128]{3,2,1,0:T(8,128)}) custom-call(f32[2,128,16,128]{3,2,1,0:T(8,128)} %echo.1), custom_call_target="tpu_custom_call" | custom-call | tf_op jit(solution)/shard_map/pack/pallas_call | solution.py:77
  2.8 0.0 collective-permute-done
  2.8 0.6 collective-permute-start.1
  3.3 0.0 copy-done.1
  3.4 0.1 pad_add_fusion
  3.4 3.9 %collective-permute-start.2 = (s32[32,64]{1,0:T(8,128)S(1)}, s32[32,64]{1,0:T(8,128)S(1)}, u32[]{:S(2)}, u32[]{:S(2)}) collective-permute-start(s32[32,64]{1,0:T(8,128)S(1)} %pad_add_fusion), channel_id=1, source_target_pairs={{0,2},{1,3},{2,0},{3,1},{4,6},{5,7},{6,4},{7,5},{8,10},{9,11},{10,... | collective-permute-start | bytes 24584 | tf_op jit(solution)/shard_map/ppermute | solution.py:420
  7.3 1.7 %collective-permute-done.2 = s32[32,64]{1,0:T(8,128)S(1)} collective-permute-done((s32[32,64]{1,0:T(8,128)S(1)}, s32[32,64]{1,0:T(8,128)S(1)}, u32[]{:S(2)}, u32[]{:S(2)}) %collective-permute-start.2) | collective-permute-done | bytes 8224 | tf_op jit(solution)/shard_map/ppermute | solution.py:420
  9.0 0.1 broadcast_select_fusion.2.mask
  9.1 1.6 %collective-permute-start.3 = (s32[32,64]{1,0:T(8,128)S(1)}, s32[32,64]{1,0:T(8,128)S(1)}, u32[]{:S(2)}, u32[]{:S(2)}) collective-permute-start(s32[32,64]{1,0:T(8,128)S(1)} %broadcast_select_fusion.2.mask), channel_id=1, source_target_pairs={{0,1},{1,0},{2,3},{3,2},{4,5},{5,4},{6,7},{7,6},{8,9},{9,8},{10,11... | collective-permute-start | bytes 24584 | tf_op jit(solution)/shard_map/ppermute | solution.py:422
  10.7 0.1 add_and_fusion
  10.8 0.1 copy.8
  10.9 0.1 reshape.47.place
  11.0 0.0 collective-permute-done.1.far
  11.0 2.7 %gram_a.1.refs_0_ = f32[32,1,2304]{2,1,0:T(1,128)S(1)} custom-call(s32[192]{0:T(256)S(1)} %reshape.47.place, f32[2,68,16,128]{3,2,1,0:T(8,128)S(1)} %get-tuple-element.15.near, f32[2,68,16,128]{3,2,1,0:T(8,128)S(1)} %collective-permute-done.1.far, s32[32,64]{1,0:T(8,128)S(1)} %broadcast_select_fusion.2.mask), custom_call_target="tpu_custom_call" | custom-call | tf_op jit(solution)/shard_map/gram_a/pallas_call | solution.py:186
  13.8 0.0 collective-permute-done.3.mask
  13.8 3.4 %gram_b.1 = f32[64,1,2304]{2,1,0:T(1,128)} custom-call(s32[192]{0:T(256)S(1)} %reshape.47.place, f32[2,68,16,128]{3,2,1,0:T(8,128)S(1)} %get-tuple-element.15.near, f32[2,68,16,128]{3,2,1,0:T(8,128)S(1)} %collective-permute-done.1.far, s32[32,64]{1,0:T(8,128)S(1)} %collective-permute-done.3.mask, f32[32,1,2304]{2,1,0:T(1,128)S(1)} %gram_a.1.refs_0_), custom_call_target="tpu_custom_call" | custom-call | tf_op jit(solution)/shard_map/gram_b/pallas_call | solution.py:186
  17.2 0.0 copy-start.5
  17.2 0.0 copy-start.3
  17.3 0.0 copy-start.4
  17.3 11.1 %all-to-all-start = ((f32[64,1,2304]{2,1,0:T(1,128)}), f32[64,1,2304]{2,1,0:T(1,128)S(1)}, u32[]{:S(2)}, u32[]{:S(2)}) async-start(f32[64,1,2304]{2,1,0:T(1,128)} %gram_b.1), calls=%async_computation | async-start | bytes 1179648 | tf_op jit(solution)/shard_map/all_to_all | solution.py:425
  28.4 0.2 dynamic-slice_reduce_fusion
  28.6 0.1 broadcast_multiply_fusion
  28.7 0.1 mul.54
  28.8 0.1 mul.57
  28.9 0.1 broadcast_in_dim.8.sr
  28.9 0.1 broadcast_in_dim.9.si
  29.0 0.1 broadcast_in_dim.10.guard
  29.1 0.1 broadcast_in_dim.11.train
  29.2 11.0 %all-to-all-done.parts = f32[64,1,2304]{2,1,0:T(1,128)S(1)} async-done(((f32[64,1,2304]{2,1,0:T(1,128)}), f32[64,1,2304]{2,1,0:T(1,128)S(1)}, u32[]{:S(2)}, u32[]{:S(2)}) %all-to-all-start) | async-done | bytes 589856 | tf_op jit(solution)/shard_map/all_to_all | solution.py:425
  40.2 3.4 %solve.1 = f32[64,1,128]{2,1,0:T(1,128)S(1)} custom-call(f32[64,1,2304]{2,1,0:T(1,128)S(1)} %all-to-all-done.parts, f32[48,128]{1,0:T(8,128)S(1)} %broadcast_in_dim.8.sr, f32[48,128]{1,0:T(8,128)S(1)} %broadcast_in_dim.9.si), custom_call_target="tpu_custom_call" | custom-call | tf_op jit(solution)/shard_map/solve/pallas_call | solution.py:243
  43.6 14.1 %all_to_all.10.w = f32[64,1,128]{2,1,0:T(1,128)S(1)} all-to-all(f32[64,1,128]{2,1,0:T(1,128)S(1)} %solve.1), channel_id=1, replica_groups={{0,8,16,24,32,40,48,56,64,72,80,88,96,104,112,120,1,9,17,25,33,41,49,57..., dimensions={0} | all-to-all | bytes 65536 | tf_op jit(solution)/shard_map/all_to_all | solution.py:431
  57.7 2.5 %power.1 = (f32[2,32,128]{2,1,0:T(8,128)S(1)}, f32[2,32,128]{2,1,0:T(8,128)S(1)}) custom-call(s32[192]{0:T(256)S(1)} %reshape.47.place, f32[2,68,16,128]{3,2,1,0:T(8,128)S(1)} %get-tuple-element.15.near, f32[2,68,16,128]{3,2,1,0:T(8,128)S(1)} %collective-permute-done.1.far, f32[64,1,128]{2,1,0:T(1,128)S(1)} %all_to_all.10.w), custom_call_target="tpu_custom_call" | custom-call | tf_op jit(solution)/shard_map/power/pallas_call | solution.py:300
  60.2 0.1 collective-permute-start.4
  60.3 1.2 %collective-permute-done.4 = f32[2,32,128]{2,1,0:T(8,128)S(1)} collective-permute-done((f32[2,32,128]{2,1,0:T(8,128)S(1)}, f32[2,32,128]{2,1,0:T(8,128)S(1)}, u32[]{:S(2)}, u32[]{:S(2)}) %collective-permute-start.4) | collective-permute-done | bytes 32800 | tf_op jit(solution)/shard_map/ppermute | solution.py:398
  61.5 0.6 collective-permute-start.5
  62.1 1.8 %collective-permute-start.6 = (f32[32,128]{1,0:T(8,128)S(1)}, f32[32,128]{1,0:T(8,128)S(1)}, u32[]{:S(2)}, u32[]{:S(2)}) collective-permute-start(f32[32,128]{1,0:T(8,128)S(1)} %get-tuple-element.30), channel_id=1, source_target_pairs={{0,2},{1,3},{2,0},{3,1},{4,6},{5,7},{6,4},{7,5},{8,10},{9,11},{10,... | collective-permute-start | bytes 49160 | tf_op jit(solution)/shard_map/ppermute | solution.py:437
  63.9 2.3 %collective-permute-start.7 = (f32[32,128]{1,0:T(8,128)S(1)}, f32[32,128]{1,0:T(8,128)S(1)}, u32[]{:S(2)}, u32[]{:S(2)}) collective-permute-start(f32[32,128]{1,0:T(8,128)S(1)} %get-tuple-element.29), channel_id=1, source_target_pairs={{0,3},{1,2},{2,1},{3,0},{4,7},{5,6},{6,5},{7,4},{8,11},{9,10},{10,... | collective-permute-start | bytes 49160 | tf_op jit(solution)/shard_map/ppermute | solution.py:437
  66.2 0.0 collective-permute-done.5.p1
  66.2 1.1 %collective-permute-done.6.p2 = f32[32,128]{1,0:T(8,128)S(1)} collective-permute-done((f32[32,128]{1,0:T(8,128)S(1)}, f32[32,128]{1,0:T(8,128)S(1)}, u32[]{:S(2)}, u32[]{:S(2)}) %collective-permute-start.6) | collective-permute-done | bytes 16416 | tf_op jit(solution)/shard_map/ppermute | solution.py:437
  67.3 1.6 %collective-permute-done.7.p3 = f32[32,128]{1,0:T(8,128)S(1)} collective-permute-done((f32[32,128]{1,0:T(8,128)S(1)}, f32[32,128]{1,0:T(8,128)S(1)}, u32[]{:S(2)}, u32[]{:S(2)}) %collective-permute-start.7) | collective-permute-done | bytes 16416 | tf_op jit(solution)/shard_map/ppermute | solution.py:437
  68.9 0.1 collective-permute-start.8
  69.0 4.1 %collective-permute-start.9 = (f32[32,128]{1,0:T(8,128)S(1)}, f32[32,128]{1,0:T(8,128)S(1)}, u32[]{:S(2)}, u32[]{:S(2)}) collective-permute-start(f32[32,128]{1,0:T(8,128)S(1)} %get-tuple-element.25), channel_id=1, source_target_pairs={{4,8},{8,4},{12,16},{16,12},{20,24},{24,20},{28,32},{32,28},{36,40... | collective-permute-start | bytes 49160 | tf_op jit(solution)/shard_map/ppermute | solution.py:444
  73.1 0.0 collective-permute-done.8.inner
  73.1 1.2 %noise.1.known = f32[3,32,512]{2,1,0:T(8,128)S(1)} custom-call(f32[32,128]{1,0:T(8,128)S(1)} %get-tuple-element.28.p0, f32[32,128]{1,0:T(8,128)S(1)} %collective-permute-done.5.p1, f32[32,128]{1,0:T(8,128)S(1)} %collective-permute-done.6.p2, f32[32,128]{1,0:T(8,128)S(1)} %collective-permute-done.7.p3, f32[32,128]{1,0:T(8,128)S(1)} %collective-permute-done.8.inner, ...), custom_call_target="tpu_custom_call" | custom-call | tf_op jit(solution)/shard_map/noise/pallas_call | solution.py:349
  74.4 1.8 %collective-permute-done.9.outer = f32[32,128]{1,0:T(8,128)S(1)} collective-permute-done((f32[32,128]{1,0:T(8,128)S(1)}, f32[32,128]{1,0:T(8,128)S(1)}, u32[]{:S(2)}, u32[]{:S(2)}) %collective-permute-start.9) | collective-permute-done | bytes 16416 | tf_op jit(solution)/shard_map/ppermute | solution.py:444
  76.2 1.7 %cfar.1 = f32[32,512]{1,0:T(8,128)} custom-call(f32[3,32,512]{2,1,0:T(8,128)S(1)} %noise.1.known, f32[32,128]{1,0:T(8,128)S(1)} %collective-permute-done.9.outer, s32[32,128]{1,0:T(8,128)S(1)} %broadcast_in_dim.10.guard, s32[32,128]{1,0:T(8,128)S(1)} %broadcast_in_dim.11.train), custom_call_target="tpu_custom_call" | custom-call | tf_op jit(solution)/shard_map/cfar/pallas_call | solution.py:374
  (11 shorter events, 0.1 us)
Async XLA Ops:
  0.0 28.4 %copy-start = (f32[128,3]{0,1:T(4,128)S(1)}, f32[128,3]{0,1:T(4,128)}, u32[]{:S(2)}) copy-start(f32[128,3]{0,1:T(4,128)} %param.9) | copy-start | bytes 4612
  0.0 3.3 %copy-start.1 = (s32[32,32]{1,0:T(8,128)S(1)}, s32[32,32]{1,0:T(8,128)}, u32[]{:S(2)}) copy-start(s32[32,32]{1,0:T(8,128)} %param.11) | copy-start | bytes 12292
  0.0 10.7 %copy-start.2 = (s32[128,3]{0,1:T(4,128)S(1)}, s32[128,3]{0,1:T(4,128)}, u32[]{:S(2)}) copy-start(s32[128,3]{0,1:T(4,128)} %param.8) | copy-start | bytes 4612
  0.0 2.8 %collective-permute-start = (s32[32,32]{1,0:T(8,128)}, s32[32,32]{1,0:T(8,128)S(1)}, u32[]{:S(2)}, u32[]{:S(2)}) collective-permute-start(s32[32,32]{1,0:T(8,128)} %param.11), channel_id=1, source_target_pairs={{0,4},{4,0},{8,12},{12,8},{16,20},{20,16},{24,28},{28,24},{32,36},... | collective-permute-start | bytes 12296 | tf_op jit(solution)/shard_map/ppermute | solution.py:398
  2.8 8.2 %collective-permute-start.1 = (f32[2,68,16,128]{3,2,1,0:T(8,128)}, f32[2,68,16,128]{3,2,1,0:T(8,128)S(1)}, u32[]{:S(2)}, u32[]{:S(2)}) collective-permute-start(f32[2,68,16,128]{3,2,1,0:T(8,128)} %get-tuple-element.17), channel_id=1, source_target_pairs={{0,4},{4,0},{8,12},{12,8},{16,20},{20,16},{24,28},{28,24},{32,36},... | collective-permute-start | bytes 3342344 | tf_op jit(solution)/shard_map/ppermute | solution.py:398
  3.4 5.6 %collective-permute-start.2 = (s32[32,64]{1,0:T(8,128)S(1)}, s32[32,64]{1,0:T(8,128)S(1)}, u32[]{:S(2)}, u32[]{:S(2)}) collective-permute-start(s32[32,64]{1,0:T(8,128)S(1)} %pad_add_fusion), channel_id=1, source_target_pairs={{0,2},{1,3},{2,0},{3,1},{4,6},{5,7},{6,4},{7,5},{8,10},{9,11},{10,... | collective-permute-start | bytes 24584 | tf_op jit(solution)/shard_map/ppermute | solution.py:420
  9.1 4.7 %collective-permute-start.3 = (s32[32,64]{1,0:T(8,128)S(1)}, s32[32,64]{1,0:T(8,128)S(1)}, u32[]{:S(2)}, u32[]{:S(2)}) collective-permute-start(s32[32,64]{1,0:T(8,128)S(1)} %broadcast_select_fusion.2.mask), channel_id=1, source_target_pairs={{0,1},{1,0},{2,3},{3,2},{4,5},{5,4},{6,7},{7,6},{8,9},{9,8},{10,11... | collective-permute-start | bytes 24584 | tf_op jit(solution)/shard_map/ppermute | solution.py:422
  17.2 11.4 %copy-start.5 = (f32[16]{0:T(128)S(1)}, f32[16]{0:T(128)}, u32[]{:S(2)}) copy-start(f32[16]{0:T(128)} %param.10) | copy-start | bytes 196
  17.2 11.8 %copy-start.3 = (s32[32]{0:T(128)S(1)}, s32[32]{0:T(128)}, u32[]{:S(2)}) copy-start(s32[32]{0:T(128)} %param.12) | copy-start | bytes 388
  17.3 11.8 %copy-start.4 = (s32[32]{0:T(128)S(1)}, s32[32]{0:T(128)}, u32[]{:S(2)}) copy-start(s32[32]{0:T(128)} %param.13) | copy-start | bytes 388
  17.3 22.9 %all-to-all-start = ((f32[64,1,2304]{2,1,0:T(1,128)}), f32[64,1,2304]{2,1,0:T(1,128)S(1)}, u32[]{:S(2)}, u32[]{:S(2)}) async-start(f32[64,1,2304]{2,1,0:T(1,128)} %gram_b.1), calls=%async_computation | async-start | bytes 1179648 | tf_op jit(solution)/shard_map/all_to_all | solution.py:425
  60.2 1.3 %collective-permute-start.4 = (f32[2,32,128]{2,1,0:T(8,128)S(1)}, f32[2,32,128]{2,1,0:T(8,128)S(1)}, u32[]{:S(2)}, u32[]{:S(2)}) collective-permute-start(f32[2,32,128]{2,1,0:T(8,128)S(1)} %get-tuple-element.22), channel_id=1, source_target_pairs={{0,4},{4,0},{8,12},{12,8},{16,20},{20,16},{24,28},{28,24},{32,36},... | collective-permute-start | bytes 98312 | tf_op jit(solution)/shard_map/ppermute | solution.py:398
  61.5 4.7 %collective-permute-start.5 = (f32[32,128]{1,0:T(8,128)S(1)}, f32[32,128]{1,0:T(8,128)S(1)}, u32[]{:S(2)}, u32[]{:S(2)}) collective-permute-start(f32[32,128]{1,0:T(8,128)S(1)} %get-tuple-element.31), channel_id=1, source_target_pairs={{0,1},{1,0},{2,3},{3,2},{4,5},{5,4},{6,7},{7,6},{8,9},{9,8},{10,11... | collective-permute-start | bytes 49160 | tf_op jit(solution)/shard_map/ppermute | solution.py:437
  62.1 5.2 %collective-permute-start.6 = (f32[32,128]{1,0:T(8,128)S(1)}, f32[32,128]{1,0:T(8,128)S(1)}, u32[]{:S(2)}, u32[]{:S(2)}) collective-permute-start(f32[32,128]{1,0:T(8,128)S(1)} %get-tuple-element.30), channel_id=1, source_target_pairs={{0,2},{1,3},{2,0},{3,1},{4,6},{5,7},{6,4},{7,5},{8,10},{9,11},{10,... | collective-permute-start | bytes 49160 | tf_op jit(solution)/shard_map/ppermute | solution.py:437
  63.9 4.9 %collective-permute-start.7 = (f32[32,128]{1,0:T(8,128)S(1)}, f32[32,128]{1,0:T(8,128)S(1)}, u32[]{:S(2)}, u32[]{:S(2)}) collective-permute-start(f32[32,128]{1,0:T(8,128)S(1)} %get-tuple-element.29), channel_id=1, source_target_pairs={{0,3},{1,2},{2,1},{3,0},{4,7},{5,6},{6,5},{7,4},{8,11},{9,10},{10,... | collective-permute-start | bytes 49160 | tf_op jit(solution)/shard_map/ppermute | solution.py:437
  68.9 4.2 %collective-permute-start.8 = (f32[32,128]{1,0:T(8,128)S(1)}, f32[32,128]{1,0:T(8,128)S(1)}, u32[]{:S(2)}, u32[]{:S(2)}) collective-permute-start(f32[32,128]{1,0:T(8,128)S(1)} %broadcast_select_fusion.1), channel_id=1, source_target_pairs={{0,4},{4,0},{8,12},{12,8},{16,20},{20,16},{24,28},{28,24},{32,36},... | collective-permute-start | bytes 49160 | tf_op jit(solution)/shard_map/ppermute | solution.py:398
  69.0 7.2 %collective-permute-start.9 = (f32[32,128]{1,0:T(8,128)S(1)}, f32[32,128]{1,0:T(8,128)S(1)}, u32[]{:S(2)}, u32[]{:S(2)}) collective-permute-start(f32[32,128]{1,0:T(8,128)S(1)} %get-tuple-element.25), channel_id=1, source_target_pairs={{4,8},{8,4},{12,16},{16,12},{20,24},{24,20},{28,32},{32,28},{36,40... | collective-permute-start | bytes 49160 | tf_op jit(solution)/shard_map/ppermute | solution.py:444

commit v9 on v8

--- a/solution.py
+++ b/solution.py
@@ -18,7 +18,7 @@
 XN = 4
 YN = 4
 ZN = 4
-WINDOW = 68
+WINDOW = 20
 PACKED = ST * ST
 UNROLL = 4
 f32 = jnp.float32
@@ -54,19 +54,20 @@
     core, _ = core_and_dop()
     copies = []
     for out, half in ((near, core), (send, 1 - core)):
-        first = half * 64
-        for start, at, count in (
-            (first, 2, 64),
-            ((first + BINS - 2) % BINS, 0, 2),
-            ((first + 64) % BINS, 66, 2),
-        ):
-            copies.append(
-                pltpu.make_async_copy(
-                    echo.at[:, pl.ds(start, count)],
-                    out.at[:, pl.ds(at, count)],
-                    sems.at[len(copies)],
+        for z in range(ZN):
+            first = z * 32 + half * 16
+            for start, at, count in (
+                (first, 2, 16),
+                ((first + BINS - 2) % BINS, 0, 2),
+                ((first + 16) % BINS, 18, 2),
+            ):
+                copies.append(
+                    pltpu.make_async_copy(
+                        echo.at[:, pl.ds(start, count)],
+                        out.at[:, pl.ds(z * WINDOW + at, count)],
+                        sems.at[len(copies)],
+                    )
                 )
-            )
     for c in copies:
         c.start()
     for c in copies:
@@ -76,10 +77,10 @@
 def pack(echo):
     return pl.pallas_call(
         pack_kernel,
-        out_shape=[jax.ShapeDtypeStruct((2, WINDOW, CH, GATES), f32)] * 2,
+        out_shape=[jax.ShapeDtypeStruct((2, ZN * WINDOW, CH, GATES), f32)] * 2,
         in_specs=[pl.BlockSpec(memory_space=pltpu.HBM)],
         out_specs=[VM] * 2,
-        scratch_shapes=[pltpu.SemaphoreType.DMA((6,))],
+        scratch_shapes=[pltpu.SemaphoreType.DMA((6 * ZN,))],
         name="pack",
         compiler_params=pltpu.CompilerParams(vmem_limit_bytes=52 * 2**20),
     )(echo)
@@ -87,30 +88,36 @@
 
 def places(triplet):
     core, _ = core_and_dop()
-    mine = lax.dynamic_slice_in_dim(triplet, core * 64, 64, 0)
-    return ((mine - core * 64 + BINS + 2) & (BINS - 1)).reshape(64 * SLOTS)
-
-
-def gram_kernel(second, place, near, far, mask, *refs):
+    mine = lax.dynamic_index_in_dim(triplet.reshape(ZN, 2, 16, SLOTS), core, 1, keepdims=False)
+    group = iota((ZN, 16, SLOTS), 0)
+    where = group * WINDOW + ((mine - (group * 32 + core * 16) + BINS + 2) & (BINS - 1))
+    return where.reshape(ZN * 16 * SLOTS)
+
+
+def gram_kernel(second, place, near, far, *refs):
+    masks = refs[: 1 if second else 2]
     if second:
-        done, whole, kept, out, sems = refs
+        done, whole, kept, out, sems = refs[1:]
     else:
-        out, kept = refs
+        out, kept = refs[2:]
     core, dop = core_and_dop()
-    group = (dop + 1) % 2 if second else dop % 2
     block = dop * (GATES // BLOCK) + (iota((64, 2 * GATES), 1) % GATES) // BLOCK
     block = block + 32 * (iota((64, 2 * GATES), 1) // GATES)
     pick = (iota((64, 2 * GATES), 0) == block).astype(f32)
-    kept[...] = 1.0 - jnp.dot(mask[...].astype(f32), pick, preferred_element_type=f32)
+    left = 1.0 - jnp.dot(rows(*[m[...] for m in masks]).astype(f32), pick, preferred_element_type=f32)
+    for k in range(2):
+        kept[k] = left[16 * k : 16 * k + 16]
     zero = jnp.zeros((16, 4 * GATES), bf16)
-
-    def operands(i):
-        m = kept[i : i + 1]
+    base = 2 if second else 0
+
+    def operands(k, i):
+        z = dop ^ (base + k)
+        m = kept[k, pl.ds(i, 1), :]
         mn = jnp.broadcast_to(m[:, :GATES], (CH, GATES)).astype(bf16)
         mf = jnp.broadcast_to(m[:, GATES:], (CH, GATES)).astype(bf16)
         hi, lo, left, right, rest, last = [], [], [], [], [], []
         for t in range(SLOTS):
-            s = place[(group * 32 + i) * SLOTS + t]
+            s = place[(z * 16 + i) * SLOTS + t]
             un, uf, vn, vf = split(near[0, s]), split(far[0, s]), split(near[1, s]), split(far[1, s])
             hi.append(lanes(un[0], uf[0], vn[0], vf[0]))
             lo.append(lanes(un[1], uf[1], vn[1], vf[1]))
@@ -130,7 +137,8 @@
     lane16 = iota((CH, GATES), 1)
     mine8 = iota((8, GATES), 1) // 16 == iota((8, GATES), 0)
 
-    def store(q, p):
+    def store(k, i, p):
+        q = k * 16 + i
         p0, p1 = p[:16], pltpu.roll(p[16:32], 48, 1)
         p2 = pltpu.roll(p[32:], 96, 1)
         tail = [pltpu.roll(p2[h : h + 8], 0, 1, stride=16, stride_axis=0) for h in (0, 8)]
@@ -141,9 +149,9 @@
             extra = jnp.sum(jnp.where(mine8, tail[j], 0.0), 0, keepdims=True)
             out[q, :, (16 + j) * GATES : (17 + j) * GATES] = extra
 
-    def pair(i):
-        ha, wa, la = operands(i)
-        hb, wb, lb = operands(i + 1)
+    def pair(k, i):
+        ha, wa, la = operands(k, i)
+        hb, wb, lb = operands(k, i + 1)
         rhs = rows(*ha, zero, *hb, zero, *wa, zero, *wb, zero)
         dims = (((1,), (1,)), ((), ()))
         g = lax.dot_general(rows(la, lb), rhs, dims, preferred_element_type=f32)
@@ -155,40 +163,41 @@
         re = jnp.where(first, ga[:ST], gb[:ST])
         im = jnp.where(first, ga[ST:], gb[ST:])
         p = jnp.where(low, re, im)
-        store(i, p)
-        store(i + 1, pltpu.roll(p, HALF, 1))
+        store(k, i, p)
+        store(k, i + 1, pltpu.roll(p, HALF, 1))
 
     copies = []
 
-    def ship(value, first, at, count):
+    def ship(value, k):
+        first = pl.multiple_of((dop ^ k) * 16, 16)
         copies.append(
             pltpu.make_async_copy(
-                value.at[pl.ds(first, count)],
-                whole.at[pl.ds(pl.multiple_of(at + first, 16), count)],
-                sems.at[len(copies)],
+                value.at[pl.ds((k % 2) * 16, 16)], whole.at[pl.ds(first, 16)], sems.at[k]
             )
         )
         copies[-1].start()
 
     if second:
-        ship(done, 0, (1 - group) * 32, 32)
-    for i in range(0, 32, 2):
-        pair(i)
-        if second and i in (14, 30):
-            ship(out, i - 14, group * 32, 16)
+        ship(done, 0)
+        ship(done, 1)
+    for k in range(2):
+        for i in range(0, 16, 2):
+            pair(k, i)
+        if second:
+            ship(out, 2 + k)
     for c in copies:
         c.wait()
 
 
-def gram(second, place, near, far, *extra):
+def gram(second, place, near, far, extra):
     block = (32, 1, PACKED)
-    kept = pltpu.VMEM((32, 2 * GATES), f32)
+    kept = pltpu.VMEM((2, 16, 2 * GATES), f32)
     return pl.pallas_call(
         functools.partial(gram_kernel, second),
-        out_shape=jax.ShapeDtypeStruct((64, 1, PACKED) if second else block, f32),
-        in_specs=[SM] + [VM] * (4 if second else 3),
-        out_specs=pl.BlockSpec(memory_space=pl.ANY) if second else VM,
-        scratch_shapes=[kept, pltpu.VMEM(block, f32), pltpu.SemaphoreType.DMA((3,))] if second else [kept],
+        out_shape=pltpu.HBM((64, 1, PACKED), f32) if second else jax.ShapeDtypeStruct(block, f32),
+        in_specs=[SM] + [VM] * 4,
+        out_specs=pl.BlockSpec(memory_space=pltpu.HBM) if second else VM,
+        scratch_shapes=[kept, pltpu.VMEM(block, f32), pltpu.SemaphoreType.DMA((4,))] if second else [kept],
         name="gram_b" if second else "gram_a",
         compiler_params=pltpu.CompilerParams(vmem_limit_bytes=VMEM_LIMIT),
     )(place, near, far, *extra)
@@ -256,8 +265,9 @@
     row = iota((8, GATES), 0)
     lane = iota((8, GATES), 1)
 
-    def one(i):
-        wt = jnp.broadcast_to(w[i], (8, GATES))
+    def one(k, i):
+        z = dop ^ k
+        wt = jnp.broadcast_to(w[z * 16 + i], (8, GATES))
         turned = jnp.where(
             lane < ST,
             -pltpu.roll(wt, GATES - ST, 1),
@@ -272,7 +282,7 @@
         rhs = [[], [], []]
         for p in range(2):
             for t in range(SLOTS):
-                s = place[i * SLOTS + t]
+                s = place[(z * 16 + i) * SLOTS + t]
                 x = lanes(near[p, s], far[p, s])
                 hi, rest = split(x)
                 x = x - hi.astype(f32)
@@ -286,9 +296,10 @@
         return re * re + im * im
 
     def step(j, c):
-        k = (j // 4) ^ (dop % 2)
-        y = rows(*[one(j * 8 + n) for n in range(8)])
-        at = pl.ds(pl.multiple_of((j % 4) * 8, 8), 8)
+        k = j // 2
+        i = (j % 2) * 8
+        y = rows(*[one(k, i + n) for n in range(8)])
+        at = pl.ds(pl.multiple_of(i, 8), 8)
         own[k, at, :] = y[:, :GATES]
         other[k, at, :] = y[:, GATES:]
         return c
@@ -299,7 +310,7 @@
 def power(place, near, far, w):
     return pl.pallas_call(
         power_kernel,
-        out_shape=[jax.ShapeDtypeStruct((2, 32, GATES), f32)] * 2,
+        out_shape=[jax.ShapeDtypeStruct((ZN, 16, GATES), f32)] * 2,
         in_specs=[SM] + [VM] * 3,
         out_specs=[VM] * 2,
         name="power",
@@ -329,10 +340,14 @@
     core, dop = core_and_dop()
     rank = lax.axis_index("range")
     for k, ref in enumerate((p0, p1, p2, p3)):
-        line[1 + (dop ^ k)] = ref[...]
-    line[5 * (1 - core)] = inner[...]
-    line[5 * core] = jnp.zeros((32, GATES), f32)
-    p = lanes(*[line[j] for j in range(6)])
+        at = 1 + (dop ^ k)
+        line[at, core] = ref[0]
+        line[at, 1 - core] = ref[1]
+    at = 5 * (1 - core)
+    line[at, 1 - core] = inner[0]
+    line[at, core] = inner[1]
+    line[5 * core] = jnp.zeros((2, 16, GATES), f32)
+    p = lanes(*[rows(line[j, 0], line[j, 1]) for j in range(6)])
     g = guard[:, :1]
     t = train[:, :1]
     left, right = window_sums(p, g, t)
@@ -351,7 +366,7 @@
         out_shape=jax.ShapeDtypeStruct((3, 32, 4 * GATES), f32),
         in_specs=[VM] * 7,
         out_specs=VM,
-        scratch_shapes=[pltpu.VMEM((6, 32, GATES), f32)],
+        scratch_shapes=[pltpu.VMEM((6, 2, 16, GATES), f32)],
         name="noise",
         compiler_params=pltpu.CompilerParams(vmem_limit_bytes=VMEM_LIMIT),
     )(*pieces, inner, guard, train)
@@ -359,9 +374,10 @@
 
 def cfar_kernel(known, outer, guard, train, out, line):
     core, _ = core_and_dop()
-    line[core] = outer[...]
-    line[1 - core] = jnp.zeros((32, GATES), f32)
-    p = lanes(line[0], line[1])
+    line[core, 1 - core] = outer[0]
+    line[core, core] = outer[1]
+    line[1 - core] = jnp.zeros((2, 16, GATES), f32)
+    p = lanes(*[rows(line[j, 0], line[j, 1]) for j in range(2)])
     left, right = window_sums(p, guard[:, :1], train[:, :1])
     sums = known[1]
     head = sums[:, :GATES] + jnp.where(core == 0, left[:, GATES:], 0.0)
@@ -376,7 +392,7 @@
         out_shape=jax.ShapeDtypeStruct((32, 4 * GATES), f32),
         in_specs=[VM] * 4,
         out_specs=VM,
-        scratch_shapes=[pltpu.VMEM((2, 32, GATES), f32)],
+        scratch_shapes=[pltpu.VMEM((2, 2, 16, GATES), f32)],
         name="cfar",
         compiler_params=pltpu.CompilerParams(vmem_limit_bytes=VMEM_LIMIT),
     )(known, outer, guard, train)
@@ -400,7 +416,7 @@
 
 def steering(bin_taper, phases):
     core, dop = core_and_dop()
-    b = core * 64 + dop * 16 + lax.axis_index("range") // 2
+    b = dop * 32 + core * 16 + lax.axis_index("range") // 2
     taper = lax.dynamic_index_in_dim(bin_taper, b, 0, keepdims=False)
 
     def lay(values):
@@ -416,12 +432,11 @@
     near, far = pack(echoes)
     far, other = lax.optimization_barrier((far, other))
     far = swap(far)
-    mine = lanes(excluded, other)
-    across = lax.ppermute(mine, "dop", flipped(2))
-    m0 = jnp.where(dop // 2 == core, mine, across)
-    m1 = lax.ppermute(m0, "dop", flipped(1))
-    part = gram(False, place, near, far, m0)
-    part = gram(True, place, near, far, m1, part)
+    mine = lax.dynamic_slice_in_dim(lanes(excluded, other), core * 16, 16, 0)
+    m1 = lax.ppermute(mine, "dop", flipped(1))
+    m2 = lax.ppermute(rows(mine, m1), "dop", flipped(2))
+    part = gram(False, place, near, far, [mine, m1])
+    part = gram(True, place, near, far, [m2, part])
     part = lax.all_to_all(part, BOTH, 0, 0, tiled=True, axis_index_groups=SAME_CORE)
     sr, si = steering(bin_taper, phases)
     guard = jnp.broadcast_to(guard_len[:, None], (32, GATES))
@@ -431,9 +446,7 @@
     w = lax.all_to_all(w, BOTH, 0, 0, tiled=True, axis_index_groups=SAME_CORE)
     own, away = power(place, near, far, w)
     came = swap(away)
-    pieces = [
-        jnp.where((dop // 2) ^ (k // 2) == core, own[k % 2], came[k % 2]) for k in range(ZN)
-    ]
+    pieces = [jnp.stack([own[k], came[k]]) for k in range(ZN)]
     pieces = [pieces[0]] + [lax.ppermute(pieces[k], "dop", flipped(k)) for k in (1, 2, 3)]
     p0, p1, p2, p3 = pieces
     ranges = lax.axis_size("range")

time: 78.5 us -> 76.3 us (0.972)
  waiting for transfers between devices: 18.4 us -> 16.9 us
  starting transfers between devices: 26.2 us -> 24.8 us
    all_to_all x1, starting transfers between devices: 11.1 us -> 10 us  [shards(): lax.all_to_all(part, BOTH, 0, 0, tiled=True, axis_index_groups=SAME_CORE)]
  transfers between devices with their start and end apart: 11 -> 11, of which waited for: 6 -> 7; matrix products, arithmetic and copies ran while one was open for 2% -> 2% of each run, Pallas kernels for 9% -> 9%
where the time goes in v9:
time: 76.3 us; the launch traced here: 75.7 us
  starting transfers between devices  24.8 us (33%)
  Pallas kernels  18 us (24%)
  waiting for transfers between devices  16.9 us (22%)
  blocking collectives  14.1 us (18%)
  local copies, waits for them, and re-layouts  1.47 us (2%)
    all_to_all x1, blocking collectives, shards(): w = lax.all_to_all(w, BOTH, 0, 0, tiled=True, axis_index_groups=SAME_CORE)  14.1 us
    all_to_all x1, waiting for transfers between devices, shards(): lax.all_to_all(part, BOTH, 0, 0, tiled=True, axis_index_groups=SAME_CORE)  10.5 us
    all_to_all x1, starting transfers between devices, shards(): lax.all_to_all(part, BOTH, 0, 0, tiled=True, axis_index_groups=SAME_CORE)  10 us
    pallas_call x2, Pallas kernels, gram(): pl.pallas_call(functools.partial(gram_kernel, second), out_shape=pltpu.HB...  6.15 us
    ppermute x1, starting transfers between devices, shards(): outer = lax.ppermute(jnp.where(core == 0, head, tail), 'range', pairs)  4.12 us
    ppermute x3, starting transfers between devices, shards(): lax.ppermute(pieces[k], 'dop', flipped(k))  4.09 us
    ppermute x1, starting transfers between devices, shards(): m2 = lax.ppermute(rows(mine, m1), 'dop', flipped(2))  3.88 us
    pallas_call x1, Pallas kernels, solve(): pl.pallas_call(solve_kernel, out_shape=jax.ShapeDtypeStruct((64, 1, GATES...  3.37 us
  transfers between devices with their start and end apart: 11, of which 7 were waited for; matrix products, arithmetic and copies ran while one was open for 2% of the time, Pallas kernels for 9%

profile of v9, /device:TPU:8, one launch (start us, length us, event | category | flops | bytes accessed | tf_op | source)
XLA Modules:
  0.0 75.7 jit_solution(2993396507401067648)
XLA Ops:
  0.0 0.1 collective-permute-start
  0.1 3.0 %pack.1 = (f32[2,80,16,128]{3,2,1,0:T(8,128)S(1)}, f32[2,80,16,128]{3,2,1,0:T(8,128)}) custom-call(f32[2,128,16,128]{3,2,1,0:T(8,128)} %echo.1), custom_call_target="tpu_custom_call" | custom-call | tf_op jit(solution)/shard_map/pack/pallas_call | solution.py:78
  3.1 0.0 collective-permute-done
  3.1 0.6 collective-permute-start.1
  3.7 0.1 reshape.43
  3.8 0.1 fusion.refs_0_
  3.9 1.9 %collective-permute-start.2 = (s32[16,64]{1,0:T(8,128)S(1)}, s32[16,64]{1,0:T(8,128)S(1)}, u32[]{:S(2)}, u32[]{:S(2)}) collective-permute-start(s32[16,64]{1,0:T(8,128)S(1)} %fusion.refs_0_), channel_id=1, source_target_pairs={{0,1},{1,0},{2,3},{3,2},{4,5},{5,4},{6,7},{7,6},{8,9},{9,8},{10,11... | collective-permute-start | bytes 12296 | tf_op jit(solution)/shard_map/ppermute | solution.py:436
  5.8 0.1 copy.9
  5.9 0.1 squeeze.6
  6.1 0.1 iota.18
  6.1 0.1 iota.19
  6.3 0.1 iota.15
  6.4 0.1 iota.16
  6.5 1.1 %collective-permute-done.2.refs_1_ = s32[16,64]{1,0:T(8,128)S(1)} collective-permute-done((s32[16,64]{1,0:T(8,128)S(1)}, s32[16,64]{1,0:T(8,128)S(1)}, u32[]{:S(2)}, u32[]{:S(2)}) %collective-permute-start.2) | collective-permute-done | bytes 4128 | tf_op jit(solution)/shard_map/ppermute | solution.py:436
  7.6 3.9 %collective-permute-start.3 = (s32[32,64]{1,0:T(8,128)S(1)}, s32[32,64]{1,0:T(8,128)S(1)}, u32[]{:S(2)}, u32[]{:S(2)}) collective-permute-start(s32[32,64]{1,0:T(8,128)S(1)} %pad_add_fusion), channel_id=1, source_target_pairs={{0,2},{1,3},{2,0},{3,1},{4,6},{5,7},{6,4},{7,5},{8,10},{9,11},{10,... | collective-permute-start | bytes 24584 | tf_op jit(solution)/shard_map/ppermute | solution.py:437
  11.5 0.0 collective-permute-done.1.far
  11.5 2.7 %gram_a.1.refs_1_ = f32[32,1,2304]{2,1,0:T(1,128)S(1)} custom-call(s32[192]{0:T(256)S(1)} %and_add_fusion.place, f32[2,80,16,128]{3,2,1,0:T(8,128)S(1)} %get-tuple-element.15.near, f32[2,80,16,128]{3,2,1,0:T(8,128)S(1)} %collective-permute-done.1.far, s32[16,64]{1,0:T(8,128)S(1)} %fusion.refs_0_, s32[16,64]{1,0:T(8,128)S(1)} %collective-permute-done.2.refs_1_), custom_call_target="tpu_custom_call" | custom-call | tf_op jit(solution)/shard_map/gram_a/pallas_call | solution.py:195
  14.2 0.0 copy-start.5
  14.2 0.0 copy-start.3
  14.2 0.0 copy-start.4
  14.2 0.0 collective-permute-done.3.refs_0_
  14.2 3.4 %gram_b.1 = f32[64,1,2304]{2,1,0:T(1,128)} custom-call(s32[192]{0:T(256)S(1)} %and_add_fusion.place, f32[2,80,16,128]{3,2,1,0:T(8,128)S(1)} %get-tuple-element.15.near, f32[2,80,16,128]{3,2,1,0:T(8,128)S(1)} %collective-permute-done.1.far, s32[32,64]{1,0:T(8,128)S(1)} %collective-permute-done.3.refs_0_, f32[32,1,2304]{2,1,0:T(1,128)S(1)} %gram_a.1.refs_1_), custom_call_target="tpu_custom_call" | custom-call | tf_op jit(solution)/shard_map/gram_b/pallas_call | solution.py:195
  17.7 10.0 %all-to-all-start = ((f32[64,1,2304]{2,1,0:T(1,128)}), f32[64,1,2304]{2,1,0:T(1,128)S(1)}, u32[]{:S(2)}, u32[]{:S(2)}) async-start(f32[64,1,2304]{2,1,0:T(1,128)} %gram_b.1), calls=%async_computation | async-start | bytes 1179648 | tf_op jit(solution)/shard_map/all_to_all | solution.py:440
  27.7 0.2 dynamic-slice_reduce_fusion
  28.0 0.1 broadcast_multiply_fusion
  28.0 0.1 mul.72
  28.1 0.1 mul.75
  28.2 0.1 broadcast_in_dim.8.sr
  28.3 0.1 broadcast_in_dim.9.si
  28.3 0.1 broadcast_in_dim.10.guard
  28.4 0.1 broadcast_in_dim.11.train
  28.5 10.5 %all-to-all-done.parts = f32[64,1,2304]{2,1,0:T(1,128)S(1)} async-done(((f32[64,1,2304]{2,1,0:T(1,128)}), f32[64,1,2304]{2,1,0:T(1,128)S(1)}, u32[]{:S(2)}, u32[]{:S(2)}) %all-to-all-start) | async-done | bytes 589856 | tf_op jit(solution)/shard_map/all_to_all | solution.py:440
  39.0 3.4 %solve.1 = f32[64,1,128]{2,1,0:T(1,128)S(1)} custom-call(f32[64,1,2304]{2,1,0:T(1,128)S(1)} %all-to-all-done.parts, f32[48,128]{1,0:T(8,128)S(1)} %broadcast_in_dim.8.sr, f32[48,128]{1,0:T(8,128)S(1)} %broadcast_in_dim.9.si), custom_call_target="tpu_custom_call" | custom-call | tf_op jit(solution)/shard_map/solve/pallas_call | solution.py:252
  42.4 14.1 %all_to_all.10.w = f32[64,1,128]{2,1,0:T(1,128)S(1)} all-to-all(f32[64,1,128]{2,1,0:T(1,128)S(1)} %solve.1), channel_id=1, replica_groups={{0,8,16,24,32,40,48,56,64,72,80,88,96,104,112,120,1,9,17,25,33,41,49,57..., dimensions={0} | all-to-all | bytes 65536 | tf_op jit(solution)/shard_map/all_to_all | solution.py:446
  56.5 2.6 %power.1 = (f32[4,16,128]{2,1,0:T(8,128)S(1)}, f32[4,16,128]{2,1,0:T(8,128)S(1)}) custom-call(s32[192]{0:T(256)S(1)} %and_add_fusion.place, f32[2,80,16,128]{3,2,1,0:T(8,128)S(1)} %get-tuple-element.15.near, f32[2,80,16,128]{3,2,1,0:T(8,128)S(1)} %collective-permute-done.1.far, f32[64,1,128]{2,1,0:T(1,128)S(1)} %all_to_all.10.w), custom_call_target="tpu_custom_call" | custom-call | tf_op jit(solution)/shard_map/power/pallas_call | solution.py:311
  59.0 0.1 collective-permute-start.4
  59.2 1.2 %collective-permute-done.4 = f32[4,16,128]{2,1,0:T(8,128)S(1)} collective-permute-done((f32[4,16,128]{2,1,0:T(8,128)S(1)}, f32[4,16,128]{2,1,0:T(8,128)S(1)}, u32[]{:S(2)}, u32[]{:S(2)}) %collective-permute-start.4) | collective-permute-done | bytes 32800 | tf_op jit(solution)/shard_map/ppermute | solution.py:414
  60.3 0.9 %collective-permute-start.7 = (f32[2,16,128]{2,1,0:T(8,128)S(1)}, f32[2,16,128]{2,1,0:T(8,128)S(1)}, u32[]{:S(2)}, u32[]{:S(2)}) collective-permute-start(f32[2,16,128]{2,1,0:T(8,128)S(1)} %pad_maximum_fusion.3), channel_id=1, source_target_pairs={{0,3},{1,2},{2,1},{3,0},{4,7},{5,6},{6,5},{7,4},{8,11},{9,10},{10,... | collective-permute-start | bytes 49160 | tf_op jit(solution)/shard_map/ppermute | solution.py:450
  61.3 1.7 %collective-permute-start.6 = (f32[2,16,128]{2,1,0:T(8,128)S(1)}, f32[2,16,128]{2,1,0:T(8,128)S(1)}, u32[]{:S(2)}, u32[]{:S(2)}) collective-permute-start(f32[2,16,128]{2,1,0:T(8,128)S(1)} %pad_maximum_fusion.2), channel_id=1, source_target_pairs={{0,2},{1,3},{2,0},{3,1},{4,6},{5,7},{6,4},{7,5},{8,10},{9,11},{10,... | collective-permute-start | bytes 49160 | tf_op jit(solution)/shard_map/ppermute | solution.py:450
  63.0 1.5 %collective-permute-start.5 = (f32[2,16,128]{2,1,0:T(8,128)S(1)}, f32[2,16,128]{2,1,0:T(8,128)S(1)}, u32[]{:S(2)}, u32[]{:S(2)}) collective-permute-start(f32[2,16,128]{2,1,0:T(8,128)S(1)} %pad_maximum_fusion.1), channel_id=1, source_target_pairs={{0,1},{1,0},{2,3},{3,2},{4,5},{5,4},{6,7},{7,6},{8,9},{9,8},{10,11... | collective-permute-start | bytes 49160 | tf_op jit(solution)/shard_map/ppermute | solution.py:450
  64.4 0.9 %collective-permute-done.7.p3 = f32[2,16,128]{2,1,0:T(8,128)S(1)} collective-permute-done((f32[2,16,128]{2,1,0:T(8,128)S(1)}, f32[2,16,128]{2,1,0:T(8,128)S(1)}, u32[]{:S(2)}, u32[]{:S(2)}) %collective-permute-start.7) | collective-permute-done | bytes 16416 | tf_op jit(solution)/shard_map/ppermute | solution.py:450
  65.3 1.2 %collective-permute-done.6.p2 = f32[2,16,128]{2,1,0:T(8,128)S(1)} collective-permute-done((f32[2,16,128]{2,1,0:T(8,128)S(1)}, f32[2,16,128]{2,1,0:T(8,128)S(1)}, u32[]{:S(2)}, u32[]{:S(2)}) %collective-permute-start.6) | collective-permute-done | bytes 16416 | tf_op jit(solution)/shard_map/ppermute | solution.py:450
  66.5 0.2 collective-permute-done.5.p1
  66.7 0.1 collective-permute-start.8
  66.8 4.1 %collective-permute-start.9 = (f32[2,16,128]{2,1,0:T(8,128)S(1)}, f32[2,16,128]{2,1,0:T(8,128)S(1)}, u32[]{:S(2)}, u32[]{:S(2)}) collective-permute-start(f32[2,16,128]{2,1,0:T(8,128)S(1)} %get-tuple-element.25), channel_id=1, source_target_pairs={{4,8},{8,4},{12,16},{16,12},{20,24},{24,20},{28,32},{32,28},{36,40... | collective-permute-start | bytes 49160 | tf_op jit(solution)/shard_map/ppermute | solution.py:457
  71.0 1.2 %noise.1.known = f32[3,32,512]{2,1,0:T(8,128)S(1)} custom-call(f32[2,16,128]{2,1,0:T(8,128)S(1)} %get-tuple-element.36.p0, f32[2,16,128]{2,1,0:T(8,128)S(1)} %collective-permute-done.5.p1, f32[2,16,128]{2,1,0:T(8,128)S(1)} %collective-permute-done.6.p2, f32[2,16,128]{2,1,0:T(8,128)S(1)} %collective-permute-done.7.p3, ...), custom_call_target="tpu_custom_call" | custom-call | tf_op jit(solution)/shard_map/noise/pallas_call | solution.py:364
  72.2 1.8 %collective-permute-done.9.outer = f32[2,16,128]{2,1,0:T(8,128)S(1)} collective-permute-done((f32[2,16,128]{2,1,0:T(8,128)S(1)}, f32[2,16,128]{2,1,0:T(8,128)S(1)}, u32[]{:S(2)}, u32[]{:S(2)}) %collective-permute-start.9) | collective-permute-done | bytes 16416 | tf_op jit(solution)/shard_map/ppermute | solution.py:457
  74.0 1.7 %cfar.1 = f32[32,512]{1,0:T(8,128)} custom-call(f32[3,32,512]{2,1,0:T(8,128)S(1)} %noise.1.known, f32[2,16,128]{2,1,0:T(8,128)S(1)} %collective-permute-done.9.outer, s32[32,128]{1,0:T(8,128)S(1)} %broadcast_in_dim.10.guard, s32[32,128]{1,0:T(8,128)S(1)} %broadcast_in_dim.11.train), custom_call_target="tpu_custom_call" | custom-call | tf_op jit(solution)/shard_map/cfar/pallas_call | solution.py:390
  (23 shorter events, 0.1 us)
Async XLA Ops:
  0.0 27.7 %copy-start = (f32[128,3]{0,1:T(4,128)S(1)}, f32[128,3]{0,1:T(4,128)}, u32[]{:S(2)}) copy-start(f32[128,3]{0,1:T(4,128)} %param.9) | copy-start | bytes 4612
  0.0 3.8 %copy-start.1 = (s32[32,32]{1,0:T(8,128)S(1)}, s32[32,32]{1,0:T(8,128)}, u32[]{:S(2)}) copy-start(s32[32,32]{1,0:T(8,128)} %param.11) | copy-start | bytes 12292
  0.0 3.7 %copy-start.2 = (s32[128,3]{0,1:T(4,128)S(1)}, s32[128,3]{0,1:T(4,128)}, u32[]{:S(2)}) copy-start(s32[128,3]{0,1:T(4,128)} %param.8) | copy-start | bytes 4612
  0.0 3.1 %collective-permute-start = (s32[32,32]{1,0:T(8,128)}, s32[32,32]{1,0:T(8,128)S(1)}, u32[]{:S(2)}, u32[]{:S(2)}) collective-permute-start(s32[32,32]{1,0:T(8,128)} %param.11), channel_id=1, source_target_pairs={{0,4},{4,0},{8,12},{12,8},{16,20},{20,16},{24,28},{28,24},{32,36},... | collective-permute-start | bytes 12296 | tf_op jit(solution)/shard_map/ppermute | solution.py:414
  3.1 8.3 %collective-permute-start.1 = (f32[2,80,16,128]{3,2,1,0:T(8,128)}, f32[2,80,16,128]{3,2,1,0:T(8,128)S(1)}, u32[]{:S(2)}, u32[]{:S(2)}) collective-permute-start(f32[2,80,16,128]{3,2,1,0:T(8,128)} %get-tuple-element.17), channel_id=1, source_target_pairs={{0,4},{4,0},{8,12},{12,8},{16,20},{20,16},{24,28},{28,24},{32,36},... | collective-permute-start | bytes 3932168 | tf_op jit(solution)/shard_map/ppermute | solution.py:414
  3.9 3.7 %collective-permute-start.2 = (s32[16,64]{1,0:T(8,128)S(1)}, s32[16,64]{1,0:T(8,128)S(1)}, u32[]{:S(2)}, u32[]{:S(2)}) collective-permute-start(s32[16,64]{1,0:T(8,128)S(1)} %fusion.refs_0_), channel_id=1, source_target_pairs={{0,1},{1,0},{2,3},{3,2},{4,5},{5,4},{6,7},{7,6},{8,9},{9,8},{10,11... | collective-permute-start | bytes 12296 | tf_op jit(solution)/shard_map/ppermute | solution.py:436
  7.6 6.7 %collective-permute-start.3 = (s32[32,64]{1,0:T(8,128)S(1)}, s32[32,64]{1,0:T(8,128)S(1)}, u32[]{:S(2)}, u32[]{:S(2)}) collective-permute-start(s32[32,64]{1,0:T(8,128)S(1)} %pad_add_fusion), channel_id=1, source_target_pairs={{0,2},{1,3},{2,0},{3,1},{4,6},{5,7},{6,4},{7,5},{8,10},{9,11},{10,... | collective-permute-start | bytes 24584 | tf_op jit(solution)/shard_map/ppermute | solution.py:437
  14.2 13.7 %copy-start.5 = (f32[16]{0:T(128)S(1)}, f32[16]{0:T(128)}, u32[]{:S(2)}) copy-start(f32[16]{0:T(128)} %param.10) | copy-start | bytes 196
  14.2 14.1 %copy-start.3 = (s32[32]{0:T(128)S(1)}, s32[32]{0:T(128)}, u32[]{:S(2)}) copy-start(s32[32]{0:T(128)} %param.12) | copy-start | bytes 388
  14.2 14.2 %copy-start.4 = (s32[32]{0:T(128)S(1)}, s32[32]{0:T(128)}, u32[]{:S(2)}) copy-start(s32[32]{0:T(128)} %param.13) | copy-start | bytes 388
  17.7 21.3 %all-to-all-start = ((f32[64,1,2304]{2,1,0:T(1,128)}), f32[64,1,2304]{2,1,0:T(1,128)S(1)}, u32[]{:S(2)}, u32[]{:S(2)}) async-start(f32[64,1,2304]{2,1,0:T(1,128)} %gram_b.1), calls=%async_computation | async-start | bytes 1179648 | tf_op jit(solution)/shard_map/all_to_all | solution.py:440
  59.0 1.3 %collective-permute-start.4 = (f32[4,16,128]{2,1,0:T(8,128)S(1)}, f32[4,16,128]{2,1,0:T(8,128)S(1)}, u32[]{:S(2)}, u32[]{:S(2)}) collective-permute-start(f32[4,16,128]{2,1,0:T(8,128)S(1)} %get-tuple-element.22), channel_id=1, source_target_pairs={{0,4},{4,0},{8,12},{12,8},{16,20},{20,16},{24,28},{28,24},{32,36},... | collective-permute-start | bytes 98312 | tf_op jit(solution)/shard_map/ppermute | solution.py:414
  60.3 5.0 %collective-permute-start.7 = (f32[2,16,128]{2,1,0:T(8,128)S(1)}, f32[2,16,128]{2,1,0:T(8,128)S(1)}, u32[]{:S(2)}, u32[]{:S(2)}) collective-permute-start(f32[2,16,128]{2,1,0:T(8,128)S(1)} %pad_maximum_fusion.3), channel_id=1, source_target_pairs={{0,3},{1,2},{2,1},{3,0},{4,7},{5,6},{6,5},{7,4},{8,11},{9,10},{10,... | collective-permute-start | bytes 49160 | tf_op jit(solution)/shard_map/ppermute | solution.py:450
  61.3 5.2 %collective-permute-start.6 = (f32[2,16,128]{2,1,0:T(8,128)S(1)}, f32[2,16,128]{2,1,0:T(8,128)S(1)}, u32[]{:S(2)}, u32[]{:S(2)}) collective-permute-start(f32[2,16,128]{2,1,0:T(8,128)S(1)} %pad_maximum_fusion.2), channel_id=1, source_target_pairs={{0,2},{1,3},{2,0},{3,1},{4,6},{5,7},{6,4},{7,5},{8,10},{9,11},{10,... | collective-permute-start | bytes 49160 | tf_op jit(solution)/shard_map/ppermute | solution.py:450
  63.0 3.7 %collective-permute-start.5 = (f32[2,16,128]{2,1,0:T(8,128)S(1)}, f32[2,16,128]{2,1,0:T(8,128)S(1)}, u32[]{:S(2)}, u32[]{:S(2)}) collective-permute-start(f32[2,16,128]{2,1,0:T(8,128)S(1)} %pad_maximum_fusion.1), channel_id=1, source_target_pairs={{0,1},{1,0},{2,3},{3,2},{4,5},{5,4},{6,7},{7,6},{8,9},{9,8},{10,11... | collective-permute-start | bytes 49160 | tf_op jit(solution)/shard_map/ppermute | solution.py:450
  66.7 4.2 %collective-permute-start.8 = (f32[2,16,128]{2,1,0:T(8,128)S(1)}, f32[2,16,128]{2,1,0:T(8,128)S(1)}, u32[]{:S(2)}, u32[]{:S(2)}) collective-permute-start(f32[2,16,128]{2,1,0:T(8,128)S(1)} %broadcast_select_fusion.1), channel_id=1, source_target_pairs={{0,4},{4,0},{8,12},{12,8},{16,20},{20,16},{24,28},{28,24},{32,36},... | collective-permute-start | bytes 49160 | tf_op jit(solution)/shard_map/ppermute | solution.py:414
  66.8 7.2 %collective-permute-start.9 = (f32[2,16,128]{2,1,0:T(8,128)S(1)}, f32[2,16,128]{2,1,0:T(8,128)S(1)}, u32[]{:S(2)}, u32[]{:S(2)}) collective-permute-start(f32[2,16,128]{2,1,0:T(8,128)S(1)} %get-tuple-element.25), channel_id=1, source_target_pairs={{4,8},{8,4},{12,16},{16,12},{20,24},{24,20},{28,32},{32,28},{36,40... | collective-permute-start | bytes 49160 | tf_op jit(solution)/shard_map/ppermute | solution.py:457

commit v10 on v9

--- a/solution.py
+++ b/solution.py
@@ -203,6 +203,33 @@
     )(place, near, far, *extra)
 
 
+def plus(a, b):
+    return a[0] + b[0], a[1] + b[1]
+
+
+def minus(a, b):
+    return a[0] - b[0], a[1] - b[1]
+
+
+def times(a, b):
+    return a[0] * b[0] - a[1] * b[1], a[0] * b[1] + a[1] * b[0]
+
+
+def inner(a, b):
+    return a[0] * b[0] + a[1] * b[1], a[0] * b[1] - a[1] * b[0]
+
+
+def half_inverse(a, d, b):
+    inv = 1.0 / (a * d - (b[0] * b[0] + b[1] * b[1]))
+    a, d, b = a * inv, d * inv, (b[0] * inv, b[1] * inv)
+
+    def apply(u, v):
+        bv, bu = times(b, v), inner(b, u)
+        return (d * u[0] - bv[0], d * u[1] - bv[1]), (a * v[0] - bu[0], a * v[1] - bu[1])
+
+    return apply
+
+
 def solve_kernel(parts, sr, si, out):
     row = iota((ST, GATES), 0)
     lane = iota((ST, GATES), 1)
@@ -218,27 +245,33 @@
     im = jnp.where(row < lane, p, jnp.where(row == lane, 0.0, -full))
     are = jnp.where(lane < ST, re, sr[...])
     aim = jnp.where(lane < ST, im, si[...])
-    for k in range(0, ST, 2):
-        i0 = jnp.full((ST, GATES), k, jnp.int32)
-        i1 = jnp.full((ST, GATES), k + 1, jnp.int32)
-        c0r = jnp.take_along_axis(are, i0, 1)
-        c0i = jnp.take_along_axis(aim, i0, 1)
-        c1r = jnp.take_along_axis(are, i1, 1)
-        c1i = jnp.take_along_axis(aim, i1, 1)
-        r0, q0 = are[k : k + 1], aim[k : k + 1]
-        r1, q1 = are[k + 1 : k + 2], aim[k + 1 : k + 2]
-        a, d = c0r[k : k + 1], c1r[k + 1 : k + 2]
-        br, bi = c1r[k : k + 1], c1i[k : k + 1]
-        inv = 1.0 / (a * d - (br * br + bi * bi))
-        a, d, br, bi = a * inv, d * inv, br * inv, bi * inv
-        n0r = d * r0 - (br * r1 - bi * q1)
-        n0i = d * q0 - (br * q1 + bi * r1)
-        n1r = a * r1 - (br * r0 + bi * q0)
-        n1i = a * q1 - (br * q0 - bi * r0)
-        ur = (c0r * n0r - c0i * n0i) + (c1r * n1r - c1i * n1i)
-        ui = (c0r * n0i + c0i * n0r) + (c1r * n1i + c1i * n1r)
-        are = jnp.where(row == k, n0r, jnp.where(row == k + 1, n1r, are - ur))
-        aim = jnp.where(row == k, n0i, jnp.where(row == k + 1, n1i, aim - ui))
+    for k in range(0, ST, 4):
+        cols = []
+        for j in range(4):
+            at = jnp.full((ST, GATES), k + j, jnp.int32)
+            cols.append((jnp.take_along_axis(are, at, 1), jnp.take_along_axis(aim, at, 1)))
+        piv = [[(c[0][k + i : k + i + 1], c[1][k + i : k + i + 1]) for c in cols] for i in range(4)]
+        r = [(are[k + i : k + i + 1], aim[k + i : k + i + 1]) for i in range(4)]
+        first = half_inverse(piv[0][0][0], piv[1][1][0], piv[0][1])
+        x = first(r[0], r[1])
+        y2 = first(piv[0][2], piv[1][2])
+        y3 = first(piv[0][3], piv[1][3])
+        t2 = minus(piv[2][2], plus(inner(piv[0][2], y2[0]), inner(piv[1][2], y2[1])))
+        t3 = minus(piv[3][3], plus(inner(piv[0][3], y3[0]), inner(piv[1][3], y3[1])))
+        t23 = minus(piv[2][3], plus(inner(piv[0][2], y3[0]), inner(piv[1][2], y3[1])))
+        r2 = minus(r[2], plus(inner(piv[0][2], x[0]), inner(piv[1][2], x[1])))
+        r3 = minus(r[3], plus(inner(piv[0][3], x[0]), inner(piv[1][3], x[1])))
+        n2, n3 = half_inverse(t2[0], t3[0], t23)(r2, r3)
+        n0 = minus(x[0], plus(times(y2[0], n2), times(y3[0], n3)))
+        n1 = minus(x[1], plus(times(y2[1], n2), times(y3[1], n3)))
+        new = (n0, n1, n2, n3)
+        ur, ui = times(cols[0], n0)
+        for j in range(1, 4):
+            ur, ui = plus((ur, ui), times(cols[j], new[j]))
+        are, aim = are - ur, aim - ui
+        for j in range(4):
+            are = jnp.where(row == k + j, new[j][0], are)
+            aim = jnp.where(row == k + j, new[j][1], aim)
     pad = jnp.zeros((GATES - ST, GATES), f32)
     wr = rows(are, pad).T[ST : ST + 1]
     wi = rows(aim, pad).T[ST : ST + 1]
@@ -336,7 +369,7 @@
     return left, right
 
 
-def noise_kernel(p0, p1, p2, p3, inner, guard, train, out, line):
+def noise_kernel(p0, p1, p2, p3, inner, guard, train, whole, edge, line, ready, sem):
     core, dop = core_and_dop()
     rank = lax.axis_index("range")
     for k, ref in enumerate((p0, p1, p2, p3)):
@@ -355,47 +388,67 @@
     pos = rank * (4 * GATES) + iota((32, 4 * GATES), 1)
     left_count = jnp.maximum(jnp.minimum(pos - g - 1, TOTAL - 1) - jnp.maximum(pos - g - t, 0) + 1, 0)
     right_count = jnp.maximum(jnp.minimum(pos + g + t, TOTAL - 1) - jnp.maximum(pos + g + 1, 0) + 1, 0)
-    out[0] = p[:, lo:hi]
-    out[1] = left[:, lo:hi] + right[:, lo:hi]
-    out[2] = (left_count + right_count).astype(f32)
+    sums = left[:, lo:hi] + right[:, lo:hi]
+    count = (left_count + right_count).astype(f32)
+    p = p[:, lo:hi]
+    ready[...] = p / (sums / count + EPS)
+    copy = pltpu.make_async_copy(ready, whole, sem)
+    copy.start()
+    for j, value in enumerate((p, sums, count)):
+        edge[j] = jnp.where(core == 0, value[:, :GATES], value[:, 3 * GATES :])
+    copy.wait()
 
 
 def noise(pieces, inner, guard, train):
     return pl.pallas_call(
         noise_kernel,
-        out_shape=jax.ShapeDtypeStruct((3, 32, 4 * GATES), f32),
+        out_shape=[
+            pltpu.HBM((32, 4 * GATES), f32),
+            jax.ShapeDtypeStruct((3, 32, GATES), f32),
+        ],
         in_specs=[VM] * 7,
-        out_specs=VM,
-        scratch_shapes=[pltpu.VMEM((6, 2, 16, GATES), f32)],
+        out_specs=[pl.BlockSpec(memory_space=pltpu.HBM), VM],
+        scratch_shapes=[
+            pltpu.VMEM((6, 2, 16, GATES), f32),
+            pltpu.VMEM((32, 4 * GATES), f32),
+            pltpu.SemaphoreType.DMA,
+        ],
         name="noise",
         compiler_params=pltpu.CompilerParams(vmem_limit_bytes=VMEM_LIMIT),
     )(*pieces, inner, guard, train)
 
 
-def cfar_kernel(known, outer, guard, train, out, line):
+def cfar_kernel(whole, edge, outer, guard, train, out, line, ready, sem):
     core, _ = core_and_dop()
     line[core, 1 - core] = outer[0]
     line[core, core] = outer[1]
     line[1 - core] = jnp.zeros((2, 16, GATES), f32)
     p = lanes(*[rows(line[j, 0], line[j, 1]) for j in range(2)])
     left, right = window_sums(p, guard[:, :1], train[:, :1])
-    sums = known[1]
-    head = sums[:, :GATES] + jnp.where(core == 0, left[:, GATES:], 0.0)
-    tail = sums[:, 3 * GATES :] + jnp.where(core == 1, right[:, :GATES], 0.0)
-    sums = lanes(head, sums[:, GATES : 3 * GATES], tail)
-    out[...] = known[0] / (sums / known[2] + EPS)
+    sums = edge[1] + jnp.where(core == 0, left[:, GATES:], right[:, :GATES])
+    ready[...] = edge[0] / (sums / edge[2] + EPS)
+    at = pl.multiple_of(core * (3 * GATES), GATES)
+    copy = pltpu.make_async_copy(ready, out.at[:, pl.ds(at, GATES)], sem)
+    copy.start()
+    copy.wait()
 
 
 def cfar(known, outer, guard, train):
+    hbm = pl.BlockSpec(memory_space=pltpu.HBM)
     return pl.pallas_call(
         cfar_kernel,
-        out_shape=jax.ShapeDtypeStruct((32, 4 * GATES), f32),
-        in_specs=[VM] * 4,
-        out_specs=VM,
-        scratch_shapes=[pltpu.VMEM((2, 2, 16, GATES), f32)],
+        out_shape=pltpu.HBM((32, 4 * GATES), f32),
+        in_specs=[hbm] + [VM] * 4,
+        out_specs=hbm,
+        scratch_shapes=[
+            pltpu.VMEM((2, 2, 16, GATES), f32),
+            pltpu.VMEM((32, GATES), f32),
+            pltpu.SemaphoreType.DMA,
+        ],
+        input_output_aliases={0: 0},
         name="cfar",
         compiler_params=pltpu.CompilerParams(vmem_limit_bytes=VMEM_LIMIT),
-    )(known, outer, guard, train)
+    )(*known, outer, guard, train)
 
 
 BOTH = ("range", "dop")

time: 76.3 us -> 75.4 us (0.988)
    pallas_call x1, Pallas kernels: 3.37 us -> 2.51 us  [solve(): pl.pallas_call(solve_kernel, out_shape=jax.ShapeDtypeStruct((64, 1, GATES...]
  transfers between devices with their start and end apart: 11 -> 11, of which waited for: 7 -> 7; matrix products, arithmetic and copies ran while one was open for 2% -> 2% of each run, Pallas kernels for 9% -> 10%
where the time goes in v10:
time: 75.4 us; the launch traced here: 74.8 us
  starting transfers between devices  24.8 us (33%)
  Pallas kernels  17.8 us (24%)
  waiting for transfers between devices  16.2 us (21%)
  blocking collectives  14.1 us (19%)
  local copies, waits for them, and re-layouts  1.47 us (2%)
    all_to_all x1, blocking collectives, shards(): w = lax.all_to_all(w, BOTH, 0, 0, tiled=True, axis_index_groups=SAME_CORE)  14.1 us
    all_to_all x1, waiting for transfers between devices, shards(): lax.all_to_all(part, BOTH, 0, 0, tiled=True, axis_index_groups=SAME_CORE)  10.5 us
    all_to_all x1, starting transfers between devices, shards(): lax.all_to_all(part, BOTH, 0, 0, tiled=True, axis_index_groups=SAME_CORE)  9.97 us
    pallas_call x2, Pallas kernels, gram(): pl.pallas_call(functools.partial(gram_kernel, second), out_shape=pltpu.HB...  6.17 us
    ppermute x1, starting transfers between devices, shards(): outer = lax.ppermute(jnp.where(core == 0, head, tail), 'range', pairs)  4.11 us
    ppermute x3, starting transfers between devices, shards(): lax.ppermute(pieces[k], 'dop', flipped(k))  4.09 us
    ppermute x1, starting transfers between devices, shards(): m2 = lax.ppermute(rows(mine, m1), 'dop', flipped(2))  3.88 us
    pallas_call x1, Pallas kernels, pack(): pl.pallas_call(pack_kernel, out_shape=[jax.ShapeDtypeStruct((2, ZN * WIND...  2.99 us
  transfers between devices with their start and end apart: 11, of which 7 were waited for; matrix products, arithmetic and copies ran while one was open for 2% of the time, Pallas kernels for 10%

profile of v10, /device:TPU:8, one launch (start us, length us, event | category | flops | bytes accessed | tf_op | source)
XLA Modules:
  0.0 74.8 jit_solution(5636539513862518357)
XLA Ops:
  0.0 0.1 collective-permute-start
  0.1 3.0 %pack.1 = (f32[2,80,16,128]{3,2,1,0:T(8,128)S(1)}, f32[2,80,16,128]{3,2,1,0:T(8,128)}) custom-call(f32[2,128,16,128]{3,2,1,0:T(8,128)} %echo.1), custom_call_target="tpu_custom_call" | custom-call | tf_op jit(solution)/shard_map/pack/pallas_call | solution.py:78
  3.1 0.0 collective-permute-done
  3.1 0.6 collective-permute-start.1
  3.7 0.1 reshape.43
  3.8 0.1 fusion.refs_0_
  3.9 1.9 %collective-permute-start.2 = (s32[16,64]{1,0:T(8,128)S(1)}, s32[16,64]{1,0:T(8,128)S(1)}, u32[]{:S(2)}, u32[]{:S(2)}) collective-permute-start(s32[16,64]{1,0:T(8,128)S(1)} %fusion.refs_0_), channel_id=1, source_target_pairs={{0,1},{1,0},{2,3},{3,2},{4,5},{5,4},{6,7},{7,6},{8,9},{9,8},{10,11... | collective-permute-start | bytes 12296 | tf_op jit(solution)/shard_map/ppermute | solution.py:489
  5.8 0.1 copy.10
  5.9 0.1 squeeze.6
  6.1 0.1 iota.18
  6.1 0.1 iota.19
  6.3 0.1 iota.15
  6.4 0.1 iota.16
  6.5 1.1 %collective-permute-done.2.refs_1_ = s32[16,64]{1,0:T(8,128)S(1)} collective-permute-done((s32[16,64]{1,0:T(8,128)S(1)}, s32[16,64]{1,0:T(8,128)S(1)}, u32[]{:S(2)}, u32[]{:S(2)}) %collective-permute-start.2) | collective-permute-done | bytes 4128 | tf_op jit(solution)/shard_map/ppermute | solution.py:489
  7.6 3.9 %collective-permute-start.3 = (s32[32,64]{1,0:T(8,128)S(1)}, s32[32,64]{1,0:T(8,128)S(1)}, u32[]{:S(2)}, u32[]{:S(2)}) collective-permute-start(s32[32,64]{1,0:T(8,128)S(1)} %pad_add_fusion), channel_id=1, source_target_pairs={{0,2},{1,3},{2,0},{3,1},{4,6},{5,7},{6,4},{7,5},{8,10},{9,11},{10,... | collective-permute-start | bytes 24584 | tf_op jit(solution)/shard_map/ppermute | solution.py:490
  11.5 0.0 collective-permute-done.1.far
  11.5 2.7 %gram_a.1.refs_1_ = f32[32,1,2304]{2,1,0:T(1,128)S(1)} custom-call(s32[192]{0:T(256)S(1)} %and_add_fusion.place, f32[2,80,16,128]{3,2,1,0:T(8,128)S(1)} %get-tuple-element.17.near, f32[2,80,16,128]{3,2,1,0:T(8,128)S(1)} %collective-permute-done.1.far, s32[16,64]{1,0:T(8,128)S(1)} %fusion.refs_0_, s32[16,64]{1,0:T(8,128)S(1)} %collective-permute-done.2.refs_1_), custom_call_target="tpu_custom_call" | custom-call | tf_op jit(solution)/shard_map/gram_a/pallas_call | solution.py:195
  14.2 0.0 copy-start.5
  14.2 0.0 copy-start.3
  14.2 0.0 copy-start.4
  14.2 3.4 %gram_b.1 = f32[64,1,2304]{2,1,0:T(1,128)} custom-call(s32[192]{0:T(256)S(1)} %and_add_fusion.place, f32[2,80,16,128]{3,2,1,0:T(8,128)S(1)} %get-tuple-element.17.near, f32[2,80,16,128]{3,2,1,0:T(8,128)S(1)} %collective-permute-done.1.far, s32[32,64]{1,0:T(8,128)S(1)} %collective-permute-done.3.refs_0_, f32[32,1,2304]{2,1,0:T(1,128)S(1)} %gram_a.1.refs_1_), custom_call_target="tpu_custom_call" | custom-call | tf_op jit(solution)/shard_map/gram_b/pallas_call | solution.py:195
  17.7 10.0 %all-to-all-start = ((f32[64,1,2304]{2,1,0:T(1,128)}), f32[64,1,2304]{2,1,0:T(1,128)S(1)}, u32[]{:S(2)}, u32[]{:S(2)}) async-start(f32[64,1,2304]{2,1,0:T(1,128)} %gram_b.1), calls=%async_computation | async-start | bytes 1179648 | tf_op jit(solution)/shard_map/all_to_all | solution.py:493
  27.7 0.2 dynamic-slice_reduce_fusion
  27.9 0.1 broadcast_multiply_fusion
  28.0 0.1 mul.72
  28.1 0.1 mul.75
  28.2 0.1 broadcast_in_dim.8.sr
  28.2 0.1 broadcast_in_dim.9.si
  28.3 0.1 broadcast_in_dim.10.guard
  28.4 0.1 broadcast_in_dim.11.train
  28.5 10.5 %all-to-all-done.parts = f32[64,1,2304]{2,1,0:T(1,128)S(1)} async-done(((f32[64,1,2304]{2,1,0:T(1,128)}), f32[64,1,2304]{2,1,0:T(1,128)S(1)}, u32[]{:S(2)}, u32[]{:S(2)}) %all-to-all-start) | async-done | bytes 589856 | tf_op jit(solution)/shard_map/all_to_all | solution.py:493
  39.0 2.5 %solve.1 = f32[64,1,128]{2,1,0:T(1,128)S(1)} custom-call(f32[64,1,2304]{2,1,0:T(1,128)S(1)} %all-to-all-done.parts, f32[48,128]{1,0:T(8,128)S(1)} %broadcast_in_dim.8.sr, f32[48,128]{1,0:T(8,128)S(1)} %broadcast_in_dim.9.si), custom_call_target="tpu_custom_call" | custom-call | tf_op jit(solution)/shard_map/solve/pallas_call | solution.py:285
  41.5 14.1 %all_to_all.10.w = f32[64,1,128]{2,1,0:T(1,128)S(1)} all-to-all(f32[64,1,128]{2,1,0:T(1,128)S(1)} %solve.1), channel_id=1, replica_groups={{0,8,16,24,32,40,48,56,64,72,80,88,96,104,112,120,1,9,17,25,33,41,49,57..., dimensions={0} | all-to-all | bytes 65536 | tf_op jit(solution)/shard_map/all_to_all | solution.py:499
  55.6 2.6 %power.1 = (f32[4,16,128]{2,1,0:T(8,128)S(1)}, f32[4,16,128]{2,1,0:T(8,128)S(1)}) custom-call(s32[192]{0:T(256)S(1)} %and_add_fusion.place, f32[2,80,16,128]{3,2,1,0:T(8,128)S(1)} %get-tuple-element.17.near, f32[2,80,16,128]{3,2,1,0:T(8,128)S(1)} %collective-permute-done.1.far, f32[64,1,128]{2,1,0:T(1,128)S(1)} %all_to_all.10.w), custom_call_target="tpu_custom_call" | custom-call | tf_op jit(solution)/shard_map/power/pallas_call | solution.py:344
  58.2 0.1 collective-permute-start.4
  58.3 1.2 %collective-permute-done.4 = f32[4,16,128]{2,1,0:T(8,128)S(1)} collective-permute-done((f32[4,16,128]{2,1,0:T(8,128)S(1)}, f32[4,16,128]{2,1,0:T(8,128)S(1)}, u32[]{:S(2)}, u32[]{:S(2)}) %collective-permute-start.4) | collective-permute-done | bytes 32800 | tf_op jit(solution)/shard_map/ppermute | solution.py:467
  59.5 0.9 %collective-permute-start.7 = (f32[2,16,128]{2,1,0:T(8,128)S(1)}, f32[2,16,128]{2,1,0:T(8,128)S(1)}, u32[]{:S(2)}, u32[]{:S(2)}) collective-permute-start(f32[2,16,128]{2,1,0:T(8,128)S(1)} %pad_maximum_fusion.3), channel_id=1, source_target_pairs={{0,3},{1,2},{2,1},{3,0},{4,7},{5,6},{6,5},{7,4},{8,11},{9,10},{10,... | collective-permute-start | bytes 49160 | tf_op jit(solution)/shard_map/ppermute | solution.py:503
  60.4 1.7 %collective-permute-start.6 = (f32[2,16,128]{2,1,0:T(8,128)S(1)}, f32[2,16,128]{2,1,0:T(8,128)S(1)}, u32[]{:S(2)}, u32[]{:S(2)}) collective-permute-start(f32[2,16,128]{2,1,0:T(8,128)S(1)} %pad_maximum_fusion.2), channel_id=1, source_target_pairs={{0,2},{1,3},{2,0},{3,1},{4,6},{5,7},{6,4},{7,5},{8,10},{9,11},{10,... | collective-permute-start | bytes 49160 | tf_op jit(solution)/shard_map/ppermute | solution.py:503
  62.1 1.5 %collective-permute-start.5 = (f32[2,16,128]{2,1,0:T(8,128)S(1)}, f32[2,16,128]{2,1,0:T(8,128)S(1)}, u32[]{:S(2)}, u32[]{:S(2)}) collective-permute-start(f32[2,16,128]{2,1,0:T(8,128)S(1)} %pad_maximum_fusion.1), channel_id=1, source_target_pairs={{0,1},{1,0},{2,3},{3,2},{4,5},{5,4},{6,7},{7,6},{8,9},{9,8},{10,11... | collective-permute-start | bytes 49160 | tf_op jit(solution)/shard_map/ppermute | solution.py:503
  63.6 0.9 %collective-permute-done.7.p3 = f32[2,16,128]{2,1,0:T(8,128)S(1)} collective-permute-done((f32[2,16,128]{2,1,0:T(8,128)S(1)}, f32[2,16,128]{2,1,0:T(8,128)S(1)}, u32[]{:S(2)}, u32[]{:S(2)}) %collective-permute-start.7) | collective-permute-done | bytes 16416 | tf_op jit(solution)/shard_map/ppermute | solution.py:503
  64.4 1.2 %collective-permute-done.6.p2 = f32[2,16,128]{2,1,0:T(8,128)S(1)} collective-permute-done((f32[2,16,128]{2,1,0:T(8,128)S(1)}, f32[2,16,128]{2,1,0:T(8,128)S(1)}, u32[]{:S(2)}, u32[]{:S(2)}) %collective-permute-start.6) | collective-permute-done | bytes 16416 | tf_op jit(solution)/shard_map/ppermute | solution.py:503
  65.6 0.2 collective-permute-done.5.p1
  65.9 0.1 collective-permute-start.8
  65.9 4.1 %collective-permute-start.9 = (f32[2,16,128]{2,1,0:T(8,128)S(1)}, f32[2,16,128]{2,1,0:T(8,128)S(1)}, u32[]{:S(2)}, u32[]{:S(2)}) collective-permute-start(f32[2,16,128]{2,1,0:T(8,128)S(1)} %get-tuple-element.29), channel_id=1, source_target_pairs={{4,8},{8,4},{12,16},{16,12},{20,24},{24,20},{28,32},{32,28},{36,40... | collective-permute-start | bytes 49160 | tf_op jit(solution)/shard_map/ppermute | solution.py:510
  70.1 0.0 collective-permute-done.8.inner
  70.1 1.8 %noise.1 = (f32[32,512]{1,0:T(8,128)}, f32[3,32,128]{2,1,0:T(8,128)S(1)}) custom-call(f32[2,16,128]{2,1,0:T(8,128)S(1)} %get-tuple-element.40.p0, f32[2,16,128]{2,1,0:T(8,128)S(1)} %collective-permute-done.5.p1, f32[2,16,128]{2,1,0:T(8,128)S(1)} %collective-permute-done.6.p2, f32[2,16,128]{2,1,0:T(8,128)S(1)} %collective-permute-done.7.p3, ...), custom_call_target="tpu_custom_call" | custom-call | tf_op jit(solution)/shard_map/noise/pallas_call | solution.py:403
  71.9 1.2 %collective-permute-done.9.outer = f32[2,16,128]{2,1,0:T(8,128)S(1)} collective-permute-done((f32[2,16,128]{2,1,0:T(8,128)S(1)}, f32[2,16,128]{2,1,0:T(8,128)S(1)}, u32[]{:S(2)}, u32[]{:S(2)}) %collective-permute-start.9) | collective-permute-done | bytes 16416 | tf_op jit(solution)/shard_map/ppermute | solution.py:510
  73.1 1.7 %cfar.1 = f32[32,512]{1,0:T(8,128)} custom-call(f32[32,512]{1,0:T(8,128)} %get-tuple-element.27.whole, f32[3,32,128]{2,1,0:T(8,128)S(1)} %get-tuple-element.28.edge, f32[2,16,128]{2,1,0:T(8,128)S(1)} %collective-permute-done.9.outer, s32[32,128]{1,0:T(8,128)S(1)} %broadcast_in_dim.10.guard, ...), custom_call_target="tpu_custom_call", output_to_operand_aliasing={{}: (0, {})} | custom-call | tf_op jit(solution)/shard_map/cfar/pallas_call | solution.py:438
  (23 shorter events, 0.1 us)
Async XLA Ops:
  0.0 27.7 %copy-start = (f32[128,3]{0,1:T(4,128)S(1)}, f32[128,3]{0,1:T(4,128)}, u32[]{:S(2)}) copy-start(f32[128,3]{0,1:T(4,128)} %param.9) | copy-start | bytes 4612
  0.0 3.8 %copy-start.1 = (s32[32,32]{1,0:T(8,128)S(1)}, s32[32,32]{1,0:T(8,128)}, u32[]{:S(2)}) copy-start(s32[32,32]{1,0:T(8,128)} %param.11) | copy-start | bytes 12292
  0.0 3.7 %copy-start.2 = (s32[128,3]{0,1:T(4,128)S(1)}, s32[128,3]{0,1:T(4,128)}, u32[]{:S(2)}) copy-start(s32[128,3]{0,1:T(4,128)} %param.8) | copy-start | bytes 4612
  0.0 3.1 %collective-permute-start = (s32[32,32]{1,0:T(8,128)}, s32[32,32]{1,0:T(8,128)S(1)}, u32[]{:S(2)}, u32[]{:S(2)}) collective-permute-start(s32[32,32]{1,0:T(8,128)} %param.11), channel_id=1, source_target_pairs={{0,4},{4,0},{8,12},{12,8},{16,20},{20,16},{24,28},{28,24},{32,36},... | collective-permute-start | bytes 12296 | tf_op jit(solution)/shard_map/ppermute | solution.py:467
  3.1 8.3 %collective-permute-start.1 = (f32[2,80,16,128]{3,2,1,0:T(8,128)}, f32[2,80,16,128]{3,2,1,0:T(8,128)S(1)}, u32[]{:S(2)}, u32[]{:S(2)}) collective-permute-start(f32[2,80,16,128]{3,2,1,0:T(8,128)} %get-tuple-element.19), channel_id=1, source_target_pairs={{0,4},{4,0},{8,12},{12,8},{16,20},{20,16},{24,28},{28,24},{32,36},... | collective-permute-start | bytes 3932168 | tf_op jit(solution)/shard_map/ppermute | solution.py:467
  3.9 3.7 %collective-permute-start.2 = (s32[16,64]{1,0:T(8,128)S(1)}, s32[16,64]{1,0:T(8,128)S(1)}, u32[]{:S(2)}, u32[]{:S(2)}) collective-permute-start(s32[16,64]{1,0:T(8,128)S(1)} %fusion.refs_0_), channel_id=1, source_target_pairs={{0,1},{1,0},{2,3},{3,2},{4,5},{5,4},{6,7},{7,6},{8,9},{9,8},{10,11... | collective-permute-start | bytes 12296 | tf_op jit(solution)/shard_map/ppermute | solution.py:489
  7.6 6.7 %collective-permute-start.3 = (s32[32,64]{1,0:T(8,128)S(1)}, s32[32,64]{1,0:T(8,128)S(1)}, u32[]{:S(2)}, u32[]{:S(2)}) collective-permute-start(s32[32,64]{1,0:T(8,128)S(1)} %pad_add_fusion), channel_id=1, source_target_pairs={{0,2},{1,3},{2,0},{3,1},{4,6},{5,7},{6,4},{7,5},{8,10},{9,11},{10,... | collective-permute-start | bytes 24584 | tf_op jit(solution)/shard_map/ppermute | solution.py:490
  14.2 13.7 %copy-start.5 = (f32[16]{0:T(128)S(1)}, f32[16]{0:T(128)}, u32[]{:S(2)}) copy-start(f32[16]{0:T(128)} %param.10) | copy-start | bytes 196
  14.2 14.1 %copy-start.3 = (s32[32]{0:T(128)S(1)}, s32[32]{0:T(128)}, u32[]{:S(2)}) copy-start(s32[32]{0:T(128)} %param.12) | copy-start | bytes 388
  14.2 14.2 %copy-start.4 = (s32[32]{0:T(128)S(1)}, s32[32]{0:T(128)}, u32[]{:S(2)}) copy-start(s32[32]{0:T(128)} %param.13) | copy-start | bytes 388
  17.7 21.3 %all-to-all-start = ((f32[64,1,2304]{2,1,0:T(1,128)}), f32[64,1,2304]{2,1,0:T(1,128)S(1)}, u32[]{:S(2)}, u32[]{:S(2)}) async-start(f32[64,1,2304]{2,1,0:T(1,128)} %gram_b.1), calls=%async_computation | async-start | bytes 1179648 | tf_op jit(solution)/shard_map/all_to_all | solution.py:493
  58.2 1.3 %collective-permute-start.4 = (f32[4,16,128]{2,1,0:T(8,128)S(1)}, f32[4,16,128]{2,1,0:T(8,128)S(1)}, u32[]{:S(2)}, u32[]{:S(2)}) collective-permute-start(f32[4,16,128]{2,1,0:T(8,128)S(1)} %get-tuple-element.24), channel_id=1, source_target_pairs={{0,4},{4,0},{8,12},{12,8},{16,20},{20,16},{24,28},{28,24},{32,36},... | collective-permute-start | bytes 98312 | tf_op jit(solution)/shard_map/ppermute | solution.py:467
  59.5 5.0 %collective-permute-start.7 = (f32[2,16,128]{2,1,0:T(8,128)S(1)}, f32[2,16,128]{2,1,0:T(8,128)S(1)}, u32[]{:S(2)}, u32[]{:S(2)}) collective-permute-start(f32[2,16,128]{2,1,0:T(8,128)S(1)} %pad_maximum_fusion.3), channel_id=1, source_target_pairs={{0,3},{1,2},{2,1},{3,0},{4,7},{5,6},{6,5},{7,4},{8,11},{9,10},{10,... | collective-permute-start | bytes 49160 | tf_op jit(solution)/shard_map/ppermute | solution.py:503
  60.4 5.2 %collective-permute-start.6 = (f32[2,16,128]{2,1,0:T(8,128)S(1)}, f32[2,16,128]{2,1,0:T(8,128)S(1)}, u32[]{:S(2)}, u32[]{:S(2)}) collective-permute-start(f32[2,16,128]{2,1,0:T(8,128)S(1)} %pad_maximum_fusion.2), channel_id=1, source_target_pairs={{0,2},{1,3},{2,0},{3,1},{4,6},{5,7},{6,4},{7,5},{8,10},{9,11},{10,... | collective-permute-start | bytes 49160 | tf_op jit(solution)/shard_map/ppermute | solution.py:503
  62.1 3.7 %collective-permute-start.5 = (f32[2,16,128]{2,1,0:T(8,128)S(1)}, f32[2,16,128]{2,1,0:T(8,128)S(1)}, u32[]{:S(2)}, u32[]{:S(2)}) collective-permute-start(f32[2,16,128]{2,1,0:T(8,128)S(1)} %pad_maximum_fusion.1), channel_id=1, source_target_pairs={{0,1},{1,0},{2,3},{3,2},{4,5},{5,4},{6,7},{7,6},{8,9},{9,8},{10,11... | collective-permute-start | bytes 49160 | tf_op jit(solution)/shard_map/ppermute | solution.py:503
  65.9 4.2 %collective-permute-start.8 = (f32[2,16,128]{2,1,0:T(8,128)S(1)}, f32[2,16,128]{2,1,0:T(8,128)S(1)}, u32[]{:S(2)}, u32[]{:S(2)}) collective-permute-start(f32[2,16,128]{2,1,0:T(8,128)S(1)} %broadcast_select_fusion.1), channel_id=1, source_target_pairs={{0,4},{4,0},{8,12},{12,8},{16,20},{20,16},{24,28},{28,24},{32,36},... | collective-permute-start | bytes 49160 | tf_op jit(solution)/shard_map/ppermute | solution.py:467
  65.9 7.2 %collective-permute-start.9 = (f32[2,16,128]{2,1,0:T(8,128)S(1)}, f32[2,16,128]{2,1,0:T(8,128)S(1)}, u32[]{:S(2)}, u32[]{:S(2)}) collective-permute-start(f32[2,16,128]{2,1,0:T(8,128)S(1)} %get-tuple-element.29), channel_id=1, source_target_pairs={{4,8},{8,4},{12,16},{16,12},{20,24},{24,20},{28,32},{32,28},{36,40... | collective-permute-start | bytes 49160 | tf_op jit(solution)/shard_map/ppermute | solution.py:510

commit v11 on v10

--- a/solution.py
+++ b/solution.py
@@ -351,21 +351,36 @@
     )(place, near, far, w)
 
 
-def window_sums(p, g, t):
+def window_sums(p, g, t, left_tiles, right_tiles):
     width = p.shape[1]
     total = p
-    acc = jnp.where((t & 1) == 1, p, 0.0)
-    for k in range(1, 7):
-        total = total + pltpu.roll(total, width - (1 << (k - 1)), 1)
-        acc = jnp.where((t >> k) & 1 == 1, total + pltpu.roll(acc, width - (1 << k), 1), acc)
-    right = acc
-    shift = g + 1
-    for k in range(3):
-        right = jnp.where((shift >> k) & 1 == 1, pltpu.roll(right, width - (1 << k), 1), right)
-    left = acc
-    shift = g + t
-    for k in range(7):
-        left = jnp.where((shift >> k) & 1 == 1, pltpu.roll(left, 1 << k, 1), left)
+    acc = None
+    for bit in (0, 2, 4):
+        k = 1 << bit
+        digit = (t >> bit) & 3
+        shifted = [total] + [pltpu.roll(total, width - j * k, 1) for j in (1, 2, 3)]
+        two = shifted[0] + shifted[1]
+        three = two + shifted[2]
+        part = jnp.where(digit == 1, total, jnp.where(digit == 2, two, three))
+        if acc is None:
+            acc = jnp.where(digit == 0, 0.0, part)
+        else:
+            moved = [pltpu.roll(acc, width - j * k, 1) for j in (1, 2, 3)]
+            moved = jnp.where(digit == 1, moved[0], jnp.where(digit == 2, moved[1], moved[2]))
+            acc = jnp.where(digit == 0, acc, part + moved)
+        total = two + (shifted[2] + shifted[3])
+    acc = jnp.where(t == 64, total, acc)
+    tiles = [acc[:, j : j + GATES] for j in range(0, width, GATES)]
+    lane = iota(tiles[0].shape, 1)
+
+    def taken(j, other, shift, inside):
+        at = (lane + shift) & (GATES - 1)
+        here = jnp.take_along_axis(tiles[j], at, 1)
+        return jnp.where(inside, here, jnp.take_along_axis(tiles[other], at, 1))
+
+    back, ahead = -(g + t), g + 1
+    left = [taken(j, j - 1, back, lane + back >= 0) for j in left_tiles]
+    right = [taken(j, j + 1, ahead, lane + ahead < GATES) for j in right_tiles]
     return left, right
 
 
@@ -383,12 +398,12 @@
     p = lanes(*[rows(line[j, 0], line[j, 1]) for j in range(6)])
     g = guard[:, :1]
     t = train[:, :1]
-    left, right = window_sums(p, g, t)
+    left, right = window_sums(p, g, t, (1, 2, 3, 4), (1, 2, 3, 4))
     lo, hi = GATES, GATES + 4 * GATES
     pos = rank * (4 * GATES) + iota((32, 4 * GATES), 1)
     left_count = jnp.maximum(jnp.minimum(pos - g - 1, TOTAL - 1) - jnp.maximum(pos - g - t, 0) + 1, 0)
     right_count = jnp.maximum(jnp.minimum(pos + g + t, TOTAL - 1) - jnp.maximum(pos + g + 1, 0) + 1, 0)
-    sums = left[:, lo:hi] + right[:, lo:hi]
+    sums = lanes(*left) + lanes(*right)
     count = (left_count + right_count).astype(f32)
     p = p[:, lo:hi]
     ready[...] = p / (sums / count + EPS)
@@ -424,8 +439,8 @@
     line[core, core] = outer[1]
     line[1 - core] = jnp.zeros((2, 16, GATES), f32)
     p = lanes(*[rows(line[j, 0], line[j, 1]) for j in range(2)])
-    left, right = window_sums(p, guard[:, :1], train[:, :1])
-    sums = edge[1] + jnp.where(core == 0, left[:, GATES:], right[:, :GATES])
+    left, right = window_sums(p, guard[:, :1], train[:, :1], (1,), (0,))
+    sums = edge[1] + jnp.where(core == 0, left[0], right[0])
     ready[...] = edge[0] / (sums / edge[2] + EPS)
     at = pl.multiple_of(core * (3 * GATES), GATES)
     copy = pltpu.make_async_copy(ready, out.at[:, pl.ds(at, GATES)], sem)

time: 75.4 us -> 74.8 us (level)
  Pallas kernels: 17.8 us -> 16.8 us
where the time goes in v11:
time: 74.8 us; the launch traced here: 74.2 us
  starting transfers between devices  24.8 us (33%)
  Pallas kernels  16.8 us (22%)
  waiting for transfers between devices  16.6 us (22%)
  blocking collectives  14.1 us (19%)
  local copies, waits for them, and re-layouts  1.47 us (2%)
    all_to_all x1, blocking collectives, shards(): w = lax.all_to_all(w, BOTH, 0, 0, tiled=True, axis_index_groups=SAME_CORE)  14.1 us
    all_to_all x1, waiting for transfers between devices, shards(): lax.all_to_all(part, BOTH, 0, 0, tiled=True, axis_index_groups=SAME_CORE)  10.5 us
    all_to_all x1, starting transfers between devices, shards(): lax.all_to_all(part, BOTH, 0, 0, tiled=True, axis_index_groups=SAME_CORE)  9.97 us
    pallas_call x2, Pallas kernels, gram(): pl.pallas_call(functools.partial(gram_kernel, second), out_shape=pltpu.HB...  6.17 us
    ppermute x1, starting transfers between devices, shards(): outer = lax.ppermute(jnp.where(core == 0, head, tail), 'range', pairs)  4.11 us
    ppermute x3, starting transfers between devices, shards(): lax.ppermute(pieces[k], 'dop', flipped(k))  4.09 us
    ppermute x1, starting transfers between devices, shards(): m2 = lax.ppermute(rows(mine, m1), 'dop', flipped(2))  3.88 us
    pallas_call x1, Pallas kernels, pack(): pl.pallas_call(pack_kernel, out_shape=[jax.ShapeDtypeStruct((2, ZN * WIND...  2.99 us
  transfers between devices with their start and end apart: 11, of which 7 were waited for; matrix products, arithmetic and copies ran while one was open for 2% of the time, Pallas kernels for 10%

profile of v11, /device:TPU:8, one launch (start us, length us, event | category | flops | bytes accessed | tf_op | source)
XLA Modules:
  0.0 74.2 jit_solution(10775146159618870491)
XLA Ops:
  0.0 0.1 collective-permute-start
  0.1 3.0 %pack.1 = (f32[2,80,16,128]{3,2,1,0:T(8,128)S(1)}, f32[2,80,16,128]{3,2,1,0:T(8,128)}) custom-call(f32[2,128,16,128]{3,2,1,0:T(8,128)} %echo.1), custom_call_target="tpu_custom_call" | custom-call | tf_op jit(solution)/shard_map/pack/pallas_call | solution.py:78
  3.1 0.0 collective-permute-done
  3.1 0.6 collective-permute-start.1
  3.7 0.1 reshape.43
  3.8 0.1 fusion.refs_0_
  3.9 1.9 %collective-permute-start.2 = (s32[16,64]{1,0:T(8,128)S(1)}, s32[16,64]{1,0:T(8,128)S(1)}, u32[]{:S(2)}, u32[]{:S(2)}) collective-permute-start(s32[16,64]{1,0:T(8,128)S(1)} %fusion.refs_0_), channel_id=1, source_target_pairs={{0,1},{1,0},{2,3},{3,2},{4,5},{5,4},{6,7},{7,6},{8,9},{9,8},{10,11... | collective-permute-start | bytes 12296 | tf_op jit(solution)/shard_map/ppermute | solution.py:504
  5.8 0.1 copy.10
  5.9 0.1 squeeze.6
  6.1 0.1 iota.18
  6.1 0.1 iota.19
  6.3 0.1 iota.15
  6.4 0.1 iota.16
  6.5 1.1 %collective-permute-done.2.refs_1_ = s32[16,64]{1,0:T(8,128)S(1)} collective-permute-done((s32[16,64]{1,0:T(8,128)S(1)}, s32[16,64]{1,0:T(8,128)S(1)}, u32[]{:S(2)}, u32[]{:S(2)}) %collective-permute-start.2) | collective-permute-done | bytes 4128 | tf_op jit(solution)/shard_map/ppermute | solution.py:504
  7.6 3.9 %collective-permute-start.3 = (s32[32,64]{1,0:T(8,128)S(1)}, s32[32,64]{1,0:T(8,128)S(1)}, u32[]{:S(2)}, u32[]{:S(2)}) collective-permute-start(s32[32,64]{1,0:T(8,128)S(1)} %pad_add_fusion), channel_id=1, source_target_pairs={{0,2},{1,3},{2,0},{3,1},{4,6},{5,7},{6,4},{7,5},{8,10},{9,11},{10,... | collective-permute-start | bytes 24584 | tf_op jit(solution)/shard_map/ppermute | solution.py:505
  11.5 0.0 collective-permute-done.1.far
  11.5 2.7 %gram_a.1.refs_1_ = f32[32,1,2304]{2,1,0:T(1,128)S(1)} custom-call(s32[192]{0:T(256)S(1)} %and_add_fusion.place, f32[2,80,16,128]{3,2,1,0:T(8,128)S(1)} %get-tuple-element.17.near, f32[2,80,16,128]{3,2,1,0:T(8,128)S(1)} %collective-permute-done.1.far, s32[16,64]{1,0:T(8,128)S(1)} %fusion.refs_0_, s32[16,64]{1,0:T(8,128)S(1)} %collective-permute-done.2.refs_1_), custom_call_target="tpu_custom_call" | custom-call | tf_op jit(solution)/shard_map/gram_a/pallas_call | solution.py:195
  14.2 0.0 copy-start.5
  14.2 0.0 copy-start.3
  14.2 0.0 copy-start.4
  14.2 0.0 collective-permute-done.3.refs_0_
  14.2 3.4 %gram_b.1 = f32[64,1,2304]{2,1,0:T(1,128)} custom-call(s32[192]{0:T(256)S(1)} %and_add_fusion.place, f32[2,80,16,128]{3,2,1,0:T(8,128)S(1)} %get-tuple-element.17.near, f32[2,80,16,128]{3,2,1,0:T(8,128)S(1)} %collective-permute-done.1.far, s32[32,64]{1,0:T(8,128)S(1)} %collective-permute-done.3.refs_0_, f32[32,1,2304]{2,1,0:T(1,128)S(1)} %gram_a.1.refs_1_), custom_call_target="tpu_custom_call" | custom-call | tf_op jit(solution)/shard_map/gram_b/pallas_call | solution.py:195
  17.7 10.0 %all-to-all-start = ((f32[64,1,2304]{2,1,0:T(1,128)}), f32[64,1,2304]{2,1,0:T(1,128)S(1)}, u32[]{:S(2)}, u32[]{:S(2)}) async-start(f32[64,1,2304]{2,1,0:T(1,128)} %gram_b.1), calls=%async_computation | async-start | bytes 1179648 | tf_op jit(solution)/shard_map/all_to_all | solution.py:508
  27.7 0.2 dynamic-slice_reduce_fusion
  27.9 0.1 broadcast_multiply_fusion
  28.0 0.1 mul.72
  28.1 0.1 mul.75
  28.2 0.1 broadcast_in_dim.8.sr
  28.2 0.1 broadcast_in_dim.9.si
  28.3 0.1 broadcast_in_dim.10.guard
  28.4 0.1 broadcast_in_dim.11.train
  28.5 10.5 %all-to-all-done.parts = f32[64,1,2304]{2,1,0:T(1,128)S(1)} async-done(((f32[64,1,2304]{2,1,0:T(1,128)}), f32[64,1,2304]{2,1,0:T(1,128)S(1)}, u32[]{:S(2)}, u32[]{:S(2)}) %all-to-all-start) | async-done | bytes 589856 | tf_op jit(solution)/shard_map/all_to_all | solution.py:508
  39.0 2.5 %solve.1 = f32[64,1,128]{2,1,0:T(1,128)S(1)} custom-call(f32[64,1,2304]{2,1,0:T(1,128)S(1)} %all-to-all-done.parts, f32[48,128]{1,0:T(8,128)S(1)} %broadcast_in_dim.8.sr, f32[48,128]{1,0:T(8,128)S(1)} %broadcast_in_dim.9.si), custom_call_target="tpu_custom_call" | custom-call | tf_op jit(solution)/shard_map/solve/pallas_call | solution.py:285
  41.5 14.1 %all_to_all.10.w = f32[64,1,128]{2,1,0:T(1,128)S(1)} all-to-all(f32[64,1,128]{2,1,0:T(1,128)S(1)} %solve.1), channel_id=1, replica_groups={{0,8,16,24,32,40,48,56,64,72,80,88,96,104,112,120,1,9,17,25,33,41,49,57..., dimensions={0} | all-to-all | bytes 65536 | tf_op jit(solution)/shard_map/all_to_all | solution.py:514
  55.6 2.6 %power.1 = (f32[4,16,128]{2,1,0:T(8,128)S(1)}, f32[4,16,128]{2,1,0:T(8,128)S(1)}) custom-call(s32[192]{0:T(256)S(1)} %and_add_fusion.place, f32[2,80,16,128]{3,2,1,0:T(8,128)S(1)} %get-tuple-element.17.near, f32[2,80,16,128]{3,2,1,0:T(8,128)S(1)} %collective-permute-done.1.far, f32[64,1,128]{2,1,0:T(1,128)S(1)} %all_to_all.10.w), custom_call_target="tpu_custom_call" | custom-call | tf_op jit(solution)/shard_map/power/pallas_call | solution.py:344
  58.2 0.1 collective-permute-start.4
  58.3 1.2 %collective-permute-done.4 = f32[4,16,128]{2,1,0:T(8,128)S(1)} collective-permute-done((f32[4,16,128]{2,1,0:T(8,128)S(1)}, f32[4,16,128]{2,1,0:T(8,128)S(1)}, u32[]{:S(2)}, u32[]{:S(2)}) %collective-permute-start.4) | collective-permute-done | bytes 32800 | tf_op jit(solution)/shard_map/ppermute | solution.py:482
  59.5 0.9 %collective-permute-start.7 = (f32[2,16,128]{2,1,0:T(8,128)S(1)}, f32[2,16,128]{2,1,0:T(8,128)S(1)}, u32[]{:S(2)}, u32[]{:S(2)}) collective-permute-start(f32[2,16,128]{2,1,0:T(8,128)S(1)} %pad_maximum_fusion.3), channel_id=1, source_target_pairs={{0,3},{1,2},{2,1},{3,0},{4,7},{5,6},{6,5},{7,4},{8,11},{9,10},{10,... | collective-permute-start | bytes 49160 | tf_op jit(solution)/shard_map/ppermute | solution.py:518
  60.4 1.7 %collective-permute-start.6 = (f32[2,16,128]{2,1,0:T(8,128)S(1)}, f32[2,16,128]{2,1,0:T(8,128)S(1)}, u32[]{:S(2)}, u32[]{:S(2)}) collective-permute-start(f32[2,16,128]{2,1,0:T(8,128)S(1)} %pad_maximum_fusion.2), channel_id=1, source_target_pairs={{0,2},{1,3},{2,0},{3,1},{4,6},{5,7},{6,4},{7,5},{8,10},{9,11},{10,... | collective-permute-start | bytes 49160 | tf_op jit(solution)/shard_map/ppermute | solution.py:518
  62.1 1.5 %collective-permute-start.5 = (f32[2,16,128]{2,1,0:T(8,128)S(1)}, f32[2,16,128]{2,1,0:T(8,128)S(1)}, u32[]{:S(2)}, u32[]{:S(2)}) collective-permute-start(f32[2,16,128]{2,1,0:T(8,128)S(1)} %pad_maximum_fusion.1), channel_id=1, source_target_pairs={{0,1},{1,0},{2,3},{3,2},{4,5},{5,4},{6,7},{7,6},{8,9},{9,8},{10,11... | collective-permute-start | bytes 49160 | tf_op jit(solution)/shard_map/ppermute | solution.py:518
  63.6 0.9 %collective-permute-done.7.p3 = f32[2,16,128]{2,1,0:T(8,128)S(1)} collective-permute-done((f32[2,16,128]{2,1,0:T(8,128)S(1)}, f32[2,16,128]{2,1,0:T(8,128)S(1)}, u32[]{:S(2)}, u32[]{:S(2)}) %collective-permute-start.7) | collective-permute-done | bytes 16416 | tf_op jit(solution)/shard_map/ppermute | solution.py:518
  64.4 1.2 %collective-permute-done.6.p2 = f32[2,16,128]{2,1,0:T(8,128)S(1)} collective-permute-done((f32[2,16,128]{2,1,0:T(8,128)S(1)}, f32[2,16,128]{2,1,0:T(8,128)S(1)}, u32[]{:S(2)}, u32[]{:S(2)}) %collective-permute-start.6) | collective-permute-done | bytes 16416 | tf_op jit(solution)/shard_map/ppermute | solution.py:518
  65.7 0.2 collective-permute-done.5.p1
  65.9 0.1 collective-permute-start.8
  66.0 4.1 %collective-permute-start.9 = (f32[2,16,128]{2,1,0:T(8,128)S(1)}, f32[2,16,128]{2,1,0:T(8,128)S(1)}, u32[]{:S(2)}, u32[]{:S(2)}) collective-permute-start(f32[2,16,128]{2,1,0:T(8,128)S(1)} %get-tuple-element.29), channel_id=1, source_target_pairs={{4,8},{8,4},{12,16},{16,12},{20,24},{24,20},{28,32},{32,28},{36,40... | collective-permute-start | bytes 49160 | tf_op jit(solution)/shard_map/ppermute | solution.py:525
  70.1 1.5 %noise.1 = (f32[32,512]{1,0:T(8,128)}, f32[3,32,128]{2,1,0:T(8,128)S(1)}) custom-call(f32[2,16,128]{2,1,0:T(8,128)S(1)} %get-tuple-element.40.p0, f32[2,16,128]{2,1,0:T(8,128)S(1)} %collective-permute-done.5.p1, f32[2,16,128]{2,1,0:T(8,128)S(1)} %collective-permute-done.6.p2, f32[2,16,128]{2,1,0:T(8,128)S(1)} %collective-permute-done.7.p3, ...), custom_call_target="tpu_custom_call" | custom-call | tf_op jit(solution)/shard_map/noise/pallas_call | solution.py:418
  71.6 1.5 %collective-permute-done.9.outer = f32[2,16,128]{2,1,0:T(8,128)S(1)} collective-permute-done((f32[2,16,128]{2,1,0:T(8,128)S(1)}, f32[2,16,128]{2,1,0:T(8,128)S(1)}, u32[]{:S(2)}, u32[]{:S(2)}) %collective-permute-start.9) | collective-permute-done | bytes 16416 | tf_op jit(solution)/shard_map/ppermute | solution.py:525
  73.1 1.1 %cfar.1 = f32[32,512]{1,0:T(8,128)} custom-call(f32[32,512]{1,0:T(8,128)} %get-tuple-element.27.whole, f32[3,32,128]{2,1,0:T(8,128)S(1)} %get-tuple-element.28.edge, f32[2,16,128]{2,1,0:T(8,128)S(1)} %collective-permute-done.9.outer, s32[32,128]{1,0:T(8,128)S(1)} %broadcast_in_dim.10.guard, ...), custom_call_target="tpu_custom_call", output_to_operand_aliasing={{}: (0, {})} | custom-call | tf_op jit(solution)/shard_map/cfar/pallas_call | solution.py:453
  (23 shorter events, 0.1 us)
Async XLA Ops:
  0.0 27.7 %copy-start = (f32[128,3]{0,1:T(4,128)S(1)}, f32[128,3]{0,1:T(4,128)}, u32[]{:S(2)}) copy-start(f32[128,3]{0,1:T(4,128)} %param.9) | copy-start | bytes 4612
  0.0 3.8 %copy-start.1 = (s32[32,32]{1,0:T(8,128)S(1)}, s32[32,32]{1,0:T(8,128)}, u32[]{:S(2)}) copy-start(s32[32,32]{1,0:T(8,128)} %param.11) | copy-start | bytes 12292
  0.0 3.7 %copy-start.2 = (s32[128,3]{0,1:T(4,128)S(1)}, s32[128,3]{0,1:T(4,128)}, u32[]{:S(2)}) copy-start(s32[128,3]{0,1:T(4,128)} %param.8) | copy-start | bytes 4612
  0.0 3.1 %collective-permute-start = (s32[32,32]{1,0:T(8,128)}, s32[32,32]{1,0:T(8,128)S(1)}, u32[]{:S(2)}, u32[]{:S(2)}) collective-permute-start(s32[32,32]{1,0:T(8,128)} %param.11), channel_id=1, source_target_pairs={{0,4},{4,0},{8,12},{12,8},{16,20},{20,16},{24,28},{28,24},{32,36},... | collective-permute-start | bytes 12296 | tf_op jit(solution)/shard_map/ppermute | solution.py:482
  3.1 8.3 %collective-permute-start.1 = (f32[2,80,16,128]{3,2,1,0:T(8,128)}, f32[2,80,16,128]{3,2,1,0:T(8,128)S(1)}, u32[]{:S(2)}, u32[]{:S(2)}) collective-permute-start(f32[2,80,16,128]{3,2,1,0:T(8,128)} %get-tuple-element.19), channel_id=1, source_target_pairs={{0,4},{4,0},{8,12},{12,8},{16,20},{20,16},{24,28},{28,24},{32,36},... | collective-permute-start | bytes 3932168 | tf_op jit(solution)/shard_map/ppermute | solution.py:482
  3.9 3.7 %collective-permute-start.2 = (s32[16,64]{1,0:T(8,128)S(1)}, s32[16,64]{1,0:T(8,128)S(1)}, u32[]{:S(2)}, u32[]{:S(2)}) collective-permute-start(s32[16,64]{1,0:T(8,128)S(1)} %fusion.refs_0_), channel_id=1, source_target_pairs={{0,1},{1,0},{2,3},{3,2},{4,5},{5,4},{6,7},{7,6},{8,9},{9,8},{10,11... | collective-permute-start | bytes 12296 | tf_op jit(solution)/shard_map/ppermute | solution.py:504
  7.6 6.7 %collective-permute-start.3 = (s32[32,64]{1,0:T(8,128)S(1)}, s32[32,64]{1,0:T(8,128)S(1)}, u32[]{:S(2)}, u32[]{:S(2)}) collective-permute-start(s32[32,64]{1,0:T(8,128)S(1)} %pad_add_fusion), channel_id=1, source_target_pairs={{0,2},{1,3},{2,0},{3,1},{4,6},{5,7},{6,4},{7,5},{8,10},{9,11},{10,... | collective-permute-start | bytes 24584 | tf_op jit(solution)/shard_map/ppermute | solution.py:505
  14.2 13.7 %copy-start.5 = (f32[16]{0:T(128)S(1)}, f32[16]{0:T(128)}, u32[]{:S(2)}) copy-start(f32[16]{0:T(128)} %param.10) | copy-start | bytes 196
  14.2 14.1 %copy-start.3 = (s32[32]{0:T(128)S(1)}, s32[32]{0:T(128)}, u32[]{:S(2)}) copy-start(s32[32]{0:T(128)} %param.12) | copy-start | bytes 388
  14.2 14.2 %copy-start.4 = (s32[32]{0:T(128)S(1)}, s32[32]{0:T(128)}, u32[]{:S(2)}) copy-start(s32[32]{0:T(128)} %param.13) | copy-start | bytes 388
  17.7 21.3 %all-to-all-start = ((f32[64,1,2304]{2,1,0:T(1,128)}), f32[64,1,2304]{2,1,0:T(1,128)S(1)}, u32[]{:S(2)}, u32[]{:S(2)}) async-start(f32[64,1,2304]{2,1,0:T(1,128)} %gram_b.1), calls=%async_computation | async-start | bytes 1179648 | tf_op jit(solution)/shard_map/all_to_all | solution.py:508
  58.2 1.3 %collective-permute-start.4 = (f32[4,16,128]{2,1,0:T(8,128)S(1)}, f32[4,16,128]{2,1,0:T(8,128)S(1)}, u32[]{:S(2)}, u32[]{:S(2)}) collective-permute-start(f32[4,16,128]{2,1,0:T(8,128)S(1)} %get-tuple-element.24), channel_id=1, source_target_pairs={{0,4},{4,0},{8,12},{12,8},{16,20},{20,16},{24,28},{28,24},{32,36},... | collective-permute-start | bytes 98312 | tf_op jit(solution)/shard_map/ppermute | solution.py:482
  59.5 5.0 %collective-permute-start.7 = (f32[2,16,128]{2,1,0:T(8,128)S(1)}, f32[2,16,128]{2,1,0:T(8,128)S(1)}, u32[]{:S(2)}, u32[]{:S(2)}) collective-permute-start(f32[2,16,128]{2,1,0:T(8,128)S(1)} %pad_maximum_fusion.3), channel_id=1, source_target_pairs={{0,3},{1,2},{2,1},{3,0},{4,7},{5,6},{6,5},{7,4},{8,11},{9,10},{10,... | collective-permute-start | bytes 49160 | tf_op jit(solution)/shard_map/ppermute | solution.py:518
  60.4 5.2 %collective-permute-start.6 = (f32[2,16,128]{2,1,0:T(8,128)S(1)}, f32[2,16,128]{2,1,0:T(8,128)S(1)}, u32[]{:S(2)}, u32[]{:S(2)}) collective-permute-start(f32[2,16,128]{2,1,0:T(8,128)S(1)} %pad_maximum_fusion.2), channel_id=1, source_target_pairs={{0,2},{1,3},{2,0},{3,1},{4,6},{5,7},{6,4},{7,5},{8,10},{9,11},{10,... | collective-permute-start | bytes 49160 | tf_op jit(solution)/shard_map/ppermute | solution.py:518
  62.1 3.7 %collective-permute-start.5 = (f32[2,16,128]{2,1,0:T(8,128)S(1)}, f32[2,16,128]{2,1,0:T(8,128)S(1)}, u32[]{:S(2)}, u32[]{:S(2)}) collective-permute-start(f32[2,16,128]{2,1,0:T(8,128)S(1)} %pad_maximum_fusion.1), channel_id=1, source_target_pairs={{0,1},{1,0},{2,3},{3,2},{4,5},{5,4},{6,7},{7,6},{8,9},{9,8},{10,11... | collective-permute-start | bytes 49160 | tf_op jit(solution)/shard_map/ppermute | solution.py:518
  65.9 4.2 %collective-permute-start.8 = (f32[2,16,128]{2,1,0:T(8,128)S(1)}, f32[2,16,128]{2,1,0:T(8,128)S(1)}, u32[]{:S(2)}, u32[]{:S(2)}) collective-permute-start(f32[2,16,128]{2,1,0:T(8,128)S(1)} %broadcast_select_fusion.1), channel_id=1, source_target_pairs={{0,4},{4,0},{8,12},{12,8},{16,20},{20,16},{24,28},{28,24},{32,36},... | collective-permute-start | bytes 49160 | tf_op jit(solution)/shard_map/ppermute | solution.py:482
  66.0 7.2 %collective-permute-start.9 = (f32[2,16,128]{2,1,0:T(8,128)S(1)}, f32[2,16,128]{2,1,0:T(8,128)S(1)}, u32[]{:S(2)}, u32[]{:S(2)}) collective-permute-start(f32[2,16,128]{2,1,0:T(8,128)S(1)} %get-tuple-element.29), channel_id=1, source_target_pairs={{4,8},{8,4},{12,16},{16,12},{20,24},{24,20},{28,32},{32,28},{36,40... | collective-permute-start | bytes 49160 | tf_op jit(solution)/shard_map/ppermute | solution.py:525

commit v12 on v11

--- a/solution.py
+++ b/solution.py
@@ -20,7 +20,7 @@
 ZN = 4
 WINDOW = 20
 PACKED = ST * ST
-UNROLL = 4
+UNROLL = 8
 f32 = jnp.float32
 bf16 = jnp.bfloat16
 VMEM_LIMIT = 16 * 2**20
@@ -292,7 +292,7 @@
     )(parts, sr, si)
 
 
-def power_kernel(place, near, far, w, own, other):
+def power_kernel(place, near, far, w, out):
     core, dop = core_and_dop()
     zero = jnp.zeros((32, 2 * GATES), bf16)
     row = iota((8, GATES), 0)
@@ -333,8 +333,8 @@
         i = (j % 2) * 8
         y = rows(*[one(k, i + n) for n in range(8)])
         at = pl.ds(pl.multiple_of(i, 8), 8)
-        own[k, at, :] = y[:, :GATES]
-        other[k, at, :] = y[:, GATES:]
+        out[k, 0, at, :] = y[:, :GATES]
+        out[k, 1, at, :] = y[:, GATES:]
         return c
 
     lax.fori_loop(0, 8, step, 0, unroll=UNROLL)
@@ -343,9 +343,9 @@
 def power(place, near, far, w):
     return pl.pallas_call(
         power_kernel,
-        out_shape=[jax.ShapeDtypeStruct((ZN, 16, GATES), f32)] * 2,
+        out_shape=jax.ShapeDtypeStruct((ZN, 2, 16, GATES), f32),
         in_specs=[SM] + [VM] * 3,
-        out_specs=[VM] * 2,
+        out_specs=VM,
         name="power",
         compiler_params=pltpu.CompilerParams(vmem_limit_bytes=VMEM_LIMIT),
     )(place, near, far, w)
@@ -384,16 +384,19 @@
     return left, right
 
 
-def noise_kernel(p0, p1, p2, p3, inner, guard, train, whole, edge, line, ready, sem):
+def noise_kernel(p0, p1, p2, p3, guard, train, whole, edge, line, ready, sem):
     core, dop = core_and_dop()
     rank = lax.axis_index("range")
     for k, ref in enumerate((p0, p1, p2, p3)):
         at = 1 + (dop ^ k)
         line[at, core] = ref[0]
         line[at, 1 - core] = ref[1]
-    at = 5 * (1 - core)
-    line[at, 1 - core] = inner[0]
-    line[at, core] = inner[1]
+    source = dop ^ (3 * core)
+    for slot, half in ((2, core), (3, 1 - core)):
+        value = p0[slot]
+        for k, ref in ((1, p1), (2, p2), (3, p3)):
+            value = jnp.where(source == k, ref[slot], value)
+        line[5 * (1 - core), half] = value
     line[5 * core] = jnp.zeros((2, 16, GATES), f32)
     p = lanes(*[rows(line[j, 0], line[j, 1]) for j in range(6)])
     g = guard[:, :1]
@@ -414,14 +417,14 @@
     copy.wait()
 
 
-def noise(pieces, inner, guard, train):
+def noise(pieces, guard, train):
     return pl.pallas_call(
         noise_kernel,
         out_shape=[
             pltpu.HBM((32, 4 * GATES), f32),
             jax.ShapeDtypeStruct((3, 32, GATES), f32),
         ],
-        in_specs=[VM] * 7,
+        in_specs=[VM] * 6,
         out_specs=[pl.BlockSpec(memory_space=pltpu.HBM), VM],
         scratch_shapes=[
             pltpu.VMEM((6, 2, 16, GATES), f32),
@@ -430,7 +433,7 @@
         ],
         name="noise",
         compiler_params=pltpu.CompilerParams(vmem_limit_bytes=VMEM_LIMIT),
-    )(*pieces, inner, guard, train)
+    )(*pieces, guard, train)
 
 
 def cfar_kernel(whole, edge, outer, guard, train, out, line, ready, sem):
@@ -512,18 +515,17 @@
     sr, si, guard, train = lax.optimization_barrier((sr, si, guard, train))
     w = solve(part, sr, si)
     w = lax.all_to_all(w, BOTH, 0, 0, tiled=True, axis_index_groups=SAME_CORE)
-    own, away = power(place, near, far, w)
-    came = swap(away)
-    pieces = [jnp.stack([own[k], came[k]]) for k in range(ZN)]
+    mine = power(place, near, far, w)
+    came = swap(mine)
+    pieces = [jnp.stack([mine[k, 0], came[k, 1], mine[k, 1], came[k, 0]]) for k in range(ZN)]
     pieces = [pieces[0]] + [lax.ppermute(pieces[k], "dop", flipped(k)) for k in (1, 2, 3)]
-    p0, p1, p2, p3 = pieces
     ranges = lax.axis_size("range")
+    p0, p1, p2, p3 = [p[:2] for p in pieces]
     tail = jnp.where(dop == 0, p3, jnp.where(dop == 1, p2, jnp.where(dop == 2, p1, p0)))
     head = jnp.where(dop == 0, p0, jnp.where(dop == 1, p1, jnp.where(dop == 2, p2, p3)))
-    inner = swap(jnp.where(core == 0, tail, head))
     pairs = [(i, i + 1 if i % 2 else i - 1) for i in range(1, ranges - 1)]
     outer = lax.ppermute(jnp.where(core == 0, head, tail), "range", pairs)
-    return cfar(noise(pieces, inner, guard, train), outer, guard, train)
+    return cfar(noise(pieces, guard, train), outer, guard, train)
 
 
 def solution(mesh):

time: 74.8 us -> 74.6 us (level)
  waiting for transfers between devices: 16.6 us -> 18.6 us
  starting transfers between devices: 24.8 us -> 23 us
    ppermute x1, starting transfers between devices: 4.11 us -> 2.27 us  [shards(): outer = lax.ppermute(jnp.where(core == 0, head, tail), 'range', pairs)]
    ppermute x1, waiting for transfers between devices: 1.5 us -> 3.34 us  [shards(): outer = lax.ppermute(jnp.where(core == 0, head, tail), 'range', pairs)]
  transfers between devices with their start and end apart: 11 -> 10, of which waited for: 7 -> 7; matrix products, arithmetic and copies ran while one was open for 2% -> 2% of each run, Pallas kernels for 10% -> 10%
where the time goes in v12:
time: 74.6 us; the launch traced here: 74.3 us
  starting transfers between devices  23 us (31%)
  waiting for transfers between devices  18.6 us (25%)
  Pallas kernels  16.8 us (23%)
  blocking collectives  14.1 us (19%)
  local copies, waits for them, and re-layouts  1.47 us (2%)
    all_to_all x1, blocking collectives, shards(): w = lax.all_to_all(w, BOTH, 0, 0, tiled=True, axis_index_groups=SAME_CORE)  14.1 us
    all_to_all x1, waiting for transfers between devices, shards(): lax.all_to_all(part, BOTH, 0, 0, tiled=True, axis_index_groups=SAME_CORE)  10.5 us
    all_to_all x1, starting transfers between devices, shards(): lax.all_to_all(part, BOTH, 0, 0, tiled=True, axis_index_groups=SAME_CORE)  9.98 us
    pallas_call x2, Pallas kernels, gram(): pl.pallas_call(functools.partial(gram_kernel, second), out_shape=pltpu.HB...  6.16 us
    ppermute x3, starting transfers between devices, shards(): lax.ppermute(pieces[k], 'dop', flipped(k))  4.17 us
    ppermute x1, starting transfers between devices, shards(): m2 = lax.ppermute(rows(mine, m1), 'dop', flipped(2))  3.88 us
    ppermute x1, waiting for transfers between devices, shards(): outer = lax.ppermute(jnp.where(core == 0, head, tail), 'range', pairs)  3.34 us
    pallas_call x1, Pallas kernels, pack(): pl.pallas_call(pack_kernel, out_shape=[jax.ShapeDtypeStruct((2, ZN * WIND...  3 us
  transfers between devices with their start and end apart: 10, of which 7 were waited for; matrix products, arithmetic and copies ran while one was open for 2% of the time, Pallas kernels for 10%

profile of v12, /device:TPU:8, one launch (start us, length us, event | category | flops | bytes accessed | tf_op | source)
XLA Modules:
  0.0 74.3 jit_solution(18270045034803554473)
XLA Ops:
  0.0 0.1 collective-permute-start
  0.1 3.0 %pack.1 = (f32[2,80,16,128]{3,2,1,0:T(8,128)S(1)}, f32[2,80,16,128]{3,2,1,0:T(8,128)}) custom-call(f32[2,128,16,128]{3,2,1,0:T(8,128)} %echo.1), custom_call_target="tpu_custom_call" | custom-call | tf_op jit(solution)/shard_map/pack/pallas_call | solution.py:78
  3.1 0.0 collective-permute-done
  3.1 0.6 collective-permute-start.1
  3.7 0.0 copy-done.2
  3.7 0.1 reshape.43
  3.8 0.1 fusion.refs_0_
  3.9 1.9 %collective-permute-start.2 = (s32[16,64]{1,0:T(8,128)S(1)}, s32[16,64]{1,0:T(8,128)S(1)}, u32[]{:S(2)}, u32[]{:S(2)}) collective-permute-start(s32[16,64]{1,0:T(8,128)S(1)} %fusion.refs_0_), channel_id=1, source_target_pairs={{0,1},{1,0},{2,3},{3,2},{4,5},{5,4},{6,7},{7,6},{8,9},{9,8},{10,11... | collective-permute-start | bytes 12296 | tf_op jit(solution)/shard_map/ppermute | solution.py:507
  5.9 0.1 copy.10
  6.0 0.1 squeeze.6
  6.1 0.1 iota.18
  6.2 0.1 iota.19
  6.3 0.1 iota.15
  6.4 0.1 iota.16
  6.5 1.1 %collective-permute-done.2.refs_1_ = s32[16,64]{1,0:T(8,128)S(1)} collective-permute-done((s32[16,64]{1,0:T(8,128)S(1)}, s32[16,64]{1,0:T(8,128)S(1)}, u32[]{:S(2)}, u32[]{:S(2)}) %collective-permute-start.2) | collective-permute-done | bytes 4128 | tf_op jit(solution)/shard_map/ppermute | solution.py:507
  7.6 3.9 %collective-permute-start.3 = (s32[32,64]{1,0:T(8,128)S(1)}, s32[32,64]{1,0:T(8,128)S(1)}, u32[]{:S(2)}, u32[]{:S(2)}) collective-permute-start(s32[32,64]{1,0:T(8,128)S(1)} %pad_add_fusion), channel_id=1, source_target_pairs={{0,2},{1,3},{2,0},{3,1},{4,6},{5,7},{6,4},{7,5},{8,10},{9,11},{10,... | collective-permute-start | bytes 24584 | tf_op jit(solution)/shard_map/ppermute | solution.py:508
  11.5 0.0 collective-permute-done.1.far
  11.5 2.7 %gram_a.1.refs_1_ = f32[32,1,2304]{2,1,0:T(1,128)S(1)} custom-call(s32[192]{0:T(256)S(1)} %and_add_fusion.place, f32[2,80,16,128]{3,2,1,0:T(8,128)S(1)} %get-tuple-element.15.near, f32[2,80,16,128]{3,2,1,0:T(8,128)S(1)} %collective-permute-done.1.far, s32[16,64]{1,0:T(8,128)S(1)} %fusion.refs_0_, s32[16,64]{1,0:T(8,128)S(1)} %collective-permute-done.2.refs_1_), custom_call_target="tpu_custom_call" | custom-call | tf_op jit(solution)/shard_map/gram_a/pallas_call | solution.py:195
  14.2 0.0 copy-start.5
  14.2 0.0 copy-start.3
  14.2 0.0 copy-start.4
  14.2 0.0 collective-permute-done.3.refs_0_
  14.3 3.4 %gram_b.1 = f32[64,1,2304]{2,1,0:T(1,128)} custom-call(s32[192]{0:T(256)S(1)} %and_add_fusion.place, f32[2,80,16,128]{3,2,1,0:T(8,128)S(1)} %get-tuple-element.15.near, f32[2,80,16,128]{3,2,1,0:T(8,128)S(1)} %collective-permute-done.1.far, s32[32,64]{1,0:T(8,128)S(1)} %collective-permute-done.3.refs_0_, f32[32,1,2304]{2,1,0:T(1,128)S(1)} %gram_a.1.refs_1_), custom_call_target="tpu_custom_call" | custom-call | tf_op jit(solution)/shard_map/gram_b/pallas_call | solution.py:195
  17.7 10.0 %all-to-all-start = ((f32[64,1,2304]{2,1,0:T(1,128)}), f32[64,1,2304]{2,1,0:T(1,128)S(1)}, u32[]{:S(2)}, u32[]{:S(2)}) async-start(f32[64,1,2304]{2,1,0:T(1,128)} %gram_b.1), calls=%async_computation | async-start | bytes 1179648 | tf_op jit(solution)/shard_map/all_to_all | solution.py:511
  27.7 0.2 dynamic-slice_reduce_fusion
  28.0 0.1 broadcast_multiply_fusion
  28.0 0.1 mul.72
  28.1 0.1 mul.75
  28.2 0.1 broadcast_in_dim.8.sr
  28.3 0.1 broadcast_in_dim.9.si
  28.3 0.1 broadcast_in_dim.10.guard
  28.4 0.1 broadcast_in_dim.11.train
  28.5 10.5 %all-to-all-done.parts = f32[64,1,2304]{2,1,0:T(1,128)S(1)} async-done(((f32[64,1,2304]{2,1,0:T(1,128)}), f32[64,1,2304]{2,1,0:T(1,128)S(1)}, u32[]{:S(2)}, u32[]{:S(2)}) %all-to-all-start) | async-done | bytes 589856 | tf_op jit(solution)/shard_map/all_to_all | solution.py:511
  39.0 2.5 %solve.1 = f32[64,1,128]{2,1,0:T(1,128)S(1)} custom-call(f32[64,1,2304]{2,1,0:T(1,128)S(1)} %all-to-all-done.parts, f32[48,128]{1,0:T(8,128)S(1)} %broadcast_in_dim.8.sr, f32[48,128]{1,0:T(8,128)S(1)} %broadcast_in_dim.9.si), custom_call_target="tpu_custom_call" | custom-call | tf_op jit(solution)/shard_map/solve/pallas_call | solution.py:285
  41.5 14.1 %all_to_all.10.w = f32[64,1,128]{2,1,0:T(1,128)S(1)} all-to-all(f32[64,1,128]{2,1,0:T(1,128)S(1)} %solve.1), channel_id=1, replica_groups={{0,8,16,24,32,40,48,56,64,72,80,88,96,104,112,120,1,9,17,25,33,41,49,57..., dimensions={0} | all-to-all | bytes 65536 | tf_op jit(solution)/shard_map/all_to_all | solution.py:517
  55.6 2.5 %power.1 = f32[4,2,16,128]{3,2,1,0:T(8,128)S(1)} custom-call(s32[192]{0:T(256)S(1)} %and_add_fusion.place, f32[2,80,16,128]{3,2,1,0:T(8,128)S(1)} %get-tuple-element.15.near, f32[2,80,16,128]{3,2,1,0:T(8,128)S(1)} %collective-permute-done.1.far, f32[64,1,128]{2,1,0:T(1,128)S(1)} %all_to_all.10.w), custom_call_target="tpu_custom_call" | custom-call | tf_op jit(solution)/shard_map/power/pallas_call | solution.py:344
  58.1 0.1 collective-permute-start.4
  58.2 1.2 %collective-permute-done.4 = f32[4,2,16,128]{3,2,1,0:T(8,128)S(1)} collective-permute-done((f32[4,2,16,128]{3,2,1,0:T(8,128)S(1)}, f32[4,2,16,128]{3,2,1,0:T(8,128)S(1)}, u32[]{:S(2)}, u32[]{:S(2)}) %collective-permute-start.4) | collective-permute-done | bytes 65568 | tf_op jit(solution)/shard_map/ppermute | solution.py:485
  59.5 1.0 %collective-permute-start.7 = (f32[4,16,128]{2,1,0:T(8,128)S(1)}, f32[4,16,128]{2,1,0:T(8,128)S(1)}, u32[]{:S(2)}, u32[]{:S(2)}) collective-permute-start(f32[4,16,128]{2,1,0:T(8,128)S(1)} %pad_maximum_fusion.3), channel_id=1, source_target_pairs={{0,3},{1,2},{2,1},{3,0},{4,7},{5,6},{6,5},{7,4},{8,11},{9,10},{10,... | collective-permute-start | bytes 98312 | tf_op jit(solution)/shard_map/ppermute | solution.py:521
  60.5 1.7 %collective-permute-start.6 = (f32[4,16,128]{2,1,0:T(8,128)S(1)}, f32[4,16,128]{2,1,0:T(8,128)S(1)}, u32[]{:S(2)}, u32[]{:S(2)}) collective-permute-start(f32[4,16,128]{2,1,0:T(8,128)S(1)} %pad_maximum_fusion.2), channel_id=1, source_target_pairs={{0,2},{1,3},{2,0},{3,1},{4,6},{5,7},{6,4},{7,5},{8,10},{9,11},{10,... | collective-permute-start | bytes 98312 | tf_op jit(solution)/shard_map/ppermute | solution.py:521
  62.2 1.5 %collective-permute-start.5 = (f32[4,16,128]{2,1,0:T(8,128)S(1)}, f32[4,16,128]{2,1,0:T(8,128)S(1)}, u32[]{:S(2)}, u32[]{:S(2)}) collective-permute-start(f32[4,16,128]{2,1,0:T(8,128)S(1)} %pad_maximum_fusion.1), channel_id=1, source_target_pairs={{0,1},{1,0},{2,3},{3,2},{4,5},{5,4},{6,7},{7,6},{8,9},{9,8},{10,11... | collective-permute-start | bytes 98312 | tf_op jit(solution)/shard_map/ppermute | solution.py:521
  63.6 1.4 %collective-permute-done.7.p3 = f32[4,16,128]{2,1,0:T(8,128)S(1)} collective-permute-done((f32[4,16,128]{2,1,0:T(8,128)S(1)}, f32[4,16,128]{2,1,0:T(8,128)S(1)}, u32[]{:S(2)}, u32[]{:S(2)}) %collective-permute-start.7) | collective-permute-done | bytes 32800 | tf_op jit(solution)/shard_map/ppermute | solution.py:521
  65.0 0.9 %collective-permute-done.6.p2 = f32[4,16,128]{2,1,0:T(8,128)S(1)} collective-permute-done((f32[4,16,128]{2,1,0:T(8,128)S(1)}, f32[4,16,128]{2,1,0:T(8,128)S(1)}, u32[]{:S(2)}, u32[]{:S(2)}) %collective-permute-start.6) | collective-permute-done | bytes 32800 | tf_op jit(solution)/shard_map/ppermute | solution.py:521
  65.9 0.2 collective-permute-done.5.p1
  66.1 2.3 %collective-permute-start.8 = (f32[2,16,128]{2,1,0:T(8,128)S(1)}, f32[2,16,128]{2,1,0:T(8,128)S(1)}, u32[]{:S(2)}, u32[]{:S(2)}) collective-permute-start(f32[2,16,128]{2,1,0:T(8,128)S(1)} %select_select_fusion), channel_id=1, source_target_pairs={{4,8},{8,4},{12,16},{16,12},{20,24},{24,20},{28,32},{32,28},{36,40... | collective-permute-start | bytes 49160 | tf_op jit(solution)/shard_map/ppermute | solution.py:527
  68.4 1.5 %noise.1 = (f32[32,512]{1,0:T(8,128)}, f32[3,32,128]{2,1,0:T(8,128)S(1)}) custom-call(f32[4,16,128]{2,1,0:T(8,128)S(1)} %pad_maximum_fusion.p0, f32[4,16,128]{2,1,0:T(8,128)S(1)} %collective-permute-done.5.p1, f32[4,16,128]{2,1,0:T(8,128)S(1)} %collective-permute-done.6.p2, f32[4,16,128]{2,1,0:T(8,128)S(1)} %collective-permute-done.7.p3, ...), custom_call_target="tpu_custom_call" | custom-call | tf_op jit(solution)/shard_map/noise/pallas_call | solution.py:421
  69.9 3.3 %collective-permute-done.8.outer = f32[2,16,128]{2,1,0:T(8,128)S(1)} collective-permute-done((f32[2,16,128]{2,1,0:T(8,128)S(1)}, f32[2,16,128]{2,1,0:T(8,128)S(1)}, u32[]{:S(2)}, u32[]{:S(2)}) %collective-permute-start.8) | collective-permute-done | bytes 16416 | tf_op jit(solution)/shard_map/ppermute | solution.py:527
  73.3 1.1 %cfar.1 = f32[32,512]{1,0:T(8,128)} custom-call(f32[32,512]{1,0:T(8,128)} %get-tuple-element.23.whole, f32[3,32,128]{2,1,0:T(8,128)S(1)} %get-tuple-element.24.edge, f32[2,16,128]{2,1,0:T(8,128)S(1)} %collective-permute-done.8.outer, s32[32,128]{1,0:T(8,128)S(1)} %broadcast_in_dim.10.guard, ...), custom_call_target="tpu_custom_call", output_to_operand_aliasing={{}: (0, {})} | custom-call | tf_op jit(solution)/shard_map/cfar/pallas_call | solution.py:456
  (21 shorter events, 0.1 us)
Async XLA Ops:
  0.0 27.7 %copy-start = (f32[128,3]{0,1:T(4,128)S(1)}, f32[128,3]{0,1:T(4,128)}, u32[]{:S(2)}) copy-start(f32[128,3]{0,1:T(4,128)} %param.9) | copy-start | bytes 4612
  0.0 3.8 %copy-start.1 = (s32[32,32]{1,0:T(8,128)S(1)}, s32[32,32]{1,0:T(8,128)}, u32[]{:S(2)}) copy-start(s32[32,32]{1,0:T(8,128)} %param.11) | copy-start | bytes 12292
  0.0 3.7 %copy-start.2 = (s32[128,3]{0,1:T(4,128)S(1)}, s32[128,3]{0,1:T(4,128)}, u32[]{:S(2)}) copy-start(s32[128,3]{0,1:T(4,128)} %param.8) | copy-start | bytes 4612
  0.0 3.1 %collective-permute-start = (s32[32,32]{1,0:T(8,128)}, s32[32,32]{1,0:T(8,128)S(1)}, u32[]{:S(2)}, u32[]{:S(2)}) collective-permute-start(s32[32,32]{1,0:T(8,128)} %param.11), channel_id=1, source_target_pairs={{0,4},{4,0},{8,12},{12,8},{16,20},{20,16},{24,28},{28,24},{32,36},... | collective-permute-start | bytes 12296 | tf_op jit(solution)/shard_map/ppermute | solution.py:485
  3.1 8.3 %collective-permute-start.1 = (f32[2,80,16,128]{3,2,1,0:T(8,128)}, f32[2,80,16,128]{3,2,1,0:T(8,128)S(1)}, u32[]{:S(2)}, u32[]{:S(2)}) collective-permute-start(f32[2,80,16,128]{3,2,1,0:T(8,128)} %get-tuple-element.17), channel_id=1, source_target_pairs={{0,4},{4,0},{8,12},{12,8},{16,20},{20,16},{24,28},{28,24},{32,36},... | collective-permute-start | bytes 3932168 | tf_op jit(solution)/shard_map/ppermute | solution.py:485
  3.9 3.7 %collective-permute-start.2 = (s32[16,64]{1,0:T(8,128)S(1)}, s32[16,64]{1,0:T(8,128)S(1)}, u32[]{:S(2)}, u32[]{:S(2)}) collective-permute-start(s32[16,64]{1,0:T(8,128)S(1)} %fusion.refs_0_), channel_id=1, source_target_pairs={{0,1},{1,0},{2,3},{3,2},{4,5},{5,4},{6,7},{7,6},{8,9},{9,8},{10,11... | collective-permute-start | bytes 12296 | tf_op jit(solution)/shard_map/ppermute | solution.py:507
  7.6 6.7 %collective-permute-start.3 = (s32[32,64]{1,0:T(8,128)S(1)}, s32[32,64]{1,0:T(8,128)S(1)}, u32[]{:S(2)}, u32[]{:S(2)}) collective-permute-start(s32[32,64]{1,0:T(8,128)S(1)} %pad_add_fusion), channel_id=1, source_target_pairs={{0,2},{1,3},{2,0},{3,1},{4,6},{5,7},{6,4},{7,5},{8,10},{9,11},{10,... | collective-permute-start | bytes 24584 | tf_op jit(solution)/shard_map/ppermute | solution.py:508
  14.2 13.7 %copy-start.5 = (f32[16]{0:T(128)S(1)}, f32[16]{0:T(128)}, u32[]{:S(2)}) copy-start(f32[16]{0:T(128)} %param.10) | copy-start | bytes 196
  14.2 14.1 %copy-start.3 = (s32[32]{0:T(128)S(1)}, s32[32]{0:T(128)}, u32[]{:S(2)}) copy-start(s32[32]{0:T(128)} %param.12) | copy-start | bytes 388
  14.2 14.2 %copy-start.4 = (s32[32]{0:T(128)S(1)}, s32[32]{0:T(128)}, u32[]{:S(2)}) copy-start(s32[32]{0:T(128)} %param.13) | copy-start | bytes 388
  17.7 21.3 %all-to-all-start = ((f32[64,1,2304]{2,1,0:T(1,128)}), f32[64,1,2304]{2,1,0:T(1,128)S(1)}, u32[]{:S(2)}, u32[]{:S(2)}) async-start(f32[64,1,2304]{2,1,0:T(1,128)} %gram_b.1), calls=%async_computation | async-start | bytes 1179648 | tf_op jit(solution)/shard_map/all_to_all | solution.py:511
  58.1 1.3 %collective-permute-start.4 = (f32[4,2,16,128]{3,2,1,0:T(8,128)S(1)}, f32[4,2,16,128]{3,2,1,0:T(8,128)S(1)}, u32[]{:S(2)}, u32[]{:S(2)}) collective-permute-start(f32[4,2,16,128]{3,2,1,0:T(8,128)S(1)} %power.1), channel_id=1, source_target_pairs={{0,4},{4,0},{8,12},{12,8},{16,20},{20,16},{24,28},{28,24},{32,36},... | collective-permute-start | bytes 196616 | tf_op jit(solution)/shard_map/ppermute | solution.py:485
  59.5 5.6 %collective-permute-start.7 = (f32[4,16,128]{2,1,0:T(8,128)S(1)}, f32[4,16,128]{2,1,0:T(8,128)S(1)}, u32[]{:S(2)}, u32[]{:S(2)}) collective-permute-start(f32[4,16,128]{2,1,0:T(8,128)S(1)} %pad_maximum_fusion.3), channel_id=1, source_target_pairs={{0,3},{1,2},{2,1},{3,0},{4,7},{5,6},{6,5},{7,4},{8,11},{9,10},{10,... | collective-permute-start | bytes 98312 | tf_op jit(solution)/shard_map/ppermute | solution.py:521
  60.5 5.4 %collective-permute-start.6 = (f32[4,16,128]{2,1,0:T(8,128)S(1)}, f32[4,16,128]{2,1,0:T(8,128)S(1)}, u32[]{:S(2)}, u32[]{:S(2)}) collective-permute-start(f32[4,16,128]{2,1,0:T(8,128)S(1)} %pad_maximum_fusion.2), channel_id=1, source_target_pairs={{0,2},{1,3},{2,0},{3,1},{4,6},{5,7},{6,4},{7,5},{8,10},{9,11},{10,... | collective-permute-start | bytes 98312 | tf_op jit(solution)/shard_map/ppermute | solution.py:521
  62.2 3.9 %collective-permute-start.5 = (f32[4,16,128]{2,1,0:T(8,128)S(1)}, f32[4,16,128]{2,1,0:T(8,128)S(1)}, u32[]{:S(2)}, u32[]{:S(2)}) collective-permute-start(f32[4,16,128]{2,1,0:T(8,128)S(1)} %pad_maximum_fusion.1), channel_id=1, source_target_pairs={{0,1},{1,0},{2,3},{3,2},{4,5},{5,4},{6,7},{7,6},{8,9},{9,8},{10,11... | collective-permute-start | bytes 98312 | tf_op jit(solution)/shard_map/ppermute | solution.py:521
  66.1 7.2 %collective-permute-start.8 = (f32[2,16,128]{2,1,0:T(8,128)S(1)}, f32[2,16,128]{2,1,0:T(8,128)S(1)}, u32[]{:S(2)}, u32[]{:S(2)}) collective-permute-start(f32[2,16,128]{2,1,0:T(8,128)S(1)} %select_select_fusion), channel_id=1, source_target_pairs={{4,8},{8,4},{12,16},{16,12},{20,24},{24,20},{28,32},{32,28},{36,40... | collective-permute-start | bytes 49160 | tf_op jit(solution)/shard_map/ppermute | solution.py:527

commit v13 on v12

--- a/solution.py
+++ b/solution.py
@@ -50,10 +50,10 @@
     return jnp.concatenate(parts, 0)
 
 
-def pack_kernel(echo, near, send, sems):
+def pack_kernel(echo, near, send, stage, sems):
     core, _ = core_and_dop()
-    copies = []
-    for out, half in ((near, core), (send, 1 - core)):
+    loads = []
+    for out, half in ((stage, 1 - core), (near, core)):
         for z in range(ZN):
             first = z * 32 + half * 16
             for start, at, count in (
@@ -61,26 +61,36 @@
                 ((first + BINS - 2) % BINS, 0, 2),
                 ((first + 16) % BINS, 18, 2),
             ):
-                copies.append(
+                loads.append(
                     pltpu.make_async_copy(
                         echo.at[:, pl.ds(start, count)],
                         out.at[:, pl.ds(z * WINDOW + at, count)],
-                        sems.at[len(copies)],
+                        sems.at[len(loads)],
                     )
                 )
-    for c in copies:
+    for c in loads:
         c.start()
-    for c in copies:
+    stores = []
+    for z in range(ZN):
+        for c in loads[3 * z : 3 * z + 3]:
+            c.wait()
+        part = pl.ds(z * WINDOW, WINDOW)
+        stores.append(
+            pltpu.make_async_copy(stage.at[:, part], send.at[:, part], sems.at[6 * ZN + z])
+        )
+        stores[-1].start()
+    for c in loads[3 * ZN :] + stores:
         c.wait()
 
 
 def pack(echo):
+    packed = (2, ZN * WINDOW, CH, GATES)
     return pl.pallas_call(
         pack_kernel,
-        out_shape=[jax.ShapeDtypeStruct((2, ZN * WINDOW, CH, GATES), f32)] * 2,
+        out_shape=[jax.ShapeDtypeStruct(packed, f32), pltpu.HBM(packed, f32)],
         in_specs=[pl.BlockSpec(memory_space=pltpu.HBM)],
-        out_specs=[VM] * 2,
-        scratch_shapes=[pltpu.SemaphoreType.DMA((6 * ZN,))],
+        out_specs=[VM, pl.BlockSpec(memory_space=pltpu.HBM)],
+        scratch_shapes=[pltpu.VMEM(packed, f32), pltpu.SemaphoreType.DMA((7 * ZN,))],
         name="pack",
         compiler_params=pltpu.CompilerParams(vmem_limit_bytes=52 * 2**20),
     )(echo)
@@ -233,9 +243,11 @@
 def solve_kernel(parts, sr, si, out):
     row = iota((ST, GATES), 0)
     lane = iota((ST, GATES), 1)
-    line = []
-    for j in range(PACKED // GATES):
-        line.append(jnp.sum(parts[:, 0, j * GATES : (j + 1) * GATES], 0, keepdims=True) * (1.0 / TOTAL))
+    total = parts[0]
+    for j in range(1, 64):
+        total = total + parts[j]
+    total = total * (1.0 / TOTAL)
+    line = [total[:, j : j + GATES] for j in range(0, PACKED, GATES)]
     main = rows(*line[:16])
     corner = rows(*[pltpu.roll(line[16 + j // 8], (GATES + 32 - 16 * (j % 8)) % GATES, 1) for j in range(16)])
     p2 = jnp.where(lane[:16] < 32, pltpu.roll(main, 32, 1), corner)

time: 74.6 us -> 73.8 us (0.989)
  Pallas kernels: 16.8 us -> 16 us
  transfers between devices with their start and end apart: 10 -> 10, of which waited for: 7 -> 7; matrix products, arithmetic and copies ran while one was open for 2% -> 2% of each run, Pallas kernels for 10% -> 9%
where the time goes in v13:
time: 73.8 us; the launch traced here: 73.5 us
  starting transfers between devices  23 us (31%)
  waiting for transfers between devices  18.6 us (25%)
  Pallas kernels  16 us (22%)
  blocking collectives  14.1 us (19%)
  local copies, waits for them, and re-layouts  1.47 us (2%)
    all_to_all x1, blocking collectives, shards(): w = lax.all_to_all(w, BOTH, 0, 0, tiled=True, axis_index_groups=SAME_CORE)  14.1 us
    all_to_all x1, waiting for transfers between devices, shards(): lax.all_to_all(part, BOTH, 0, 0, tiled=True, axis_index_groups=SAME_CORE)  10.5 us
    all_to_all x1, starting transfers between devices, shards(): lax.all_to_all(part, BOTH, 0, 0, tiled=True, axis_index_groups=SAME_CORE)  9.98 us
    pallas_call x2, Pallas kernels, gram(): pl.pallas_call(functools.partial(gram_kernel, second), out_shape=pltpu.HB...  6.17 us
    ppermute x3, starting transfers between devices, shards(): lax.ppermute(pieces[k], 'dop', flipped(k))  4.17 us
    ppermute x1, starting transfers between devices, shards(): m2 = lax.ppermute(rows(mine, m1), 'dop', flipped(2))  3.88 us
    ppermute x1, waiting for transfers between devices, shards(): outer = lax.ppermute(jnp.where(core == 0, head, tail), 'range', pairs)  3.33 us
    pallas_call x1, Pallas kernels, power(): pl.pallas_call(power_kernel, out_shape=jax.ShapeDtypeStruct((ZN, 2, 16, G...  2.51 us
  transfers between devices with their start and end apart: 10, of which 7 were waited for; matrix products, arithmetic and copies ran while one was open for 2% of the time, Pallas kernels for 9%

profile of v13, /device:TPU:8, one launch (start us, length us, event | category | flops | bytes accessed | tf_op | source)
XLA Modules:
  0.0 73.5 jit_solution(18193545023950985948)
XLA Ops:
  0.0 0.1 collective-permute-start
  0.1 2.3 %pack.1 = (f32[2,80,16,128]{3,2,1,0:T(8,128)S(1)}, f32[2,80,16,128]{3,2,1,0:T(8,128)}) custom-call(f32[2,128,16,128]{3,2,1,0:T(8,128)} %echo.1), custom_call_target="tpu_custom_call" | custom-call | tf_op jit(solution)/shard_map/pack/pallas_call | solution.py:88
  2.4 0.0 collective-permute-done
  2.4 0.6 collective-permute-start.1
  3.0 0.0 copy-done.2
  3.0 0.1 reshape.43
  3.2 0.1 fusion.refs_0_
  3.2 1.9 %collective-permute-start.2 = (s32[16,64]{1,0:T(8,128)S(1)}, s32[16,64]{1,0:T(8,128)S(1)}, u32[]{:S(2)}, u32[]{:S(2)}) collective-permute-start(s32[16,64]{1,0:T(8,128)S(1)} %fusion.refs_0_), channel_id=1, source_target_pairs={{0,1},{1,0},{2,3},{3,2},{4,5},{5,4},{6,7},{7,6},{8,9},{9,8},{10,11... | collective-permute-start | bytes 12296 | tf_op jit(solution)/shard_map/ppermute | solution.py:519
  5.2 0.1 copy.10
  5.3 0.1 squeeze.6
  5.4 0.1 iota.18
  5.5 0.1 iota.19
  5.6 0.1 iota.15
  5.7 0.1 iota.16
  5.8 1.1 %collective-permute-done.2.refs_1_ = s32[16,64]{1,0:T(8,128)S(1)} collective-permute-done((s32[16,64]{1,0:T(8,128)S(1)}, s32[16,64]{1,0:T(8,128)S(1)}, u32[]{:S(2)}, u32[]{:S(2)}) %collective-permute-start.2) | collective-permute-done | bytes 4128 | tf_op jit(solution)/shard_map/ppermute | solution.py:519
  6.9 3.9 %collective-permute-start.3 = (s32[32,64]{1,0:T(8,128)S(1)}, s32[32,64]{1,0:T(8,128)S(1)}, u32[]{:S(2)}, u32[]{:S(2)}) collective-permute-start(s32[32,64]{1,0:T(8,128)S(1)} %pad_add_fusion), channel_id=1, source_target_pairs={{0,2},{1,3},{2,0},{3,1},{4,6},{5,7},{6,4},{7,5},{8,10},{9,11},{10,... | collective-permute-start | bytes 24584 | tf_op jit(solution)/shard_map/ppermute | solution.py:520
  10.8 0.0 collective-permute-done.1.far
  10.8 2.7 %gram_a.1.refs_1_ = f32[32,1,2304]{2,1,0:T(1,128)S(1)} custom-call(s32[192]{0:T(256)S(1)} %and_add_fusion.place, f32[2,80,16,128]{3,2,1,0:T(8,128)S(1)} %get-tuple-element.15.near, f32[2,80,16,128]{3,2,1,0:T(8,128)S(1)} %collective-permute-done.1.far, s32[16,64]{1,0:T(8,128)S(1)} %fusion.refs_0_, s32[16,64]{1,0:T(8,128)S(1)} %collective-permute-done.2.refs_1_), custom_call_target="tpu_custom_call" | custom-call | tf_op jit(solution)/shard_map/gram_a/pallas_call | solution.py:205
  13.5 0.0 copy-start.5
  13.5 0.0 copy-start.3
  13.6 0.0 copy-start.4
  13.6 0.0 collective-permute-done.3.refs_0_
  13.6 3.4 %gram_b.1 = f32[64,1,2304]{2,1,0:T(1,128)} custom-call(s32[192]{0:T(256)S(1)} %and_add_fusion.place, f32[2,80,16,128]{3,2,1,0:T(8,128)S(1)} %get-tuple-element.15.near, f32[2,80,16,128]{3,2,1,0:T(8,128)S(1)} %collective-permute-done.1.far, s32[32,64]{1,0:T(8,128)S(1)} %collective-permute-done.3.refs_0_, f32[32,1,2304]{2,1,0:T(1,128)S(1)} %gram_a.1.refs_1_), custom_call_target="tpu_custom_call" | custom-call | tf_op jit(solution)/shard_map/gram_b/pallas_call | solution.py:205
  17.0 10.0 %all-to-all-start = ((f32[64,1,2304]{2,1,0:T(1,128)}), f32[64,1,2304]{2,1,0:T(1,128)S(1)}, u32[]{:S(2)}, u32[]{:S(2)}) async-start(f32[64,1,2304]{2,1,0:T(1,128)} %gram_b.1), calls=%async_computation | async-start | bytes 1179648 | tf_op jit(solution)/shard_map/all_to_all | solution.py:523
  27.1 0.2 dynamic-slice_reduce_fusion
  27.3 0.1 broadcast_multiply_fusion
  27.4 0.1 mul.72
  27.4 0.1 mul.75
  27.5 0.1 broadcast_in_dim.8.sr
  27.6 0.1 broadcast_in_dim.9.si
  27.7 0.1 broadcast_in_dim.10.guard
  27.7 0.1 broadcast_in_dim.11.train
  27.8 10.5 %all-to-all-done.parts = f32[64,1,2304]{2,1,0:T(1,128)S(1)} async-done(((f32[64,1,2304]{2,1,0:T(1,128)}), f32[64,1,2304]{2,1,0:T(1,128)S(1)}, u32[]{:S(2)}, u32[]{:S(2)}) %all-to-all-start) | async-done | bytes 589856 | tf_op jit(solution)/shard_map/all_to_all | solution.py:523
  38.3 2.4 %solve.1 = f32[64,1,128]{2,1,0:T(1,128)S(1)} custom-call(f32[64,1,2304]{2,1,0:T(1,128)S(1)} %all-to-all-done.parts, f32[48,128]{1,0:T(8,128)S(1)} %broadcast_in_dim.8.sr, f32[48,128]{1,0:T(8,128)S(1)} %broadcast_in_dim.9.si), custom_call_target="tpu_custom_call" | custom-call | tf_op jit(solution)/shard_map/solve/pallas_call | solution.py:297
  40.7 14.1 %all_to_all.10.w = f32[64,1,128]{2,1,0:T(1,128)S(1)} all-to-all(f32[64,1,128]{2,1,0:T(1,128)S(1)} %solve.1), channel_id=1, replica_groups={{0,8,16,24,32,40,48,56,64,72,80,88,96,104,112,120,1,9,17,25,33,41,49,57..., dimensions={0} | all-to-all | bytes 65536 | tf_op jit(solution)/shard_map/all_to_all | solution.py:529
  54.8 2.5 %power.1 = f32[4,2,16,128]{3,2,1,0:T(8,128)S(1)} custom-call(s32[192]{0:T(256)S(1)} %and_add_fusion.place, f32[2,80,16,128]{3,2,1,0:T(8,128)S(1)} %get-tuple-element.15.near, f32[2,80,16,128]{3,2,1,0:T(8,128)S(1)} %collective-permute-done.1.far, f32[64,1,128]{2,1,0:T(1,128)S(1)} %all_to_all.10.w), custom_call_target="tpu_custom_call" | custom-call | tf_op jit(solution)/shard_map/power/pallas_call | solution.py:356
  57.3 0.1 collective-permute-start.4
  57.4 1.2 %collective-permute-done.4 = f32[4,2,16,128]{3,2,1,0:T(8,128)S(1)} collective-permute-done((f32[4,2,16,128]{3,2,1,0:T(8,128)S(1)}, f32[4,2,16,128]{3,2,1,0:T(8,128)S(1)}, u32[]{:S(2)}, u32[]{:S(2)}) %collective-permute-start.4) | collective-permute-done | bytes 65568 | tf_op jit(solution)/shard_map/ppermute | solution.py:497
  58.7 1.0 %collective-permute-start.7 = (f32[4,16,128]{2,1,0:T(8,128)S(1)}, f32[4,16,128]{2,1,0:T(8,128)S(1)}, u32[]{:S(2)}, u32[]{:S(2)}) collective-permute-start(f32[4,16,128]{2,1,0:T(8,128)S(1)} %pad_maximum_fusion.3), channel_id=1, source_target_pairs={{0,3},{1,2},{2,1},{3,0},{4,7},{5,6},{6,5},{7,4},{8,11},{9,10},{10,... | collective-permute-start | bytes 98312 | tf_op jit(solution)/shard_map/ppermute | solution.py:533
  59.7 1.7 %collective-permute-start.6 = (f32[4,16,128]{2,1,0:T(8,128)S(1)}, f32[4,16,128]{2,1,0:T(8,128)S(1)}, u32[]{:S(2)}, u32[]{:S(2)}) collective-permute-start(f32[4,16,128]{2,1,0:T(8,128)S(1)} %pad_maximum_fusion.2), channel_id=1, source_target_pairs={{0,2},{1,3},{2,0},{3,1},{4,6},{5,7},{6,4},{7,5},{8,10},{9,11},{10,... | collective-permute-start | bytes 98312 | tf_op jit(solution)/shard_map/ppermute | solution.py:533
  61.4 1.5 %collective-permute-start.5 = (f32[4,16,128]{2,1,0:T(8,128)S(1)}, f32[4,16,128]{2,1,0:T(8,128)S(1)}, u32[]{:S(2)}, u32[]{:S(2)}) collective-permute-start(f32[4,16,128]{2,1,0:T(8,128)S(1)} %pad_maximum_fusion.1), channel_id=1, source_target_pairs={{0,1},{1,0},{2,3},{3,2},{4,5},{5,4},{6,7},{7,6},{8,9},{9,8},{10,11... | collective-permute-start | bytes 98312 | tf_op jit(solution)/shard_map/ppermute | solution.py:533
  62.8 1.4 %collective-permute-done.7.p3 = f32[4,16,128]{2,1,0:T(8,128)S(1)} collective-permute-done((f32[4,16,128]{2,1,0:T(8,128)S(1)}, f32[4,16,128]{2,1,0:T(8,128)S(1)}, u32[]{:S(2)}, u32[]{:S(2)}) %collective-permute-start.7) | collective-permute-done | bytes 32800 | tf_op jit(solution)/shard_map/ppermute | solution.py:533
  64.2 0.9 %collective-permute-done.6.p2 = f32[4,16,128]{2,1,0:T(8,128)S(1)} collective-permute-done((f32[4,16,128]{2,1,0:T(8,128)S(1)}, f32[4,16,128]{2,1,0:T(8,128)S(1)}, u32[]{:S(2)}, u32[]{:S(2)}) %collective-permute-start.6) | collective-permute-done | bytes 32800 | tf_op jit(solution)/shard_map/ppermute | solution.py:533
  65.1 0.2 collective-permute-done.5.p1
  65.3 2.3 %collective-permute-start.8 = (f32[2,16,128]{2,1,0:T(8,128)S(1)}, f32[2,16,128]{2,1,0:T(8,128)S(1)}, u32[]{:S(2)}, u32[]{:S(2)}) collective-permute-start(f32[2,16,128]{2,1,0:T(8,128)S(1)} %select_select_fusion), channel_id=1, source_target_pairs={{4,8},{8,4},{12,16},{16,12},{20,24},{24,20},{28,32},{32,28},{36,40... | collective-permute-start | bytes 49160 | tf_op jit(solution)/shard_map/ppermute | solution.py:539
  67.6 1.5 %noise.1 = (f32[32,512]{1,0:T(8,128)}, f32[3,32,128]{2,1,0:T(8,128)S(1)}) custom-call(f32[4,16,128]{2,1,0:T(8,128)S(1)} %pad_maximum_fusion.p0, f32[4,16,128]{2,1,0:T(8,128)S(1)} %collective-permute-done.5.p1, f32[4,16,128]{2,1,0:T(8,128)S(1)} %collective-permute-done.6.p2, f32[4,16,128]{2,1,0:T(8,128)S(1)} %collective-permute-done.7.p3, ...), custom_call_target="tpu_custom_call" | custom-call | tf_op jit(solution)/shard_map/noise/pallas_call | solution.py:433
  69.1 3.3 %collective-permute-done.8.outer = f32[2,16,128]{2,1,0:T(8,128)S(1)} collective-permute-done((f32[2,16,128]{2,1,0:T(8,128)S(1)}, f32[2,16,128]{2,1,0:T(8,128)S(1)}, u32[]{:S(2)}, u32[]{:S(2)}) %collective-permute-start.8) | collective-permute-done | bytes 16416 | tf_op jit(solution)/shard_map/ppermute | solution.py:539
  72.5 1.1 %cfar.1 = f32[32,512]{1,0:T(8,128)} custom-call(f32[32,512]{1,0:T(8,128)} %get-tuple-element.23.whole, f32[3,32,128]{2,1,0:T(8,128)S(1)} %get-tuple-element.24.edge, f32[2,16,128]{2,1,0:T(8,128)S(1)} %collective-permute-done.8.outer, s32[32,128]{1,0:T(8,128)S(1)} %broadcast_in_dim.10.guard, ...), custom_call_target="tpu_custom_call", output_to_operand_aliasing={{}: (0, {})} | custom-call | tf_op jit(solution)/shard_map/cfar/pallas_call | solution.py:468
  (21 shorter events, 0.1 us)
Async XLA Ops:
  0.0 27.0 %copy-start = (f32[128,3]{0,1:T(4,128)S(1)}, f32[128,3]{0,1:T(4,128)}, u32[]{:S(2)}) copy-start(f32[128,3]{0,1:T(4,128)} %param.9) | copy-start | bytes 4612
  0.0 3.1 %copy-start.1 = (s32[32,32]{1,0:T(8,128)S(1)}, s32[32,32]{1,0:T(8,128)}, u32[]{:S(2)}) copy-start(s32[32,32]{1,0:T(8,128)} %param.11) | copy-start | bytes 12292
  0.0 3.0 %copy-start.2 = (s32[128,3]{0,1:T(4,128)S(1)}, s32[128,3]{0,1:T(4,128)}, u32[]{:S(2)}) copy-start(s32[128,3]{0,1:T(4,128)} %param.8) | copy-start | bytes 4612
  0.0 2.4 %collective-permute-start = (s32[32,32]{1,0:T(8,128)}, s32[32,32]{1,0:T(8,128)S(1)}, u32[]{:S(2)}, u32[]{:S(2)}) collective-permute-start(s32[32,32]{1,0:T(8,128)} %param.11), channel_id=1, source_target_pairs={{0,4},{4,0},{8,12},{12,8},{16,20},{20,16},{24,28},{28,24},{32,36},... | collective-permute-start | bytes 12296 | tf_op jit(solution)/shard_map/ppermute | solution.py:497
  2.4 8.4 %collective-permute-start.1 = (f32[2,80,16,128]{3,2,1,0:T(8,128)}, f32[2,80,16,128]{3,2,1,0:T(8,128)S(1)}, u32[]{:S(2)}, u32[]{:S(2)}) collective-permute-start(f32[2,80,16,128]{3,2,1,0:T(8,128)} %get-tuple-element.17), channel_id=1, source_target_pairs={{0,4},{4,0},{8,12},{12,8},{16,20},{20,16},{24,28},{28,24},{32,36},... | collective-permute-start | bytes 3932168 | tf_op jit(solution)/shard_map/ppermute | solution.py:497
  3.2 3.7 %collective-permute-start.2 = (s32[16,64]{1,0:T(8,128)S(1)}, s32[16,64]{1,0:T(8,128)S(1)}, u32[]{:S(2)}, u32[]{:S(2)}) collective-permute-start(s32[16,64]{1,0:T(8,128)S(1)} %fusion.refs_0_), channel_id=1, source_target_pairs={{0,1},{1,0},{2,3},{3,2},{4,5},{5,4},{6,7},{7,6},{8,9},{9,8},{10,11... | collective-permute-start | bytes 12296 | tf_op jit(solution)/shard_map/ppermute | solution.py:519
  6.9 6.7 %collective-permute-start.3 = (s32[32,64]{1,0:T(8,128)S(1)}, s32[32,64]{1,0:T(8,128)S(1)}, u32[]{:S(2)}, u32[]{:S(2)}) collective-permute-start(s32[32,64]{1,0:T(8,128)S(1)} %pad_add_fusion), channel_id=1, source_target_pairs={{0,2},{1,3},{2,0},{3,1},{4,6},{5,7},{6,4},{7,5},{8,10},{9,11},{10,... | collective-permute-start | bytes 24584 | tf_op jit(solution)/shard_map/ppermute | solution.py:520
  13.5 13.7 %copy-start.5 = (f32[16]{0:T(128)S(1)}, f32[16]{0:T(128)}, u32[]{:S(2)}) copy-start(f32[16]{0:T(128)} %param.10) | copy-start | bytes 196
  13.5 14.1 %copy-start.3 = (s32[32]{0:T(128)S(1)}, s32[32]{0:T(128)}, u32[]{:S(2)}) copy-start(s32[32]{0:T(128)} %param.12) | copy-start | bytes 388
  13.6 14.2 %copy-start.4 = (s32[32]{0:T(128)S(1)}, s32[32]{0:T(128)}, u32[]{:S(2)}) copy-start(s32[32]{0:T(128)} %param.13) | copy-start | bytes 388
  17.0 21.3 %all-to-all-start = ((f32[64,1,2304]{2,1,0:T(1,128)}), f32[64,1,2304]{2,1,0:T(1,128)S(1)}, u32[]{:S(2)}, u32[]{:S(2)}) async-start(f32[64,1,2304]{2,1,0:T(1,128)} %gram_b.1), calls=%async_computation | async-start | bytes 1179648 | tf_op jit(solution)/shard_map/all_to_all | solution.py:523
  57.3 1.3 %collective-permute-start.4 = (f32[4,2,16,128]{3,2,1,0:T(8,128)S(1)}, f32[4,2,16,128]{3,2,1,0:T(8,128)S(1)}, u32[]{:S(2)}, u32[]{:S(2)}) collective-permute-start(f32[4,2,16,128]{3,2,1,0:T(8,128)S(1)} %power.1), channel_id=1, source_target_pairs={{0,4},{4,0},{8,12},{12,8},{16,20},{20,16},{24,28},{28,24},{32,36},... | collective-permute-start | bytes 196616 | tf_op jit(solution)/shard_map/ppermute | solution.py:497
  58.7 5.6 %collective-permute-start.7 = (f32[4,16,128]{2,1,0:T(8,128)S(1)}, f32[4,16,128]{2,1,0:T(8,128)S(1)}, u32[]{:S(2)}, u32[]{:S(2)}) collective-permute-start(f32[4,16,128]{2,1,0:T(8,128)S(1)} %pad_maximum_fusion.3), channel_id=1, source_target_pairs={{0,3},{1,2},{2,1},{3,0},{4,7},{5,6},{6,5},{7,4},{8,11},{9,10},{10,... | collective-permute-start | bytes 98312 | tf_op jit(solution)/shard_map/ppermute | solution.py:533
  59.7 5.4 %collective-permute-start.6 = (f32[4,16,128]{2,1,0:T(8,128)S(1)}, f32[4,16,128]{2,1,0:T(8,128)S(1)}, u32[]{:S(2)}, u32[]{:S(2)}) collective-permute-start(f32[4,16,128]{2,1,0:T(8,128)S(1)} %pad_maximum_fusion.2), channel_id=1, source_target_pairs={{0,2},{1,3},{2,0},{3,1},{4,6},{5,7},{6,4},{7,5},{8,10},{9,11},{10,... | collective-permute-start | bytes 98312 | tf_op jit(solution)/shard_map/ppermute | solution.py:533
  61.4 3.9 %collective-permute-start.5 = (f32[4,16,128]{2,1,0:T(8,128)S(1)}, f32[4,16,128]{2,1,0:T(8,128)S(1)}, u32[]{:S(2)}, u32[]{:S(2)}) collective-permute-start(f32[4,16,128]{2,1,0:T(8,128)S(1)} %pad_maximum_fusion.1), channel_id=1, source_target_pairs={{0,1},{1,0},{2,3},{3,2},{4,5},{5,4},{6,7},{7,6},{8,9},{9,8},{10,11... | collective-permute-start | bytes 98312 | tf_op jit(solution)/shard_map/ppermute | solution.py:533
  65.3 7.2 %collective-permute-start.8 = (f32[2,16,128]{2,1,0:T(8,128)S(1)}, f32[2,16,128]{2,1,0:T(8,128)S(1)}, u32[]{:S(2)}, u32[]{:S(2)}) collective-permute-start(f32[2,16,128]{2,1,0:T(8,128)S(1)} %select_select_fusion), channel_id=1, source_target_pairs={{4,8},{8,4},{12,16},{16,12},{20,24},{24,20},{28,32},{32,28},{36,40... | collective-permute-start | bytes 49160 | tf_op jit(solution)/shard_map/ppermute | solution.py:539

commit v14 on v13

--- a/solution.py
+++ b/solution.py
@@ -105,9 +105,9 @@
 
 
 def gram_kernel(second, place, near, far, *refs):
-    masks = refs[: 1 if second else 2]
+    masks = refs[:2]
     if second:
-        done, whole, kept, out, sems = refs[1:]
+        done, whole, kept, out, sems = refs[2:]
     else:
         out, kept = refs[2:]
     core, dop = core_and_dop()
@@ -205,7 +205,7 @@
     return pl.pallas_call(
         functools.partial(gram_kernel, second),
         out_shape=pltpu.HBM((64, 1, PACKED), f32) if second else jax.ShapeDtypeStruct(block, f32),
-        in_specs=[SM] + [VM] * 4,
+        in_specs=[SM] + [VM] * (2 + len(extra)),
         out_specs=pl.BlockSpec(memory_space=pltpu.HBM) if second else VM,
         scratch_shapes=[kept, pltpu.VMEM(block, f32), pltpu.SemaphoreType.DMA((4,))] if second else [kept],
         name="gram_b" if second else "gram_a",
@@ -516,10 +516,9 @@
     far, other = lax.optimization_barrier((far, other))
     far = swap(far)
     mine = lax.dynamic_slice_in_dim(lanes(excluded, other), core * 16, 16, 0)
-    m1 = lax.ppermute(mine, "dop", flipped(1))
-    m2 = lax.ppermute(rows(mine, m1), "dop", flipped(2))
+    m1, m2, m3 = [lax.ppermute(mine, "dop", flipped(k)) for k in (1, 2, 3)]
     part = gram(False, place, near, far, [mine, m1])
-    part = gram(True, place, near, far, [m2, part])
+    part = gram(True, place, near, far, [m2, m3, part])
     part = lax.all_to_all(part, BOTH, 0, 0, tiled=True, axis_index_groups=SAME_CORE)
     sr, si = steering(bin_taper, phases)
     guard = jnp.broadcast_to(guard_len[:, None], (32, GATES))

time: 73.8 us -> 74.2 us (level)
  waiting for transfers between devices: 18.6 us -> 20.7 us
  starting transfers between devices: 23 us -> 21.3 us
    all_to_all x1, starting transfers between devices: 9.98 us -> 8.56 us  [shards(): lax.all_to_all(part, BOTH, 0, 0, tiled=True, axis_index_groups=SAME_CORE)]
    all_to_all x1, waiting for transfers between devices: 10.5 us -> 11.7 us  [shards(): lax.all_to_all(part, BOTH, 0, 0, tiled=True, axis_index_groups=SAME_CORE)]
    ppermute x2 -> x3, waiting for transfers between devices: 1.07 us -> 2.05 us  [shards(): m1, m2, m3 = [lax.ppermute(mine, 'dop', flipped(k)) for k in (1, 2, 3)]]
    ppermute x2 -> x3, starting transfers between devices: 5.82 us -> 5.52 us  [shards(): m1, m2, m3 = [lax.ppermute(mine, 'dop', flipped(k)) for k in (1, 2, 3)]]
  transfers between devices with their start and end apart: 10 -> 11, of which waited for: 7 -> 7; matrix products, arithmetic and copies ran while one was open for 2% -> 2% of each run, Pallas kernels for 9% -> 9%
where the time goes in v14:
time: 74.2 us; the launch traced here: 73.9 us
  starting transfers between devices  21.3 us (29%)
  waiting for transfers between devices  20.7 us (28%)
  Pallas kernels  16 us (22%)
  blocking collectives  14.1 us (19%)
  local copies, waits for them, and re-layouts  1.46 us (2%)
    all_to_all x1, blocking collectives, shards(): w = lax.all_to_all(w, BOTH, 0, 0, tiled=True, axis_index_groups=SAME_CORE)  14.1 us
    all_to_all x1, waiting for transfers between devices, shards(): lax.all_to_all(part, BOTH, 0, 0, tiled=True, axis_index_groups=SAME_CORE)  11.7 us
    all_to_all x1, starting transfers between devices, shards(): lax.all_to_all(part, BOTH, 0, 0, tiled=True, axis_index_groups=SAME_CORE)  8.56 us
    pallas_call x2, Pallas kernels, gram(): pl.pallas_call(functools.partial(gram_kernel, second), out_shape=pltpu.HB...  6.17 us
    ppermute x3, starting transfers between devices, shards(): m1, m2, m3 = [lax.ppermute(mine, 'dop', flipped(k)) for k in (1, 2, 3)]  5.52 us
    ppermute x3, starting transfers between devices, shards(): lax.ppermute(pieces[k], 'dop', flipped(k))  4.17 us
    ppermute x1, waiting for transfers between devices, shards(): outer = lax.ppermute(jnp.where(core == 0, head, tail), 'range', pairs)  3.33 us
    pallas_call x1, Pallas kernels, power(): pl.pallas_call(power_kernel, out_shape=jax.ShapeDtypeStruct((ZN, 2, 16, G...  2.5 us
  transfers between devices with their start and end apart: 11, of which 7 were waited for; matrix products, arithmetic and copies ran while one was open for 2% of the time, Pallas kernels for 9%

profile of v14, /device:TPU:8, one launch (start us, length us, event | category | flops | bytes accessed | tf_op | source)
XLA Modules:
  0.0 73.9 jit_solution(8273887573302248256)
XLA Ops:
  0.0 0.1 collective-permute-start
  0.1 2.3 %pack.1 = (f32[2,80,16,128]{3,2,1,0:T(8,128)S(1)}, f32[2,80,16,128]{3,2,1,0:T(8,128)}) custom-call(f32[2,128,16,128]{3,2,1,0:T(8,128)} %echo.1), custom_call_target="tpu_custom_call" | custom-call | tf_op jit(solution)/shard_map/pack/pallas_call | solution.py:88
  2.4 0.0 collective-permute-done
  2.4 0.6 collective-permute-start.1
  3.0 0.1 reshape.43
  3.1 0.1 copy.10
  3.2 0.1 squeeze.6
  3.4 0.1 iota.18
  3.4 0.1 iota.19
  3.6 0.1 iota.15
  3.7 0.1 iota.16
  3.8 0.1 fusion.refs_0_
  3.9 1.9 %collective-permute-start.4 = (s32[16,64]{1,0:T(8,128)S(1)}, s32[16,64]{1,0:T(8,128)S(1)}, u32[]{:S(2)}, u32[]{:S(2)}) collective-permute-start(s32[16,64]{1,0:T(8,128)S(1)} %fusion.refs_0_), channel_id=1, source_target_pairs={{0,1},{1,0},{2,3},{3,2},{4,5},{5,4},{6,7},{7,6},{8,9},{9,8},{10,11... | collective-permute-start | bytes 12296 | tf_op jit(solution)/shard_map/ppermute | solution.py:519
  5.8 3.6 %collective-permute-start.2 = (s32[16,64]{1,0:T(8,128)S(1)}, s32[16,64]{1,0:T(8,128)S(1)}, u32[]{:S(2)}, u32[]{:S(2)}) collective-permute-start(s32[16,64]{1,0:T(8,128)S(1)} %fusion.refs_0_), channel_id=1, source_target_pairs={{0,2},{1,3},{2,0},{3,1},{4,6},{5,7},{6,4},{7,5},{8,10},{9,11},{10,... | collective-permute-start | bytes 12296 | tf_op jit(solution)/shard_map/ppermute | solution.py:519
  9.4 0.0 collective-permute-start.3
  9.4 0.0 collective-permute-done.4.refs_1_
  9.4 2.7 %gram_a.1.refs_2_ = f32[32,1,2304]{2,1,0:T(1,128)S(1)} custom-call(s32[192]{0:T(256)S(1)} %and_add_fusion.place, f32[2,80,16,128]{3,2,1,0:T(8,128)S(1)} %get-tuple-element.15.near, f32[2,80,16,128]{3,2,1,0:T(8,128)S(1)} %collective-permute-done.1.far, s32[16,64]{1,0:T(8,128)S(1)} %fusion.refs_0_, s32[16,64]{1,0:T(8,128)S(1)} %collective-permute-done.4.refs_1_), custom_call_target="tpu_custom_call" | custom-call | tf_op jit(solution)/shard_map/gram_a/pallas_call | solution.py:205
  12.2 0.0 copy-start.5
  12.2 0.0 copy-start.3
  12.2 0.0 copy-start.4
  12.2 0.0 collective-permute-done.2.refs_0_
  12.2 2.0 %collective-permute-done.3.refs_1_ = s32[16,64]{1,0:T(8,128)S(1)} collective-permute-done((s32[16,64]{1,0:T(8,128)S(1)}, s32[16,64]{1,0:T(8,128)S(1)}, u32[]{:S(2)}, u32[]{:S(2)}) %collective-permute-start.3) | collective-permute-done | bytes 4128 | tf_op jit(solution)/shard_map/ppermute | solution.py:519
  14.3 3.4 %gram_b.1 = f32[64,1,2304]{2,1,0:T(1,128)} custom-call(s32[192]{0:T(256)S(1)} %and_add_fusion.place, f32[2,80,16,128]{3,2,1,0:T(8,128)S(1)} %get-tuple-element.15.near, f32[2,80,16,128]{3,2,1,0:T(8,128)S(1)} %collective-permute-done.1.far, s32[16,64]{1,0:T(8,128)S(1)} %collective-permute-done.2.refs_0_, s32[16,64]{1,0:T(8,128)S(1)} %collective-permute-done.3.refs_1_, ...), custom_call_target="tpu_custom_call" | custom-call | tf_op jit(solution)/shard_map/gram_b/pallas_call | solution.py:205
  17.7 8.6 %all-to-all-start = ((f32[64,1,2304]{2,1,0:T(1,128)}), f32[64,1,2304]{2,1,0:T(1,128)S(1)}, u32[]{:S(2)}, u32[]{:S(2)}) async-start(f32[64,1,2304]{2,1,0:T(1,128)} %gram_b.1), calls=%async_computation | async-start | bytes 1179648 | tf_op jit(solution)/shard_map/all_to_all | solution.py:522
  26.3 0.2 dynamic-slice_reduce_fusion
  26.6 0.1 broadcast_multiply_fusion
  26.6 0.1 mul.72
  26.7 0.1 mul.75
  26.8 0.1 broadcast_in_dim.8.sr
  26.9 0.1 broadcast_in_dim.9.si
  26.9 0.1 broadcast_in_dim.10.guard
  27.0 0.1 broadcast_in_dim.11.train
  27.1 11.7 %all-to-all-done.parts = f32[64,1,2304]{2,1,0:T(1,128)S(1)} async-done(((f32[64,1,2304]{2,1,0:T(1,128)}), f32[64,1,2304]{2,1,0:T(1,128)S(1)}, u32[]{:S(2)}, u32[]{:S(2)}) %all-to-all-start) | async-done | bytes 589856 | tf_op jit(solution)/shard_map/all_to_all | solution.py:522
  38.7 2.4 %solve.1 = f32[64,1,128]{2,1,0:T(1,128)S(1)} custom-call(f32[64,1,2304]{2,1,0:T(1,128)S(1)} %all-to-all-done.parts, f32[48,128]{1,0:T(8,128)S(1)} %broadcast_in_dim.8.sr, f32[48,128]{1,0:T(8,128)S(1)} %broadcast_in_dim.9.si), custom_call_target="tpu_custom_call" | custom-call | tf_op jit(solution)/shard_map/solve/pallas_call | solution.py:297
  41.1 14.1 %all_to_all.10.w = f32[64,1,128]{2,1,0:T(1,128)S(1)} all-to-all(f32[64,1,128]{2,1,0:T(1,128)S(1)} %solve.1), channel_id=1, replica_groups={{0,8,16,24,32,40,48,56,64,72,80,88,96,104,112,120,1,9,17,25,33,41,49,57..., dimensions={0} | all-to-all | bytes 65536 | tf_op jit(solution)/shard_map/all_to_all | solution.py:528
  55.2 2.5 %power.1 = f32[4,2,16,128]{3,2,1,0:T(8,128)S(1)} custom-call(s32[192]{0:T(256)S(1)} %and_add_fusion.place, f32[2,80,16,128]{3,2,1,0:T(8,128)S(1)} %get-tuple-element.15.near, f32[2,80,16,128]{3,2,1,0:T(8,128)S(1)} %collective-permute-done.1.far, f32[64,1,128]{2,1,0:T(1,128)S(1)} %all_to_all.10.w), custom_call_target="tpu_custom_call" | custom-call | tf_op jit(solution)/shard_map/power/pallas_call | solution.py:356
  57.7 0.1 collective-permute-start.5
  57.8 1.2 %collective-permute-done.5 = f32[4,2,16,128]{3,2,1,0:T(8,128)S(1)} collective-permute-done((f32[4,2,16,128]{3,2,1,0:T(8,128)S(1)}, f32[4,2,16,128]{3,2,1,0:T(8,128)S(1)}, u32[]{:S(2)}, u32[]{:S(2)}) %collective-permute-start.5) | collective-permute-done | bytes 65568 | tf_op jit(solution)/shard_map/ppermute | solution.py:497
  59.1 1.0 %collective-permute-start.8 = (f32[4,16,128]{2,1,0:T(8,128)S(1)}, f32[4,16,128]{2,1,0:T(8,128)S(1)}, u32[]{:S(2)}, u32[]{:S(2)}) collective-permute-start(f32[4,16,128]{2,1,0:T(8,128)S(1)} %pad_maximum_fusion.3), channel_id=1, source_target_pairs={{0,3},{1,2},{2,1},{3,0},{4,7},{5,6},{6,5},{7,4},{8,11},{9,10},{10,... | collective-permute-start | bytes 98312 | tf_op jit(solution)/shard_map/ppermute | solution.py:532
  60.1 1.7 %collective-permute-start.7 = (f32[4,16,128]{2,1,0:T(8,128)S(1)}, f32[4,16,128]{2,1,0:T(8,128)S(1)}, u32[]{:S(2)}, u32[]{:S(2)}) collective-permute-start(f32[4,16,128]{2,1,0:T(8,128)S(1)} %pad_maximum_fusion.2), channel_id=1, source_target_pairs={{0,2},{1,3},{2,0},{3,1},{4,6},{5,7},{6,4},{7,5},{8,10},{9,11},{10,... | collective-permute-start | bytes 98312 | tf_op jit(solution)/shard_map/ppermute | solution.py:532
  61.8 1.5 %collective-permute-start.6 = (f32[4,16,128]{2,1,0:T(8,128)S(1)}, f32[4,16,128]{2,1,0:T(8,128)S(1)}, u32[]{:S(2)}, u32[]{:S(2)}) collective-permute-start(f32[4,16,128]{2,1,0:T(8,128)S(1)} %pad_maximum_fusion.1), channel_id=1, source_target_pairs={{0,1},{1,0},{2,3},{3,2},{4,5},{5,4},{6,7},{7,6},{8,9},{9,8},{10,11... | collective-permute-start | bytes 98312 | tf_op jit(solution)/shard_map/ppermute | solution.py:532
  63.2 1.4 %collective-permute-done.8.p3 = f32[4,16,128]{2,1,0:T(8,128)S(1)} collective-permute-done((f32[4,16,128]{2,1,0:T(8,128)S(1)}, f32[4,16,128]{2,1,0:T(8,128)S(1)}, u32[]{:S(2)}, u32[]{:S(2)}) %collective-permute-start.8) | collective-permute-done | bytes 32800 | tf_op jit(solution)/shard_map/ppermute | solution.py:532
  64.6 0.9 %collective-permute-done.7.p2 = f32[4,16,128]{2,1,0:T(8,128)S(1)} collective-permute-done((f32[4,16,128]{2,1,0:T(8,128)S(1)}, f32[4,16,128]{2,1,0:T(8,128)S(1)}, u32[]{:S(2)}, u32[]{:S(2)}) %collective-permute-start.7) | collective-permute-done | bytes 32800 | tf_op jit(solution)/shard_map/ppermute | solution.py:532
  65.5 0.2 collective-permute-done.6.p1
  65.7 2.3 %collective-permute-start.9 = (f32[2,16,128]{2,1,0:T(8,128)S(1)}, f32[2,16,128]{2,1,0:T(8,128)S(1)}, u32[]{:S(2)}, u32[]{:S(2)}) collective-permute-start(f32[2,16,128]{2,1,0:T(8,128)S(1)} %select_select_fusion), channel_id=1, source_target_pairs={{4,8},{8,4},{12,16},{16,12},{20,24},{24,20},{28,32},{32,28},{36,40... | collective-permute-start | bytes 49160 | tf_op jit(solution)/shard_map/ppermute | solution.py:538
  68.0 1.5 %noise.1 = (f32[32,512]{1,0:T(8,128)}, f32[3,32,128]{2,1,0:T(8,128)S(1)}) custom-call(f32[4,16,128]{2,1,0:T(8,128)S(1)} %pad_maximum_fusion.p0, f32[4,16,128]{2,1,0:T(8,128)S(1)} %collective-permute-done.6.p1, f32[4,16,128]{2,1,0:T(8,128)S(1)} %collective-permute-done.7.p2, f32[4,16,128]{2,1,0:T(8,128)S(1)} %collective-permute-done.8.p3, ...), custom_call_target="tpu_custom_call" | custom-call | tf_op jit(solution)/shard_map/noise/pallas_call | solution.py:433
  69.5 3.3 %collective-permute-done.9.outer = f32[2,16,128]{2,1,0:T(8,128)S(1)} collective-permute-done((f32[2,16,128]{2,1,0:T(8,128)S(1)}, f32[2,16,128]{2,1,0:T(8,128)S(1)}, u32[]{:S(2)}, u32[]{:S(2)}) %collective-permute-start.9) | collective-permute-done | bytes 16416 | tf_op jit(solution)/shard_map/ppermute | solution.py:538
  72.9 1.1 %cfar.1 = f32[32,512]{1,0:T(8,128)} custom-call(f32[32,512]{1,0:T(8,128)} %get-tuple-element.23.whole, f32[3,32,128]{2,1,0:T(8,128)S(1)} %get-tuple-element.24.edge, f32[2,16,128]{2,1,0:T(8,128)S(1)} %collective-permute-done.9.outer, s32[32,128]{1,0:T(8,128)S(1)} %broadcast_in_dim.10.guard, ...), custom_call_target="tpu_custom_call", output_to_operand_aliasing={{}: (0, {})} | custom-call | tf_op jit(solution)/shard_map/cfar/pallas_call | solution.py:468
  (22 shorter events, 0.1 us)
Async XLA Ops:
  0.0 26.3 %copy-start = (f32[128,3]{0,1:T(4,128)S(1)}, f32[128,3]{0,1:T(4,128)}, u32[]{:S(2)}) copy-start(f32[128,3]{0,1:T(4,128)} %param.9) | copy-start | bytes 4612
  0.0 3.8 %copy-start.1 = (s32[32,32]{1,0:T(8,128)S(1)}, s32[32,32]{1,0:T(8,128)}, u32[]{:S(2)}) copy-start(s32[32,32]{1,0:T(8,128)} %param.11) | copy-start | bytes 12292
  0.0 3.0 %copy-start.2 = (s32[128,3]{0,1:T(4,128)S(1)}, s32[128,3]{0,1:T(4,128)}, u32[]{:S(2)}) copy-start(s32[128,3]{0,1:T(4,128)} %param.8) | copy-start | bytes 4612
  0.0 2.4 %collective-permute-start = (s32[32,32]{1,0:T(8,128)}, s32[32,32]{1,0:T(8,128)S(1)}, u32[]{:S(2)}, u32[]{:S(2)}) collective-permute-start(s32[32,32]{1,0:T(8,128)} %param.11), channel_id=1, source_target_pairs={{0,4},{4,0},{8,12},{12,8},{16,20},{20,16},{24,28},{28,24},{32,36},... | collective-permute-start | bytes 12296 | tf_op jit(solution)/shard_map/ppermute | solution.py:497
  2.4 7.0 %collective-permute-start.1 = (f32[2,80,16,128]{3,2,1,0:T(8,128)}, f32[2,80,16,128]{3,2,1,0:T(8,128)S(1)}, u32[]{:S(2)}, u32[]{:S(2)}) collective-permute-start(f32[2,80,16,128]{3,2,1,0:T(8,128)} %get-tuple-element.17), channel_id=1, source_target_pairs={{0,4},{4,0},{8,12},{12,8},{16,20},{20,16},{24,28},{28,24},{32,36},... | collective-permute-start | bytes 3932168 | tf_op jit(solution)/shard_map/ppermute | solution.py:497
  3.9 5.5 %collective-permute-start.4 = (s32[16,64]{1,0:T(8,128)S(1)}, s32[16,64]{1,0:T(8,128)S(1)}, u32[]{:S(2)}, u32[]{:S(2)}) collective-permute-start(s32[16,64]{1,0:T(8,128)S(1)} %fusion.refs_0_), channel_id=1, source_target_pairs={{0,1},{1,0},{2,3},{3,2},{4,5},{5,4},{6,7},{7,6},{8,9},{9,8},{10,11... | collective-permute-start | bytes 12296 | tf_op jit(solution)/shard_map/ppermute | solution.py:519
  5.8 6.4 %collective-permute-start.2 = (s32[16,64]{1,0:T(8,128)S(1)}, s32[16,64]{1,0:T(8,128)S(1)}, u32[]{:S(2)}, u32[]{:S(2)}) collective-permute-start(s32[16,64]{1,0:T(8,128)S(1)} %fusion.refs_0_), channel_id=1, source_target_pairs={{0,2},{1,3},{2,0},{3,1},{4,6},{5,7},{6,4},{7,5},{8,10},{9,11},{10,... | collective-permute-start | bytes 12296 | tf_op jit(solution)/shard_map/ppermute | solution.py:519
  9.4 4.9 %collective-permute-start.3 = (s32[16,64]{1,0:T(8,128)S(1)}, s32[16,64]{1,0:T(8,128)S(1)}, u32[]{:S(2)}, u32[]{:S(2)}) collective-permute-start(s32[16,64]{1,0:T(8,128)S(1)} %fusion.refs_0_), channel_id=1, source_target_pairs={{0,3},{1,2},{2,1},{3,0},{4,7},{5,6},{6,5},{7,4},{8,11},{9,10},{10,... | collective-permute-start | bytes 12296 | tf_op jit(solution)/shard_map/ppermute | solution.py:519
  12.2 14.3 %copy-start.5 = (f32[16]{0:T(128)S(1)}, f32[16]{0:T(128)}, u32[]{:S(2)}) copy-start(f32[16]{0:T(128)} %param.10) | copy-start | bytes 196
  12.2 14.7 %copy-start.3 = (s32[32]{0:T(128)S(1)}, s32[32]{0:T(128)}, u32[]{:S(2)}) copy-start(s32[32]{0:T(128)} %param.12) | copy-start | bytes 388
  12.2 14.8 %copy-start.4 = (s32[32]{0:T(128)S(1)}, s32[32]{0:T(128)}, u32[]{:S(2)}) copy-start(s32[32]{0:T(128)} %param.13) | copy-start | bytes 388
  17.7 21.0 %all-to-all-start = ((f32[64,1,2304]{2,1,0:T(1,128)}), f32[64,1,2304]{2,1,0:T(1,128)S(1)}, u32[]{:S(2)}, u32[]{:S(2)}) async-start(f32[64,1,2304]{2,1,0:T(1,128)} %gram_b.1), calls=%async_computation | async-start | bytes 1179648 | tf_op jit(solution)/shard_map/all_to_all | solution.py:522
  57.7 1.3 %collective-permute-start.5 = (f32[4,2,16,128]{3,2,1,0:T(8,128)S(1)}, f32[4,2,16,128]{3,2,1,0:T(8,128)S(1)}, u32[]{:S(2)}, u32[]{:S(2)}) collective-permute-start(f32[4,2,16,128]{3,2,1,0:T(8,128)S(1)} %power.1), channel_id=1, source_target_pairs={{0,4},{4,0},{8,12},{12,8},{16,20},{20,16},{24,28},{28,24},{32,36},... | collective-permute-start | bytes 196616 | tf_op jit(solution)/shard_map/ppermute | solution.py:497
  59.1 5.6 %collective-permute-start.8 = (f32[4,16,128]{2,1,0:T(8,128)S(1)}, f32[4,16,128]{2,1,0:T(8,128)S(1)}, u32[]{:S(2)}, u32[]{:S(2)}) collective-permute-start(f32[4,16,128]{2,1,0:T(8,128)S(1)} %pad_maximum_fusion.3), channel_id=1, source_target_pairs={{0,3},{1,2},{2,1},{3,0},{4,7},{5,6},{6,5},{7,4},{8,11},{9,10},{10,... | collective-permute-start | bytes 98312 | tf_op jit(solution)/shard_map/ppermute | solution.py:532
  60.1 5.4 %collective-permute-start.7 = (f32[4,16,128]{2,1,0:T(8,128)S(1)}, f32[4,16,128]{2,1,0:T(8,128)S(1)}, u32[]{:S(2)}, u32[]{:S(2)}) collective-permute-start(f32[4,16,128]{2,1,0:T(8,128)S(1)} %pad_maximum_fusion.2), channel_id=1, source_target_pairs={{0,2},{1,3},{2,0},{3,1},{4,6},{5,7},{6,4},{7,5},{8,10},{9,11},{10,... | collective-permute-start | bytes 98312 | tf_op jit(solution)/shard_map/ppermute | solution.py:532
  61.8 3.9 %collective-permute-start.6 = (f32[4,16,128]{2,1,0:T(8,128)S(1)}, f32[4,16,128]{2,1,0:T(8,128)S(1)}, u32[]{:S(2)}, u32[]{:S(2)}) collective-permute-start(f32[4,16,128]{2,1,0:T(8,128)S(1)} %pad_maximum_fusion.1), channel_id=1, source_target_pairs={{0,1},{1,0},{2,3},{3,2},{4,5},{5,4},{6,7},{7,6},{8,9},{9,8},{10,11... | collective-permute-start | bytes 98312 | tf_op jit(solution)/shard_map/ppermute | solution.py:532
  65.7 7.2 %collective-permute-start.9 = (f32[2,16,128]{2,1,0:T(8,128)S(1)}, f32[2,16,128]{2,1,0:T(8,128)S(1)}, u32[]{:S(2)}, u32[]{:S(2)}) collective-permute-start(f32[2,16,128]{2,1,0:T(8,128)S(1)} %select_select_fusion), channel_id=1, source_target_pairs={{4,8},{8,4},{12,16},{16,12},{20,24},{24,20},{28,32},{32,28},{36,40... | collective-permute-start | bytes 49160 | tf_op jit(solution)/shard_map/ppermute | solution.py:538

commit v15 on v13

--- a/solution.py
+++ b/solution.py
@@ -110,7 +110,7 @@
         done, whole, kept, out, sems = refs[1:]
     else:
         out, kept = refs[2:]
-    core, dop = core_and_dop()
+    _, dop = core_and_dop()
     block = dop * (GATES // BLOCK) + (iota((64, 2 * GATES), 1) % GATES) // BLOCK
     block = block + 32 * (iota((64, 2 * GATES), 1) // GATES)
     pick = (iota((64, 2 * GATES), 0) == block).astype(f32)
@@ -142,7 +142,6 @@
     row = iota((ST, GATES), 0)
     lane = iota((ST, GATES), 1)
     low = row >= lane % HALF
-    high = row <= lane % HALF
     first = lane < HALF
     lane16 = iota((CH, GATES), 1)
     mine8 = iota((8, GATES), 1) // 16 == iota((8, GATES), 0)
@@ -305,7 +304,7 @@
 
 
 def power_kernel(place, near, far, w, out):
-    core, dop = core_and_dop()
+    _, dop = core_and_dop()
     zero = jnp.zeros((32, 2 * GATES), bf16)
     row = iota((8, GATES), 0)
     lane = iota((8, GATES), 1)
@@ -530,7 +529,9 @@
     mine = power(place, near, far, w)
     came = swap(mine)
     pieces = [jnp.stack([mine[k, 0], came[k, 1], mine[k, 1], came[k, 0]]) for k in range(ZN)]
-    pieces = [pieces[0]] + [lax.ppermute(pieces[k], "dop", flipped(k)) for k in (1, 2, 3)]
+    p2 = lax.ppermute(pieces[2], "dop", flipped(2))
+    p1, p3 = [lax.ppermute(pieces[k], "dop", flipped(k)) for k in (1, 3)]
+    pieces = [pieces[0], p1, p2, p3]
     ranges = lax.axis_size("range")
     p0, p1, p2, p3 = [p[:2] for p in pieces]
     tail = jnp.where(dop == 0, p3, jnp.where(dop == 1, p2, jnp.where(dop == 2, p1, p0)))

time: 73.8 us -> 73.8 us (level)
  no operation moved by 1% of the time
where the time goes in v15:
time: 73.8 us; the launch traced here: 73.5 us
  starting transfers between devices  23 us (31%)
  waiting for transfers between devices  18.6 us (25%)
  Pallas kernels  16 us (22%)
  blocking collectives  14.1 us (19%)
  local copies, waits for them, and re-layouts  1.47 us (2%)
    all_to_all x1, blocking collectives, shards(): w = lax.all_to_all(w, BOTH, 0, 0, tiled=True, axis_index_groups=SAME_CORE)  14.1 us
    all_to_all x1, waiting for transfers between devices, shards(): lax.all_to_all(part, BOTH, 0, 0, tiled=True, axis_index_groups=SAME_CORE)  10.5 us
    all_to_all x1, starting transfers between devices, shards(): lax.all_to_all(part, BOTH, 0, 0, tiled=True, axis_index_groups=SAME_CORE)  9.98 us
    pallas_call x2, Pallas kernels, gram(): pl.pallas_call(functools.partial(gram_kernel, second), out_shape=pltpu.HB...  6.16 us
    ppermute x1, starting transfers between devices, shards(): m2 = lax.ppermute(rows(mine, m1), 'dop', flipped(2))  3.88 us
    ppermute x1, waiting for transfers between devices, shards(): outer = lax.ppermute(jnp.where(core == 0, head, tail), 'range', pairs)  3.34 us
    pallas_call x1, Pallas kernels, power(): pl.pallas_call(power_kernel, out_shape=jax.ShapeDtypeStruct((ZN, 2, 16, G...  2.5 us
    ppermute x2, starting transfers between devices, shards(): p1, p3 = [lax.ppermute(pieces[k], 'dop', flipped(k)) for k in (1, 3)]  2.5 us
  transfers between devices with their start and end apart: 10, of which 7 were waited for; matrix products, arithmetic and copies ran while one was open for 2% of the time, Pallas kernels for 9%

profile of v15, /device:TPU:8, one launch (start us, length us, event | category | flops | bytes accessed | tf_op | source)
XLA Modules:
  0.0 73.5 jit_solution(18193545023950985948)
XLA Ops:
  0.0 0.1 collective-permute-start
  0.1 2.3 %pack.1 = (f32[2,80,16,128]{3,2,1,0:T(8,128)S(1)}, f32[2,80,16,128]{3,2,1,0:T(8,128)}) custom-call(f32[2,128,16,128]{3,2,1,0:T(8,128)} %echo.1), custom_call_target="tpu_custom_call" | custom-call | tf_op jit(solution)/shard_map/pack/pallas_call | solution.py:88
  2.4 0.0 collective-permute-done
  2.4 0.6 collective-permute-start.1
  3.0 0.1 reshape.43
  3.2 0.1 fusion.refs_0_
  3.2 1.9 %collective-permute-start.2 = (s32[16,64]{1,0:T(8,128)S(1)}, s32[16,64]{1,0:T(8,128)S(1)}, u32[]{:S(2)}, u32[]{:S(2)}) collective-permute-start(s32[16,64]{1,0:T(8,128)S(1)} %fusion.refs_0_), channel_id=1, source_target_pairs={{0,1},{1,0},{2,3},{3,2},{4,5},{5,4},{6,7},{7,6},{8,9},{9,8},{10,11... | collective-permute-start | bytes 12296 | tf_op jit(solution)/shard_map/ppermute | solution.py:518
  5.2 0.1 copy.10
  5.3 0.1 squeeze.6
  5.4 0.1 iota.18
  5.5 0.1 iota.19
  5.6 0.1 iota.15
  5.7 0.1 iota.16
  5.8 1.1 %collective-permute-done.2.refs_1_ = s32[16,64]{1,0:T(8,128)S(1)} collective-permute-done((s32[16,64]{1,0:T(8,128)S(1)}, s32[16,64]{1,0:T(8,128)S(1)}, u32[]{:S(2)}, u32[]{:S(2)}) %collective-permute-start.2) | collective-permute-done | bytes 4128 | tf_op jit(solution)/shard_map/ppermute | solution.py:518
  6.9 3.9 %collective-permute-start.3 = (s32[32,64]{1,0:T(8,128)S(1)}, s32[32,64]{1,0:T(8,128)S(1)}, u32[]{:S(2)}, u32[]{:S(2)}) collective-permute-start(s32[32,64]{1,0:T(8,128)S(1)} %pad_add_fusion), channel_id=1, source_target_pairs={{0,2},{1,3},{2,0},{3,1},{4,6},{5,7},{6,4},{7,5},{8,10},{9,11},{10,... | collective-permute-start | bytes 24584 | tf_op jit(solution)/shard_map/ppermute | solution.py:519
  10.8 0.0 collective-permute-done.1.far
  10.8 2.7 %gram_a.1.refs_1_ = f32[32,1,2304]{2,1,0:T(1,128)S(1)} custom-call(s32[192]{0:T(256)S(1)} %and_add_fusion.place, f32[2,80,16,128]{3,2,1,0:T(8,128)S(1)} %get-tuple-element.15.near, f32[2,80,16,128]{3,2,1,0:T(8,128)S(1)} %collective-permute-done.1.far, s32[16,64]{1,0:T(8,128)S(1)} %fusion.refs_0_, s32[16,64]{1,0:T(8,128)S(1)} %collective-permute-done.2.refs_1_), custom_call_target="tpu_custom_call" | custom-call | tf_op jit(solution)/shard_map/gram_a/pallas_call | solution.py:204
  13.5 0.0 copy-start.5
  13.5 0.0 copy-start.3
  13.6 0.0 copy-start.4
  13.6 0.0 collective-permute-done.3.refs_0_
  13.6 3.4 %gram_b.1 = f32[64,1,2304]{2,1,0:T(1,128)} custom-call(s32[192]{0:T(256)S(1)} %and_add_fusion.place, f32[2,80,16,128]{3,2,1,0:T(8,128)S(1)} %get-tuple-element.15.near, f32[2,80,16,128]{3,2,1,0:T(8,128)S(1)} %collective-permute-done.1.far, s32[32,64]{1,0:T(8,128)S(1)} %collective-permute-done.3.refs_0_, f32[32,1,2304]{2,1,0:T(1,128)S(1)} %gram_a.1.refs_1_), custom_call_target="tpu_custom_call" | custom-call | tf_op jit(solution)/shard_map/gram_b/pallas_call | solution.py:204
  17.0 10.0 %all-to-all-start = ((f32[64,1,2304]{2,1,0:T(1,128)}), f32[64,1,2304]{2,1,0:T(1,128)S(1)}, u32[]{:S(2)}, u32[]{:S(2)}) async-start(f32[64,1,2304]{2,1,0:T(1,128)} %gram_b.1), calls=%async_computation | async-start | bytes 1179648 | tf_op jit(solution)/shard_map/all_to_all | solution.py:522
  27.0 0.0 copy-done
  27.0 0.2 dynamic-slice_reduce_fusion
  27.3 0.1 broadcast_multiply_fusion
  27.4 0.1 mul.72
  27.4 0.1 mul.75
  27.5 0.1 broadcast_in_dim.8.sr
  27.6 0.1 broadcast_in_dim.9.si
  27.7 0.1 broadcast_in_dim.10.guard
  27.7 0.1 broadcast_in_dim.11.train
  27.8 10.5 %all-to-all-done.parts = f32[64,1,2304]{2,1,0:T(1,128)S(1)} async-done(((f32[64,1,2304]{2,1,0:T(1,128)}), f32[64,1,2304]{2,1,0:T(1,128)S(1)}, u32[]{:S(2)}, u32[]{:S(2)}) %all-to-all-start) | async-done | bytes 589856 | tf_op jit(solution)/shard_map/all_to_all | solution.py:522
  38.3 2.4 %solve.1 = f32[64,1,128]{2,1,0:T(1,128)S(1)} custom-call(f32[64,1,2304]{2,1,0:T(1,128)S(1)} %all-to-all-done.parts, f32[48,128]{1,0:T(8,128)S(1)} %broadcast_in_dim.8.sr, f32[48,128]{1,0:T(8,128)S(1)} %broadcast_in_dim.9.si), custom_call_target="tpu_custom_call" | custom-call | tf_op jit(solution)/shard_map/solve/pallas_call | solution.py:296
  40.7 14.1 %all_to_all.10.w = f32[64,1,128]{2,1,0:T(1,128)S(1)} all-to-all(f32[64,1,128]{2,1,0:T(1,128)S(1)} %solve.1), channel_id=1, replica_groups={{0,8,16,24,32,40,48,56,64,72,80,88,96,104,112,120,1,9,17,25,33,41,49,57..., dimensions={0} | all-to-all | bytes 65536 | tf_op jit(solution)/shard_map/all_to_all | solution.py:528
  54.8 2.5 %power.1 = f32[4,2,16,128]{3,2,1,0:T(8,128)S(1)} custom-call(s32[192]{0:T(256)S(1)} %and_add_fusion.place, f32[2,80,16,128]{3,2,1,0:T(8,128)S(1)} %get-tuple-element.15.near, f32[2,80,16,128]{3,2,1,0:T(8,128)S(1)} %collective-permute-done.1.far, f32[64,1,128]{2,1,0:T(1,128)S(1)} %all_to_all.10.w), custom_call_target="tpu_custom_call" | custom-call | tf_op jit(solution)/shard_map/power/pallas_call | solution.py:355
  57.3 0.1 collective-permute-start.4
  57.4 1.2 %collective-permute-done.4 = f32[4,2,16,128]{3,2,1,0:T(8,128)S(1)} collective-permute-done((f32[4,2,16,128]{3,2,1,0:T(8,128)S(1)}, f32[4,2,16,128]{3,2,1,0:T(8,128)S(1)}, u32[]{:S(2)}, u32[]{:S(2)}) %collective-permute-start.4) | collective-permute-done | bytes 65568 | tf_op jit(solution)/shard_map/ppermute | solution.py:496
  58.7 1.0 %collective-permute-start.7 = (f32[4,16,128]{2,1,0:T(8,128)S(1)}, f32[4,16,128]{2,1,0:T(8,128)S(1)}, u32[]{:S(2)}, u32[]{:S(2)}) collective-permute-start(f32[4,16,128]{2,1,0:T(8,128)S(1)} %pad_maximum_fusion.3), channel_id=1, source_target_pairs={{0,3},{1,2},{2,1},{3,0},{4,7},{5,6},{6,5},{7,4},{8,11},{9,10},{10,... | collective-permute-start | bytes 98312 | tf_op jit(solution)/shard_map/ppermute | solution.py:533
  59.7 1.7 %collective-permute-start.6 = (f32[4,16,128]{2,1,0:T(8,128)S(1)}, f32[4,16,128]{2,1,0:T(8,128)S(1)}, u32[]{:S(2)}, u32[]{:S(2)}) collective-permute-start(f32[4,16,128]{2,1,0:T(8,128)S(1)} %pad_maximum_fusion.2), channel_id=1, source_target_pairs={{0,2},{1,3},{2,0},{3,1},{4,6},{5,7},{6,4},{7,5},{8,10},{9,11},{10,... | collective-permute-start | bytes 98312 | tf_op jit(solution)/shard_map/ppermute | solution.py:532
  61.4 1.5 %collective-permute-start.5 = (f32[4,16,128]{2,1,0:T(8,128)S(1)}, f32[4,16,128]{2,1,0:T(8,128)S(1)}, u32[]{:S(2)}, u32[]{:S(2)}) collective-permute-start(f32[4,16,128]{2,1,0:T(8,128)S(1)} %pad_maximum_fusion.1), channel_id=1, source_target_pairs={{0,1},{1,0},{2,3},{3,2},{4,5},{5,4},{6,7},{7,6},{8,9},{9,8},{10,11... | collective-permute-start | bytes 98312 | tf_op jit(solution)/shard_map/ppermute | solution.py:533
  62.8 1.4 %collective-permute-done.7.p3 = f32[4,16,128]{2,1,0:T(8,128)S(1)} collective-permute-done((f32[4,16,128]{2,1,0:T(8,128)S(1)}, f32[4,16,128]{2,1,0:T(8,128)S(1)}, u32[]{:S(2)}, u32[]{:S(2)}) %collective-permute-start.7) | collective-permute-done | bytes 32800 | tf_op jit(solution)/shard_map/ppermute | solution.py:533
  64.2 0.9 %collective-permute-done.6.p2 = f32[4,16,128]{2,1,0:T(8,128)S(1)} collective-permute-done((f32[4,16,128]{2,1,0:T(8,128)S(1)}, f32[4,16,128]{2,1,0:T(8,128)S(1)}, u32[]{:S(2)}, u32[]{:S(2)}) %collective-permute-start.6) | collective-permute-done | bytes 32800 | tf_op jit(solution)/shard_map/ppermute | solution.py:532
  65.1 0.2 collective-permute-done.5.p1
  65.3 2.3 %collective-permute-start.8 = (f32[2,16,128]{2,1,0:T(8,128)S(1)}, f32[2,16,128]{2,1,0:T(8,128)S(1)}, u32[]{:S(2)}, u32[]{:S(2)}) collective-permute-start(f32[2,16,128]{2,1,0:T(8,128)S(1)} %select_select_fusion), channel_id=1, source_target_pairs={{4,8},{8,4},{12,16},{16,12},{20,24},{24,20},{28,32},{32,28},{36,40... | collective-permute-start | bytes 49160 | tf_op jit(solution)/shard_map/ppermute | solution.py:540
  67.6 1.5 %noise.1 = (f32[32,512]{1,0:T(8,128)}, f32[3,32,128]{2,1,0:T(8,128)S(1)}) custom-call(f32[4,16,128]{2,1,0:T(8,128)S(1)} %pad_maximum_fusion.p0, f32[4,16,128]{2,1,0:T(8,128)S(1)} %collective-permute-done.5.p1, f32[4,16,128]{2,1,0:T(8,128)S(1)} %collective-permute-done.6.p2, f32[4,16,128]{2,1,0:T(8,128)S(1)} %collective-permute-done.7.p3, ...), custom_call_target="tpu_custom_call" | custom-call | tf_op jit(solution)/shard_map/noise/pallas_call | solution.py:432
  69.1 3.3 %collective-permute-done.8.outer = f32[2,16,128]{2,1,0:T(8,128)S(1)} collective-permute-done((f32[2,16,128]{2,1,0:T(8,128)S(1)}, f32[2,16,128]{2,1,0:T(8,128)S(1)}, u32[]{:S(2)}, u32[]{:S(2)}) %collective-permute-start.8) | collective-permute-done | bytes 16416 | tf_op jit(solution)/shard_map/ppermute | solution.py:540
  72.5 1.1 %cfar.1 = f32[32,512]{1,0:T(8,128)} custom-call(f32[32,512]{1,0:T(8,128)} %get-tuple-element.23.whole, f32[3,32,128]{2,1,0:T(8,128)S(1)} %get-tuple-element.24.edge, f32[2,16,128]{2,1,0:T(8,128)S(1)} %collective-permute-done.8.outer, s32[32,128]{1,0:T(8,128)S(1)} %broadcast_in_dim.10.guard, ...), custom_call_target="tpu_custom_call", output_to_operand_aliasing={{}: (0, {})} | custom-call | tf_op jit(solution)/shard_map/cfar/pallas_call | solution.py:467
  (21 shorter events, 0.1 us)
Async XLA Ops:
  0.0 27.0 %copy-start = (f32[128,3]{0,1:T(4,128)S(1)}, f32[128,3]{0,1:T(4,128)}, u32[]{:S(2)}) copy-start(f32[128,3]{0,1:T(4,128)} %param.9) | copy-start | bytes 4612
  0.0 3.1 %copy-start.1 = (s32[32,32]{1,0:T(8,128)S(1)}, s32[32,32]{1,0:T(8,128)}, u32[]{:S(2)}) copy-start(s32[32,32]{1,0:T(8,128)} %param.11) | copy-start | bytes 12292
  0.0 3.0 %copy-start.2 = (s32[128,3]{0,1:T(4,128)S(1)}, s32[128,3]{0,1:T(4,128)}, u32[]{:S(2)}) copy-start(s32[128,3]{0,1:T(4,128)} %param.8) | copy-start | bytes 4612
  0.0 2.4 %collective-permute-start = (s32[32,32]{1,0:T(8,128)}, s32[32,32]{1,0:T(8,128)S(1)}, u32[]{:S(2)}, u32[]{:S(2)}) collective-permute-start(s32[32,32]{1,0:T(8,128)} %param.11), channel_id=1, source_target_pairs={{0,4},{4,0},{8,12},{12,8},{16,20},{20,16},{24,28},{28,24},{32,36},... | collective-permute-start | bytes 12296 | tf_op jit(solution)/shard_map/ppermute | solution.py:496
  2.4 8.4 %collective-permute-start.1 = (f32[2,80,16,128]{3,2,1,0:T(8,128)}, f32[2,80,16,128]{3,2,1,0:T(8,128)S(1)}, u32[]{:S(2)}, u32[]{:S(2)}) collective-permute-start(f32[2,80,16,128]{3,2,1,0:T(8,128)} %get-tuple-element.17), channel_id=1, source_target_pairs={{0,4},{4,0},{8,12},{12,8},{16,20},{20,16},{24,28},{28,24},{32,36},... | collective-permute-start | bytes 3932168 | tf_op jit(solution)/shard_map/ppermute | solution.py:496
  3.2 3.7 %collective-permute-start.2 = (s32[16,64]{1,0:T(8,128)S(1)}, s32[16,64]{1,0:T(8,128)S(1)}, u32[]{:S(2)}, u32[]{:S(2)}) collective-permute-start(s32[16,64]{1,0:T(8,128)S(1)} %fusion.refs_0_), channel_id=1, source_target_pairs={{0,1},{1,0},{2,3},{3,2},{4,5},{5,4},{6,7},{7,6},{8,9},{9,8},{10,11... | collective-permute-start | bytes 12296 | tf_op jit(solution)/shard_map/ppermute | solution.py:518
  6.9 6.7 %collective-permute-start.3 = (s32[32,64]{1,0:T(8,128)S(1)}, s32[32,64]{1,0:T(8,128)S(1)}, u32[]{:S(2)}, u32[]{:S(2)}) collective-permute-start(s32[32,64]{1,0:T(8,128)S(1)} %pad_add_fusion), channel_id=1, source_target_pairs={{0,2},{1,3},{2,0},{3,1},{4,6},{5,7},{6,4},{7,5},{8,10},{9,11},{10,... | collective-permute-start | bytes 24584 | tf_op jit(solution)/shard_map/ppermute | solution.py:519
  13.5 13.7 %copy-start.5 = (f32[16]{0:T(128)S(1)}, f32[16]{0:T(128)}, u32[]{:S(2)}) copy-start(f32[16]{0:T(128)} %param.10) | copy-start | bytes 196
  13.5 14.1 %copy-start.3 = (s32[32]{0:T(128)S(1)}, s32[32]{0:T(128)}, u32[]{:S(2)}) copy-start(s32[32]{0:T(128)} %param.12) | copy-start | bytes 388
  13.6 14.2 %copy-start.4 = (s32[32]{0:T(128)S(1)}, s32[32]{0:T(128)}, u32[]{:S(2)}) copy-start(s32[32]{0:T(128)} %param.13) | copy-start | bytes 388
  17.0 21.3 %all-to-all-start = ((f32[64,1,2304]{2,1,0:T(1,128)}), f32[64,1,2304]{2,1,0:T(1,128)S(1)}, u32[]{:S(2)}, u32[]{:S(2)}) async-start(f32[64,1,2304]{2,1,0:T(1,128)} %gram_b.1), calls=%async_computation | async-start | bytes 1179648 | tf_op jit(solution)/shard_map/all_to_all | solution.py:522
  57.3 1.3 %collective-permute-start.4 = (f32[4,2,16,128]{3,2,1,0:T(8,128)S(1)}, f32[4,2,16,128]{3,2,1,0:T(8,128)S(1)}, u32[]{:S(2)}, u32[]{:S(2)}) collective-permute-start(f32[4,2,16,128]{3,2,1,0:T(8,128)S(1)} %power.1), channel_id=1, source_target_pairs={{0,4},{4,0},{8,12},{12,8},{16,20},{20,16},{24,28},{28,24},{32,36},... | collective-permute-start | bytes 196616 | tf_op jit(solution)/shard_map/ppermute | solution.py:496
  58.7 5.6 %collective-permute-start.7 = (f32[4,16,128]{2,1,0:T(8,128)S(1)}, f32[4,16,128]{2,1,0:T(8,128)S(1)}, u32[]{:S(2)}, u32[]{:S(2)}) collective-permute-start(f32[4,16,128]{2,1,0:T(8,128)S(1)} %pad_maximum_fusion.3), channel_id=1, source_target_pairs={{0,3},{1,2},{2,1},{3,0},{4,7},{5,6},{6,5},{7,4},{8,11},{9,10},{10,... | collective-permute-start | bytes 98312 | tf_op jit(solution)/shard_map/ppermute | solution.py:533
  59.7 5.4 %collective-permute-start.6 = (f32[4,16,128]{2,1,0:T(8,128)S(1)}, f32[4,16,128]{2,1,0:T(8,128)S(1)}, u32[]{:S(2)}, u32[]{:S(2)}) collective-permute-start(f32[4,16,128]{2,1,0:T(8,128)S(1)} %pad_maximum_fusion.2), channel_id=1, source_target_pairs={{0,2},{1,3},{2,0},{3,1},{4,6},{5,7},{6,4},{7,5},{8,10},{9,11},{10,... | collective-permute-start | bytes 98312 | tf_op jit(solution)/shard_map/ppermute | solution.py:532
  61.4 3.9 %collective-permute-start.5 = (f32[4,16,128]{2,1,0:T(8,128)S(1)}, f32[4,16,128]{2,1,0:T(8,128)S(1)}, u32[]{:S(2)}, u32[]{:S(2)}) collective-permute-start(f32[4,16,128]{2,1,0:T(8,128)S(1)} %pad_maximum_fusion.1), channel_id=1, source_target_pairs={{0,1},{1,0},{2,3},{3,2},{4,5},{5,4},{6,7},{7,6},{8,9},{9,8},{10,11... | collective-permute-start | bytes 98312 | tf_op jit(solution)/shard_map/ppermute | solution.py:533
  65.3 7.2 %collective-permute-start.8 = (f32[2,16,128]{2,1,0:T(8,128)S(1)}, f32[2,16,128]{2,1,0:T(8,128)S(1)}, u32[]{:S(2)}, u32[]{:S(2)}) collective-permute-start(f32[2,16,128]{2,1,0:T(8,128)S(1)} %select_select_fusion), channel_id=1, source_target_pairs={{4,8},{8,4},{12,16},{16,12},{20,24},{24,20},{28,32},{32,28},{36,40... | collective-permute-start | bytes 49160 | tf_op jit(solution)/shard_map/ppermute | solution.py:540
